TPU v7x, 32 devices: a whole 2x2x4 slice. The times are simulated.
32 devices in a mesh: dp: 4 (over x, core), fsdp: 8 (over z, y).
Axes of the slice: x: 2, y: 2, z: 4, core: 2. Of those that a mesh axis runs over, the one named last changes fastest.
Arguments:
- tokens: bfloat16 [25088, 1024], P(('dp', 'fsdp')), may hold values from -6 to 6
- scale_codes: int32 [128], P(('dp', 'fsdp')), may hold values from 0 to 15
- w_qkv: float32 [1024, 3072], P('fsdp'), may hold values from -0.1875 to 0.1875
- b_q: float32 [1024], P('fsdp'), may hold values from -3 to 3
- b_v: float32 [1024], P('fsdp'), may hold values from -3 to 3
- w_out: float32 [1024, 1024], P('fsdp'), may hold values from -1.5 to 1.5
- b_out: float32 [1024], P('fsdp'), may hold values from -3 to 3
- gain_one: float32 [1024], P('fsdp'), may hold values from 0.5 to 1.5
- shift_one: float32 [1024], P('fsdp'), may hold values from -2 to 2
- w_fc1: float32 [1024, 4096], P('fsdp'), may hold values from -0.1875 to 0.1875
- b_fc1: float32 [4096], P('fsdp'), may hold values from -3 to 3
- w_fc2: float32 [4096, 1024], P('fsdp'), may hold values from -0.09375 to 0.09375
- b_fc2: float32 [1024], P('fsdp'), may hold values from -3 to 3
- gain_two: float32 [1024], P('fsdp'), may hold values from 0.5 to 1.5
- shift_two: float32 [1024], P('fsdp'), may hold values from -2 to 2
- cotangent: bfloat16 [25088, 1024], P(('dp', 'fsdp')), may hold values from -6 to 6
Outputs:
- block_out: bfloat16 [25088, 1024], P(('dp', 'fsdp'))
- grad_tokens: float32 [25088, 1024], P(('dp', 'fsdp'))
- grad_w_qkv: float32 [1024, 3072], P('fsdp')
- grad_b_q: float32 [1024], P('fsdp')
- grad_b_v: float32 [1024], P('fsdp')
- grad_w_out: float32 [1024, 1024], P('fsdp')
- grad_b_out: float32 [1024], P('fsdp')
- grad_gain_one: float32 [1024], P('fsdp')
- grad_shift_one: float32 [1024], P('fsdp')
- grad_w_fc1: float32 [1024, 4096], P('fsdp')
- grad_b_fc1: float32 [4096], P('fsdp')
- grad_w_fc2: float32 [4096, 1024], P('fsdp')
- grad_b_fc2: float32 [1024], P('fsdp')
- grad_gain_two: float32 [1024], P('fsdp')
- grad_shift_two: float32 [1024], P('fsdp')
All inputs are finite; a program needn't handle non-finite values.
Results may differ from a plain program's by a relative error of at most 0.015.
Values may be sent and summed in bfloat16 or wider, within the bound.
No kernel may reach another device: no remote copies, remote signals or barrier semaphores. Data moves between devices by JAX's collectives and lax.ppermute only.
A program may use at most 256 MiB of HBM per device.

v0:
```python
import math

import jax
import jax.numpy as jnp
from jax import lax
from jax.experimental import pallas as pl
from jax.experimental.pallas import tpu as pltpu
from jax.sharding import PartitionSpec as P

HEADS = 16
GRID = 14
NSCALE = 16
norm_eps = 1e-06
half = jnp.bfloat16
full = jnp.float32


def xor_swap(value, axis, size, mask):
    return lax.ppermute(value, axis, [(i, i ^ mask) for i in range(size)])


def core_swap(value):
    return xor_swap(value, "dp", 4, 1)


def x_swap(value):
    return xor_swap(value, "dp", 4, 2)


def masks(bits):
    found = [0]
    for bit in bits:
        found = found + [m | (1 << bit) for m in found]
    return found


class Order:
    def __init__(self, value):
        self.value = value

    def at(self, value):
        value, self.value = lax.optimization_barrier((value, self.value))
        return value

    def land(self, value, *sent):
        value, flights = self.at((value, [s.flight for s in sent]))
        for s, flight in zip(sent, flights, strict=True):
            s.accept(flight)
        return value


class Sent:
    def __init__(self, flight):
        self.flight = flight

    def accept(self, value):
        self.value = value


class Gather:
    def __init__(self, seq, piece, n, bits):
        self.seq, self.held, self.n, self.bits = seq, piece[None], n, list(bits)

    def launch(self):
        self.held = self.seq.at(self.held)
        self.flight = xor_swap(self.held, "fsdp", self.n, 1 << self.bits.pop(0))

    def accept(self, value):
        self.got = value

    def join(self):
        self.held = jnp.concatenate([self.held, self.got])
        return self.held


def rounded_sum(terms, kind=half):
    return sum(t.astype(full) for t in terms).astype(kind)


class Reduce:
    def __init__(self, seq, terms, n, kind=half):
        self.kind = kind
        self.seq, self.n, self.axes = seq, n, list(range(n.bit_length() - 1))
        self.terms = [t.reshape((2,) * len(self.axes) + t.shape[1:]) for t in terms]

    def launch(self, bit=None, more=()):
        bit = self.axes[0] if bit is None else bit
        axis = self.axes.index(bit)
        self.axes.pop(axis)
        low, high = [
            [lax.index_in_dim(t, side, axis, keepdims=False) for t in self.terms] for side in (0, 1)
        ]
        self.terms = low
        self.flight = xor_swap(self.seq.at(rounded_sum([*high, *more], self.kind)), "fsdp", self.n, 1 << bit)

    def accept(self, value):
        self.terms = [*self.terms, value]

    def rest(self):
        while self.axes:
            self.launch()
            self.seq.land((), self)
        return self

    def piece(self):
        return rounded_sum(self.terms, self.kind)


class Spread:
    def __init__(self, seq, piece):
        self.seq, self.pieces = seq, [seq.at(piece)]
        self.flight = [core_swap(self.pieces[0]), x_swap(self.pieces[0])]

    def cross(self):
        self.flight = [core_swap(self.seq.at(self.pieces[2]))]

    def accept(self, value):
        self.pieces += value


ANYWHERE = pl.BlockSpec(memory_space=pl.ANY)
ON_CHIP = pl.BlockSpec(memory_space=pltpu.VMEM)
SCALARS = pl.BlockSpec(memory_space=pltpu.SMEM)


def dot(left, right, dim_left, dim_right):
    return lax.dot_general(
        left, right, (((dim_left,), (dim_right,)), ((), ())), preferred_element_type=full
    )


def call(kernel, name, operands, in_specs, outs, out_specs, scratch):
    return pl.pallas_call(
        kernel,
        out_shape=[jax.ShapeDtypeStruct(shape, kind) for shape, kind in outs],
        in_specs=in_specs,
        out_specs=out_specs,
        scratch_shapes=scratch,
        compiler_params=pltpu.CompilerParams(vmem_limit_bytes=58 * 2**20),
        name=name,
    )(*operands)


def loop(count, body, unroll=1):
    def step(i, carry):
        body(i)
        return carry

    lax.fori_loop(0, count, step, 0, unroll=unroll)


def tile(i, size):
    return pl.ds(pl.multiple_of(i * size, size), size)


def bring(src, dst, sem):
    pltpu.make_async_copy(src, dst, sem).start()


def arrived(dst, sem):
    pltpu.make_async_copy(dst, dst, sem).wait()


def fetch(parts, order_ref, place, sem):
    base = 0
    for part in parts:

        def start(r, part=part, base=base):
            shard = r if order_ref is None else order_ref[base + r]
            pltpu.make_async_copy(part.at[r], place(shard), sem).start()

        loop(part.shape[0], start)
        base += part.shape[0]


def head_rows(s, q, n, rows, quarter):
    per = n // 4
    return pl.multiple_of(((s // per) ^ q) * quarter + (s % per) * rows, rows)


def pair_scores(q2, k2):
    first = lax.broadcasted_iota(jnp.int32, q2.shape, 1) < q2.shape[1] // 2
    both = apart(q2, first)
    return both, dot(k2, both, 1, 1), first


def apart(value, first):
    zero = jnp.zeros_like(value)
    return jnp.concatenate([jnp.where(first, value, zero), jnp.where(first, zero, value)])


def attention_forward(order, normed, bias, weights, n_img, patches, factor):
    groups, n_parts = len(weights), len(weights[0])
    wide = weights[0][0].shape[2]
    count, width = normed.shape
    rows = width // sum(part.shape[0] for part in weights[0])
    padded = count // n_img
    quarter = wide // 3

    def kernel(order_ref, normed_ref, bias_ref, *refs):
        w_refs, refs = refs[: groups * n_parts], refs[groups * n_parts :]
        qkv_refs, mixed_refs, refs = refs[:groups], refs[groups : 2 * groups], refs[2 * groups :]
        lse_refs, (w_held, sems) = refs[:groups], refs[groups:]
        for g in range(groups):
            fetch(
                [w.at[:, pl.ds(0, rows)] for w in w_refs[g * n_parts : (g + 1) * n_parts]],
                order_ref,
                lambda s, g=g: w_held.at[g, pl.ds(pl.multiple_of(s * rows, rows), rows)],
                sems.at[g],
            )
        for g in range(groups):
            pltpu.make_async_copy(w_held.at[g], w_held.at[g], sems.at[g]).wait()

            def project(t, g=g):
                at = tile(t, quarter)
                product = dot(normed_ref[...], w_held[g, :, at], 1, 0)
                qkv_refs[g][:, at] = (product + bias_ref[g, :, at]).astype(half)

            loop(3, project)

            def attend(i, g=g):
                at = tile(i // 2, padded)
                lanes = [pl.ds(pl.multiple_of(t * quarter + (i % 2) * 128, 128), 128) for t in range(3)]
                q2 = qkv_refs[g][at, lanes[0]] * factor
                k2 = qkv_refs[g][at, lanes[1]]
                v2 = qkv_refs[g][at, lanes[2]]
                _, scores, first = pair_scores(q2, k2)
                key = lax.broadcasted_iota(jnp.int32, scores.shape, 0)
                scores = jnp.where(key < patches, scores, -1e30)
                top = jnp.max(scores, axis=0, keepdims=True)
                raised = jnp.exp(scores - top)
                total = jnp.sum(raised, axis=0, keepdims=True)
                lse_refs[g][i] = top + jnp.log(total)
                out = dot((raised * (1.0 / total)).astype(half), v2, 0, 0)
                mixed_refs[g][at, lanes[0]] = jnp.where(first, out[:padded], out[padded:]).astype(half)

            loop(2 * n_img, attend, 2 * n_img)

    return call(
        kernel,
        "attention_forward",
        (order, normed, bias, *(part for w in weights for part in w)),
        [SCALARS, ON_CHIP, ON_CHIP] + [ANYWHERE] * (groups * n_parts),
        [((count, wide), half)] * groups
        + [((count, quarter), half)] * groups
        + [((2 * n_img, 1, 2 * padded), full)] * groups,
        [ON_CHIP] * (3 * groups),
        [pltpu.VMEM((groups, width, wide), half), pltpu.SemaphoreType.DMA((groups,))],
    )


def layer_norm(value, gain, shift):
    center = jnp.mean(value, axis=-1, keepdims=True)
    offset = value - center
    spread = jnp.mean(offset * offset, axis=-1, keepdims=True)
    return offset * lax.rsqrt(spread + norm_eps) * gain + shift


def layer_norm_back(value, grad, gain):
    center = jnp.mean(value, axis=-1, keepdims=True)
    offset = value - center
    scale = lax.rsqrt(jnp.mean(offset * offset, axis=-1, keepdims=True) + norm_eps)
    unit = offset * scale
    scaled = grad * gain
    inner = jnp.mean(scaled * unit, axis=-1, keepdims=True)
    return scale * (scaled - jnp.mean(scaled, axis=-1, keepdims=True) - unit * inner), grad * unit


def load_out(order_ref, out_refs, held, sem, n, rows, quarter):
    q = order_ref[n]
    for j in range(4):
        column = pl.multiple_of((q ^ j) * quarter, quarter)
        fetch(
            [out_refs[j % 2].at[:, :, pl.ds(j // 2 * quarter, quarter)]],
            order_ref,
            lambda s, column=column: held.at[
                pl.ds(head_rows(s, q, n, rows, quarter), rows), pl.ds(column, quarter)
            ],
            sem,
        )


CHUNK = 16
ROWS = 64


def attention_out(order, x_zero, mixed, outs, bias, gain, shift):
    count, width = x_zero.shape
    n, rows, _ = outs[0].shape
    quarter = mixed[0].shape[1]

    def kernel(order_ref, x_ref, bias_ref, gain_ref, shift_ref, *refs):
        mixed_refs, out_refs = refs[:4], refs[4:6]
        after_ref, normed_ref, held, x_held, sems = refs[6:]
        bring(x_ref, x_held, sems.at[1])
        load_out(order_ref, out_refs, held, sems.at[0], n, rows, quarter)
        together = jnp.concatenate([m[...] for m in mixed_refs], axis=1)
        pltpu.make_async_copy(held, held, sems.at[0]).wait()
        after_ref[...] = dot(together, held[...], 1, 0)
        arrived(x_held, sems.at[1])

        def finish(i):
            at = tile(i, CHUNK)
            after = x_held[at] + (after_ref[at] + bias_ref[...])
            after_ref[at] = after
            normed_ref[at] = layer_norm(after, gain_ref[...], shift_ref[...]).astype(half)

        loop(count // CHUNK, finish, 13)

    return call(
        kernel,
        "attention_out",
        (order, x_zero, bias, gain, shift, *mixed, *outs),
        [SCALARS, ANYWHERE] + [ON_CHIP] * 7 + [ANYWHERE] * 2,
        [((count, width), full), ((count, width), half)],
        [ON_CHIP] * 2,
        [
            pltpu.VMEM((width, width), half),
            pltpu.VMEM((count, width), full),
            pltpu.SemaphoreType.DMA((2,)),
        ],
    )


def mlp(order, normed, cot, bias, up_all, down_all, down_start, carried=None, ending=None):
    count, width = normed.shape
    n, rows, _ = up_all.shape
    hidden = bias.shape[1]
    share = hidden // n
    step = min(512, hidden)
    steps = hidden // step
    more = [*(carried or []), *(ending[:1] if ending else [])]
    last = list(ending[1:]) if ending else []

    def kernel(order_ref, bias_ref, *refs):
        last_refs, refs = refs[: len(last)], refs[len(last) :]
        normed_ref, cot_ref, up_ref, down_ref, refs = *refs[:4], refs[4:]
        more_refs, refs = refs[: len(more)], refs[len(more) :]
        g_up_ref, g_down_ref, g_bias_ref, back_ref, end_ref, refs = *refs[:5], refs[5:]
        held, refs = refs[: len(more)], refs[len(more) :]
        rows_in, cots, out, back, up, down, pre, act, act_half, pre_half, g_up, g_down, sems = refs
        bring(normed_ref, rows_in, sems.at[3])
        fetch(
            [up_ref.at[:, :, pl.ds(0, hidden)]],
            None,
            lambda s: up.at[pl.ds(pl.multiple_of(s * rows, rows), rows)],
            sems.at[0],
        )
        bring(cot_ref, cots, sems.at[4])
        fetch(
            [down_ref.at[:, :, pl.ds(down_start, width)]],
            None,
            lambda s: down.at[pl.ds(pl.multiple_of(s * share, share), share)],
            sems.at[1],
        )
        for k in range(len(more)):
            bring(more_refs[k], held[k], sems.at[5 + k])
        arrived(rows_in, sems.at[3])
        arrived(up, sems.at[0])
        for t in range(steps):
            at = pl.ds(t * step, step)
            pre[...] = dot(rows_in[...], up[:, at], 1, 0)
            if not t:
                arrived(cots, sems.at[4])
                arrived(down, sems.at[1])
            act[...] = dot(cots[...], down[at, :], 1, 1)

            def gelu(i, at=at):
                some = tile(i, 2 * CHUNK)
                x = pre[some] + bias_ref[:, at]
                below = 0.5 * (1.0 + lax.erf(x * math.sqrt(0.5)))
                density = jnp.exp(-0.5 * x * x) * (1.0 / math.sqrt(2.0 * math.pi))
                act_half[some] = (x * below).astype(half)
                pre_half[some] = (act[some] * (below + x * density)).astype(half)

            loop(count // CHUNK // 2, gelu)
            p = pre_half[...]
            h = act_half[...]
            more_back = dot(p, up[:, at], 1, 1)
            more_out = dot(h, down[at, :], 1, 0)
            if t:
                back[...] += more_back
                out[...] += more_out
            elif carried:
                arrived(held[0], sems.at[5])
                arrived(held[1], sems.at[6])
                out[...] = held[0][...] + more_out
                back[...] = held[1][...] + more_back
            else:
                out[...] = more_out
                back[...] = more_back
            if t == steps - 1:
                bring(back, back_ref, sems.at[3])
                if not ending:
                    bring(out, end_ref, sems.at[4])
            g_down[at, :] = dot(h, cots[...], 0, 0).astype(half)
            if t == steps - 1:

                def send_down(r):
                    at = pl.multiple_of(order_ref[r] * share, share)
                    bring(g_down.at[pl.ds(at, share)], g_down_ref.at[r], sems.at[2])

                loop(n, send_down)
            g_up[:, at] = dot(rows_in[...], p, 0, 0).astype(half)
            g_bias_ref[:, at] = jnp.sum(p.astype(full), axis=0, keepdims=True)

        def send_up(r):
            at = pl.multiple_of(order_ref[r] * rows, rows)
            bring(g_up.at[pl.ds(at, rows)], g_up_ref.at[r], sems.at[0])

        loop(n, send_up)
        if ending:
            arrived(held[2], sems.at[7])

            def finish(i):
                at = tile(i, 2 * CHUNK)
                end_ref[at] = (held[2][at] + (out[at] + last_refs[0][...])).astype(half)

            loop(count // CHUNK // 2, finish)
        else:
            arrived(end_ref, sems.at[4])
        arrived(back_ref, sems.at[3])
        arrived(g_down_ref, sems.at[2])
        arrived(g_up_ref, sems.at[0])

    sums = pltpu.VMEM((count, width), full)
    wide = pltpu.VMEM((count, width), half)
    square = pltpu.VMEM((width, hidden), half)
    return call(
        kernel,
        "mlp",
        (order, bias, *last, normed, cot, up_all, down_all, *more),
        [SCALARS] + [ON_CHIP] * (1 + len(last)) + [ANYWHERE] * (4 + len(more)),
        [
            ((n, rows, hidden), half),
            ((n, share, width), half),
            ((1, hidden), full),
            ((count, width), full),
            ((count, width), half if ending else full),
        ],
        [ANYWHERE, ANYWHERE, ON_CHIP, ANYWHERE, ON_CHIP if ending else ANYWHERE],
        [
            *([sums] * len(more)),
            wide,
            wide,
            sums,
            sums,
            square,
            pltpu.VMEM((hidden, width), half),
            pltpu.VMEM((count, step), full),
            pltpu.VMEM((count, step), full),
            pltpu.VMEM((count, step), half),
            pltpu.VMEM((count, step), half),
            square,
            pltpu.VMEM((hidden, width), half),
            pltpu.SemaphoreType.DMA((5 + len(more),)),
        ],
    )


def attention_out_back(order, grad, after, cot, gain, mixed, outs):
    count, width = after.shape
    n, rows, _ = outs[0].shape
    quarter = mixed[0].shape[1]

    def kernel(order_ref, grad_ref, after_ref, cot_ref, gain_ref, *refs):
        mixed_refs, out_refs, refs = refs[:4], refs[4:6], refs[6:]
        after_grad_ref, mixed_grad_refs, g_out_ref, sums_ref = refs[0], refs[1:5], refs[5], refs[6]
        held, branch, terms, grad, after, cot, mixes, sems = refs[7:]
        block = count // 4
        for k in range(4):
            some = pl.ds(k * block, block)
            bring(grad_ref.at[some], grad.at[some], sems.at[1 + k])
            bring(after_ref.at[some], after.at[some], sems.at[5 + k])
            bring(cot_ref.at[some], cot.at[some], sems.at[9 + k])
        load_out(order_ref, out_refs, held, sems.at[0], n, rows, quarter)
        for j in range(4):
            bring(mixed_refs[j], mixes.at[j], sems.at[13])
        terms[...] = jnp.zeros_like(terms)

        def fold(value):
            return jnp.sum(value.reshape(CHUNK // 8, 8, width), axis=0)

        def back(i, k):
            at = pl.ds(pl.multiple_of(k * block + i * CHUNK, CHUNK), CHUNK)
            incoming = grad[at]
            part, gain_terms = layer_norm_back(after[at], incoming, gain_ref[...])
            own = cot[at].astype(full)
            total = own + part
            after_grad_ref[at] = total
            rounded = total.astype(half)
            branch[at] = rounded
            terms[0] += fold(rounded.astype(full))
            terms[1] += fold(gain_terms)
            terms[2] += fold(incoming)
            terms[3] += fold(own)

        for k in range(4):
            some = pl.ds(k * block, block)
            arrived(grad.at[some], sems.at[1 + k])
            arrived(after.at[some], sems.at[5 + k])
            arrived(cot.at[some], sems.at[9 + k])
            loop(block // CHUNK, lambda i, k=k: back(i, k), 13)
        for k in range(4):
            sums_ref[k] = jnp.sum(terms[k], axis=0, keepdims=True)
        arrived(held, sems.at[0])
        arrived(mixes, sems.at[13])
        for j in range(4):
            mixed_grad_refs[j][...] = dot(branch[...], held[j * quarter : (j + 1) * quarter], 1, 1).astype(half)
            g_out_ref[j * quarter : (j + 1) * quarter] = dot(mixes[j], branch[...], 0, 0).astype(half)

    return call(
        kernel,
        "attention_out_back",
        (order, grad, after, cot, gain, *mixed, *outs),
        [SCALARS] + [ANYWHERE] * 3 + [ON_CHIP] + [ANYWHERE] * 6,
        [((count, width), full)]
        + [((count, quarter), half)] * 4
        + [((width, width), half), ((4, 1, width), full)],
        [ON_CHIP] * 7,
        [
            pltpu.VMEM((width, width), half),
            pltpu.VMEM((count, width), half),
            pltpu.VMEM((4, 8, width), full),
            pltpu.VMEM((count, width), full),
            pltpu.VMEM((count, width), full),
            pltpu.VMEM((count, width), half),
            pltpu.VMEM((4, count, quarter), half),
            pltpu.SemaphoreType.DMA((14,)),
        ],
    )


def attention_back(order, normed, qkvs, lses, mixed_grads, g_out, which, n_img, patches, factor, n):
    groups = len(qkvs)
    count, width = normed.shape
    wide = qkvs[0].shape[1]
    quarter = wide // 3
    padded = count // n_img
    rows = width // n

    def kernel(order_ref, normed_ref, g_out_ref, *refs):
        qkv_refs, mg_refs, refs = refs[:groups], refs[groups : 2 * groups], refs[2 * groups :]
        lse_refs, refs = refs[:groups], refs[groups:]
        g_w_refs, proj_refs, sums_ref = refs[:groups], refs[groups : 2 * groups], refs[2 * groups]
        g_w, normed_held, g_out_held, sems = refs[2 * groups + 1 :]
        q = order_ref[n]
        bring(g_out_ref, g_out_held, sems.at[groups])
        bring(normed_ref, normed_held, sems.at[groups + 1])
        for g in range(groups):

            def attend(i, g=g):
                at = tile(i // 2, padded)
                lanes = [pl.ds(pl.multiple_of(t * quarter + (i % 2) * 128, 128), 128) for t in range(3)]
                q2 = qkv_refs[g][at, lanes[0]] * factor
                k2 = qkv_refs[g][at, lanes[1]]
                v2 = qkv_refs[g][at, lanes[2]]
                both, scores, first = pair_scores(q2, k2)
                key = lax.broadcasted_iota(jnp.int32, scores.shape, 0)
                probs = jnp.where(key < patches, jnp.exp(scores - lse_refs[g][i]), 0.0)
                o_both = apart(mg_refs[g][at, lanes[0]], first)
                g_probs = dot(v2, o_both, 1, 1)
                weighted = jnp.sum(probs * g_probs, axis=0, keepdims=True)
                g_scores = (probs * (g_probs - weighted)).astype(half)
                g_query = dot(g_scores, k2, 0, 0)
                g_query = jnp.where(first, g_query[:padded], g_query[padded:]) * factor
                proj_refs[g][at, lanes[0]] = g_query.astype(half)
                proj_refs[g][at, lanes[1]] = dot(g_scores, both, 1, 0).astype(half)
                proj_refs[g][at, lanes[2]] = dot(probs.astype(half), o_both, 1, 0).astype(half)

            loop(2 * n_img, attend, 4)
            if not g:
                arrived(g_out_held, sems.at[groups])
                arrived(normed_held, sems.at[groups + 1])

            def send_out(r, g=g):
                at = head_rows(order_ref[r], q, n, rows, quarter)
                column = pl.multiple_of((q ^ which[g]) * quarter, quarter)
                pltpu.make_async_copy(
                    g_out_held.at[pl.ds(at, rows), pl.ds(column, quarter)],
                    g_w_refs[g].at[r, :, pl.ds(wide, quarter)],
                    sems.at[g],
                ).start()

            loop(n, send_out)

            def weigh(t, g=g):
                at = tile(t, quarter)
                some = proj_refs[g][:, at]
                g_w[g, :, at] = dot(normed_held[...], some, 0, 0).astype(half)
                sums_ref[g, :, at] = jnp.sum(some.astype(full), axis=0, keepdims=True)

            loop(3, weigh)

            def send(r, g=g):
                at = pl.multiple_of(order_ref[r] * rows, rows)
                pltpu.make_async_copy(
                    g_w.at[g, pl.ds(at, rows)], g_w_refs[g].at[r, :, pl.ds(0, wide)], sems.at[g]
                ).start()

            loop(n, send)
        for g in range(groups):
            pltpu.make_async_copy(g_w_refs[g], g_w_refs[g], sems.at[g]).wait()

    return call(
        kernel,
        "attention_back",
        (order, normed, g_out, *qkvs, *mixed_grads, *lses),
        [SCALARS] + [ANYWHERE] * 2 + [ON_CHIP] * (3 * groups),
        [((n, rows, wide + quarter), half)] * groups
        + [((count, wide), half)] * groups
        + [((groups, 1, wide), full)],
        [ANYWHERE] * groups + [ON_CHIP] * (groups + 1),
        [
            pltpu.VMEM((groups, width, wide), half),
            pltpu.VMEM((count, width), half),
            pltpu.VMEM((width, width), half),
            pltpu.SemaphoreType.DMA((groups + 2,)),
        ],
    )


def input_back(order, x_zero, after_grad, gain, projs, weights):
    count, width = x_zero.shape
    wide = weights[0][0].shape[2]
    rows = width // sum(part.shape[0] for part in weights[0])
    parts = [part for w in weights for part in w]
    n_parts = len(weights[0])

    def kernel(order_ref, x_ref, after_ref, gain_ref, *refs):
        proj_refs, w_refs = refs[:4], refs[4 : 4 + len(parts)]
        token_ref, sums_ref, held, terms, x_held, after_held, sems = refs[4 + len(parts) :]
        for j in range(4):
            fetch(
                [w.at[:, pl.ds(0, rows)] for w in w_refs[j * n_parts : (j + 1) * n_parts]],
                order_ref,
                lambda s, j=j: held.at[j, pl.ds(pl.multiple_of(s * rows, rows), rows)],
                sems.at[j],
            )
        bring(x_ref, x_held, sems.at[4])
        bring(after_ref, after_held, sems.at[5])
        for j in range(4):
            arrived(held.at[j], sems.at[j])
            product = dot(proj_refs[j][...], held[j], 1, 1)
            if j == 0:
                token_ref[...] = product
            else:
                token_ref[...] += product
        arrived(x_held, sems.at[4])
        arrived(after_held, sems.at[5])
        terms[...] = jnp.zeros_like(terms)

        def fold(value):
            return jnp.sum(value.reshape(ROWS // 8, 8, width), axis=0)

        def back(i):
            at = tile(i, ROWS)
            incoming = token_ref[at]
            part, gain_terms = layer_norm_back(x_held[at], incoming, gain_ref[...])
            token_ref[at] = after_held[at] + part
            terms[0] += fold(gain_terms)
            terms[1] += fold(incoming)

        loop(count // ROWS, back)
        for k in range(2):
            sums_ref[k] = jnp.sum(terms[k], axis=0, keepdims=True)

    return call(
        kernel,
        "input_back",
        (order, x_zero, after_grad, gain, *projs, *parts),
        [SCALARS] + [ANYWHERE] * 2 + [ON_CHIP] * 5 + [ANYWHERE] * len(parts),
        [((count, width), full), ((2, 1, width), full)],
        [ON_CHIP] * 2,
        [
            pltpu.VMEM((4, width, wide), half),
            pltpu.VMEM((2, 8, width), full),
            pltpu.VMEM((count, width), full),
            pltpu.VMEM((count, width), full),
            pltpu.SemaphoreType.DMA((6,)),
        ],
    )


def payloads(which, w_fc1, w_fc2):
    rows, ff = w_fc1.shape
    full_share, width = w_fc2.shape
    share = full_share // 4
    n = ff // full_share
    hidden = n * share
    own, across = which
    if share % 128:
        fc1 = [lax.dynamic_slice(w_fc1, (0, (4 * s + own) * share), (rows, share)) for s in range(n)]
        fc2 = [lax.dynamic_slice(w_fc2, (g * share, 0), (share, width)).astype(half) for g in which]
        rest = jnp.concatenate([*fc1, fc2[0].reshape(rows, -1).astype(full)], axis=1)
        return rest.astype(half), fc2[1]

    def kernel(which_ref, fc1_ref, fc2_ref, rest_ref, two_ref):
        for s in range(n):
            at = pl.ds(pl.multiple_of((4 * s + which_ref[0]) * share, share), share)
            rest_ref[:, s * share : (s + 1) * share] = fc1_ref[:, at].astype(half)
        rest_ref[:, hidden : hidden + width] = fc2_ref[tile(which_ref[0], share), :].astype(half)
        two_ref[...] = fc2_ref[tile(which_ref[1], share), :].astype(half)

    return call(
        kernel,
        "payloads",
        (jnp.stack(which), w_fc1, w_fc2),
        [SCALARS] + [ON_CHIP] * 2,
        [((rows, hidden + width), half), ((share, width), half)],
        [ON_CHIP] * 2,
        [],
    )


def natural_quarters(q, pieces):
    once = [jnp.where((q & 1) == 1, pieces[i ^ 1], pieces[i]) for i in range(4)]
    return [jnp.where(q >= 2, once[i ^ 2], once[i]) for i in range(4)]


def finish_mlp(q, pieces, n):
    _, rows, width = pieces[0].shape
    share = width // n
    if share % 128:
        pieces = natural_quarters(q, pieces)
        fc1 = jnp.stack([p[0].reshape(rows, n, share) for p in pieces], axis=2).reshape(rows, 4 * width)
        return fc1.astype(full), jnp.concatenate([p[1] for p in pieces]).astype(full)

    def kernel(q_ref, *refs):
        fc1_ref, fc2_ref = refs[4:]
        for j in range(4):
            g = q_ref[0] ^ j
            for s in range(n):
                at = pl.ds(pl.multiple_of((4 * s + g) * share, share), share)
                fc1_ref[:, at] = refs[j][0, :, s * share : (s + 1) * share].astype(full)
            fc2_ref[tile(g, rows), :] = refs[j][1].astype(full)

    return call(
        kernel,
        "finish_mlp",
        (q[None], *pieces),
        [SCALARS] + [ON_CHIP] * 4,
        [((rows, 4 * width), full), ((4 * rows, width), full)],
        [ON_CHIP] * 2,
        [],
    )


def finish_attention(q, pieces):
    rows, width = pieces[0].shape
    quarter = width // 4

    def kernel(q_ref, *refs):
        qkv_ref, out_ref = refs[4:]
        for j in range(4):
            g = q_ref[0] ^ j
            for t in range(3):
                at = pl.ds(pl.multiple_of(t * width + g * quarter, quarter), quarter)
                qkv_ref[:, at] = refs[j][:, t * quarter : (t + 1) * quarter].astype(full)
            out_ref[:, tile(g, quarter)] = refs[j][:, 3 * quarter :].astype(full)

    return call(
        kernel,
        "finish_attention",
        (q[None], *pieces),
        [SCALARS] + [ON_CHIP] * 4,
        [((rows, 3 * width), full), ((rows, width), full)],
        [ON_CHIP] * 2,
        [],
    )


BELOW = 16


def first_payload(q, w_qkv, vectors):
    rows, columns = w_qkv.shape
    width = columns // 3
    quarter = width // 4
    wide = 3 * quarter

    def kernel(q_ref, w_ref, *refs):
        out_ref, held, low, sem = refs[len(vectors) :]
        for t in range(3):
            at = pl.multiple_of(t * width + q_ref[0] * quarter, quarter)
            pltpu.make_async_copy(
                w_ref.at[:, pl.ds(at, quarter)], held.at[:, pl.ds(t * quarter, quarter)], sem.at[0]
            ).start()
        low[...] = jnp.zeros_like(low)
        for k, vector in enumerate(refs[: len(vectors)]):
            low[k : k + 1, : vector.shape[1]] = vector[...]
        out_ref[rows:] = low[...].astype(half)
        pltpu.make_async_copy(held, held, sem.at[0]).wait()
        out_ref[:rows] = held[...].astype(half)

    return call(
        kernel,
        "first_payload",
        (q[None], w_qkv, *(v[None] for v in vectors)),
        [SCALARS, ANYWHERE] + [ON_CHIP] * len(vectors),
        [((rows + BELOW, wide), half)],
        [ON_CHIP],
        [pltpu.VMEM((rows, wide), full), pltpu.VMEM((BELOW, wide), full), pltpu.SemaphoreType.DMA((1,))],
    )[0]


def unpack_vectors(order, parts, n, rows, share):
    width = n * rows
    quarter = width // 4
    if rows % 128 or share % 128:
        q = order[n]
        held = jnp.concatenate([p[:, rows:] for p in parts]).astype(full)
        held = held[jnp.zeros((n,), jnp.int32).at[order[:n]].set(jnp.arange(n, dtype=jnp.int32))]
        groups = jnp.arange(4, dtype=jnp.int32) ^ q
        vectors = jnp.stack([held[:, k, :rows].reshape(1, width) for k in range(8)])
        units = held[:, 8, : 4 * share].reshape(n, 4, share).transpose(1, 0, 2)[groups]
        ends = [vectors[k].reshape(4, 1, quarter)[groups] for k in range(2)]
        return vectors, units.reshape(4, 1, width), jnp.concatenate([ends[0], 0 * ends[0], ends[1]], axis=2)

    def kernel(order_ref, *refs):
        part_refs, (vector_ref, fc1_ref, qkv_ref, held, wider, sem) = refs[: len(parts)], refs[len(parts) :]
        base = 0
        for part in part_refs:
            size = part.shape[0]
            pltpu.make_async_copy(part.at[:, pl.ds(rows, BELOW)], held.at[pl.ds(base, size)], sem.at[0]).start()
            base += size
        pltpu.make_async_copy(held, held, sem.at[0]).wait()
        wider[...] = held[...].astype(full)
        q = order_ref[n]
        for r in range(n):
            at = tile(order_ref[r], rows)
            for k in range(8):
                vector_ref[k, :, at] = wider[r, k : k + 1, :rows]
            for j in range(4):
                fc1_ref[j, :, tile(order_ref[r], share)] = wider[r, 8:9, tile(q ^ j, share)]
        for j in range(4):
            at = tile(q ^ j, quarter)
            qkv_ref[j, :, :quarter] = vector_ref[0, :, at]
            qkv_ref[j, :, quarter : 2 * quarter] = jnp.zeros((1, quarter), full)
            qkv_ref[j, :, 2 * quarter :] = vector_ref[1, :, at]

    return call(
        kernel,
        "unpack_vectors",
        (order, *parts),
        [SCALARS] + [ANYWHERE] * len(parts),
        [((8, 1, width), full), ((4, 1, width), full), ((4, 1, 3 * quarter), full)],
        [ON_CHIP] * 3,
        [
            pltpu.VMEM((n, BELOW, 3 * quarter), half),
            pltpu.VMEM((n, BELOW, 3 * quarter), full),
            pltpu.SemaphoreType.DMA((1,)),
        ],
    )


def pack_sums(order, n, rows, share, proj_sums, unit_sums, wide_sums):
    width = n * rows
    quarter = width // 4
    if rows % 128 or share % 128:
        groups = jnp.arange(4, dtype=jnp.int32) ^ order[n]
        proj = jnp.concatenate(proj_sums)[groups]
        units = jnp.concatenate(unit_sums)[groups].reshape(4, n, share)
        flat = [proj[:, :, :quarter].reshape(width), proj[:, :, 2 * quarter :].reshape(width)]
        two, one = wide_sums
        flat += [two[0], one[0], one[1], two[3], two[1], two[2]]
        flat = [v.reshape(n, 1, rows) for v in flat]
        stacked = [jnp.pad(v, ((0, 0), (0, 0), (0, 128 - rows))) for v in flat]
        stacked.append(jnp.pad(units.transpose(1, 0, 2), ((0, 0), (0, 4), (0, 128 - share))))
        return jnp.concatenate(stacked, axis=1)[order[:n]]

    def kernel(order_ref, proj_a, proj_b, unit_a, unit_b, two_ref, one_ref, out_ref, proj, units):
        proj[:2], proj[2:] = proj_a[...], proj_b[...]
        units[:2], units[2:] = unit_a[...], unit_b[...]
        q = order_ref[n]
        per = n // 4
        for r in range(n):
            s = order_ref[r]
            j = (s // per) ^ q
            at = tile(s, rows)
            inside = pl.multiple_of((s % per) * rows, rows)
            out_ref[r, 0:1] = proj[j, :, pl.ds(inside, rows)]
            out_ref[r, 1:2] = proj[j, :, pl.ds(2 * quarter + inside, rows)]
            for k, (ref, row) in enumerate(
                ((two_ref, 0), (one_ref, 0), (one_ref, 1), (two_ref, 3), (two_ref, 1), (two_ref, 2))
            ):
                out_ref[r, 2 + k : 3 + k] = ref[row, :, at]
            for g in range(4):
                out_ref[r, 8 + g : 9 + g] = units[q ^ g, :, tile(s, share)]
            out_ref[r, 12:] = jnp.zeros((4, rows), full)

    sums_two, sums_one = wide_sums
    return call(
        kernel,
        "pack_sums",
        (order, *proj_sums, *unit_sums, sums_two, sums_one),
        [SCALARS] + [ON_CHIP] * 6,
        [((n, 16, rows), full)],
        [ON_CHIP],
        [pltpu.VMEM((4, 1, 3 * quarter), full), pltpu.VMEM((4, 1, width), full)],
    )[0]


def table(codes, width):
    ratio = 0.3 * jnp.exp(codes.astype(full) * (math.log(10.0 / 0.3) / (NSCALE - 1)))
    quarter = width // 4
    omega = jnp.exp(jnp.arange(quarter).astype(full) * (-math.log(10000.0) / quarter))
    steps = jnp.arange(GRID, dtype=jnp.int32).astype(full)
    angle = ratio[:, None, None] * steps[None, :, None] * omega[None, None, :]
    return jnp.concatenate([jnp.sin(angle), jnp.cos(angle)], axis=-1)


def local(
    tokens,
    scale_codes,
    w_qkv,
    b_q,
    b_v,
    w_out,
    b_out,
    gain_one,
    shift_one,
    w_fc1,
    b_fc1,
    w_fc2,
    b_fc2,
    gain_two,
    shift_two,
    cotangent,
):
    n = lax.axis_size("fsdp")
    q = lax.axis_index("dp")
    f = lax.axis_index("fsdp")
    row_count, width = tokens.shape
    rows = width // n
    ff = b_fc1.shape[0] * n
    ffq = ff // n // 4
    hidden = n * ffq
    quarter = width // 4
    n_img = scale_codes.shape[0]
    patches = row_count // n_img
    padded = -(-patches // 16) * 16
    factor = 1.0 / math.sqrt(width // HEADS)
    seq = Order(q)
    bits = list(reversed(range(n.bit_length() - 1)))
    near = min(1, len(bits) - 1)
    shard_order = jnp.asarray(masks(bits), jnp.int32) ^ f
    group_order = jnp.arange(4, dtype=jnp.int32) ^ q
    order = jnp.concatenate([shard_order, q[None]])

    def last_three(chain):
        while len(chain.bits) > 3:
            chain.launch()
            seq.land((), chain)
            chain.join()
        return chain

    small = [b_q, b_v, b_out, gain_one, shift_one, b_fc2, gain_two, shift_two, b_fc1]
    qkv = last_three(Gather(seq, first_payload(q, w_qkv, small), n, bits))
    qkv.launch()
    rest_own, two_own = payloads([seq.at(q), q ^ 2], w_fc1, w_fc2)
    rest_own, two_own = seq.land((rest_own, two_own), qkv)
    rest = Sent(lax.all_gather(rest_own, "fsdp", axis=0, tiled=False))
    two = Sent(lax.all_gather(two_own, "fsdp", axis=0, tiled=False))
    out_own = [lax.dynamic_slice(w_out, (0, g * quarter), (rows, quarter)) for g in (q, q ^ 2)]
    out = last_three(Gather(seq, jnp.concatenate(out_own, axis=1).astype(half), n, bits))

    def spread_rows(value):
        split = value.reshape(n_img, patches, width)
        return jnp.pad(split, ((0, 0), (0, padded - patches), (0, 0)))

    def compact(value):
        return value.reshape(n_img, padded, width)[:, :patches].reshape(row_count, width)

    qkv.join()
    qkv.launch()
    spread_tokens = seq.land(spread_rows(seq.at(tokens)), qkv)
    qkv_near = qkv.join()
    qkv.launch()
    near_b, near_c = Sent(core_swap(qkv.held)), Sent(x_swap(qkv.held))
    out.launch()
    places = table(scale_codes, width)
    row_place = jnp.broadcast_to(places[:, :, None], (n_img, GRID, GRID, width // 2))
    col_place = jnp.broadcast_to(places[:, None], (n_img, GRID, GRID, width // 2))
    place = jnp.concatenate([row_place, col_place], axis=-1).reshape(n_img, patches, width)
    place = jnp.pad(place, ((0, 0), (0, padded - patches), (0, 0)))
    x_zero = (seq.at(spread_tokens).astype(full) + place).reshape(-1, width)
    x_zero = seq.land(x_zero, qkv, near_b, out)
    qkv_far = seq.at(qkv.got)
    far_b, far_c = Sent(core_swap(qkv_far)), Sent(x_swap(qkv_far))
    out.join()
    out.launch()
    vectors, bias_fc1, bias_qkv = unpack_vectors(seq.at(order), (qkv_near, qkv_far), n, rows, ffq)
    _, _, full_bout, gain_one_f, shift_one_f, full_bfc2, gain_two_f, shift_two_f = vectors
    normed_one = layer_norm(x_zero, gain_one_f, shift_one_f).astype(half)
    normed_one = seq.land(normed_one, far_b)

    first = attention_forward(
        seq.at(order), normed_one, bias_qkv[:2], ((qkv_near, qkv_far), (near_b.value, far_b.value)),
        n_img, patches, factor,
    )
    first = (seq.land(first[0], near_c, far_c, out), *first[1:])
    near_c, far_c = seq.at((near_c.value, far_c.value))
    near_d, far_d = Sent(core_swap(near_c)), Sent(core_swap(far_c))
    out.join()
    out.launch()
    cot = seq.land(spread_rows(cotangent).reshape(-1, width), near_d, far_d)
    second = attention_forward(
        seq.at(order), normed_one, bias_qkv[2:], ((near_c, far_c), (near_d.value, far_d.value)),
        n_img, patches, factor,
    )
    second = (seq.land(second[0], out), *second[1:])
    out_a = seq.at(out.join())
    out_b = Sent(core_swap(out_a))
    seq.land((), out_b)
    outs = (out_a, out_b.value)
    qkv_parts = (
        (qkv_near, qkv_far), (near_b.value, far_b.value), (near_c, far_c), (near_d.value, far_d.value)
    )
    qkvs = (*first[:2], *second[:2])
    mixed = (*first[2:4], *second[2:4])
    lses = (*first[4:], *second[4:])
    after_attn, normed_two = attention_out(
        seq.at(order), x_zero, mixed, outs, full_bout, gain_two_f, shift_two_f
    )
    normed_two = seq.land(normed_two, rest)
    rest_a = seq.at(rest.value)
    rest_b = Sent(core_swap(rest_a))
    up_c = Sent(x_swap(seq.at(rest_a[:, :, :hidden])))
    seq.land((), rest_b)

    up_g1, down_g1, g_bias_1, back_sum, out_sum = mlp(
        seq.at(order), normed_two, cot, bias_fc1[1], rest_b.value, rest_b.value, hidden
    )
    up_g0, down_g0, g_bias_0, back_sum, out_sum = mlp(
        order, normed_two, cot, bias_fc1[0], rest_a, rest_a, hidden, (out_sum, back_sum)
    )
    up_g0 = seq.land(up_g0, up_c, two)
    up_g1 = seq.at(up_g1)
    up_got = Sent(core_swap(up_g1))
    down_g1 = seq.at(down_g1)
    down_got = Sent(core_swap(down_g1))
    seq.land((), up_got)
    red_up = Reduce(seq, (up_g0, up_got.value), n)
    red_up.launch()
    seq.land((), down_got)
    red_down = Reduce(seq, (down_g0, down_got.value), n)
    red_down.launch(near)
    up_c, two = seq.at((up_c.value, two.value))
    up_d, two_d = Sent(core_swap(up_c)), Sent(core_swap(two))
    up_g2, down_g2, g_bias_2, back_sum, out_sum = mlp(
        seq.at(order), normed_two, cot, bias_fc1[2], up_c, two, 0, (out_sum, back_sum)
    )
    up_g2 = seq.land(up_g2, up_d, two_d, red_up, red_down)
    red_up.launch()
    red_down.launch()
    up_g3, down_g3, g_bias_3, grad_two_in, block = mlp(
        seq.at(order), normed_two, cot, bias_fc1[3], up_d.value, two_d.value, 0,
        (out_sum, back_sum), (after_attn, full_bfc2),
    )
    up_g3 = seq.land(up_g3, red_up, red_down)
    up_got = Sent(core_swap(up_g3))
    down_g3 = seq.at(down_g3)
    down_got = Sent(core_swap(down_g3))
    red_up.launch()
    red_down.launch()
    seq.land((), up_got)
    two_up = Reduce(seq, (up_g2, up_got.value), n)
    two_up.launch()
    seq.land((), down_got)
    two_down = Reduce(seq, (down_g2, down_got.value), n)
    two_down.launch(near)

    after_grad, mg0, mg1, mg2, mg3, g_out, sums_two = attention_out_back(
        seq.at(order), grad_two_in, after_attn, cot, gain_two_f, mixed, outs
    )
    mg2 = seq.at(mg2)
    g_w2, g_w3, proj2, proj3, sums_b = attention_back(
        seq.at(order), normed_one, qkvs[2:], lses[2:], (mg2, mg3), g_out, (2, 3), n_img, patches, factor, n
    )
    g_w3 = seq.land(g_w3, red_up, red_down, two_up, two_down)
    w_3 = Sent(core_swap(g_w3))
    two_up.launch()
    two_down.launch()
    seq.land((), w_3)
    middle = n // 2
    half_shape = (2,) * (len(bits) - 1)
    w_high = Sent(x_swap(seq.at(rounded_sum([g_w2[middle:], w_3.value[middle:]]))))
    g_w0, g_w1, proj0, proj1, sums_a = attention_back(
        seq.at(order), normed_one, qkvs[:2], lses[:2], (mg0, mg1), g_out, (0, 1), n_img, patches, factor, n
    )
    g_w1 = seq.land(g_w1, two_up, two_down, w_high)
    w_1 = Sent(core_swap(g_w1))
    two_up.launch()
    two_down.launch()
    seq.land((), w_1)
    red_w = Reduce(seq, (g_w0, w_1.value), n)
    red_w.launch(0, [w_high.value.reshape(half_shape + w_high.value.shape[1:])])
    w_low = Sent(x_swap(seq.at(rounded_sum([g_w2[:middle], w_3.value[:middle]]))))
    tokens_grad, sums_one = input_back(
        seq.at(order), x_zero, after_grad, gain_one_f, (proj0, proj1, proj2, proj3), qkv_parts
    )
    sums_one = seq.land(sums_one, two_up, two_down, red_w, w_low)
    red_w.terms = [*red_w.terms, w_low.value.reshape(half_shape + w_low.value.shape[1:])]
    while len(red_w.axes) > 2:
        red_w.launch()
        seq.land((), red_w)
    red_w.launch()
    packed = pack_sums(
        seq.at(order),
        n,
        rows,
        ffq,
        (sums_a, sums_b),
        (jnp.stack([g_bias_0, g_bias_1]), jnp.stack([g_bias_2, g_bias_3])),
        (sums_two, sums_one),
    )
    packed = seq.at(packed)
    peers = Sent([xor_swap(packed, "dp", 4, m) for m in (1, 2, 3)])
    crossing = jnp.stack([two_up.rest().piece(), two_down.rest().piece()])
    cross = Sent(x_swap(seq.at(crossing)))
    seq.land((), peers, red_w)
    if red_w.axes:
        red_w.launch()
    sums = Reduce(seq, (packed, *peers.value), n, full)
    while len(sums.axes) > 2:
        sums.launch()
        seq.land((), sums)
    if len(sums.axes) > 1:
        sums.launch()
        seq.land((), sums, cross)
    else:
        seq.land((), cross)
    owned = [rounded_sum([*red_up.rest().terms, cross.value[0]]), rounded_sum([*red_down.rest().terms, cross.value[1]])]
    mlp_spread = Spread(seq, jnp.stack(owned))
    sums.launch()
    seq.land((), sums, *([red_w] if len(bits) > 1 else []))
    w_spread = Spread(seq, red_w.piece())
    small_sums = sums.piece()
    block, tokens_grad = seq.at((block, tokens_grad))
    block_out, grad_tokens = seq.land((compact(block), compact(tokens_grad)), mlp_spread)
    mlp_spread.cross()
    small_sums = seq.land(small_sums, mlp_spread, w_spread)
    w_spread.cross()
    mlp_pieces = seq.at(mlp_spread.pieces)
    out_fc1, out_fc2 = finish_mlp(q, mlp_pieces, n)
    out_fc2 = seq.land(out_fc2, w_spread)
    out_qkv, out_out = finish_attention(seq.value, w_spread.pieces)
    small_out = [small_sums[k, :rows] for k in range(8)]
    out_bfc1 = small_sums[8:12, :ffq].reshape(-1)
    o_bq, o_bv, o_bout, o_gone, o_sone, o_bfc2, o_gtwo, o_stwo = small_out
    return (
        block_out,
        grad_tokens,
        out_qkv,
        o_bq,
        o_bv,
        out_out,
        o_bout,
        o_gone,
        o_sone,
        out_fc1,
        out_bfc1,
        out_fc2,
        o_bfc2,
        o_gtwo,
        o_stwo,
    )


def solution(mesh):
    rows_split = P(("dp", "fsdp"), None)
    matrix = P("fsdp", None)
    vector = P("fsdp")
    return jax.shard_map(
        local,
        mesh=mesh,
        in_specs=(
            rows_split, P(("dp", "fsdp")), matrix, vector, vector, matrix, vector, vector, vector,
            matrix, vector, matrix, vector, vector, vector, rows_split,
        ),
        out_specs=(
            rows_split, rows_split, matrix, vector, vector, matrix, vector, vector, vector,
            matrix, vector, matrix, vector, vector, vector,
        ),
        check_vma=False,
    )
```

profile of v0, /device:TPU:0, one launch (start us, length us, event | category | flops | bytes accessed | tf_op | source)
XLA Modules:
  0.0 418.3 jit_solution(6800643596099256900)
XLA Ops:
  7.2 2.6 first_payload.1
  9.8 4.1 collective-permute-start
  14.5 3.3 payloads.1
  17.8 6.5 %collective-permute-done = bf16[1,144,768]{2,1,0:T(8,128)(2,1)S(1)} collective-permute-done((bf16[1,144,768]{2,1,0:T(8,128)(2,1)}, bf16[1,144,768]{2,1,0:T(8,128)(2,1)S(1)}, u32[]{:S(2)}, u32[]{:S(2)}) %collective-permute-start) | collective-permute-done | bytes 221216 | tf_op jit(solution)/shard_map/ppermute | solution.py:19
  27.5 3.6 copy.32
  31.1 2.1 reshape.461
  41.3 6.6 %collective-permute-start.4 = (bf16[1,128,512]{2,1,0:T(8,128)(2,1)S(1)}, bf16[1,128,512]{2,1,0:T(8,128)(2,1)S(1)}, u32[]{:S(2)}, u32[]{:S(2)}) collective-permute-start(bf16[1,128,512]{2,1,0:T(8,128)(2,1)S(1)} %pad_maximum_fusion.7), channel_id=1, source_target_pairs={{0,4},{1,5},{2,6},{3,7},{4,0},{5,1},{6,2},{7,3},{8,12},{9,13},{10,... | collective-permute-start | bytes 393224 | tf_op jit(solution)/shard_map/ppermute | solution.py:19
  48.7 11.6 %collective-permute-done.4 = bf16[1,128,512]{2,1,0:T(8,128)(2,1)S(1)} collective-permute-done((bf16[1,128,512]{2,1,0:T(8,128)(2,1)S(1)}, bf16[1,128,512]{2,1,0:T(8,128)(2,1)S(1)}, u32[]{:S(2)}, u32[]{:S(2)}) %collective-permute-start.4) | collective-permute-done | bytes 131104 | tf_op jit(solution)/shard_map/ppermute | solution.py:19
  63.8 2.3 unpack_vectors.1
  71.5 10.5 %attention_forward.2 = (bf16[832,768]{1,0:T(8,128)(2,1)}, bf16[832,768]{1,0:T(8,128)(2,1)}, bf16[832,256]{1,0:T(8,128)(2,1)}, bf16[832,256]{1,0:T(8,128)(2,1)}, ...) custom-call(s32[9]{0:T(128)} %pad_add_fusion.1.order_ref, bf16[832,1024]{1,0:T(8,128)(2,1)} %add_convert_fusion.normed_ref, ...), custom_call_target="tpu_custom_call" | custom-call | tf_op jit(solution)/shard_map/attention_forward/pallas_call | solution.py:133
  82.0 8.8 %collective-permute-done.8 = bf16[2,128,512]{2,1,0:T(8,128)(2,1)S(1)} collective-permute-done((bf16[2,128,512]{2,1,0:T(8,128)(2,1)S(1)}, bf16[2,128,512]{2,1,0:T(8,128)(2,1)S(1)}, u32[]{:S(2)}, u32[]{:S(2)}) %collective-permute-start.8) | collective-permute-done | bytes 262176 | tf_op jit(solution)/shard_map/ppermute | solution.py:19
  96.2 10.5 %attention_forward.3 = (bf16[832,768]{1,0:T(8,128)(2,1)}, bf16[832,768]{1,0:T(8,128)(2,1)}, bf16[832,256]{1,0:T(8,128)(2,1)}, bf16[832,256]{1,0:T(8,128)(2,1)}, ...) custom-call(s32[9]{0:T(128)} %pad_add_fusion.1.order_ref, bf16[832,1024]{1,0:T(8,128)(2,1)} %add_convert_fusion.normed_ref, ...), custom_call_target="tpu_custom_call" | custom-call | tf_op jit(solution)/shard_map/attention_forward/pallas_call | solution.py:133
  108.0 2.6 collective-permute-done.12.refs_5_
  111.7 9.6 %attention_out.1 = (f32[832,1024]{1,0:T(8,128)}, bf16[832,1024]{1,0:T(8,128)(2,1)}) custom-call(s32[9]{0:T(128)} %pad_add_fusion.1.order_ref, f32[832,1024]{1,0:T(8,128)} %bitcast.229, f32[1,1024]{1,0:T(1,128)} %get-tuple-element.603.bias_ref, f32[1,1024]{1,0:T(1,128)} %get-tuple-element.602.gain_ref, f32[1,1024]{1,0:T(1,128)} %get-tuple-element.601.shift_ref, ...), custom_call_target="tpu_custom_call" | custom-call | tf_op jit(solution)/shard_map/attention_out/pallas_call | solution.py:133
  121.5 3.1 slice.528
  125.8 3.1 collective-permute-done.13.refs_2_.refs_3_
  128.8 19.2 %mlp.4 = (bf16[8,128,1024]{2,1,0:T(8,128)(2,1)}, bf16[8,128,1024]{2,1,0:T(8,128)(2,1)}, f32[1,1024]{1,0:T(1,128)}, f32[832,1024]{1,0:T(8,128)}, f32[832,1024]{1,0:T(8,128)}) custom-call(s32[9]{0:T(128)} %pad_add_fusion.1.order_ref, f32[1,1024]{1,0:T(1,128)} %get-tuple-element.608.bias_ref, bf16[832,1024]{1,0:T(8,128)(2,1)} %get-tuple-element.374.refs_0_.refs_1_, ...), custom_call_target="tpu_custom_call" | custom-call | tf_op jit(solution)/shard_map/mlp/pallas_call | solution.py:133
  148.1 20.2 %mlp.5 = (bf16[8,128,1024]{2,1,0:T(8,128)(2,1)}, bf16[8,128,1024]{2,1,0:T(8,128)(2,1)}, f32[1,1024]{1,0:T(1,128)}, f32[832,1024]{1,0:T(8,128)}, f32[832,1024]{1,0:T(8,128)}) custom-call(s32[9]{0:T(128)} %pad_add_fusion.1.order_ref, f32[1,1024]{1,0:T(1,128)} %get-tuple-element.609.bias_ref, bf16[832,1024]{1,0:T(8,128)(2,1)} %get-tuple-element.374.refs_0_.refs_1_, ...), custom_call_target="tpu_custom_call" | custom-call | tf_op jit(solution)/shard_map/mlp/pallas_call | solution.py:133
  170.2 2.5 collective-permute-done.14.refs_2_
  173.2 3.9 collective-permute-done.16
  177.1 2.4 add_convert_fusion.7
  183.4 20.1 %mlp.6 = (bf16[8,128,1024]{2,1,0:T(8,128)(2,1)}, bf16[8,128,1024]{2,1,0:T(8,128)(2,1)}, f32[1,1024]{1,0:T(1,128)}, f32[832,1024]{1,0:T(8,128)}, f32[832,1024]{1,0:T(8,128)}) custom-call(s32[9]{0:T(128)} %pad_add_fusion.1.order_ref, f32[1,1024]{1,0:T(1,128)} %get-tuple-element.607.bias_ref, bf16[832,1024]{1,0:T(8,128)(2,1)} %get-tuple-element.374.refs_0_.refs_1_, ...), custom_call_target="tpu_custom_call" | custom-call | tf_op jit(solution)/shard_map/mlp/pallas_call | solution.py:133
  203.5 4.2 %collective-permute-done.20 = bf16[2,2,128,1024]{3,2,1,0:T(8,128)(2,1)} collective-permute-done((bf16[2,2,128,1024]{3,2,1,0:T(8,128)(2,1)}, bf16[2,2,128,1024]{3,2,1,0:T(8,128)(2,1)}, u32[]{:S(2)}, u32[]{:S(2)}) %collective-permute-start.20) | collective-permute-done | bytes 1048608 | tf_op jit(solution)/shard_map/ppermute | solution.py:19
  207.8 2.5 fusion.6
  213.0 20.8 %mlp.7 = (bf16[8,128,1024]{2,1,0:T(8,128)(2,1)}, bf16[8,128,1024]{2,1,0:T(8,128)(2,1)}, f32[1,1024]{1,0:T(1,128)}, f32[832,1024]{1,0:T(8,128)}, bf16[832,1024]{1,0:T(8,128)(2,1)}) custom-call(s32[9]{0:T(128)} %pad_add_fusion.1.order_ref, f32[1,1024]{1,0:T(1,128)} %get-tuple-element.606.bias_ref, f32[1,1024]{1,0:T(1,128)} %get-tuple-element.600.refs_0_, ...), custom_call_target="tpu_custom_call" | custom-call | tf_op jit(solution)/shard_map/mlp/pallas_call | solution.py:133
  234.4 2.2 fusion.21
  236.6 2.1 fusion.22
  239.1 2.1 collective-permute-done.23
  245.4 2.7 collective-permute-start.26
  248.3 11.0 %attention_out_back.1 = (f32[832,1024]{1,0:T(8,128)}, bf16[832,256]{1,0:T(8,128)(2,1)}, bf16[832,256]{1,0:T(8,128)(2,1)}, bf16[832,256]{1,0:T(8,128)(2,1)}, bf16...) custom-call(s32[9]{0:T(128)} %pad_add_fusion.1.order_ref, ...), custom_call_target="tpu_custom_call" | custom-call | tf_op jit(solution)/shard_map/attention_out_back/pallas_call | solution.py:133
  259.4 18.1 %attention_back.2 = (bf16[8,128,1024]{2,1,0:T(8,128)(2,1)}, bf16[8,128,1024]{2,1,0:T(8,128)(2,1)}, bf16[832,768]{1,0:T(8,128)(2,1)}, bf16[832,768]{1,0:T(8,128)(2,1)}, f32[2,1,768]{2,1,0:T(1,128)}) custom-call(s32[9]{0:T(128)} %pad_add_fusion.1.order_ref, bf16[832,1024]{1,0:T(8,128)(2,1)} %add_convert_fusion.normed_ref, ...), custom_call_target="tpu_custom_call" | custom-call | tf_op jit(solution)/shard_map/attention_back/pallas_call | solution.py:133
  280.8 2.4 fusion.4
  283.2 2.3 fusion.5
  285.5 2.4 add_convert_fusion.2
  289.2 2.5 collective-permute-start.30
  291.7 18.0 %attention_back.3 = (bf16[8,128,1024]{2,1,0:T(8,128)(2,1)}, bf16[8,128,1024]{2,1,0:T(8,128)(2,1)}, bf16[832,768]{1,0:T(8,128)(2,1)}, bf16[832,768]{1,0:T(8,128)(2,1)}, f32[2,1,768]{2,1,0:T(1,128)}) custom-call(s32[9]{0:T(128)} %pad_add_fusion.1.order_ref, bf16[832,1024]{1,0:T(8,128)(2,1)} %add_convert_fusion.normed_ref, ...), custom_call_target="tpu_custom_call" | custom-call | tf_op jit(solution)/shard_map/attention_back/pallas_call | solution.py:133
  309.8 3.7 collective-permute-done.32
  325.1 16.0 %input_back.1 = (f32[832,1024]{1,0:T(8,128)}, f32[2,1,1024]{2,1,0:T(1,128)}) custom-call(s32[9]{0:T(128)} %pad_add_fusion.1.order_ref, f32[832,1024]{1,0:T(8,128)} %bitcast.230, f32[832,1024]{1,0:T(8,128)} %get-tuple-element.504.after_ref, f32[1,1024]{1,0:T(1,128)} %get-tuple-element.599.gain_ref, bf16[832,768]{1,0:T(8,128)(2,1)} %get-tuple-element.505.refs_0_, ...), custom_call_target="tpu_custom_call" | custom-call | tf_op jit(solution)/shard_map/input_back/pallas_call | solution.py:133
  342.6 4.2 collective-permute-done.34
  346.8 2.5 fusion.3
  357.7 9.3 %collective-permute-done.41 = bf16[2,128,1024]{2,1,0:T(8,128)(2,1)S(1)} collective-permute-done((bf16[2,128,1024]{2,1,0:T(8,128)(2,1)}, bf16[2,128,1024]{2,1,0:T(8,128)(2,1)S(1)}, u32[]{:S(2)}, u32[]{:S(2)}) %collective-permute-start.41) | collective-permute-done | bytes 524320 | tf_op jit(solution)/shard_map/ppermute | solution.py:19
  369.8 2.6 collective-permute-done.42
  373.0 2.4 collective-permute-start.46
  376.2 2.2 fusion.25
  382.2 4.1 collective-permute-done.45
  396.7 5.9 %collective-permute-done.51.refs_2_ = bf16[128,1024]{1,0:T(8,128)(2,1)S(1)} collective-permute-done((bf16[128,1024]{1,0:T(8,128)(2,1)S(1)}, bf16[128,1024]{1,0:T(8,128)(2,1)S(1)}, u32[]{:S(2)}, u32[]{:S(2)}) %collective-permute-start.51) | collective-permute-done | bytes 262176 | tf_op jit(solution)/shard_map/ppermute | solution.py:19
  403.4 3.9 finish_mlp.1
  408.6 2.6 finish_attention.1
  (235 shorter events, 91.4 us)
Async XLA Ops:
  7.2 114.1 %all-gather.5.cloned.1.call-start = ((), (), s32[]{:S(2)}) async-start(), calls=%async_computation | async-start | bytes 4718592 | tf_op jit(solution)/shard_map/all_gather | solution.py:963
  9.8 14.5 %collective-permute-start = (bf16[1,144,768]{2,1,0:T(8,128)(2,1)}, bf16[1,144,768]{2,1,0:T(8,128)(2,1)S(1)}, u32[]{:S(2)}, u32[]{:S(2)}) collective-permute-start(bf16[1,144,768]{2,1,0:T(8,128)(2,1)} %bitcast.263), channel_id=1, source_target_pairs={{0,4},{1,5},{2,6},{3,7},{4,0},{5,1},{6,2},{7,3},{8,12},{9,13},{10,... | collective-permute-start | bytes 663560 | tf_op jit(solution)/shard_map/ppermute | solution.py:19
  24.3 145.9 %all-gather.7.cloned.1.call-start = ((), (), s32[]{:S(2)}) async-start(), calls=%async_computation.1 | async-start | bytes 2359296 | tf_op jit(solution)/shard_map/all_gather | solution.py:964
  24.5 11.4 %collective-permute-start.1 = (bf16[2,144,768]{2,1,0:T(8,128)(2,1)S(1)}, bf16[2,144,768]{2,1,0:T(8,128)(2,1)S(1)}, u32[]{:S(2)}, u32[]{:S(2)}) collective-permute-start(bf16[2,144,768]{2,1,0:T(8,128)(2,1)S(1)} %pad_maximum_fusion.5), channel_id=1, source_target_pairs={{0,2},{1,3},{2,0},{3,1},{4,6},{5,7},{6,4},{7,5},{8,10},{9,11},{10,... | collective-permute-start | bytes 1327112 | tf_op jit(solution)/shard_map/ppermute | solution.py:19
  36.8 24.4 %collective-permute-start.2 = (bf16[4,144,768]{2,1,0:T(8,128)(2,1)}, bf16[4,144,768]{2,1,0:T(8,128)(2,1)}, u32[]{:S(2)}, u32[]{:S(2)}) collective-permute-start(bf16[4,144,768]{2,1,0:T(8,128)(2,1)} %constant_dynamic-update-slice_fusion.refs_0_.refs_4_), channel_id=1, source_target_pairs={{0,1},{1,0},{2,3},{3,2},{4,5},{5,4},{6,7},{7,6},{8,9},{9,8},{10,11... | collective-permute-start | bytes 2654216 | tf_op jit(solution)/shard_map/ppermute | solution.py:19
  38.1 23.0 %collective-permute-start.3 = (bf16[4,144,768]{2,1,0:T(8,128)(2,1)}, bf16[4,144,768]{2,1,0:T(8,128)(2,1)}, u32[]{:S(2)}, u32[]{:S(2)}) collective-permute-start(bf16[4,144,768]{2,1,0:T(8,128)(2,1)} %constant_dynamic-update-slice_fusion.refs_0_.refs_4_), channel_id=1, source_target_pairs={{0,8},{8,0},{16,24},{24,16},{1,9},{9,1},{17,25},{25,17},{2,10},{10... | collective-permute-start | bytes 2654216 | tf_op jit(solution)/shard_map/ppermute | solution.py:19
  39.7 42.3 %collective-permute-start.6 = (bf16[4,144,768]{2,1,0:T(8,128)(2,1)}, bf16[4,144,768]{2,1,0:T(8,128)(2,1)}, u32[]{:S(2)}, u32[]{:S(2)}) collective-permute-start(bf16[4,144,768]{2,1,0:T(8,128)(2,1)} %constant_dynamic-update-slice_fusion.refs_0_.refs_4_), channel_id=1, source_target_pairs={{0,16},{8,24},{16,0},{24,8},{1,17},{9,25},{17,1},{25,9},{2,18},{10... | collective-permute-start | bytes 2654216 | tf_op jit(solution)/shard_map/ppermute | solution.py:19
  41.3 19.0 %collective-permute-start.4 = (bf16[1,128,512]{2,1,0:T(8,128)(2,1)S(1)}, bf16[1,128,512]{2,1,0:T(8,128)(2,1)S(1)}, u32[]{:S(2)}, u32[]{:S(2)}) collective-permute-start(bf16[1,128,512]{2,1,0:T(8,128)(2,1)S(1)} %pad_maximum_fusion.7), channel_id=1, source_target_pairs={{0,4},{1,5},{2,6},{3,7},{4,0},{5,1},{6,2},{7,3},{8,12},{9,13},{10,... | collective-permute-start | bytes 393224 | tf_op jit(solution)/shard_map/ppermute | solution.py:19
  61.1 10.4 %collective-permute-start.5 = (bf16[4,144,768]{2,1,0:T(8,128)(2,1)}, bf16[4,144,768]{2,1,0:T(8,128)(2,1)}, u32[]{:S(2)}, u32[]{:S(2)}) collective-permute-start(bf16[4,144,768]{2,1,0:T(8,128)(2,1)} %collective-permute-done.2.refs_1_.refs_5_), channel_id=1, source_target_pairs={{0,8},{8,0},{16,24},{24,16},{1,9},{9,1},{17,25},{25,17},{2,10},{10... | collective-permute-start | bytes 2654216 | tf_op jit(solution)/shard_map/ppermute | solution.py:19
  61.1 29.8 %collective-permute-start.7 = (bf16[4,144,768]{2,1,0:T(8,128)(2,1)}, bf16[4,144,768]{2,1,0:T(8,128)(2,1)}, u32[]{:S(2)}, u32[]{:S(2)}) collective-permute-start(bf16[4,144,768]{2,1,0:T(8,128)(2,1)} %collective-permute-done.2.refs_1_.refs_5_), channel_id=1, source_target_pairs={{0,16},{8,24},{16,0},{24,8},{1,17},{9,25},{17,1},{25,9},{2,18},{10... | collective-permute-start | bytes 2654216 | tf_op jit(solution)/shard_map/ppermute | solution.py:19
  66.1 24.8 %collective-permute-start.8 = (bf16[2,128,512]{2,1,0:T(8,128)(2,1)S(1)}, bf16[2,128,512]{2,1,0:T(8,128)(2,1)S(1)}, u32[]{:S(2)}, u32[]{:S(2)}) collective-permute-start(bf16[2,128,512]{2,1,0:T(8,128)(2,1)S(1)} %pad_maximum_fusion.6), channel_id=1, source_target_pairs={{0,2},{1,3},{2,0},{3,1},{4,6},{5,7},{6,4},{7,5},{8,10},{9,11},{10,... | collective-permute-start | bytes 786440 | tf_op jit(solution)/shard_map/ppermute | solution.py:19
  90.9 4.4 %collective-permute-start.9 = (bf16[4,144,768]{2,1,0:T(8,128)(2,1)}, bf16[4,144,768]{2,1,0:T(8,128)(2,1)}, u32[]{:S(2)}, u32[]{:S(2)}) collective-permute-start(bf16[4,144,768]{2,1,0:T(8,128)(2,1)} %collective-permute-done.6.refs_0_.refs_8_), channel_id=1, source_target_pairs={{0,8},{8,0},{16,24},{24,16},{1,9},{9,1},{17,25},{25,17},{2,10},{10... | collective-permute-start | bytes 2654216 | tf_op jit(solution)/shard_map/ppermute | solution.py:19
  91.4 15.3 %collective-permute-start.11 = (bf16[4,128,512]{2,1,0:T(8,128)(2,1)S(1)}, bf16[4,128,512]{2,1,0:T(8,128)(2,1)}, u32[]{:S(2)}, u32[]{:S(2)}) collective-permute-start(bf16[4,128,512]{2,1,0:T(8,128)(2,1)S(1)} %pad_maximum_fusion.2), channel_id=1, source_target_pairs={{0,1},{1,0},{2,3},{3,2},{4,5},{5,4},{6,7},{7,6},{8,9},{9,8},{10,11... | collective-permute-start | bytes 1572872 | tf_op jit(solution)/shard_map/ppermute | solution.py:19
  121.3 7.6 %collective-permute-start.13 = (bf16[8,128,2048]{2,1,0:T(8,128)(2,1)}, bf16[8,128,2048]{2,1,0:T(8,128)(2,1)}, u32[]{:S(2)}, u32[]{:S(2)}) collective-permute-start(bf16[8,128,2048]{2,1,0:T(8,128)(2,1)} %bitcast.236), channel_id=1, source_target_pairs={{0,8},{8,0},{16,24},{24,16},{1,9},{9,1},{17,25},{25,17},{2,10},{10... | collective-permute-start | bytes 12582920 | tf_op jit(solution)/shard_map/ppermute | solution.py:19
  124.6 48.1 %collective-permute-start.14 = (bf16[8,128,1024]{2,1,0:T(8,128)(2,1)}, bf16[8,128,1024]{2,1,0:T(8,128)(2,1)S(1)}, u32[]{:S(2)}, u32[]{:S(2)}) collective-permute-start(bf16[8,128,1024]{2,1,0:T(8,128)(2,1)} %slice.528), channel_id=1, source_target_pairs={{0,16},{8,24},{16,0},{24,8},{1,17},{9,25},{17,1},{25,9},{2,18},{10... | collective-permute-start | bytes 6291464 | tf_op jit(solution)/shard_map/ppermute | solution.py:19
  172.7 7.4 %collective-permute-start.15 = (bf16[8,128,1024]{2,1,0:T(8,128)(2,1)}, bf16[8,128,1024]{2,1,0:T(8,128)(2,1)S(1)}, u32[]{:S(2)}, u32[]{:S(2)}) collective-permute-start(bf16[8,128,1024]{2,1,0:T(8,128)(2,1)} %get-tuple-element.395), channel_id=1, source_target_pairs={{0,8},{8,0},{16,24},{24,16},{1,9},{9,1},{17,25},{25,17},{2,10},{10... | collective-permute-start | bytes 6291464 | tf_op jit(solution)/shard_map/ppermute | solution.py:19
  181.7 26.0 %collective-permute-start.17 = (bf16[8,128,1024]{2,1,0:T(8,128)(2,1)S(1)}, bf16[8,128,1024]{2,1,0:T(8,128)(2,1)}, u32[]{:S(2)}, u32[]{:S(2)}) collective-permute-start(bf16[8,128,1024]{2,1,0:T(8,128)(2,1)S(1)} %collective-permute-done.14.refs_2_), channel_id=1, source_target_pairs={{0,8},{8,0},{16,24},{24,16},{1,9},{9,1},{17,25},{25,17},{2,10},{10... | collective-permute-start | bytes 6291464 | tf_op jit(solution)/shard_map/ppermute | solution.py:19
  181.9 25.9 %collective-permute-start.18 = (bf16[8,128,1024]{2,1,0:T(8,128)(2,1)S(1)}, bf16[8,128,1024]{2,1,0:T(8,128)(2,1)}, u32[]{:S(2)}, u32[]{:S(2)}) collective-permute-start(bf16[8,128,1024]{2,1,0:T(8,128)(2,1)S(1)} %bitcast.243), channel_id=1, source_target_pairs={{0,8},{8,0},{16,24},{24,16},{1,9},{9,1},{17,25},{25,17},{2,10},{10... | collective-permute-start | bytes 6291464 | tf_op jit(solution)/shard_map/ppermute | solution.py:19
  182.2 25.5 %collective-permute-start.20 = (bf16[2,2,128,1024]{3,2,1,0:T(8,128)(2,1)}, bf16[2,2,128,1024]{3,2,1,0:T(8,128)(2,1)}, u32[]{:S(2)}, u32[]{:S(2)}) collective-permute-start(bf16[2,2,128,1024]{3,2,1,0:T(8,128)(2,1)} %fusion), channel_id=1, source_target_pairs={{0,2},{1,3},{2,0},{3,1},{4,6},{5,7},{6,4},{7,5},{8,10},{9,11},{10,... | collective-permute-start | bytes 3145736 | tf_op jit(solution)/shard_map/ppermute | solution.py:19
  182.2 25.5 %collective-permute-start.19 = (bf16[2,2,128,1024]{3,2,1,0:T(8,128)(2,1)S(1)}, bf16[2,2,128,1024]{3,2,1,0:T(8,128)(2,1)}, u32[]{:S(2)}, u32[]{:S(2)}) collective-permute-start(bf16[2,2,128,1024]{3,2,1,0:T(8,128)(2,1)S(1)} %bitcast.262), channel_id=1, source_target_pairs={{0,1},{1,0},{2,3},{3,2},{4,5},{5,4},{6,7},{7,6},{8,9},{9,8},{10,11... | collective-permute-start | bytes 3145736 | tf_op jit(solution)/shard_map/ppermute | solution.py:19
  210.3 23.6 %collective-permute-start.22 = (bf16[2,128,1024]{2,1,0:T(8,128)(2,1)S(1)}, bf16[2,128,1024]{2,1,0:T(8,128)(2,1)S(1)}, u32[]{:S(2)}, u32[]{:S(2)}) collective-permute-start(bf16[2,128,1024]{2,1,0:T(8,128)(2,1)S(1)} %get-tuple-element.433), channel_id=1, source_target_pairs={{0,1},{1,0},{2,3},{3,2},{4,5},{5,4},{6,7},{7,6},{8,9},{9,8},{10,11... | collective-permute-start | bytes 1572872 | tf_op jit(solution)/shard_map/ppermute | solution.py:19
  211.5 22.3 %collective-permute-start.21 = (bf16[2,128,1024]{2,1,0:T(8,128)(2,1)S(1)}, bf16[2,128,1024]{2,1,0:T(8,128)(2,1)S(1)}, u32[]{:S(2)}, u32[]{:S(2)}) collective-permute-start(bf16[2,128,1024]{2,1,0:T(8,128)(2,1)S(1)} %get-tuple-element.432), channel_id=1, source_target_pairs={{0,2},{1,3},{2,0},{3,1},{4,6},{5,7},{6,4},{7,5},{8,10},{9,11},{10,... | collective-permute-start | bytes 1572872 | tf_op jit(solution)/shard_map/ppermute | solution.py:19
  233.8 4.9 %collective-permute-start.24 = (bf16[8,128,1024]{2,1,0:T(8,128)(2,1)}, bf16[8,128,1024]{2,1,0:T(8,128)(2,1)S(1)}, u32[]{:S(2)}, u32[]{:S(2)}) collective-permute-start(bf16[8,128,1024]{2,1,0:T(8,128)(2,1)} %get-tuple-element.438), channel_id=1, source_target_pairs={{0,8},{8,0},{16,24},{24,16},{1,9},{9,1},{17,25},{25,17},{2,10},{10... | collective-permute-start | bytes 6291464 | tf_op jit(solution)/shard_map/ppermute | solution.py:19
  233.9 7.4 %collective-permute-start.23 = (bf16[8,128,1024]{2,1,0:T(8,128)(2,1)}, bf16[8,128,1024]{2,1,0:T(8,128)(2,1)S(1)}, u32[]{:S(2)}, u32[]{:S(2)}) collective-permute-start(bf16[8,128,1024]{2,1,0:T(8,128)(2,1)} %get-tuple-element.436), channel_id=1, source_target_pairs={{0,8},{8,0},{16,24},{24,16},{1,9},{9,1},{17,25},{25,17},{2,10},{10... | collective-permute-start | bytes 6291464 | tf_op jit(solution)/shard_map/ppermute | solution.py:19
  244.0 36.8 %collective-permute-start.28 = (bf16[2,2,128,1024]{3,2,1,0:T(8,128)(2,1)}, bf16[2,2,128,1024]{3,2,1,0:T(8,128)(2,1)}, u32[]{:S(2)}, u32[]{:S(2)}) collective-permute-start(bf16[2,2,128,1024]{3,2,1,0:T(8,128)(2,1)} %fusion.1), channel_id=1, source_target_pairs={{0,2},{1,3},{2,0},{3,1},{4,6},{5,7},{6,4},{7,5},{8,10},{9,11},{10,... | collective-permute-start | bytes 3145736 | tf_op jit(solution)/shard_map/ppermute | solution.py:19
  244.5 36.2 %collective-permute-start.27 = (bf16[2,2,128,1024]{3,2,1,0:T(8,128)(2,1)S(1)}, bf16[2,2,128,1024]{3,2,1,0:T(8,128)(2,1)}, u32[]{:S(2)}, u32[]{:S(2)}) collective-permute-start(bf16[2,2,128,1024]{3,2,1,0:T(8,128)(2,1)S(1)} %bitcast.261), channel_id=1, source_target_pairs={{0,1},{1,0},{2,3},{3,2},{4,5},{5,4},{6,7},{7,6},{8,9},{9,8},{10,11... | collective-permute-start | bytes 3145736 | tf_op jit(solution)/shard_map/ppermute | solution.py:19
  245.4 32.1 %collective-permute-start.26 = (bf16[128,1024]{1,0:T(8,128)(2,1)}, bf16[128,1024]{1,0:T(8,128)(2,1)S(1)}, u32[]{:S(2)}, u32[]{:S(2)}) collective-permute-start(bf16[128,1024]{1,0:T(8,128)(2,1)} %fusion.22), channel_id=1, source_target_pairs={{0,4},{1,5},{2,6},{3,7},{4,0},{5,1},{6,2},{7,3},{8,12},{9,13},{10,... | collective-permute-start | bytes 786440 | tf_op jit(solution)/shard_map/ppermute | solution.py:19
  248.1 30.7 %collective-permute-start.25 = (bf16[128,1024]{1,0:T(8,128)(2,1)}, bf16[128,1024]{1,0:T(8,128)(2,1)}, u32[]{:S(2)}, u32[]{:S(2)}) collective-permute-start(bf16[128,1024]{1,0:T(8,128)(2,1)} %fusion.21), channel_id=1, source_target_pairs={{0,4},{1,5},{2,6},{3,7},{4,0},{5,1},{6,2},{7,3},{8,12},{9,13},{10,... | collective-permute-start | bytes 786440 | tf_op jit(solution)/shard_map/ppermute | solution.py:19
  280.8 4.7 %collective-permute-start.29 = (bf16[8,128,1024]{2,1,0:T(8,128)(2,1)}, bf16[8,128,1024]{2,1,0:T(8,128)(2,1)S(1)}, u32[]{:S(2)}, u32[]{:S(2)}) collective-permute-start(bf16[8,128,1024]{2,1,0:T(8,128)(2,1)} %get-tuple-element.470), channel_id=1, source_target_pairs={{0,8},{8,0},{16,24},{24,16},{1,9},{9,1},{17,25},{25,17},{2,10},{10... | collective-permute-start | bytes 6291464 | tf_op jit(solution)/shard_map/ppermute | solution.py:19
  287.9 25.6 %collective-permute-start.32 = (bf16[4,128,1024]{2,1,0:T(8,128)(2,1)}, bf16[4,128,1024]{2,1,0:T(8,128)(2,1)S(1)}, u32[]{:S(2)}, u32[]{:S(2)}) collective-permute-start(bf16[4,128,1024]{2,1,0:T(8,128)(2,1)} %get-tuple-element.490), channel_id=1, source_target_pairs={{0,16},{8,24},{16,0},{24,8},{1,17},{9,25},{17,1},{25,9},{2,18},{10... | collective-permute-start | bytes 3145736 | tf_op jit(solution)/shard_map/ppermute | solution.py:19
  288.6 21.2 %collective-permute-start.31 = (bf16[2,128,1024]{2,1,0:T(8,128)(2,1)}, bf16[2,128,1024]{2,1,0:T(8,128)(2,1)}, u32[]{:S(2)}, u32[]{:S(2)}) collective-permute-start(bf16[2,128,1024]{2,1,0:T(8,128)(2,1)} %fusion.5), channel_id=1, source_target_pairs={{0,1},{1,0},{2,3},{3,2},{4,5},{5,4},{6,7},{7,6},{8,9},{9,8},{10,11... | collective-permute-start | bytes 1572872 | tf_op jit(solution)/shard_map/ppermute | solution.py:19
  289.2 20.5 %collective-permute-start.30 = (bf16[2,128,1024]{2,1,0:T(8,128)(2,1)}, bf16[2,128,1024]{2,1,0:T(8,128)(2,1)}, u32[]{:S(2)}, u32[]{:S(2)}) collective-permute-start(bf16[2,128,1024]{2,1,0:T(8,128)(2,1)} %fusion.4), channel_id=1, source_target_pairs={{0,2},{1,3},{2,0},{3,1},{4,6},{5,7},{6,4},{7,5},{8,10},{9,11},{10,... | collective-permute-start | bytes 1572872 | tf_op jit(solution)/shard_map/ppermute | solution.py:19
  319.5 27.2 %collective-permute-start.37 = (bf16[4,128,1024]{2,1,0:T(8,128)(2,1)}, bf16[4,128,1024]{2,1,0:T(8,128)(2,1)S(1)}, u32[]{:S(2)}, u32[]{:S(2)}) collective-permute-start(bf16[4,128,1024]{2,1,0:T(8,128)(2,1)} %get-tuple-element.514), channel_id=1, source_target_pairs={{0,16},{8,24},{16,0},{24,8},{1,17},{9,25},{17,1},{25,9},{2,18},{10... | collective-permute-start | bytes 3145736 | tf_op jit(solution)/shard_map/ppermute | solution.py:19
  320.2 26.5 %collective-permute-start.36 = (bf16[2,2,128,1024]{3,2,1,0:T(8,128)(2,1)}, bf16[2,2,128,1024]{3,2,1,0:T(8,128)(2,1)}, u32[]{:S(2)}, u32[]{:S(2)}) collective-permute-start(bf16[2,2,128,1024]{3,2,1,0:T(8,128)(2,1)} %bitcast.56), channel_id=1, source_target_pairs={{0,1},{1,0},{2,3},{3,2},{4,5},{5,4},{6,7},{7,6},{8,9},{9,8},{10,11... | collective-permute-start | bytes 3145736 | tf_op jit(solution)/shard_map/ppermute | solution.py:19
  320.9 21.7 %collective-permute-start.35 = (bf16[128,1024]{1,0:T(8,128)(2,1)}, bf16[128,1024]{1,0:T(8,128)(2,1)}, u32[]{:S(2)}, u32[]{:S(2)}) collective-permute-start(bf16[128,1024]{1,0:T(8,128)(2,1)} %fusion.20), channel_id=1, source_target_pairs={{0,4},{1,5},{2,6},{3,7},{4,0},{5,1},{6,2},{7,3},{8,12},{9,13},{10,... | collective-permute-start | bytes 786440 | tf_op jit(solution)/shard_map/ppermute | solution.py:19
  322.4 24.4 %collective-permute-start.34 = (bf16[128,1024]{1,0:T(8,128)(2,1)}, bf16[128,1024]{1,0:T(8,128)(2,1)}, u32[]{:S(2)}, u32[]{:S(2)}) collective-permute-start(bf16[128,1024]{1,0:T(8,128)(2,1)} %fusion.19), channel_id=1, source_target_pairs={{0,4},{1,5},{2,6},{3,7},{4,0},{5,1},{6,2},{7,3},{8,12},{9,13},{10,... | collective-permute-start | bytes 786440 | tf_op jit(solution)/shard_map/ppermute | solution.py:19
  350.8 6.9 %collective-permute-start.38 = (f32[8,16,128]{2,1,0:T(8,128)}, f32[8,16,128]{2,1,0:T(8,128)S(1)}, u32[]{:S(2)}, u32[]{:S(2)}) collective-permute-start(f32[8,16,128]{2,1,0:T(8,128)} %pack_sums.1), channel_id=1, source_target_pairs={{0,8},{8,0},{16,24},{24,16},{1,9},{9,1},{17,25},{25,17},{2,10},{10... | collective-permute-start | bytes 196616 | tf_op jit(solution)/shard_map/ppermute | solution.py:19
  350.8 6.9 %collective-permute-start.39 = (f32[8,16,128]{2,1,0:T(8,128)}, f32[8,16,128]{2,1,0:T(8,128)S(1)}, u32[]{:S(2)}, u32[]{:S(2)}) collective-permute-start(f32[8,16,128]{2,1,0:T(8,128)} %pack_sums.1), channel_id=1, source_target_pairs={{0,16},{8,24},{16,0},{24,8},{1,17},{9,25},{17,1},{25,9},{2,18},{10... | collective-permute-start | bytes 196616 | tf_op jit(solution)/shard_map/ppermute | solution.py:19
  352.3 5.4 %collective-permute-start.40 = (f32[8,16,128]{2,1,0:T(8,128)}, f32[8,16,128]{2,1,0:T(8,128)S(1)}, u32[]{:S(2)}, u32[]{:S(2)}) collective-permute-start(f32[8,16,128]{2,1,0:T(8,128)} %pack_sums.1), channel_id=1, source_target_pairs={{0,24},{8,16},{16,8},{24,0},{1,25},{9,17},{17,9},{25,1},{2,26},{10... | collective-permute-start | bytes 196616 | tf_op jit(solution)/shard_map/ppermute | solution.py:19
  352.7 14.3 %collective-permute-start.41 = (bf16[2,128,1024]{2,1,0:T(8,128)(2,1)}, bf16[2,128,1024]{2,1,0:T(8,128)(2,1)S(1)}, u32[]{:S(2)}, u32[]{:S(2)}) collective-permute-start(bf16[2,128,1024]{2,1,0:T(8,128)(2,1)} %fusion.3), channel_id=1, source_target_pairs={{0,2},{1,3},{2,0},{3,1},{4,6},{5,7},{6,4},{7,5},{8,10},{9,11},{10,... | collective-permute-start | bytes 1572872 | tf_op jit(solution)/shard_map/ppermute | solution.py:19
  356.2 19.2 %collective-permute-start.44 = (bf16[2,128,1024]{2,1,0:T(8,128)(2,1)S(1)}, bf16[2,128,1024]{2,1,0:T(8,128)(2,1)S(1)}, u32[]{:S(2)}, u32[]{:S(2)}) collective-permute-start(bf16[2,128,1024]{2,1,0:T(8,128)(2,1)S(1)} %pad_maximum_fusion.3), channel_id=1, source_target_pairs={{0,16},{8,24},{16,0},{24,8},{1,17},{9,25},{17,1},{25,9},{2,18},{10... | collective-permute-start | bytes 1572872 | tf_op jit(solution)/shard_map/ppermute | solution.py:19
  373.0 13.4 %collective-permute-start.46 = (bf16[128,1024]{1,0:T(8,128)(2,1)S(1)}, bf16[128,1024]{1,0:T(8,128)(2,1)S(1)}, u32[]{:S(2)}, u32[]{:S(2)}) collective-permute-start(bf16[128,1024]{1,0:T(8,128)(2,1)S(1)} %fusion.12), channel_id=1, source_target_pairs={{0,4},{1,5},{2,6},{3,7},{4,0},{5,1},{6,2},{7,3},{8,12},{9,13},{10,... | collective-permute-start | bytes 786440 | tf_op jit(solution)/shard_map/ppermute | solution.py:19
  379.2 13.7 %collective-permute-start.47 = (bf16[2,128,1024]{2,1,0:T(8,128)(2,1)}, bf16[2,128,1024]{2,1,0:T(8,128)(2,1)}, u32[]{:S(2)}, u32[]{:S(2)}) collective-permute-start(bf16[2,128,1024]{2,1,0:T(8,128)(2,1)} %pad_maximum_fusion.4.refs_0_), channel_id=1, source_target_pairs={{0,8},{8,0},{16,24},{24,16},{1,9},{9,1},{17,25},{25,17},{2,10},{10... | collective-permute-start | bytes 1572872 | tf_op jit(solution)/shard_map/ppermute | solution.py:19
  379.2 14.7 %collective-permute-start.48 = (bf16[2,128,1024]{2,1,0:T(8,128)(2,1)}, bf16[2,128,1024]{2,1,0:T(8,128)(2,1)}, u32[]{:S(2)}, u32[]{:S(2)}) collective-permute-start(bf16[2,128,1024]{2,1,0:T(8,128)(2,1)} %pad_maximum_fusion.4.refs_0_), channel_id=1, source_target_pairs={{0,16},{8,24},{16,0},{24,8},{1,17},{9,25},{17,1},{25,9},{2,18},{10... | collective-permute-start | bytes 1572872 | tf_op jit(solution)/shard_map/ppermute | solution.py:19
  380.8 5.6 %collective-permute-start.45 = (f32[16,128]{1,0:T(8,128)S(1)}, f32[16,128]{1,0:T(8,128)S(1)}, u32[]{:S(2)}, u32[]{:S(2)}) collective-permute-start(f32[16,128]{1,0:T(8,128)S(1)} %bitcast_add_fusion.3), channel_id=1, source_target_pairs={{0,4},{1,5},{2,6},{3,7},{4,0},{5,1},{6,2},{7,3},{8,12},{9,13},{10,... | collective-permute-start | bytes 24584 | tf_op jit(solution)/shard_map/ppermute | solution.py:19
  393.9 8.7 %collective-permute-start.49 = (bf16[2,128,1024]{2,1,0:T(8,128)(2,1)}, bf16[2,128,1024]{2,1,0:T(8,128)(2,1)S(1)}, u32[]{:S(2)}, u32[]{:S(2)}) collective-permute-start(bf16[2,128,1024]{2,1,0:T(8,128)(2,1)} %collective-permute-done.48.refs_2_), channel_id=1, source_target_pairs={{0,8},{8,0},{16,24},{24,16},{1,9},{9,1},{17,25},{25,17},{2,10},{10... | collective-permute-start | bytes 1572872 | tf_op jit(solution)/shard_map/ppermute | solution.py:19
  394.4 8.2 %collective-permute-start.51 = (bf16[128,1024]{1,0:T(8,128)(2,1)S(1)}, bf16[128,1024]{1,0:T(8,128)(2,1)S(1)}, u32[]{:S(2)}, u32[]{:S(2)}) collective-permute-start(bf16[128,1024]{1,0:T(8,128)(2,1)S(1)} %fusion.14.refs_0_), channel_id=1, source_target_pairs={{0,16},{8,24},{16,0},{24,8},{1,17},{9,25},{17,1},{25,9},{2,18},{10... | collective-permute-start | bytes 786440 | tf_op jit(solution)/shard_map/ppermute | solution.py:19
  402.6 5.3 %collective-permute-start.52 = (bf16[128,1024]{1,0:T(8,128)(2,1)S(1)}, bf16[128,1024]{1,0:T(8,128)(2,1)S(1)}, u32[]{:S(2)}, u32[]{:S(2)}) collective-permute-start(bf16[128,1024]{1,0:T(8,128)(2,1)S(1)} %collective-permute-done.51.refs_2_), channel_id=1, source_target_pairs={{0,8},{8,0},{16,24},{24,16},{1,9},{9,1},{17,25},{25,17},{2,10},{10... | collective-permute-start | bytes 786440 | tf_op jit(solution)/shard_map/ppermute | solution.py:19
  (50 other events, 342.8 us)
Sparse Core Ops, SparseCore 0:
  24.4 81.8 all-gather.4
  121.6 48.5 all-gather.6
where the time goes:
time: 423 us; the launch traced here: 418 us
  Pallas kernels  190 us (45%)
  waiting for transfers between devices  86.8 us (21%)
  starting transfers between devices  51.2 us (12%)
  other arithmetic  45.7 us (11%)
  local copies, waits for them, and re-layouts  29.3 us (7%)
  between operations  15 us (4%)
    pallas_call x17, Pallas kernels, call(): pl.pallas_call(kernel, out_shape=[jax.ShapeDtypeStruct(shape, kind) for s...  190 us
    ppermute x53, waiting for transfers between devices, xor_swap(): return lax.ppermute(value, axis, [(i, i ^ mask) for i in range(size)])  84.8 us
    ppermute x53, starting transfers between devices, xor_swap(): return lax.ppermute(value, axis, [(i, i ^ mask) for i in range(size)])  51.2 us
    convert_element_type x16, other arithmetic, rounded_sum(): return sum((t.astype(full) for t in terms)).astype(kind)  30.4 us
  transfers between devices with their start and end apart: 55, of which 25 were waited for; matrix products, arithmetic and copies ran while one was open for 14% of the time, Pallas kernels for 44%

commit v1 on v0

--- a/solution.py
+++ b/solution.py
@@ -1009,10 +1009,13 @@
         seq.at(order), normed_one, bias_qkv[2:], ((near_c, far_c), (near_d.value, far_d.value)),
         n_img, patches, factor,
     )
-    second = (seq.land(second[0], out), *second[1:])
+    second = (seq.land(second[0], out, rest), *second[1:])
     out_a = seq.at(out.join())
     out_b = Sent(core_swap(out_a))
     seq.land((), out_b)
+    rest_a = seq.at(rest.value)
+    rest_b = Sent(core_swap(rest_a))
+    up_c = Sent(x_swap(seq.at(rest_a[:, :, :hidden])))
     outs = (out_a, out_b.value)
     qkv_parts = (
         (qkv_near, qkv_far), (near_b.value, far_b.value), (near_c, far_c), (near_d.value, far_d.value)
@@ -1023,11 +1026,7 @@
     after_attn, normed_two = attention_out(
         seq.at(order), x_zero, mixed, outs, full_bout, gain_two_f, shift_two_f
     )
-    normed_two = seq.land(normed_two, rest)
-    rest_a = seq.at(rest.value)
-    rest_b = Sent(core_swap(rest_a))
-    up_c = Sent(x_swap(seq.at(rest_a[:, :, :hidden])))
-    seq.land((), rest_b)
+    normed_two = seq.land(normed_two, rest_b)
 
     up_g1, down_g1, g_bias_1, back_sum, out_sum = mlp(
         seq.at(order), normed_two, cot, bias_fc1[1], rest_b.value, rest_b.value, hidden
@@ -1119,32 +1118,28 @@
     peers = Sent([xor_swap(packed, "dp", 4, m) for m in (1, 2, 3)])
     crossing = jnp.stack([two_up.rest().piece(), two_down.rest().piece()])
     cross = Sent(x_swap(seq.at(crossing)))
-    seq.land((), peers, red_w)
+    seq.land((), peers, red_w, cross)
     if red_w.axes:
         red_w.launch()
-    sums = Reduce(seq, (packed, *peers.value), n, full)
-    while len(sums.axes) > 2:
-        sums.launch()
-        seq.land((), sums)
-    if len(sums.axes) > 1:
-        sums.launch()
-        seq.land((), sums, cross)
-    else:
-        seq.land((), cross)
     owned = [rounded_sum([*red_up.rest().terms, cross.value[0]]), rounded_sum([*red_down.rest().terms, cross.value[1]])]
     mlp_spread = Spread(seq, jnp.stack(owned))
+    sums = Reduce(seq, (packed, *peers.value), n, full)
+    while len(sums.axes) > 1:
+        sums.launch()
+        if len(sums.axes) > 1:
+            seq.land((), sums)
+    seq.land((), *([sums, red_w] if len(bits) > 1 else []))
+    w_spread = Spread(seq, red_w.piece())
     sums.launch()
-    seq.land((), sums, *([red_w] if len(bits) > 1 else []))
-    w_spread = Spread(seq, red_w.piece())
-    small_sums = sums.piece()
     block, tokens_grad = seq.at((block, tokens_grad))
-    block_out, grad_tokens = seq.land((compact(block), compact(tokens_grad)), mlp_spread)
+    block_out, grad_tokens = seq.land((compact(block), compact(tokens_grad)), sums, mlp_spread)
     mlp_spread.cross()
-    small_sums = seq.land(small_sums, mlp_spread, w_spread)
-    w_spread.cross()
+    small_sums = seq.land(sums.piece(), mlp_spread)
     mlp_pieces = seq.at(mlp_spread.pieces)
     out_fc1, out_fc2 = finish_mlp(q, mlp_pieces, n)
     out_fc2 = seq.land(out_fc2, w_spread)
+    w_spread.cross()
+    seq.land((), w_spread)
     out_qkv, out_out = finish_attention(seq.value, w_spread.pieces)
     small_out = [small_sums[k, :rows] for k in range(8)]
     out_bfc1 = small_sums[8:12, :ffq].reshape(-1)

time: 423 us -> 416 us (0.983)
  waiting for transfers between devices: 86.8 us -> 77.3 us
    ppermute x53, waiting for transfers between devices: 84.8 us -> 77.2 us  [xor_swap(): return lax.ppermute(value, axis, [(i, i ^ mask) for i in range(size)])]
  transfers between devices with their start and end apart: 55 -> 55, of which waited for: 25 -> 23; matrix products, arithmetic and copies ran while one was open for 14% -> 12% of each run, Pallas kernels for 44% -> 45%
where the time goes in v1:
time: 416 us; the launch traced here: 410 us
  Pallas kernels  191 us (46%)
  waiting for transfers between devices  77.3 us (19%)
  starting transfers between devices  51.9 us (12%)
  other arithmetic  45.7 us (11%)
  local copies, waits for them, and re-layouts  29.2 us (7%)
  between operations  15 us (4%)
    pallas_call x17, Pallas kernels, call(): pl.pallas_call(kernel, out_shape=[jax.ShapeDtypeStruct(shape, kind) for s...  191 us
    ppermute x53, waiting for transfers between devices, xor_swap(): return lax.ppermute(value, axis, [(i, i ^ mask) for i in range(size)])  77.2 us
    ppermute x53, starting transfers between devices, xor_swap(): return lax.ppermute(value, axis, [(i, i ^ mask) for i in range(size)])  51.8 us
    convert_element_type x16, other arithmetic, rounded_sum(): return sum((t.astype(full) for t in terms)).astype(kind)  29.8 us
  transfers between devices with their start and end apart: 55, of which 23 were waited for; matrix products, arithmetic and copies ran while one was open for 12% of the time, Pallas kernels for 45%

profile of v1, /device:TPU:0, one launch (start us, length us, event | category | flops | bytes accessed | tf_op | source)
XLA Modules:
  0.0 410.5 jit_solution(10411632323175630121)
XLA Ops:
  7.2 2.6 first_payload.1
  9.8 4.1 collective-permute-start
  14.5 3.3 payloads.1
  17.8 6.5 %collective-permute-done = bf16[1,144,768]{2,1,0:T(8,128)(2,1)S(1)} collective-permute-done((bf16[1,144,768]{2,1,0:T(8,128)(2,1)}, bf16[1,144,768]{2,1,0:T(8,128)(2,1)S(1)}, u32[]{:S(2)}, u32[]{:S(2)}) %collective-permute-start) | collective-permute-done | bytes 221216 | tf_op jit(solution)/shard_map/ppermute | solution.py:19
  27.5 3.6 copy.32
  31.1 2.1 reshape.461
  41.3 6.6 %collective-permute-start.4 = (bf16[1,128,512]{2,1,0:T(8,128)(2,1)S(1)}, bf16[1,128,512]{2,1,0:T(8,128)(2,1)S(1)}, u32[]{:S(2)}, u32[]{:S(2)}) collective-permute-start(bf16[1,128,512]{2,1,0:T(8,128)(2,1)S(1)} %pad_maximum_fusion.7), channel_id=1, source_target_pairs={{0,4},{1,5},{2,6},{3,7},{4,0},{5,1},{6,2},{7,3},{8,12},{9,13},{10,... | collective-permute-start | bytes 393224 | tf_op jit(solution)/shard_map/ppermute | solution.py:19
  48.7 11.6 %collective-permute-done.4 = bf16[1,128,512]{2,1,0:T(8,128)(2,1)S(1)} collective-permute-done((bf16[1,128,512]{2,1,0:T(8,128)(2,1)S(1)}, bf16[1,128,512]{2,1,0:T(8,128)(2,1)S(1)}, u32[]{:S(2)}, u32[]{:S(2)}) %collective-permute-start.4) | collective-permute-done | bytes 131104 | tf_op jit(solution)/shard_map/ppermute | solution.py:19
  63.8 2.3 unpack_vectors.1
  69.1 1.8 add_convert_fusion.normed_ref
  71.5 10.5 %attention_forward.2 = (bf16[832,768]{1,0:T(8,128)(2,1)}, bf16[832,768]{1,0:T(8,128)(2,1)}, bf16[832,256]{1,0:T(8,128)(2,1)}, bf16[832,256]{1,0:T(8,128)(2,1)}, ...) custom-call(s32[9]{0:T(128)} %pad_add_fusion.1.order_ref, bf16[832,1024]{1,0:T(8,128)(2,1)} %add_convert_fusion.normed_ref, ...), custom_call_target="tpu_custom_call" | custom-call | tf_op jit(solution)/shard_map/attention_forward/pallas_call | solution.py:133
  82.0 8.9 %collective-permute-done.8 = bf16[2,128,512]{2,1,0:T(8,128)(2,1)S(1)} collective-permute-done((bf16[2,128,512]{2,1,0:T(8,128)(2,1)S(1)}, bf16[2,128,512]{2,1,0:T(8,128)(2,1)S(1)}, u32[]{:S(2)}, u32[]{:S(2)}) %collective-permute-start.8) | collective-permute-done | bytes 262176 | tf_op jit(solution)/shard_map/ppermute | solution.py:19
  96.2 10.5 %attention_forward.3 = (bf16[832,768]{1,0:T(8,128)(2,1)}, bf16[832,768]{1,0:T(8,128)(2,1)}, bf16[832,256]{1,0:T(8,128)(2,1)}, bf16[832,256]{1,0:T(8,128)(2,1)}, ...) custom-call(s32[9]{0:T(128)} %pad_add_fusion.1.order_ref, bf16[832,1024]{1,0:T(8,128)(2,1)} %add_convert_fusion.normed_ref, ...), custom_call_target="tpu_custom_call" | custom-call | tf_op jit(solution)/shard_map/attention_forward/pallas_call | solution.py:133
  108.0 2.6 collective-permute-done.12.refs_5_
  110.9 3.3 slice.528
  115.8 9.8 %attention_out.1 = (f32[832,1024]{1,0:T(8,128)}, bf16[832,1024]{1,0:T(8,128)(2,1)}) custom-call(s32[9]{0:T(128)} %pad_add_fusion.1.order_ref, f32[832,1024]{1,0:T(8,128)} %bitcast.229, f32[1,1024]{1,0:T(1,128)} %get-tuple-element.601.bias_ref, f32[1,1024]{1,0:T(1,128)} %get-tuple-element.600.gain_ref, f32[1,1024]{1,0:T(1,128)} %get-tuple-element.599.shift_ref, ...), custom_call_target="tpu_custom_call" | custom-call | tf_op jit(solution)/shard_map/attention_out/pallas_call | solution.py:133
  125.6 19.2 %mlp.4 = (bf16[8,128,1024]{2,1,0:T(8,128)(2,1)}, bf16[8,128,1024]{2,1,0:T(8,128)(2,1)}, f32[1,1024]{1,0:T(1,128)}, f32[832,1024]{1,0:T(8,128)}, f32[832,1024]{1,0:T(8,128)}) custom-call(s32[9]{0:T(128)} %pad_add_fusion.1.order_ref, f32[1,1024]{1,0:T(1,128)} %get-tuple-element.606.bias_ref, bf16[832,1024]{1,0:T(8,128)(2,1)} %get-tuple-element.377.refs_0_.refs_1_, ...), custom_call_target="tpu_custom_call" | custom-call | tf_op jit(solution)/shard_map/mlp/pallas_call | solution.py:133
  144.8 20.4 %mlp.5 = (bf16[8,128,1024]{2,1,0:T(8,128)(2,1)}, bf16[8,128,1024]{2,1,0:T(8,128)(2,1)}, f32[1,1024]{1,0:T(1,128)}, f32[832,1024]{1,0:T(8,128)}, f32[832,1024]{1,0:T(8,128)}) custom-call(s32[9]{0:T(128)} %pad_add_fusion.1.order_ref, f32[1,1024]{1,0:T(1,128)} %get-tuple-element.607.bias_ref, bf16[832,1024]{1,0:T(8,128)(2,1)} %get-tuple-element.377.refs_0_.refs_1_, ...), custom_call_target="tpu_custom_call" | custom-call | tf_op jit(solution)/shard_map/mlp/pallas_call | solution.py:133
  165.9 3.9 collective-permute-done.16
  169.7 2.4 add_convert_fusion.7
  177.7 20.5 %mlp.6 = (bf16[8,128,1024]{2,1,0:T(8,128)(2,1)}, bf16[8,128,1024]{2,1,0:T(8,128)(2,1)}, f32[1,1024]{1,0:T(1,128)}, f32[832,1024]{1,0:T(8,128)}, f32[832,1024]{1,0:T(8,128)}) custom-call(s32[9]{0:T(128)} %pad_add_fusion.1.order_ref, f32[1,1024]{1,0:T(1,128)} %get-tuple-element.605.bias_ref, bf16[832,1024]{1,0:T(8,128)(2,1)} %get-tuple-element.377.refs_0_.refs_1_, ...), custom_call_target="tpu_custom_call" | custom-call | tf_op jit(solution)/shard_map/mlp/pallas_call | solution.py:133
  198.2 2.2 collective-permute-done.20
  201.3 3.2 fusion.6
  206.7 21.1 %mlp.7 = (bf16[8,128,1024]{2,1,0:T(8,128)(2,1)}, bf16[8,128,1024]{2,1,0:T(8,128)(2,1)}, f32[1,1024]{1,0:T(1,128)}, f32[832,1024]{1,0:T(8,128)}, bf16[832,1024]{1,0:T(8,128)(2,1)}) custom-call(s32[9]{0:T(128)} %pad_add_fusion.1.order_ref, f32[1,1024]{1,0:T(1,128)} %get-tuple-element.604.bias_ref, f32[1,1024]{1,0:T(1,128)} %get-tuple-element.598.refs_0_, ...), custom_call_target="tpu_custom_call" | custom-call | tf_op jit(solution)/shard_map/mlp/pallas_call | solution.py:133
  228.4 2.2 fusion.21
  230.6 2.1 fusion.22
  233.2 2.1 collective-permute-done.23
  239.9 2.1 collective-permute-start.26
  242.8 11.0 %attention_out_back.1 = (f32[832,1024]{1,0:T(8,128)}, bf16[832,256]{1,0:T(8,128)(2,1)}, bf16[832,256]{1,0:T(8,128)(2,1)}, bf16[832,256]{1,0:T(8,128)(2,1)}, bf16...) custom-call(s32[9]{0:T(128)} %pad_add_fusion.1.order_ref, ...), custom_call_target="tpu_custom_call" | custom-call | tf_op jit(solution)/shard_map/attention_out_back/pallas_call | solution.py:133
  253.8 18.1 %attention_back.2 = (bf16[8,128,1024]{2,1,0:T(8,128)(2,1)}, bf16[8,128,1024]{2,1,0:T(8,128)(2,1)}, bf16[832,768]{1,0:T(8,128)(2,1)}, bf16[832,768]{1,0:T(8,128)(2,1)}, f32[2,1,768]{2,1,0:T(1,128)}) custom-call(s32[9]{0:T(128)} %pad_add_fusion.1.order_ref, bf16[832,1024]{1,0:T(8,128)(2,1)} %add_convert_fusion.normed_ref, ...), custom_call_target="tpu_custom_call" | custom-call | tf_op jit(solution)/shard_map/attention_back/pallas_call | solution.py:133
  274.8 2.4 fusion.4
  277.2 2.3 fusion.5
  279.5 2.4 add_convert_fusion.2
  283.4 2.1 collective-permute-start.30
  285.5 18.0 %attention_back.3 = (bf16[8,128,1024]{2,1,0:T(8,128)(2,1)}, bf16[8,128,1024]{2,1,0:T(8,128)(2,1)}, bf16[832,768]{1,0:T(8,128)(2,1)}, bf16[832,768]{1,0:T(8,128)(2,1)}, f32[2,1,768]{2,1,0:T(1,128)}) custom-call(s32[9]{0:T(128)} %pad_add_fusion.1.order_ref, bf16[832,1024]{1,0:T(8,128)(2,1)} %add_convert_fusion.normed_ref, ...), custom_call_target="tpu_custom_call" | custom-call | tf_op jit(solution)/shard_map/attention_back/pallas_call | solution.py:133
  303.5 4.0 collective-permute-done.32
  308.7 2.0 fusion.20
  319.2 15.9 %input_back.1 = (f32[832,1024]{1,0:T(8,128)}, f32[2,1,1024]{2,1,0:T(1,128)}) custom-call(s32[9]{0:T(128)} %pad_add_fusion.1.order_ref, f32[832,1024]{1,0:T(8,128)} %bitcast.230, f32[832,1024]{1,0:T(8,128)} %get-tuple-element.502.after_ref, f32[1,1024]{1,0:T(1,128)} %get-tuple-element.597.gain_ref, bf16[832,768]{1,0:T(8,128)(2,1)} %get-tuple-element.503.refs_0_, ...), custom_call_target="tpu_custom_call" | custom-call | tf_op jit(solution)/shard_map/input_back/pallas_call | solution.py:133
  336.8 4.2 %collective-permute-done.34 = bf16[128,1024]{1,0:T(8,128)(2,1)} collective-permute-done((bf16[128,1024]{1,0:T(8,128)(2,1)S(1)}, bf16[128,1024]{1,0:T(8,128)(2,1)}, u32[]{:S(2)}, u32[]{:S(2)}) %collective-permute-start.34) | collective-permute-done | bytes 262176 | tf_op jit(solution)/shard_map/ppermute | solution.py:19
  343.8 1.8 fusion.3
  351.5 10.3 %collective-permute-done.39 = f32[8,16,128]{2,1,0:T(8,128)S(1)} collective-permute-done((f32[8,16,128]{2,1,0:T(8,128)}, f32[8,16,128]{2,1,0:T(8,128)S(1)}, u32[]{:S(2)}, u32[]{:S(2)}) %collective-permute-start.39) | collective-permute-done | bytes 65568 | tf_op jit(solution)/shard_map/ppermute | solution.py:19
  363.3 2.2 fusion.25
  370.3 2.2 collective-permute-start.44
  372.5 1.8 collective-permute-done.44
  374.3 8.2 %collective-permute-done.45 = bf16[128,1024]{1,0:T(8,128)(2,1)S(1)} collective-permute-done((bf16[128,1024]{1,0:T(8,128)(2,1)S(1)}, bf16[128,1024]{1,0:T(8,128)(2,1)S(1)}, u32[]{:S(2)}, u32[]{:S(2)}) %collective-permute-start.45) | collective-permute-done | bytes 262176 | tf_op jit(solution)/shard_map/ppermute | solution.py:19
  384.9 1.9 reshape.473
  393.2 3.9 finish_mlp.1
  400.8 2.6 finish_attention.1
  (235 shorter events, 86.8 us)
Async XLA Ops:
  7.2 99.6 %all-gather.5.cloned.1.call-start = ((), (), s32[]{:S(2)}) async-start(), calls=%async_computation | async-start | bytes 4718592 | tf_op jit(solution)/shard_map/all_gather | solution.py:963
  9.8 14.5 %collective-permute-start = (bf16[1,144,768]{2,1,0:T(8,128)(2,1)}, bf16[1,144,768]{2,1,0:T(8,128)(2,1)S(1)}, u32[]{:S(2)}, u32[]{:S(2)}) collective-permute-start(bf16[1,144,768]{2,1,0:T(8,128)(2,1)} %bitcast.263), channel_id=1, source_target_pairs={{0,4},{1,5},{2,6},{3,7},{4,0},{5,1},{6,2},{7,3},{8,12},{9,13},{10,... | collective-permute-start | bytes 663560 | tf_op jit(solution)/shard_map/ppermute | solution.py:19
  24.3 141.0 %all-gather.7.cloned.1.call-start = ((), (), s32[]{:S(2)}) async-start(), calls=%async_computation.1 | async-start | bytes 2359296 | tf_op jit(solution)/shard_map/all_gather | solution.py:964
  24.5 11.4 %collective-permute-start.1 = (bf16[2,144,768]{2,1,0:T(8,128)(2,1)S(1)}, bf16[2,144,768]{2,1,0:T(8,128)(2,1)S(1)}, u32[]{:S(2)}, u32[]{:S(2)}) collective-permute-start(bf16[2,144,768]{2,1,0:T(8,128)(2,1)S(1)} %pad_maximum_fusion.5), channel_id=1, source_target_pairs={{0,2},{1,3},{2,0},{3,1},{4,6},{5,7},{6,4},{7,5},{8,10},{9,11},{10,... | collective-permute-start | bytes 1327112 | tf_op jit(solution)/shard_map/ppermute | solution.py:19
  36.8 24.4 %collective-permute-start.2 = (bf16[4,144,768]{2,1,0:T(8,128)(2,1)}, bf16[4,144,768]{2,1,0:T(8,128)(2,1)}, u32[]{:S(2)}, u32[]{:S(2)}) collective-permute-start(bf16[4,144,768]{2,1,0:T(8,128)(2,1)} %constant_dynamic-update-slice_fusion.refs_0_.refs_4_), channel_id=1, source_target_pairs={{0,1},{1,0},{2,3},{3,2},{4,5},{5,4},{6,7},{7,6},{8,9},{9,8},{10,11... | collective-permute-start | bytes 2654216 | tf_op jit(solution)/shard_map/ppermute | solution.py:19
  38.1 23.0 %collective-permute-start.3 = (bf16[4,144,768]{2,1,0:T(8,128)(2,1)}, bf16[4,144,768]{2,1,0:T(8,128)(2,1)}, u32[]{:S(2)}, u32[]{:S(2)}) collective-permute-start(bf16[4,144,768]{2,1,0:T(8,128)(2,1)} %constant_dynamic-update-slice_fusion.refs_0_.refs_4_), channel_id=1, source_target_pairs={{0,8},{8,0},{16,24},{24,16},{1,9},{9,1},{17,25},{25,17},{2,10},{10... | collective-permute-start | bytes 2654216 | tf_op jit(solution)/shard_map/ppermute | solution.py:19
  39.7 42.3 %collective-permute-start.6 = (bf16[4,144,768]{2,1,0:T(8,128)(2,1)}, bf16[4,144,768]{2,1,0:T(8,128)(2,1)}, u32[]{:S(2)}, u32[]{:S(2)}) collective-permute-start(bf16[4,144,768]{2,1,0:T(8,128)(2,1)} %constant_dynamic-update-slice_fusion.refs_0_.refs_4_), channel_id=1, source_target_pairs={{0,16},{8,24},{16,0},{24,8},{1,17},{9,25},{17,1},{25,9},{2,18},{10... | collective-permute-start | bytes 2654216 | tf_op jit(solution)/shard_map/ppermute | solution.py:19
  41.3 19.0 %collective-permute-start.4 = (bf16[1,128,512]{2,1,0:T(8,128)(2,1)S(1)}, bf16[1,128,512]{2,1,0:T(8,128)(2,1)S(1)}, u32[]{:S(2)}, u32[]{:S(2)}) collective-permute-start(bf16[1,128,512]{2,1,0:T(8,128)(2,1)S(1)} %pad_maximum_fusion.7), channel_id=1, source_target_pairs={{0,4},{1,5},{2,6},{3,7},{4,0},{5,1},{6,2},{7,3},{8,12},{9,13},{10,... | collective-permute-start | bytes 393224 | tf_op jit(solution)/shard_map/ppermute | solution.py:19
  61.1 10.4 %collective-permute-start.5 = (bf16[4,144,768]{2,1,0:T(8,128)(2,1)}, bf16[4,144,768]{2,1,0:T(8,128)(2,1)}, u32[]{:S(2)}, u32[]{:S(2)}) collective-permute-start(bf16[4,144,768]{2,1,0:T(8,128)(2,1)} %collective-permute-done.2.refs_1_.refs_5_), channel_id=1, source_target_pairs={{0,8},{8,0},{16,24},{24,16},{1,9},{9,1},{17,25},{25,17},{2,10},{10... | collective-permute-start | bytes 2654216 | tf_op jit(solution)/shard_map/ppermute | solution.py:19
  61.1 29.8 %collective-permute-start.7 = (bf16[4,144,768]{2,1,0:T(8,128)(2,1)}, bf16[4,144,768]{2,1,0:T(8,128)(2,1)}, u32[]{:S(2)}, u32[]{:S(2)}) collective-permute-start(bf16[4,144,768]{2,1,0:T(8,128)(2,1)} %collective-permute-done.2.refs_1_.refs_5_), channel_id=1, source_target_pairs={{0,16},{8,24},{16,0},{24,8},{1,17},{9,25},{17,1},{25,9},{2,18},{10... | collective-permute-start | bytes 2654216 | tf_op jit(solution)/shard_map/ppermute | solution.py:19
  66.1 24.8 %collective-permute-start.8 = (bf16[2,128,512]{2,1,0:T(8,128)(2,1)S(1)}, bf16[2,128,512]{2,1,0:T(8,128)(2,1)S(1)}, u32[]{:S(2)}, u32[]{:S(2)}) collective-permute-start(bf16[2,128,512]{2,1,0:T(8,128)(2,1)S(1)} %pad_maximum_fusion.6), channel_id=1, source_target_pairs={{0,2},{1,3},{2,0},{3,1},{4,6},{5,7},{6,4},{7,5},{8,10},{9,11},{10,... | collective-permute-start | bytes 786440 | tf_op jit(solution)/shard_map/ppermute | solution.py:19
  90.9 4.4 %collective-permute-start.10 = (bf16[4,144,768]{2,1,0:T(8,128)(2,1)}, bf16[4,144,768]{2,1,0:T(8,128)(2,1)S(1)}, u32[]{:S(2)}, u32[]{:S(2)}) collective-permute-start(bf16[4,144,768]{2,1,0:T(8,128)(2,1)} %collective-permute-done.7.refs_1_.refs_9_), channel_id=1, source_target_pairs={{0,8},{8,0},{16,24},{24,16},{1,9},{9,1},{17,25},{25,17},{2,10},{10... | collective-permute-start | bytes 2654216 | tf_op jit(solution)/shard_map/ppermute | solution.py:19
  90.9 4.4 %collective-permute-start.9 = (bf16[4,144,768]{2,1,0:T(8,128)(2,1)}, bf16[4,144,768]{2,1,0:T(8,128)(2,1)}, u32[]{:S(2)}, u32[]{:S(2)}) collective-permute-start(bf16[4,144,768]{2,1,0:T(8,128)(2,1)} %collective-permute-done.6.refs_0_.refs_8_), channel_id=1, source_target_pairs={{0,8},{8,0},{16,24},{24,16},{1,9},{9,1},{17,25},{25,17},{2,10},{10... | collective-permute-start | bytes 2654216 | tf_op jit(solution)/shard_map/ppermute | solution.py:19
  91.4 15.3 %collective-permute-start.11 = (bf16[4,128,512]{2,1,0:T(8,128)(2,1)S(1)}, bf16[4,128,512]{2,1,0:T(8,128)(2,1)}, u32[]{:S(2)}, u32[]{:S(2)}) collective-permute-start(bf16[4,128,512]{2,1,0:T(8,128)(2,1)S(1)} %pad_maximum_fusion.2), channel_id=1, source_target_pairs={{0,1},{1,0},{2,3},{3,2},{4,5},{5,4},{6,7},{7,6},{8,9},{9,8},{10,11... | collective-permute-start | bytes 1572872 | tf_op jit(solution)/shard_map/ppermute | solution.py:19
  110.7 14.9 %collective-permute-start.13 = (bf16[8,128,2048]{2,1,0:T(8,128)(2,1)}, bf16[8,128,2048]{2,1,0:T(8,128)(2,1)}, u32[]{:S(2)}, u32[]{:S(2)}) collective-permute-start(bf16[8,128,2048]{2,1,0:T(8,128)(2,1)} %bitcast.236), channel_id=1, source_target_pairs={{0,8},{8,0},{16,24},{24,16},{1,9},{9,1},{17,25},{25,17},{2,10},{10... | collective-permute-start | bytes 12582920 | tf_op jit(solution)/shard_map/ppermute | solution.py:19
  114.2 51.1 %collective-permute-start.14 = (bf16[8,128,1024]{2,1,0:T(8,128)(2,1)}, bf16[8,128,1024]{2,1,0:T(8,128)(2,1)}, u32[]{:S(2)}, u32[]{:S(2)}) collective-permute-start(bf16[8,128,1024]{2,1,0:T(8,128)(2,1)} %slice.528), channel_id=1, source_target_pairs={{0,16},{8,24},{16,0},{24,8},{1,17},{9,25},{17,1},{25,9},{2,18},{10... | collective-permute-start | bytes 6291464 | tf_op jit(solution)/shard_map/ppermute | solution.py:19
  165.3 4.4 %collective-permute-start.16 = (bf16[8,128,1024]{2,1,0:T(8,128)(2,1)}, bf16[8,128,1024]{2,1,0:T(8,128)(2,1)S(1)}, u32[]{:S(2)}, u32[]{:S(2)}) collective-permute-start(bf16[8,128,1024]{2,1,0:T(8,128)(2,1)} %get-tuple-element.395), channel_id=1, source_target_pairs={{0,8},{8,0},{16,24},{24,16},{1,9},{9,1},{17,25},{25,17},{2,10},{10... | collective-permute-start | bytes 6291464 | tf_op jit(solution)/shard_map/ppermute | solution.py:19
  165.4 7.4 %collective-permute-start.15 = (bf16[8,128,1024]{2,1,0:T(8,128)(2,1)}, bf16[8,128,1024]{2,1,0:T(8,128)(2,1)S(1)}, u32[]{:S(2)}, u32[]{:S(2)}) collective-permute-start(bf16[8,128,1024]{2,1,0:T(8,128)(2,1)} %get-tuple-element.393), channel_id=1, source_target_pairs={{0,8},{8,0},{16,24},{24,16},{1,9},{9,1},{17,25},{25,17},{2,10},{10... | collective-permute-start | bytes 6291464 | tf_op jit(solution)/shard_map/ppermute | solution.py:19
  174.4 26.9 %collective-permute-start.17 = (bf16[8,128,1024]{2,1,0:T(8,128)(2,1)}, bf16[8,128,1024]{2,1,0:T(8,128)(2,1)S(1)}, u32[]{:S(2)}, u32[]{:S(2)}) collective-permute-start(bf16[8,128,1024]{2,1,0:T(8,128)(2,1)} %collective-permute-done.14.refs_2_), channel_id=1, source_target_pairs={{0,8},{8,0},{16,24},{24,16},{1,9},{9,1},{17,25},{25,17},{2,10},{10... | collective-permute-start | bytes 6291464 | tf_op jit(solution)/shard_map/ppermute | solution.py:19
  174.5 26.7 %collective-permute-start.18 = (bf16[8,128,1024]{2,1,0:T(8,128)(2,1)S(1)}, bf16[8,128,1024]{2,1,0:T(8,128)(2,1)}, u32[]{:S(2)}, u32[]{:S(2)}) collective-permute-start(bf16[8,128,1024]{2,1,0:T(8,128)(2,1)S(1)} %bitcast.243), channel_id=1, source_target_pairs={{0,8},{8,0},{16,24},{24,16},{1,9},{9,1},{17,25},{25,17},{2,10},{10... | collective-permute-start | bytes 6291464 | tf_op jit(solution)/shard_map/ppermute | solution.py:19
  174.9 25.5 %collective-permute-start.20 = (bf16[2,2,128,1024]{3,2,1,0:T(8,128)(2,1)}, bf16[2,2,128,1024]{3,2,1,0:T(8,128)(2,1)}, u32[]{:S(2)}, u32[]{:S(2)}) collective-permute-start(bf16[2,2,128,1024]{3,2,1,0:T(8,128)(2,1)} %fusion), channel_id=1, source_target_pairs={{0,2},{1,3},{2,0},{3,1},{4,6},{5,7},{6,4},{7,5},{8,10},{9,11},{10,... | collective-permute-start | bytes 3145736 | tf_op jit(solution)/shard_map/ppermute | solution.py:19
  176.2 25.0 %collective-permute-start.19 = (bf16[2,2,128,1024]{3,2,1,0:T(8,128)(2,1)S(1)}, bf16[2,2,128,1024]{3,2,1,0:T(8,128)(2,1)}, u32[]{:S(2)}, u32[]{:S(2)}) collective-permute-start(bf16[2,2,128,1024]{3,2,1,0:T(8,128)(2,1)S(1)} %bitcast.262), channel_id=1, source_target_pairs={{0,1},{1,0},{2,3},{3,2},{4,5},{5,4},{6,7},{7,6},{8,9},{9,8},{10,11... | collective-permute-start | bytes 3145736 | tf_op jit(solution)/shard_map/ppermute | solution.py:19
  204.5 23.3 %collective-permute-start.22 = (bf16[2,128,1024]{2,1,0:T(8,128)(2,1)S(1)}, bf16[2,128,1024]{2,1,0:T(8,128)(2,1)S(1)}, u32[]{:S(2)}, u32[]{:S(2)}) collective-permute-start(bf16[2,128,1024]{2,1,0:T(8,128)(2,1)S(1)} %get-tuple-element.431), channel_id=1, source_target_pairs={{0,1},{1,0},{2,3},{3,2},{4,5},{5,4},{6,7},{7,6},{8,9},{9,8},{10,11... | collective-permute-start | bytes 1572872 | tf_op jit(solution)/shard_map/ppermute | solution.py:19
  206.0 21.8 %collective-permute-start.21 = (bf16[2,128,1024]{2,1,0:T(8,128)(2,1)S(1)}, bf16[2,128,1024]{2,1,0:T(8,128)(2,1)S(1)}, u32[]{:S(2)}, u32[]{:S(2)}) collective-permute-start(bf16[2,128,1024]{2,1,0:T(8,128)(2,1)S(1)} %get-tuple-element.430), channel_id=1, source_target_pairs={{0,2},{1,3},{2,0},{3,1},{4,6},{5,7},{6,4},{7,5},{8,10},{9,11},{10,... | collective-permute-start | bytes 1572872 | tf_op jit(solution)/shard_map/ppermute | solution.py:19
  227.8 4.9 %collective-permute-start.24 = (bf16[8,128,1024]{2,1,0:T(8,128)(2,1)}, bf16[8,128,1024]{2,1,0:T(8,128)(2,1)S(1)}, u32[]{:S(2)}, u32[]{:S(2)}) collective-permute-start(bf16[8,128,1024]{2,1,0:T(8,128)(2,1)} %get-tuple-element.436), channel_id=1, source_target_pairs={{0,8},{8,0},{16,24},{24,16},{1,9},{9,1},{17,25},{25,17},{2,10},{10... | collective-permute-start | bytes 6291464 | tf_op jit(solution)/shard_map/ppermute | solution.py:19
  227.9 7.4 %collective-permute-start.23 = (bf16[8,128,1024]{2,1,0:T(8,128)(2,1)}, bf16[8,128,1024]{2,1,0:T(8,128)(2,1)S(1)}, u32[]{:S(2)}, u32[]{:S(2)}) collective-permute-start(bf16[8,128,1024]{2,1,0:T(8,128)(2,1)} %get-tuple-element.434), channel_id=1, source_target_pairs={{0,8},{8,0},{16,24},{24,16},{1,9},{9,1},{17,25},{25,17},{2,10},{10... | collective-permute-start | bytes 6291464 | tf_op jit(solution)/shard_map/ppermute | solution.py:19
  238.0 36.8 %collective-permute-start.28 = (bf16[2,2,128,1024]{3,2,1,0:T(8,128)(2,1)}, bf16[2,2,128,1024]{3,2,1,0:T(8,128)(2,1)}, u32[]{:S(2)}, u32[]{:S(2)}) collective-permute-start(bf16[2,2,128,1024]{3,2,1,0:T(8,128)(2,1)} %fusion.1), channel_id=1, source_target_pairs={{0,2},{1,3},{2,0},{3,1},{4,6},{5,7},{6,4},{7,5},{8,10},{9,11},{10,... | collective-permute-start | bytes 3145736 | tf_op jit(solution)/shard_map/ppermute | solution.py:19
  239.3 35.4 %collective-permute-start.27 = (bf16[2,2,128,1024]{3,2,1,0:T(8,128)(2,1)S(1)}, bf16[2,2,128,1024]{3,2,1,0:T(8,128)(2,1)}, u32[]{:S(2)}, u32[]{:S(2)}) collective-permute-start(bf16[2,2,128,1024]{3,2,1,0:T(8,128)(2,1)S(1)} %bitcast.261), channel_id=1, source_target_pairs={{0,1},{1,0},{2,3},{3,2},{4,5},{5,4},{6,7},{7,6},{8,9},{9,8},{10,11... | collective-permute-start | bytes 3145736 | tf_op jit(solution)/shard_map/ppermute | solution.py:19
  239.9 32.0 %collective-permute-start.26 = (bf16[128,1024]{1,0:T(8,128)(2,1)}, bf16[128,1024]{1,0:T(8,128)(2,1)S(1)}, u32[]{:S(2)}, u32[]{:S(2)}) collective-permute-start(bf16[128,1024]{1,0:T(8,128)(2,1)} %fusion.22), channel_id=1, source_target_pairs={{0,4},{1,5},{2,6},{3,7},{4,0},{5,1},{6,2},{7,3},{8,12},{9,13},{10,... | collective-permute-start | bytes 786440 | tf_op jit(solution)/shard_map/ppermute | solution.py:19
  242.0 31.6 %collective-permute-start.25 = (bf16[128,1024]{1,0:T(8,128)(2,1)}, bf16[128,1024]{1,0:T(8,128)(2,1)}, u32[]{:S(2)}, u32[]{:S(2)}) collective-permute-start(bf16[128,1024]{1,0:T(8,128)(2,1)} %fusion.21), channel_id=1, source_target_pairs={{0,4},{1,5},{2,6},{3,7},{4,0},{5,1},{6,2},{7,3},{8,12},{9,13},{10,... | collective-permute-start | bytes 786440 | tf_op jit(solution)/shard_map/ppermute | solution.py:19
  274.8 4.7 %collective-permute-start.29 = (bf16[8,128,1024]{2,1,0:T(8,128)(2,1)}, bf16[8,128,1024]{2,1,0:T(8,128)(2,1)S(1)}, u32[]{:S(2)}, u32[]{:S(2)}) collective-permute-start(bf16[8,128,1024]{2,1,0:T(8,128)(2,1)} %get-tuple-element.468), channel_id=1, source_target_pairs={{0,8},{8,0},{16,24},{24,16},{1,9},{9,1},{17,25},{25,17},{2,10},{10... | collective-permute-start | bytes 6291464 | tf_op jit(solution)/shard_map/ppermute | solution.py:19
  281.8 25.6 %collective-permute-start.32 = (bf16[4,128,1024]{2,1,0:T(8,128)(2,1)}, bf16[4,128,1024]{2,1,0:T(8,128)(2,1)S(1)}, u32[]{:S(2)}, u32[]{:S(2)}) collective-permute-start(bf16[4,128,1024]{2,1,0:T(8,128)(2,1)} %get-tuple-element.488), channel_id=1, source_target_pairs={{0,16},{8,24},{16,0},{24,8},{1,17},{9,25},{17,1},{25,9},{2,18},{10... | collective-permute-start | bytes 3145736 | tf_op jit(solution)/shard_map/ppermute | solution.py:19
  282.5 21.0 %collective-permute-start.31 = (bf16[2,128,1024]{2,1,0:T(8,128)(2,1)}, bf16[2,128,1024]{2,1,0:T(8,128)(2,1)}, u32[]{:S(2)}, u32[]{:S(2)}) collective-permute-start(bf16[2,128,1024]{2,1,0:T(8,128)(2,1)} %fusion.5), channel_id=1, source_target_pairs={{0,1},{1,0},{2,3},{3,2},{4,5},{5,4},{6,7},{7,6},{8,9},{9,8},{10,11... | collective-permute-start | bytes 1572872 | tf_op jit(solution)/shard_map/ppermute | solution.py:19
  283.4 20.1 %collective-permute-start.30 = (bf16[2,128,1024]{2,1,0:T(8,128)(2,1)}, bf16[2,128,1024]{2,1,0:T(8,128)(2,1)}, u32[]{:S(2)}, u32[]{:S(2)}) collective-permute-start(bf16[2,128,1024]{2,1,0:T(8,128)(2,1)} %fusion.4), channel_id=1, source_target_pairs={{0,2},{1,3},{2,0},{3,1},{4,6},{5,7},{6,4},{7,5},{8,10},{9,11},{10,... | collective-permute-start | bytes 1572872 | tf_op jit(solution)/shard_map/ppermute | solution.py:19
  313.5 27.4 %collective-permute-start.37 = (bf16[4,128,1024]{2,1,0:T(8,128)(2,1)}, bf16[4,128,1024]{2,1,0:T(8,128)(2,1)S(1)}, u32[]{:S(2)}, u32[]{:S(2)}) collective-permute-start(bf16[4,128,1024]{2,1,0:T(8,128)(2,1)} %get-tuple-element.512), channel_id=1, source_target_pairs={{0,16},{8,24},{16,0},{24,8},{1,17},{9,25},{17,1},{25,9},{2,18},{10... | collective-permute-start | bytes 3145736 | tf_op jit(solution)/shard_map/ppermute | solution.py:19
  314.2 26.7 %collective-permute-start.36 = (bf16[2,2,128,1024]{3,2,1,0:T(8,128)(2,1)}, bf16[2,2,128,1024]{3,2,1,0:T(8,128)(2,1)}, u32[]{:S(2)}, u32[]{:S(2)}) collective-permute-start(bf16[2,2,128,1024]{3,2,1,0:T(8,128)(2,1)} %bitcast.56), channel_id=1, source_target_pairs={{0,1},{1,0},{2,3},{3,2},{4,5},{5,4},{6,7},{7,6},{8,9},{9,8},{10,11... | collective-permute-start | bytes 3145736 | tf_op jit(solution)/shard_map/ppermute | solution.py:19
  315.1 21.7 %collective-permute-start.35 = (bf16[128,1024]{1,0:T(8,128)(2,1)}, bf16[128,1024]{1,0:T(8,128)(2,1)}, u32[]{:S(2)}, u32[]{:S(2)}) collective-permute-start(bf16[128,1024]{1,0:T(8,128)(2,1)} %fusion.20), channel_id=1, source_target_pairs={{0,4},{1,5},{2,6},{3,7},{4,0},{5,1},{6,2},{7,3},{8,12},{9,13},{10,... | collective-permute-start | bytes 786440 | tf_op jit(solution)/shard_map/ppermute | solution.py:19
  316.8 24.1 %collective-permute-start.34 = (bf16[128,1024]{1,0:T(8,128)(2,1)S(1)}, bf16[128,1024]{1,0:T(8,128)(2,1)}, u32[]{:S(2)}, u32[]{:S(2)}) collective-permute-start(bf16[128,1024]{1,0:T(8,128)(2,1)S(1)} %fusion.19), channel_id=1, source_target_pairs={{0,4},{1,5},{2,6},{3,7},{4,0},{5,1},{6,2},{7,3},{8,12},{9,13},{10,... | collective-permute-start | bytes 786440 | tf_op jit(solution)/shard_map/ppermute | solution.py:19
  347.2 14.7 %collective-permute-start.42 = (bf16[2,128,1024]{2,1,0:T(8,128)(2,1)S(1)}, bf16[2,128,1024]{2,1,0:T(8,128)(2,1)S(1)}, u32[]{:S(2)}, u32[]{:S(2)}) collective-permute-start(bf16[2,128,1024]{2,1,0:T(8,128)(2,1)S(1)} %pad_maximum_fusion.3), channel_id=1, source_target_pairs={{0,16},{8,24},{16,0},{24,8},{1,17},{9,25},{17,1},{25,9},{2,18},{10... | collective-permute-start | bytes 1572872 | tf_op jit(solution)/shard_map/ppermute | solution.py:19
  348.2 13.6 %collective-permute-start.41 = (bf16[2,128,1024]{2,1,0:T(8,128)(2,1)S(1)}, bf16[2,128,1024]{2,1,0:T(8,128)(2,1)S(1)}, u32[]{:S(2)}, u32[]{:S(2)}) collective-permute-start(bf16[2,128,1024]{2,1,0:T(8,128)(2,1)S(1)} %fusion.3), channel_id=1, source_target_pairs={{0,2},{1,3},{2,0},{3,1},{4,6},{5,7},{6,4},{7,5},{8,10},{9,11},{10,... | collective-permute-start | bytes 1572872 | tf_op jit(solution)/shard_map/ppermute | solution.py:19
  349.6 12.2 %collective-permute-start.39 = (f32[8,16,128]{2,1,0:T(8,128)}, f32[8,16,128]{2,1,0:T(8,128)S(1)}, u32[]{:S(2)}, u32[]{:S(2)}) collective-permute-start(f32[8,16,128]{2,1,0:T(8,128)} %pack_sums.1), channel_id=1, source_target_pairs={{0,16},{8,24},{16,0},{24,8},{1,17},{9,25},{17,1},{25,9},{2,18},{10... | collective-permute-start | bytes 196616 | tf_op jit(solution)/shard_map/ppermute | solution.py:19
  350.1 11.7 %collective-permute-start.40 = (f32[8,16,128]{2,1,0:T(8,128)}, f32[8,16,128]{2,1,0:T(8,128)S(1)}, u32[]{:S(2)}, u32[]{:S(2)}) collective-permute-start(f32[8,16,128]{2,1,0:T(8,128)} %pack_sums.1), channel_id=1, source_target_pairs={{0,24},{8,16},{16,8},{24,0},{1,25},{9,17},{17,9},{25,1},{2,26},{10... | collective-permute-start | bytes 196616 | tf_op jit(solution)/shard_map/ppermute | solution.py:19
  367.5 14.9 %collective-permute-start.45 = (bf16[128,1024]{1,0:T(8,128)(2,1)S(1)}, bf16[128,1024]{1,0:T(8,128)(2,1)S(1)}, u32[]{:S(2)}, u32[]{:S(2)}) collective-permute-start(bf16[128,1024]{1,0:T(8,128)(2,1)S(1)} %fusion.10), channel_id=1, source_target_pairs={{0,4},{1,5},{2,6},{3,7},{4,0},{5,1},{6,2},{7,3},{8,12},{9,13},{10,... | collective-permute-start | bytes 786440 | tf_op jit(solution)/shard_map/ppermute | solution.py:19
  368.3 21.4 %collective-permute-start.47 = (bf16[2,128,1024]{2,1,0:T(8,128)(2,1)}, bf16[2,128,1024]{2,1,0:T(8,128)(2,1)}, u32[]{:S(2)}, u32[]{:S(2)}) collective-permute-start(bf16[2,128,1024]{2,1,0:T(8,128)(2,1)} %pad_maximum_fusion.4.refs_0_), channel_id=1, source_target_pairs={{0,8},{8,0},{16,24},{24,16},{1,9},{9,1},{17,25},{25,17},{2,10},{10... | collective-permute-start | bytes 1572872 | tf_op jit(solution)/shard_map/ppermute | solution.py:19
  368.3 21.4 %collective-permute-start.48 = (bf16[2,128,1024]{2,1,0:T(8,128)(2,1)}, bf16[2,128,1024]{2,1,0:T(8,128)(2,1)}, u32[]{:S(2)}, u32[]{:S(2)}) collective-permute-start(bf16[2,128,1024]{2,1,0:T(8,128)(2,1)} %pad_maximum_fusion.4.refs_0_), channel_id=1, source_target_pairs={{0,16},{8,24},{16,0},{24,8},{1,17},{9,25},{17,1},{25,9},{2,18},{10... | collective-permute-start | bytes 1572872 | tf_op jit(solution)/shard_map/ppermute | solution.py:19
  384.5 5.2 %collective-permute-start.46 = (f32[16,128]{1,0:T(8,128)}, f32[16,128]{1,0:T(8,128)}, u32[]{:S(2)}, u32[]{:S(2)}) collective-permute-start(f32[16,128]{1,0:T(8,128)} %bitcast_add_fusion.3), channel_id=1, source_target_pairs={{0,4},{1,5},{2,6},{3,7},{4,0},{5,1},{6,2},{7,3},{8,12},{9,13},{10,... | collective-permute-start | bytes 24584 | tf_op jit(solution)/shard_map/ppermute | solution.py:19
  389.8 7.3 %collective-permute-start.50 = (bf16[128,1024]{1,0:T(8,128)(2,1)S(1)}, bf16[128,1024]{1,0:T(8,128)(2,1)S(1)}, u32[]{:S(2)}, u32[]{:S(2)}) collective-permute-start(bf16[128,1024]{1,0:T(8,128)(2,1)S(1)} %fusion.9.refs_0_), channel_id=1, source_target_pairs={{0,8},{8,0},{16,24},{24,16},{1,9},{9,1},{17,25},{25,17},{2,10},{10... | collective-permute-start | bytes 786440 | tf_op jit(solution)/shard_map/ppermute | solution.py:19
  390.3 8.3 %collective-permute-start.51 = (bf16[128,1024]{1,0:T(8,128)(2,1)S(1)}, bf16[128,1024]{1,0:T(8,128)(2,1)S(1)}, u32[]{:S(2)}, u32[]{:S(2)}) collective-permute-start(bf16[128,1024]{1,0:T(8,128)(2,1)S(1)} %fusion.9.refs_0_), channel_id=1, source_target_pairs={{0,16},{8,24},{16,0},{24,8},{1,17},{9,25},{17,1},{25,9},{2,18},{10... | collective-permute-start | bytes 786440 | tf_op jit(solution)/shard_map/ppermute | solution.py:19
  (50 other events, 356.2 us)
Sparse Core Ops, SparseCore 0:
  24.4 81.8 all-gather.4
  111.0 48.9 all-gather.6

commit v2 on v1

--- a/solution.py
+++ b/solution.py
@@ -1105,8 +1105,9 @@
         red_w.launch()
         seq.land((), red_w)
     red_w.launch()
+    two_up.terms, two_down.terms, sums_one = seq.at((two_up.terms, two_down.terms, sums_one))
     packed = pack_sums(
-        seq.at(order),
+        order,
         n,
         rows,
         ffq,
@@ -1118,28 +1119,35 @@
     peers = Sent([xor_swap(packed, "dp", 4, m) for m in (1, 2, 3)])
     crossing = jnp.stack([two_up.rest().piece(), two_down.rest().piece()])
     cross = Sent(x_swap(seq.at(crossing)))
-    seq.land((), peers, red_w, cross)
+    seq.land((), peers, red_w)
     if red_w.axes:
         red_w.launch()
-    owned = [rounded_sum([*red_up.rest().terms, cross.value[0]]), rounded_sum([*red_down.rest().terms, cross.value[1]])]
+    seq.land((), cross)
+    red_up.rest()
+    red_down.rest()
+    red_up.terms, red_down.terms, cross.value = seq.at((red_up.terms, red_down.terms, cross.value))
+    owned = [rounded_sum([*red_up.terms, cross.value[0]]), rounded_sum([*red_down.terms, cross.value[1]])]
     mlp_spread = Spread(seq, jnp.stack(owned))
     sums = Reduce(seq, (packed, *peers.value), n, full)
+    sums.launch()
+    seq.land((), *([sums, red_w] if len(bits) > 1 else [sums]))
+    w_spread = Spread(seq, red_w.piece())
     while len(sums.axes) > 1:
         sums.launch()
         if len(sums.axes) > 1:
             seq.land((), sums)
-    seq.land((), *([sums, red_w] if len(bits) > 1 else []))
-    w_spread = Spread(seq, red_w.piece())
-    sums.launch()
     block, tokens_grad = seq.at((block, tokens_grad))
-    block_out, grad_tokens = seq.land((compact(block), compact(tokens_grad)), sums, mlp_spread)
+    block_out, grad_tokens = seq.land(
+        (compact(block), compact(tokens_grad)), *([sums] if len(bits) > 1 else []), mlp_spread, w_spread
+    )
     mlp_spread.cross()
-    small_sums = seq.land(sums.piece(), mlp_spread)
+    w_spread.cross()
+    if sums.axes:
+        sums.launch()
+    seq.land((), mlp_spread, w_spread, *([sums] if len(bits) > 2 else []))
+    small_sums = sums.piece()
     mlp_pieces = seq.at(mlp_spread.pieces)
     out_fc1, out_fc2 = finish_mlp(q, mlp_pieces, n)
-    out_fc2 = seq.land(out_fc2, w_spread)
-    w_spread.cross()
-    seq.land((), w_spread)
     out_qkv, out_out = finish_attention(seq.value, w_spread.pieces)
     small_out = [small_sums[k, :rows] for k in range(8)]
     out_bfc1 = small_sums[8:12, :ffq].reshape(-1)

time: 416 us -> 430 us (1.034)
  local copies, waits for them, and re-layouts: 29.2 us -> 41.9 us
    squeeze x0 -> x13, local copies, waits for them, and re-layouts: none -> 15.1 us  [launch(): lax.index_in_dim(t, side, axis, keepdims=False)]
  transfers between devices with their start and end apart: 55 -> 55, of which waited for: 23 -> 21; matrix products, arithmetic and copies ran while one was open for 12% -> 16% of each run, Pallas kernels for 45% -> 43%
where the time goes in v2:
time: 430 us; the launch traced here: 424 us
  Pallas kernels  192 us (45%)
  waiting for transfers between devices  78.7 us (18%)
  starting transfers between devices  50.5 us (12%)
  other arithmetic  46.4 us (11%)
  local copies, waits for them, and re-layouts  41.9 us (10%)
  between operations  15.2 us (4%)
    pallas_call x17, Pallas kernels, call(): pl.pallas_call(kernel, out_shape=[jax.ShapeDtypeStruct(shape, kind) for s...  192 us
    ppermute x53, waiting for transfers between devices, xor_swap(): return lax.ppermute(value, axis, [(i, i ^ mask) for i in range(size)])  78.7 us
    ppermute x53, starting transfers between devices, xor_swap(): return lax.ppermute(value, axis, [(i, i ^ mask) for i in range(size)])  50.4 us
    convert_element_type x16, other arithmetic, rounded_sum(): return sum((t.astype(full) for t in terms)).astype(kind)  30.8 us
    squeeze x13, local copies, waits for them, and re-layouts, launch(): lax.index_in_dim(t, side, axis, keepdims=False)  15.1 us
  transfers between devices with their start and end apart: 55, of which 21 were waited for; matrix products, arithmetic and copies ran while one was open for 16% of the time, Pallas kernels for 43%

profile of v2, /device:TPU:0, one launch (start us, length us, event | category | flops | bytes accessed | tf_op | source)
XLA Modules:
  0.0 424.3 jit_solution(8355337742062882647)
XLA Ops:
  7.2 2.6 first_payload.1
  9.8 4.1 collective-permute-start
  14.5 3.3 payloads.1
  17.8 6.5 %collective-permute-done = bf16[1,144,768]{2,1,0:T(8,128)(2,1)S(1)} collective-permute-done((bf16[1,144,768]{2,1,0:T(8,128)(2,1)}, bf16[1,144,768]{2,1,0:T(8,128)(2,1)S(1)}, u32[]{:S(2)}, u32[]{:S(2)}) %collective-permute-start) | collective-permute-done | bytes 221216 | tf_op jit(solution)/shard_map/ppermute | solution.py:19
  27.5 3.6 copy.32
  31.1 2.2 reshape.433
  41.3 6.6 %collective-permute-start.4 = (bf16[1,128,512]{2,1,0:T(8,128)(2,1)S(1)}, bf16[1,128,512]{2,1,0:T(8,128)(2,1)S(1)}, u32[]{:S(2)}, u32[]{:S(2)}) collective-permute-start(bf16[1,128,512]{2,1,0:T(8,128)(2,1)S(1)} %pad_maximum_fusion.7), channel_id=1, source_target_pairs={{0,4},{1,5},{2,6},{3,7},{4,0},{5,1},{6,2},{7,3},{8,12},{9,13},{10,... | collective-permute-start | bytes 393224 | tf_op jit(solution)/shard_map/ppermute | solution.py:19
  48.7 11.6 %collective-permute-done.4 = bf16[1,128,512]{2,1,0:T(8,128)(2,1)S(1)} collective-permute-done((bf16[1,128,512]{2,1,0:T(8,128)(2,1)S(1)}, bf16[1,128,512]{2,1,0:T(8,128)(2,1)S(1)}, u32[]{:S(2)}, u32[]{:S(2)}) %collective-permute-start.4) | collective-permute-done | bytes 131104 | tf_op jit(solution)/shard_map/ppermute | solution.py:19
  63.8 2.3 unpack_vectors.1
  71.5 10.5 %attention_forward.2 = (bf16[832,768]{1,0:T(8,128)(2,1)}, bf16[832,768]{1,0:T(8,128)(2,1)}, bf16[832,256]{1,0:T(8,128)(2,1)}, bf16[832,256]{1,0:T(8,128)(2,1)}, ...) custom-call(s32[9]{0:T(128)} %pad_add_fusion.1.order_ref, bf16[832,1024]{1,0:T(8,128)(2,1)} %add_convert_fusion.normed_ref, ...), custom_call_target="tpu_custom_call" | custom-call | tf_op jit(solution)/shard_map/attention_forward/pallas_call | solution.py:133
  82.0 8.9 %collective-permute-done.8 = bf16[2,128,512]{2,1,0:T(8,128)(2,1)S(1)} collective-permute-done((bf16[2,128,512]{2,1,0:T(8,128)(2,1)S(1)}, bf16[2,128,512]{2,1,0:T(8,128)(2,1)S(1)}, u32[]{:S(2)}, u32[]{:S(2)}) %collective-permute-start.8) | collective-permute-done | bytes 262176 | tf_op jit(solution)/shard_map/ppermute | solution.py:19
  96.2 10.5 %attention_forward.3 = (bf16[832,768]{1,0:T(8,128)(2,1)}, bf16[832,768]{1,0:T(8,128)(2,1)}, bf16[832,256]{1,0:T(8,128)(2,1)}, bf16[832,256]{1,0:T(8,128)(2,1)}, ...) custom-call(s32[9]{0:T(128)} %pad_add_fusion.1.order_ref, bf16[832,1024]{1,0:T(8,128)(2,1)} %add_convert_fusion.normed_ref, ...), custom_call_target="tpu_custom_call" | custom-call | tf_op jit(solution)/shard_map/attention_forward/pallas_call | solution.py:133
  108.0 2.6 collective-permute-done.12.refs_5_
  110.8 3.3 slice.528
  115.8 9.8 %attention_out.1 = (f32[832,1024]{1,0:T(8,128)}, bf16[832,1024]{1,0:T(8,128)(2,1)}) custom-call(s32[9]{0:T(128)} %pad_add_fusion.1.order_ref, f32[832,1024]{1,0:T(8,128)} %bitcast.221, f32[1,1024]{1,0:T(1,128)} %get-tuple-element.637.bias_ref, f32[1,1024]{1,0:T(1,128)} %get-tuple-element.636.gain_ref, f32[1,1024]{1,0:T(1,128)} %get-tuple-element.635.shift_ref, ...), custom_call_target="tpu_custom_call" | custom-call | tf_op jit(solution)/shard_map/attention_out/pallas_call | solution.py:133
  125.6 19.2 %mlp.4 = (bf16[8,128,1024]{2,1,0:T(8,128)(2,1)}, bf16[8,128,1024]{2,1,0:T(8,128)(2,1)}, f32[1,1024]{1,0:T(1,128)}, f32[832,1024]{1,0:T(8,128)}, f32[832,1024]{1,0:T(8,128)}) custom-call(s32[9]{0:T(128)} %pad_add_fusion.1.order_ref, f32[1,1024]{1,0:T(1,128)} %get-tuple-element.642.bias_ref, bf16[832,1024]{1,0:T(8,128)(2,1)} %get-tuple-element.395.refs_0_.refs_1_, ...), custom_call_target="tpu_custom_call" | custom-call | tf_op jit(solution)/shard_map/mlp/pallas_call | solution.py:133
  144.9 20.4 %mlp.5 = (bf16[8,128,1024]{2,1,0:T(8,128)(2,1)}, bf16[8,128,1024]{2,1,0:T(8,128)(2,1)}, f32[1,1024]{1,0:T(1,128)}, f32[832,1024]{1,0:T(8,128)}, f32[832,1024]{1,0:T(8,128)}) custom-call(s32[9]{0:T(128)} %pad_add_fusion.1.order_ref, f32[1,1024]{1,0:T(1,128)} %get-tuple-element.643.bias_ref, bf16[832,1024]{1,0:T(8,128)(2,1)} %get-tuple-element.395.refs_0_.refs_1_, ...), custom_call_target="tpu_custom_call" | custom-call | tf_op jit(solution)/shard_map/mlp/pallas_call | solution.py:133
  165.9 3.9 collective-permute-done.16
  169.8 2.4 add_convert_fusion.7
  177.8 20.5 %mlp.6 = (bf16[8,128,1024]{2,1,0:T(8,128)(2,1)}, bf16[8,128,1024]{2,1,0:T(8,128)(2,1)}, f32[1,1024]{1,0:T(1,128)}, f32[832,1024]{1,0:T(8,128)}, f32[832,1024]{1,0:T(8,128)}) custom-call(s32[9]{0:T(128)} %pad_add_fusion.1.order_ref, f32[1,1024]{1,0:T(1,128)} %get-tuple-element.641.bias_ref, bf16[832,1024]{1,0:T(8,128)(2,1)} %get-tuple-element.395.refs_0_.refs_1_, ...), custom_call_target="tpu_custom_call" | custom-call | tf_op jit(solution)/shard_map/mlp/pallas_call | solution.py:133
  198.3 2.2 collective-permute-done.20
  201.4 3.2 fusion.6
  206.9 21.1 %mlp.7 = (bf16[8,128,1024]{2,1,0:T(8,128)(2,1)}, bf16[8,128,1024]{2,1,0:T(8,128)(2,1)}, f32[1,1024]{1,0:T(1,128)}, f32[832,1024]{1,0:T(8,128)}, bf16[832,1024]{1,0:T(8,128)(2,1)}) custom-call(s32[9]{0:T(128)} %pad_add_fusion.1.order_ref, f32[1,1024]{1,0:T(1,128)} %get-tuple-element.640.bias_ref, f32[1,1024]{1,0:T(1,128)} %get-tuple-element.634.refs_0_, ...), custom_call_target="tpu_custom_call" | custom-call | tf_op jit(solution)/shard_map/mlp/pallas_call | solution.py:133
  230.3 2.1 fusion.16
  232.8 2.6 collective-permute-done.23
  239.0 2.1 collective-permute-start.26
  241.9 11.0 %attention_out_back.1 = (f32[832,1024]{1,0:T(8,128)}, bf16[832,256]{1,0:T(8,128)(2,1)}, bf16[832,256]{1,0:T(8,128)(2,1)}, bf16[832,256]{1,0:T(8,128)(2,1)}, bf16...) custom-call(s32[9]{0:T(128)} %pad_add_fusion.1.order_ref, ...), custom_call_target="tpu_custom_call" | custom-call | tf_op jit(solution)/shard_map/attention_out_back/pallas_call | solution.py:133
  253.0 18.1 %attention_back.2 = (bf16[8,128,1024]{2,1,0:T(8,128)(2,1)}, bf16[8,128,1024]{2,1,0:T(8,128)(2,1)}, bf16[832,768]{1,0:T(8,128)(2,1)}, bf16[832,768]{1,0:T(8,128)(2,1)}, f32[2,1,768]{2,1,0:T(1,128)}) custom-call(s32[9]{0:T(128)} %pad_add_fusion.1.order_ref, bf16[832,1024]{1,0:T(8,128)(2,1)} %add_convert_fusion.normed_ref, ...), custom_call_target="tpu_custom_call" | custom-call | tf_op jit(solution)/shard_map/attention_back/pallas_call | solution.py:133
  273.9 2.4 fusion.4
  276.3 2.3 fusion.5
  278.6 2.3 add_convert_fusion.2
  282.4 2.1 collective-permute-start.30
  284.5 18.0 %attention_back.3 = (bf16[8,128,1024]{2,1,0:T(8,128)(2,1)}, bf16[8,128,1024]{2,1,0:T(8,128)(2,1)}, bf16[832,768]{1,0:T(8,128)(2,1)}, bf16[832,768]{1,0:T(8,128)(2,1)}, f32[2,1,768]{2,1,0:T(1,128)}) custom-call(s32[9]{0:T(128)} %pad_add_fusion.1.order_ref, bf16[832,1024]{1,0:T(8,128)(2,1)} %add_convert_fusion.normed_ref, ...), custom_call_target="tpu_custom_call" | custom-call | tf_op jit(solution)/shard_map/attention_back/pallas_call | solution.py:133
  302.6 4.0 collective-permute-done.32
  313.9 2.0 fusion.13
  315.9 2.0 fusion.14
  331.4 16.3 %input_back.1 = (f32[832,1024]{1,0:T(8,128)}, f32[2,1,1024]{2,1,0:T(1,128)}) custom-call(s32[9]{0:T(128)} %pad_add_fusion.1.order_ref, f32[832,1024]{1,0:T(8,128)} %bitcast.222, f32[832,1024]{1,0:T(8,128)} %get-tuple-element.520.after_ref, f32[1,1024]{1,0:T(1,128)} %get-tuple-element.633.gain_ref, bf16[832,768]{1,0:T(8,128)(2,1)} %get-tuple-element.521.refs_0_, ...), custom_call_target="tpu_custom_call" | custom-call | tf_op jit(solution)/shard_map/input_back/pallas_call | solution.py:133
  347.7 4.2 collective-permute-done.34
  352.0 2.4 fusion.3
  364.2 10.6 %collective-permute-done.39 = f32[8,16,128]{2,1,0:T(8,128)S(1)} collective-permute-done((f32[8,16,128]{2,1,0:T(8,128)}, f32[8,16,128]{2,1,0:T(8,128)S(1)}, u32[]{:S(2)}, u32[]{:S(2)}) %collective-permute-start.39) | collective-permute-done | bytes 65568 | tf_op jit(solution)/shard_map/ppermute | solution.py:19
  376.2 3.4 collective-permute-start.44
  382.9 2.2 collective-permute-done.43
  385.1 6.8 %collective-permute-done.44 = bf16[128,1024]{1,0:T(8,128)(2,1)S(1)} collective-permute-done((bf16[128,1024]{1,0:T(8,128)(2,1)S(1)}, bf16[128,1024]{1,0:T(8,128)(2,1)S(1)}, u32[]{:S(2)}, u32[]{:S(2)}) %collective-permute-start.44) | collective-permute-done | bytes 262176 | tf_op jit(solution)/shard_map/ppermute | solution.py:19
  395.6 1.9 reshape.445
  400.3 2.5 collective-permute-done.49.refs_2_
  404.9 3.8 collective-permute-done.52
  410.8 2.6 finish_attention.1
  413.4 3.9 finish_mlp.1
  (276 shorter events, 96.3 us)
Async XLA Ops:
  7.2 99.6 %all-gather.5.cloned.1.call-start = ((), (), s32[]{:S(2)}) async-start(), calls=%async_computation | async-start | bytes 4718592 | tf_op jit(solution)/shard_map/all_gather | solution.py:963
  9.8 14.5 %collective-permute-start = (bf16[1,144,768]{2,1,0:T(8,128)(2,1)}, bf16[1,144,768]{2,1,0:T(8,128)(2,1)S(1)}, u32[]{:S(2)}, u32[]{:S(2)}) collective-permute-start(bf16[1,144,768]{2,1,0:T(8,128)(2,1)} %bitcast.255), channel_id=1, source_target_pairs={{0,4},{1,5},{2,6},{3,7},{4,0},{5,1},{6,2},{7,3},{8,12},{9,13},{10,... | collective-permute-start | bytes 663560 | tf_op jit(solution)/shard_map/ppermute | solution.py:19
  24.3 141.0 %all-gather.7.cloned.1.call-start = ((), (), s32[]{:S(2)}) async-start(), calls=%async_computation.1 | async-start | bytes 2359296 | tf_op jit(solution)/shard_map/all_gather | solution.py:964
  24.5 11.4 %collective-permute-start.1 = (bf16[2,144,768]{2,1,0:T(8,128)(2,1)S(1)}, bf16[2,144,768]{2,1,0:T(8,128)(2,1)S(1)}, u32[]{:S(2)}, u32[]{:S(2)}) collective-permute-start(bf16[2,144,768]{2,1,0:T(8,128)(2,1)S(1)} %pad_maximum_fusion.5), channel_id=1, source_target_pairs={{0,2},{1,3},{2,0},{3,1},{4,6},{5,7},{6,4},{7,5},{8,10},{9,11},{10,... | collective-permute-start | bytes 1327112 | tf_op jit(solution)/shard_map/ppermute | solution.py:19
  36.7 24.4 %collective-permute-start.2 = (bf16[4,144,768]{2,1,0:T(8,128)(2,1)}, bf16[4,144,768]{2,1,0:T(8,128)(2,1)}, u32[]{:S(2)}, u32[]{:S(2)}) collective-permute-start(bf16[4,144,768]{2,1,0:T(8,128)(2,1)} %constant_dynamic-update-slice_fusion.refs_0_.refs_4_), channel_id=1, source_target_pairs={{0,1},{1,0},{2,3},{3,2},{4,5},{5,4},{6,7},{7,6},{8,9},{9,8},{10,11... | collective-permute-start | bytes 2654216 | tf_op jit(solution)/shard_map/ppermute | solution.py:19
  38.1 23.0 %collective-permute-start.3 = (bf16[4,144,768]{2,1,0:T(8,128)(2,1)}, bf16[4,144,768]{2,1,0:T(8,128)(2,1)}, u32[]{:S(2)}, u32[]{:S(2)}) collective-permute-start(bf16[4,144,768]{2,1,0:T(8,128)(2,1)} %constant_dynamic-update-slice_fusion.refs_0_.refs_4_), channel_id=1, source_target_pairs={{0,8},{8,0},{16,24},{24,16},{1,9},{9,1},{17,25},{25,17},{2,10},{10... | collective-permute-start | bytes 2654216 | tf_op jit(solution)/shard_map/ppermute | solution.py:19
  39.7 42.3 %collective-permute-start.6 = (bf16[4,144,768]{2,1,0:T(8,128)(2,1)}, bf16[4,144,768]{2,1,0:T(8,128)(2,1)}, u32[]{:S(2)}, u32[]{:S(2)}) collective-permute-start(bf16[4,144,768]{2,1,0:T(8,128)(2,1)} %constant_dynamic-update-slice_fusion.refs_0_.refs_4_), channel_id=1, source_target_pairs={{0,16},{8,24},{16,0},{24,8},{1,17},{9,25},{17,1},{25,9},{2,18},{10... | collective-permute-start | bytes 2654216 | tf_op jit(solution)/shard_map/ppermute | solution.py:19
  41.3 19.0 %collective-permute-start.4 = (bf16[1,128,512]{2,1,0:T(8,128)(2,1)S(1)}, bf16[1,128,512]{2,1,0:T(8,128)(2,1)S(1)}, u32[]{:S(2)}, u32[]{:S(2)}) collective-permute-start(bf16[1,128,512]{2,1,0:T(8,128)(2,1)S(1)} %pad_maximum_fusion.7), channel_id=1, source_target_pairs={{0,4},{1,5},{2,6},{3,7},{4,0},{5,1},{6,2},{7,3},{8,12},{9,13},{10,... | collective-permute-start | bytes 393224 | tf_op jit(solution)/shard_map/ppermute | solution.py:19
  61.1 10.4 %collective-permute-start.5 = (bf16[4,144,768]{2,1,0:T(8,128)(2,1)}, bf16[4,144,768]{2,1,0:T(8,128)(2,1)}, u32[]{:S(2)}, u32[]{:S(2)}) collective-permute-start(bf16[4,144,768]{2,1,0:T(8,128)(2,1)} %collective-permute-done.2.refs_1_.refs_5_), channel_id=1, source_target_pairs={{0,8},{8,0},{16,24},{24,16},{1,9},{9,1},{17,25},{25,17},{2,10},{10... | collective-permute-start | bytes 2654216 | tf_op jit(solution)/shard_map/ppermute | solution.py:19
  61.1 29.8 %collective-permute-start.7 = (bf16[4,144,768]{2,1,0:T(8,128)(2,1)}, bf16[4,144,768]{2,1,0:T(8,128)(2,1)}, u32[]{:S(2)}, u32[]{:S(2)}) collective-permute-start(bf16[4,144,768]{2,1,0:T(8,128)(2,1)} %collective-permute-done.2.refs_1_.refs_5_), channel_id=1, source_target_pairs={{0,16},{8,24},{16,0},{24,8},{1,17},{9,25},{17,1},{25,9},{2,18},{10... | collective-permute-start | bytes 2654216 | tf_op jit(solution)/shard_map/ppermute | solution.py:19
  66.1 24.8 %collective-permute-start.8 = (bf16[2,128,512]{2,1,0:T(8,128)(2,1)S(1)}, bf16[2,128,512]{2,1,0:T(8,128)(2,1)S(1)}, u32[]{:S(2)}, u32[]{:S(2)}) collective-permute-start(bf16[2,128,512]{2,1,0:T(8,128)(2,1)S(1)} %pad_maximum_fusion.6), channel_id=1, source_target_pairs={{0,2},{1,3},{2,0},{3,1},{4,6},{5,7},{6,4},{7,5},{8,10},{9,11},{10,... | collective-permute-start | bytes 786440 | tf_op jit(solution)/shard_map/ppermute | solution.py:19
  91.5 15.3 %collective-permute-start.11 = (bf16[4,128,512]{2,1,0:T(8,128)(2,1)S(1)}, bf16[4,128,512]{2,1,0:T(8,128)(2,1)}, u32[]{:S(2)}, u32[]{:S(2)}) collective-permute-start(bf16[4,128,512]{2,1,0:T(8,128)(2,1)S(1)} %pad_maximum_fusion.2), channel_id=1, source_target_pairs={{0,1},{1,0},{2,3},{3,2},{4,5},{5,4},{6,7},{7,6},{8,9},{9,8},{10,11... | collective-permute-start | bytes 1572872 | tf_op jit(solution)/shard_map/ppermute | solution.py:19
  110.7 15.0 %collective-permute-start.13 = (bf16[8,128,2048]{2,1,0:T(8,128)(2,1)}, bf16[8,128,2048]{2,1,0:T(8,128)(2,1)}, u32[]{:S(2)}, u32[]{:S(2)}) collective-permute-start(bf16[8,128,2048]{2,1,0:T(8,128)(2,1)} %bitcast.228), channel_id=1, source_target_pairs={{0,8},{8,0},{16,24},{24,16},{1,9},{9,1},{17,25},{25,17},{2,10},{10... | collective-permute-start | bytes 12582920 | tf_op jit(solution)/shard_map/ppermute | solution.py:19
  114.1 51.2 %collective-permute-start.14 = (bf16[8,128,1024]{2,1,0:T(8,128)(2,1)}, bf16[8,128,1024]{2,1,0:T(8,128)(2,1)}, u32[]{:S(2)}, u32[]{:S(2)}) collective-permute-start(bf16[8,128,1024]{2,1,0:T(8,128)(2,1)} %slice.528), channel_id=1, source_target_pairs={{0,16},{8,24},{16,0},{24,8},{1,17},{9,25},{17,1},{25,9},{2,18},{10... | collective-permute-start | bytes 6291464 | tf_op jit(solution)/shard_map/ppermute | solution.py:19
  165.4 7.4 %collective-permute-start.15 = (bf16[8,128,1024]{2,1,0:T(8,128)(2,1)}, bf16[8,128,1024]{2,1,0:T(8,128)(2,1)S(1)}, u32[]{:S(2)}, u32[]{:S(2)}) collective-permute-start(bf16[8,128,1024]{2,1,0:T(8,128)(2,1)} %get-tuple-element.411), channel_id=1, source_target_pairs={{0,8},{8,0},{16,24},{24,16},{1,9},{9,1},{17,25},{25,17},{2,10},{10... | collective-permute-start | bytes 6291464 | tf_op jit(solution)/shard_map/ppermute | solution.py:19
  174.5 26.9 %collective-permute-start.17 = (bf16[8,128,1024]{2,1,0:T(8,128)(2,1)}, bf16[8,128,1024]{2,1,0:T(8,128)(2,1)S(1)}, u32[]{:S(2)}, u32[]{:S(2)}) collective-permute-start(bf16[8,128,1024]{2,1,0:T(8,128)(2,1)} %collective-permute-done.14.refs_2_), channel_id=1, source_target_pairs={{0,8},{8,0},{16,24},{24,16},{1,9},{9,1},{17,25},{25,17},{2,10},{10... | collective-permute-start | bytes 6291464 | tf_op jit(solution)/shard_map/ppermute | solution.py:19
  174.7 26.8 %collective-permute-start.18 = (bf16[8,128,1024]{2,1,0:T(8,128)(2,1)S(1)}, bf16[8,128,1024]{2,1,0:T(8,128)(2,1)}, u32[]{:S(2)}, u32[]{:S(2)}) collective-permute-start(bf16[8,128,1024]{2,1,0:T(8,128)(2,1)S(1)} %bitcast.235), channel_id=1, source_target_pairs={{0,8},{8,0},{16,24},{24,16},{1,9},{9,1},{17,25},{25,17},{2,10},{10... | collective-permute-start | bytes 6291464 | tf_op jit(solution)/shard_map/ppermute | solution.py:19
  175.0 25.5 %collective-permute-start.20 = (bf16[2,2,128,1024]{3,2,1,0:T(8,128)(2,1)}, bf16[2,2,128,1024]{3,2,1,0:T(8,128)(2,1)}, u32[]{:S(2)}, u32[]{:S(2)}) collective-permute-start(bf16[2,2,128,1024]{3,2,1,0:T(8,128)(2,1)} %fusion), channel_id=1, source_target_pairs={{0,2},{1,3},{2,0},{3,1},{4,6},{5,7},{6,4},{7,5},{8,10},{9,11},{10,... | collective-permute-start | bytes 3145736 | tf_op jit(solution)/shard_map/ppermute | solution.py:19
  176.4 25.0 %collective-permute-start.19 = (bf16[2,2,128,1024]{3,2,1,0:T(8,128)(2,1)S(1)}, bf16[2,2,128,1024]{3,2,1,0:T(8,128)(2,1)}, u32[]{:S(2)}, u32[]{:S(2)}) collective-permute-start(bf16[2,2,128,1024]{3,2,1,0:T(8,128)(2,1)S(1)} %bitcast.254), channel_id=1, source_target_pairs={{0,1},{1,0},{2,3},{3,2},{4,5},{5,4},{6,7},{7,6},{8,9},{9,8},{10,11... | collective-permute-start | bytes 3145736 | tf_op jit(solution)/shard_map/ppermute | solution.py:19
  204.7 23.3 %collective-permute-start.22 = (bf16[2,128,1024]{2,1,0:T(8,128)(2,1)S(1)}, bf16[2,128,1024]{2,1,0:T(8,128)(2,1)S(1)}, u32[]{:S(2)}, u32[]{:S(2)}) collective-permute-start(bf16[2,128,1024]{2,1,0:T(8,128)(2,1)S(1)} %get-tuple-element.449), channel_id=1, source_target_pairs={{0,1},{1,0},{2,3},{3,2},{4,5},{5,4},{6,7},{7,6},{8,9},{9,8},{10,11... | collective-permute-start | bytes 1572872 | tf_op jit(solution)/shard_map/ppermute | solution.py:19
  206.2 21.8 %collective-permute-start.21 = (bf16[2,128,1024]{2,1,0:T(8,128)(2,1)S(1)}, bf16[2,128,1024]{2,1,0:T(8,128)(2,1)S(1)}, u32[]{:S(2)}, u32[]{:S(2)}) collective-permute-start(bf16[2,128,1024]{2,1,0:T(8,128)(2,1)S(1)} %get-tuple-element.448), channel_id=1, source_target_pairs={{0,2},{1,3},{2,0},{3,1},{4,6},{5,7},{6,4},{7,5},{8,10},{9,11},{10,... | collective-permute-start | bytes 1572872 | tf_op jit(solution)/shard_map/ppermute | solution.py:19
  228.1 7.4 %collective-permute-start.23 = (bf16[8,128,1024]{2,1,0:T(8,128)(2,1)}, bf16[8,128,1024]{2,1,0:T(8,128)(2,1)S(1)}, u32[]{:S(2)}, u32[]{:S(2)}) collective-permute-start(bf16[8,128,1024]{2,1,0:T(8,128)(2,1)} %get-tuple-element.452), channel_id=1, source_target_pairs={{0,8},{8,0},{16,24},{24,16},{1,9},{9,1},{17,25},{25,17},{2,10},{10... | collective-permute-start | bytes 6291464 | tf_op jit(solution)/shard_map/ppermute | solution.py:19
  237.1 36.8 %collective-permute-start.28 = (bf16[2,2,128,1024]{3,2,1,0:T(8,128)(2,1)}, bf16[2,2,128,1024]{3,2,1,0:T(8,128)(2,1)}, u32[]{:S(2)}, u32[]{:S(2)}) collective-permute-start(bf16[2,2,128,1024]{3,2,1,0:T(8,128)(2,1)} %fusion.1), channel_id=1, source_target_pairs={{0,2},{1,3},{2,0},{3,1},{4,6},{5,7},{6,4},{7,5},{8,10},{9,11},{10,... | collective-permute-start | bytes 3145736 | tf_op jit(solution)/shard_map/ppermute | solution.py:19
  238.4 35.5 %collective-permute-start.27 = (bf16[2,2,128,1024]{3,2,1,0:T(8,128)(2,1)S(1)}, bf16[2,2,128,1024]{3,2,1,0:T(8,128)(2,1)}, u32[]{:S(2)}, u32[]{:S(2)}) collective-permute-start(bf16[2,2,128,1024]{3,2,1,0:T(8,128)(2,1)S(1)} %bitcast.253), channel_id=1, source_target_pairs={{0,1},{1,0},{2,3},{3,2},{4,5},{5,4},{6,7},{7,6},{8,9},{9,8},{10,11... | collective-permute-start | bytes 3145736 | tf_op jit(solution)/shard_map/ppermute | solution.py:19
  239.0 32.0 %collective-permute-start.26 = (bf16[128,1024]{1,0:T(8,128)(2,1)}, bf16[128,1024]{1,0:T(8,128)(2,1)S(1)}, u32[]{:S(2)}, u32[]{:S(2)}) collective-permute-start(bf16[128,1024]{1,0:T(8,128)(2,1)} %fusion.16), channel_id=1, source_target_pairs={{0,4},{1,5},{2,6},{3,7},{4,0},{5,1},{6,2},{7,3},{8,12},{9,13},{10,... | collective-permute-start | bytes 786440 | tf_op jit(solution)/shard_map/ppermute | solution.py:19
  241.1 31.5 %collective-permute-start.25 = (bf16[128,1024]{1,0:T(8,128)(2,1)S(1)}, bf16[128,1024]{1,0:T(8,128)(2,1)S(1)}, u32[]{:S(2)}, u32[]{:S(2)}) collective-permute-start(bf16[128,1024]{1,0:T(8,128)(2,1)S(1)} %fusion.15), channel_id=1, source_target_pairs={{0,4},{1,5},{2,6},{3,7},{4,0},{5,1},{6,2},{7,3},{8,12},{9,13},{10,... | collective-permute-start | bytes 786440 | tf_op jit(solution)/shard_map/ppermute | solution.py:19
  273.9 4.7 %collective-permute-start.29 = (bf16[8,128,1024]{2,1,0:T(8,128)(2,1)}, bf16[8,128,1024]{2,1,0:T(8,128)(2,1)S(1)}, u32[]{:S(2)}, u32[]{:S(2)}) collective-permute-start(bf16[8,128,1024]{2,1,0:T(8,128)(2,1)} %get-tuple-element.486), channel_id=1, source_target_pairs={{0,8},{8,0},{16,24},{24,16},{1,9},{9,1},{17,25},{25,17},{2,10},{10... | collective-permute-start | bytes 6291464 | tf_op jit(solution)/shard_map/ppermute | solution.py:19
  280.9 25.6 %collective-permute-start.32 = (bf16[4,128,1024]{2,1,0:T(8,128)(2,1)}, bf16[4,128,1024]{2,1,0:T(8,128)(2,1)S(1)}, u32[]{:S(2)}, u32[]{:S(2)}) collective-permute-start(bf16[4,128,1024]{2,1,0:T(8,128)(2,1)} %get-tuple-element.506), channel_id=1, source_target_pairs={{0,16},{8,24},{16,0},{24,8},{1,17},{9,25},{17,1},{25,9},{2,18},{10... | collective-permute-start | bytes 3145736 | tf_op jit(solution)/shard_map/ppermute | solution.py:19
  281.5 21.0 %collective-permute-start.31 = (bf16[2,128,1024]{2,1,0:T(8,128)(2,1)}, bf16[2,128,1024]{2,1,0:T(8,128)(2,1)S(1)}, u32[]{:S(2)}, u32[]{:S(2)}) collective-permute-start(bf16[2,128,1024]{2,1,0:T(8,128)(2,1)} %fusion.5), channel_id=1, source_target_pairs={{0,1},{1,0},{2,3},{3,2},{4,5},{5,4},{6,7},{7,6},{8,9},{9,8},{10,11... | collective-permute-start | bytes 1572872 | tf_op jit(solution)/shard_map/ppermute | solution.py:19
  282.4 20.1 %collective-permute-start.30 = (bf16[2,128,1024]{2,1,0:T(8,128)(2,1)}, bf16[2,128,1024]{2,1,0:T(8,128)(2,1)}, u32[]{:S(2)}, u32[]{:S(2)}) collective-permute-start(bf16[2,128,1024]{2,1,0:T(8,128)(2,1)} %fusion.4), channel_id=1, source_target_pairs={{0,2},{1,3},{2,0},{3,1},{4,6},{5,7},{6,4},{7,5},{8,10},{9,11},{10,... | collective-permute-start | bytes 1572872 | tf_op jit(solution)/shard_map/ppermute | solution.py:19
  306.6 11.3 %collective-permute-start.33 = (bf16[8,128,1024]{2,1,0:T(8,128)(2,1)}, bf16[8,128,1024]{2,1,0:T(8,128)(2,1)S(1)}, u32[]{:S(2)}, u32[]{:S(2)}) collective-permute-start(bf16[8,128,1024]{2,1,0:T(8,128)(2,1)} %get-tuple-element.508), channel_id=1, source_target_pairs={{0,8},{8,0},{16,24},{24,16},{1,9},{9,1},{17,25},{25,17},{2,10},{10... | collective-permute-start | bytes 6291464 | tf_op jit(solution)/shard_map/ppermute | solution.py:19
  319.6 32.3 %collective-permute-start.37 = (bf16[4,128,1024]{2,1,0:T(8,128)(2,1)}, bf16[4,128,1024]{2,1,0:T(8,128)(2,1)}, u32[]{:S(2)}, u32[]{:S(2)}) collective-permute-start(bf16[4,128,1024]{2,1,0:T(8,128)(2,1)} %get-tuple-element.537), channel_id=1, source_target_pairs={{0,16},{8,24},{16,0},{24,8},{1,17},{9,25},{17,1},{25,9},{2,18},{10... | collective-permute-start | bytes 3145736 | tf_op jit(solution)/shard_map/ppermute | solution.py:19
  320.2 31.7 %collective-permute-start.36 = (bf16[2,2,128,1024]{3,2,1,0:T(8,128)(2,1)}, bf16[2,2,128,1024]{3,2,1,0:T(8,128)(2,1)}, u32[]{:S(2)}, u32[]{:S(2)}) collective-permute-start(bf16[2,2,128,1024]{3,2,1,0:T(8,128)(2,1)} %bitcast.56), channel_id=1, source_target_pairs={{0,1},{1,0},{2,3},{3,2},{4,5},{5,4},{6,7},{7,6},{8,9},{9,8},{10,11... | collective-permute-start | bytes 3145736 | tf_op jit(solution)/shard_map/ppermute | solution.py:19
  326.1 21.7 %collective-permute-start.35 = (bf16[128,1024]{1,0:T(8,128)(2,1)}, bf16[128,1024]{1,0:T(8,128)(2,1)}, u32[]{:S(2)}, u32[]{:S(2)}) collective-permute-start(bf16[128,1024]{1,0:T(8,128)(2,1)} %fusion.14), channel_id=1, source_target_pairs={{0,4},{1,5},{2,6},{3,7},{4,0},{5,1},{6,2},{7,3},{8,12},{9,13},{10,... | collective-permute-start | bytes 786440 | tf_op jit(solution)/shard_map/ppermute | solution.py:19
  327.8 24.1 %collective-permute-start.34 = (bf16[128,1024]{1,0:T(8,128)(2,1)}, bf16[128,1024]{1,0:T(8,128)(2,1)}, u32[]{:S(2)}, u32[]{:S(2)}) collective-permute-start(bf16[128,1024]{1,0:T(8,128)(2,1)} %fusion.13), channel_id=1, source_target_pairs={{0,4},{1,5},{2,6},{3,7},{4,0},{5,1},{6,2},{7,3},{8,12},{9,13},{10,... | collective-permute-start | bytes 786440 | tf_op jit(solution)/shard_map/ppermute | solution.py:19
  354.4 20.4 %collective-permute-start.41 = (bf16[2,128,1024]{2,1,0:T(8,128)(2,1)}, bf16[2,128,1024]{2,1,0:T(8,128)(2,1)}, u32[]{:S(2)}, u32[]{:S(2)}) collective-permute-start(bf16[2,128,1024]{2,1,0:T(8,128)(2,1)} %fusion.3), channel_id=1, source_target_pairs={{0,2},{1,3},{2,0},{3,1},{4,6},{5,7},{6,4},{7,5},{8,10},{9,11},{10,... | collective-permute-start | bytes 1572872 | tf_op jit(solution)/shard_map/ppermute | solution.py:19
  359.2 17.0 %collective-permute-start.42 = (bf16[2,128,1024]{2,1,0:T(8,128)(2,1)}, bf16[2,128,1024]{2,1,0:T(8,128)(2,1)S(1)}, u32[]{:S(2)}, u32[]{:S(2)}) collective-permute-start(bf16[2,128,1024]{2,1,0:T(8,128)(2,1)} %pad_maximum_fusion.3), channel_id=1, source_target_pairs={{0,16},{8,24},{16,0},{24,8},{1,17},{9,25},{17,1},{25,9},{2,18},{10... | collective-permute-start | bytes 1572872 | tf_op jit(solution)/shard_map/ppermute | solution.py:19
  361.3 13.5 %collective-permute-start.39 = (f32[8,16,128]{2,1,0:T(8,128)}, f32[8,16,128]{2,1,0:T(8,128)S(1)}, u32[]{:S(2)}, u32[]{:S(2)}) collective-permute-start(f32[8,16,128]{2,1,0:T(8,128)} %pack_sums.1), channel_id=1, source_target_pairs={{0,16},{8,24},{16,0},{24,8},{1,17},{9,25},{17,1},{25,9},{2,18},{10... | collective-permute-start | bytes 196616 | tf_op jit(solution)/shard_map/ppermute | solution.py:19
  362.3 12.5 %collective-permute-start.40 = (f32[8,16,128]{2,1,0:T(8,128)}, f32[8,16,128]{2,1,0:T(8,128)S(1)}, u32[]{:S(2)}, u32[]{:S(2)}) collective-permute-start(f32[8,16,128]{2,1,0:T(8,128)} %pack_sums.1), channel_id=1, source_target_pairs={{0,24},{8,16},{16,8},{24,0},{1,25},{9,17},{17,9},{25,1},{2,26},{10... | collective-permute-start | bytes 196616 | tf_op jit(solution)/shard_map/ppermute | solution.py:19
  376.2 15.8 %collective-permute-start.44 = (bf16[128,1024]{1,0:T(8,128)(2,1)S(1)}, bf16[128,1024]{1,0:T(8,128)(2,1)S(1)}, u32[]{:S(2)}, u32[]{:S(2)}) collective-permute-start(bf16[128,1024]{1,0:T(8,128)(2,1)S(1)} %fusion.12), channel_id=1, source_target_pairs={{0,4},{1,5},{2,6},{3,7},{4,0},{5,1},{6,2},{7,3},{8,12},{9,13},{10,... | collective-permute-start | bytes 786440 | tf_op jit(solution)/shard_map/ppermute | solution.py:19
  382.5 20.3 %collective-permute-start.46 = (bf16[2,128,1024]{2,1,0:T(8,128)(2,1)}, bf16[2,128,1024]{2,1,0:T(8,128)(2,1)}, u32[]{:S(2)}, u32[]{:S(2)}) collective-permute-start(bf16[2,128,1024]{2,1,0:T(8,128)(2,1)} %pad_maximum_fusion.4.refs_0_), channel_id=1, source_target_pairs={{0,8},{8,0},{16,24},{24,16},{1,9},{9,1},{17,25},{25,17},{2,10},{10... | collective-permute-start | bytes 1572872 | tf_op jit(solution)/shard_map/ppermute | solution.py:19
  382.6 20.3 %collective-permute-start.47 = (bf16[2,128,1024]{2,1,0:T(8,128)(2,1)}, bf16[2,128,1024]{2,1,0:T(8,128)(2,1)}, u32[]{:S(2)}, u32[]{:S(2)}) collective-permute-start(bf16[2,128,1024]{2,1,0:T(8,128)(2,1)} %pad_maximum_fusion.4.refs_0_), channel_id=1, source_target_pairs={{0,16},{8,24},{16,0},{24,8},{1,17},{9,25},{17,1},{25,9},{2,18},{10... | collective-permute-start | bytes 1572872 | tf_op jit(solution)/shard_map/ppermute | solution.py:19
  393.3 7.0 %collective-permute-start.48 = (bf16[128,1024]{1,0:T(8,128)(2,1)S(1)}, bf16[128,1024]{1,0:T(8,128)(2,1)}, u32[]{:S(2)}, u32[]{:S(2)}) collective-permute-start(bf16[128,1024]{1,0:T(8,128)(2,1)S(1)} %fusion.9.refs_0_), channel_id=1, source_target_pairs={{0,8},{8,0},{16,24},{24,16},{1,9},{9,1},{17,25},{25,17},{2,10},{10... | collective-permute-start | bytes 786440 | tf_op jit(solution)/shard_map/ppermute | solution.py:19
  393.5 9.3 %collective-permute-start.49 = (bf16[128,1024]{1,0:T(8,128)(2,1)S(1)}, bf16[128,1024]{1,0:T(8,128)(2,1)}, u32[]{:S(2)}, u32[]{:S(2)}) collective-permute-start(bf16[128,1024]{1,0:T(8,128)(2,1)S(1)} %fusion.9.refs_0_), channel_id=1, source_target_pairs={{0,16},{8,24},{16,0},{24,8},{1,17},{9,25},{17,1},{25,9},{2,18},{10... | collective-permute-start | bytes 786440 | tf_op jit(solution)/shard_map/ppermute | solution.py:19
  395.2 5.2 %collective-permute-start.45 = (f32[2,16,128]{2,1,0:T(8,128)}, f32[2,16,128]{2,1,0:T(8,128)S(1)}, u32[]{:S(2)}, u32[]{:S(2)}) collective-permute-start(f32[2,16,128]{2,1,0:T(8,128)} %bitcast_add_fusion), channel_id=1, source_target_pairs={{0,2},{1,3},{2,0},{3,1},{4,6},{5,7},{6,4},{7,5},{8,10},{9,11},{10,... | collective-permute-start | bytes 49160 | tf_op jit(solution)/shard_map/ppermute | solution.py:19
  402.8 5.9 %collective-permute-start.50 = (bf16[2,128,1024]{2,1,0:T(8,128)(2,1)}, bf16[2,128,1024]{2,1,0:T(8,128)(2,1)S(1)}, u32[]{:S(2)}, u32[]{:S(2)}) collective-permute-start(bf16[2,128,1024]{2,1,0:T(8,128)(2,1)} %collective-permute-done.47.refs_2_), channel_id=1, source_target_pairs={{0,8},{8,0},{16,24},{24,16},{1,9},{9,1},{17,25},{25,17},{2,10},{10... | collective-permute-start | bytes 1572872 | tf_op jit(solution)/shard_map/ppermute | solution.py:19
  402.8 5.8 %collective-permute-start.51 = (bf16[128,1024]{1,0:T(8,128)(2,1)}, bf16[128,1024]{1,0:T(8,128)(2,1)S(1)}, u32[]{:S(2)}, u32[]{:S(2)}) collective-permute-start(bf16[128,1024]{1,0:T(8,128)(2,1)} %collective-permute-done.49.refs_2_), channel_id=1, source_target_pairs={{0,8},{8,0},{16,24},{24,16},{1,9},{9,1},{17,25},{25,17},{2,10},{10... | collective-permute-start | bytes 786440 | tf_op jit(solution)/shard_map/ppermute | solution.py:19
  404.1 4.6 %collective-permute-start.52 = (f32[16,128]{1,0:T(8,128)S(1)}, f32[16,128]{1,0:T(8,128)S(1)}, u32[]{:S(2)}, u32[]{:S(2)}) collective-permute-start(f32[16,128]{1,0:T(8,128)S(1)} %bitcast_add_fusion.3), channel_id=1, source_target_pairs={{0,4},{1,5},{2,6},{3,7},{4,0},{5,1},{6,2},{7,3},{8,12},{9,13},{10,... | collective-permute-start | bytes 24584 | tf_op jit(solution)/shard_map/ppermute | solution.py:19
  (64 other events, 496.2 us)
Sparse Core Ops, SparseCore 0:
  24.4 81.8 all-gather.4
  110.9 48.9 all-gather.6

commit v3 on v1

--- a/solution.py
+++ b/solution.py
@@ -1105,8 +1105,9 @@
         red_w.launch()
         seq.land((), red_w)
     red_w.launch()
+    two_up.terms[-1], two_down.terms[-1], sums_one = seq.at((two_up.terms[-1], two_down.terms[-1], sums_one))
     packed = pack_sums(
-        seq.at(order),
+        order,
         n,
         rows,
         ffq,
@@ -1118,10 +1119,14 @@
     peers = Sent([xor_swap(packed, "dp", 4, m) for m in (1, 2, 3)])
     crossing = jnp.stack([two_up.rest().piece(), two_down.rest().piece()])
     cross = Sent(x_swap(seq.at(crossing)))
-    seq.land((), peers, red_w, cross)
+    seq.land((), red_w)
     if red_w.axes:
         red_w.launch()
-    owned = [rounded_sum([*red_up.rest().terms, cross.value[0]]), rounded_sum([*red_down.rest().terms, cross.value[1]])]
+    seq.land((), peers, cross)
+    owned = [
+        rounded_sum([*red_up.rest().terms, cross.value[0]]),
+        rounded_sum([*red_down.rest().terms, cross.value[1]]),
+    ]
     mlp_spread = Spread(seq, jnp.stack(owned))
     sums = Reduce(seq, (packed, *peers.value), n, full)
     while len(sums.axes) > 1:
@@ -1132,14 +1137,11 @@
     w_spread = Spread(seq, red_w.piece())
     sums.launch()
     block, tokens_grad = seq.at((block, tokens_grad))
-    block_out, grad_tokens = seq.land((compact(block), compact(tokens_grad)), sums, mlp_spread)
+    block_out, grad_tokens = seq.land((compact(block), compact(tokens_grad)), sums, mlp_spread, w_spread)
     mlp_spread.cross()
-    small_sums = seq.land(sums.piece(), mlp_spread)
-    mlp_pieces = seq.at(mlp_spread.pieces)
-    out_fc1, out_fc2 = finish_mlp(q, mlp_pieces, n)
-    out_fc2 = seq.land(out_fc2, w_spread)
     w_spread.cross()
-    seq.land((), w_spread)
+    small_sums = seq.land(sums.piece(), mlp_spread, w_spread)
+    out_fc1, out_fc2 = finish_mlp(q, mlp_spread.pieces, n)
     out_qkv, out_out = finish_attention(seq.value, w_spread.pieces)
     small_out = [small_sums[k, :rows] for k in range(8)]
     out_bfc1 = small_sums[8:12, :ffq].reshape(-1)

time: 416 us -> 416 us (level)
  transfers between devices with their start and end apart: 55 -> 55, of which waited for: 23 -> 23; matrix products, arithmetic and copies ran while one was open for 12% -> 12% of each run, Pallas kernels for 45% -> 44%
where the time goes in v3:
time: 416 us; the launch traced here: 411 us
  Pallas kernels  191 us (46%)
  waiting for transfers between devices  79.1 us (19%)
  starting transfers between devices  51.4 us (12%)
  other arithmetic  46.4 us (11%)
  local copies, waits for them, and re-layouts  27.7 us (7%)
  between operations  15 us (4%)
    pallas_call x17, Pallas kernels, call(): pl.pallas_call(kernel, out_shape=[jax.ShapeDtypeStruct(shape, kind) for s...  191 us
    ppermute x53, waiting for transfers between devices, xor_swap(): return lax.ppermute(value, axis, [(i, i ^ mask) for i in range(size)])  79 us
    ppermute x53, starting transfers between devices, xor_swap(): return lax.ppermute(value, axis, [(i, i ^ mask) for i in range(size)])  51.4 us
    convert_element_type x16, other arithmetic, rounded_sum(): return sum((t.astype(full) for t in terms)).astype(kind)  30.5 us
  transfers between devices with their start and end apart: 55, of which 23 were waited for; matrix products, arithmetic and copies ran while one was open for 12% of the time, Pallas kernels for 44%

profile of v3, /device:TPU:0, one launch (start us, length us, event | category | flops | bytes accessed | tf_op | source)
XLA Modules:
  0.0 410.9 jit_solution(17444048479815492506)
XLA Ops:
  7.2 2.6 first_payload.1
  9.8 4.1 collective-permute-start
  14.5 3.3 payloads.1
  17.8 6.5 %collective-permute-done = bf16[1,144,768]{2,1,0:T(8,128)(2,1)S(1)} collective-permute-done((bf16[1,144,768]{2,1,0:T(8,128)(2,1)}, bf16[1,144,768]{2,1,0:T(8,128)(2,1)S(1)}, u32[]{:S(2)}, u32[]{:S(2)}) %collective-permute-start) | collective-permute-done | bytes 221216 | tf_op jit(solution)/shard_map/ppermute | solution.py:19
  27.5 3.6 copy.32
  31.1 2.2 reshape.461
  41.3 6.6 %collective-permute-start.4 = (bf16[1,128,512]{2,1,0:T(8,128)(2,1)S(1)}, bf16[1,128,512]{2,1,0:T(8,128)(2,1)S(1)}, u32[]{:S(2)}, u32[]{:S(2)}) collective-permute-start(bf16[1,128,512]{2,1,0:T(8,128)(2,1)S(1)} %pad_maximum_fusion.7), channel_id=1, source_target_pairs={{0,4},{1,5},{2,6},{3,7},{4,0},{5,1},{6,2},{7,3},{8,12},{9,13},{10,... | collective-permute-start | bytes 393224 | tf_op jit(solution)/shard_map/ppermute | solution.py:19
  48.7 11.6 %collective-permute-done.4 = bf16[1,128,512]{2,1,0:T(8,128)(2,1)S(1)} collective-permute-done((bf16[1,128,512]{2,1,0:T(8,128)(2,1)S(1)}, bf16[1,128,512]{2,1,0:T(8,128)(2,1)S(1)}, u32[]{:S(2)}, u32[]{:S(2)}) %collective-permute-start.4) | collective-permute-done | bytes 131104 | tf_op jit(solution)/shard_map/ppermute | solution.py:19
  63.8 2.3 unpack_vectors.1
  71.5 10.5 %attention_forward.2 = (bf16[832,768]{1,0:T(8,128)(2,1)}, bf16[832,768]{1,0:T(8,128)(2,1)}, bf16[832,256]{1,0:T(8,128)(2,1)}, bf16[832,256]{1,0:T(8,128)(2,1)}, ...) custom-call(s32[9]{0:T(128)} %pad_add_fusion.1.order_ref, bf16[832,1024]{1,0:T(8,128)(2,1)} %add_convert_fusion.normed_ref, ...), custom_call_target="tpu_custom_call" | custom-call | tf_op jit(solution)/shard_map/attention_forward/pallas_call | solution.py:133
  82.0 8.9 %collective-permute-done.8 = bf16[2,128,512]{2,1,0:T(8,128)(2,1)S(1)} collective-permute-done((bf16[2,128,512]{2,1,0:T(8,128)(2,1)S(1)}, bf16[2,128,512]{2,1,0:T(8,128)(2,1)S(1)}, u32[]{:S(2)}, u32[]{:S(2)}) %collective-permute-start.8) | collective-permute-done | bytes 262176 | tf_op jit(solution)/shard_map/ppermute | solution.py:19
  96.2 10.5 %attention_forward.3 = (bf16[832,768]{1,0:T(8,128)(2,1)}, bf16[832,768]{1,0:T(8,128)(2,1)}, bf16[832,256]{1,0:T(8,128)(2,1)}, bf16[832,256]{1,0:T(8,128)(2,1)}, ...) custom-call(s32[9]{0:T(128)} %pad_add_fusion.1.order_ref, bf16[832,1024]{1,0:T(8,128)(2,1)} %add_convert_fusion.normed_ref, ...), custom_call_target="tpu_custom_call" | custom-call | tf_op jit(solution)/shard_map/attention_forward/pallas_call | solution.py:133
  108.0 2.6 collective-permute-done.12.refs_5_
  110.9 3.3 slice.528
  115.8 9.8 %attention_out.1 = (f32[832,1024]{1,0:T(8,128)}, bf16[832,1024]{1,0:T(8,128)(2,1)}) custom-call(s32[9]{0:T(128)} %pad_add_fusion.1.order_ref, f32[832,1024]{1,0:T(8,128)} %bitcast.229, f32[1,1024]{1,0:T(1,128)} %get-tuple-element.591.bias_ref, f32[1,1024]{1,0:T(1,128)} %get-tuple-element.590.gain_ref, f32[1,1024]{1,0:T(1,128)} %get-tuple-element.589.shift_ref, ...), custom_call_target="tpu_custom_call" | custom-call | tf_op jit(solution)/shard_map/attention_out/pallas_call | solution.py:133
  125.6 19.2 %mlp.4 = (bf16[8,128,1024]{2,1,0:T(8,128)(2,1)}, bf16[8,128,1024]{2,1,0:T(8,128)(2,1)}, f32[1,1024]{1,0:T(1,128)}, f32[832,1024]{1,0:T(8,128)}, f32[832,1024]{1,0:T(8,128)}) custom-call(s32[9]{0:T(128)} %pad_add_fusion.1.order_ref, f32[1,1024]{1,0:T(1,128)} %get-tuple-element.596.bias_ref, bf16[832,1024]{1,0:T(8,128)(2,1)} %get-tuple-element.372.refs_0_.refs_1_, ...), custom_call_target="tpu_custom_call" | custom-call | tf_op jit(solution)/shard_map/mlp/pallas_call | solution.py:133
  144.9 20.4 %mlp.5 = (bf16[8,128,1024]{2,1,0:T(8,128)(2,1)}, bf16[8,128,1024]{2,1,0:T(8,128)(2,1)}, f32[1,1024]{1,0:T(1,128)}, f32[832,1024]{1,0:T(8,128)}, f32[832,1024]{1,0:T(8,128)}) custom-call(s32[9]{0:T(128)} %pad_add_fusion.1.order_ref, f32[1,1024]{1,0:T(1,128)} %get-tuple-element.597.bias_ref, bf16[832,1024]{1,0:T(8,128)(2,1)} %get-tuple-element.372.refs_0_.refs_1_, ...), custom_call_target="tpu_custom_call" | custom-call | tf_op jit(solution)/shard_map/mlp/pallas_call | solution.py:133
  165.9 3.9 collective-permute-done.16
  169.8 2.4 add_convert_fusion.7
  177.8 20.5 %mlp.6 = (bf16[8,128,1024]{2,1,0:T(8,128)(2,1)}, bf16[8,128,1024]{2,1,0:T(8,128)(2,1)}, f32[1,1024]{1,0:T(1,128)}, f32[832,1024]{1,0:T(8,128)}, f32[832,1024]{1,0:T(8,128)}) custom-call(s32[9]{0:T(128)} %pad_add_fusion.1.order_ref, f32[1,1024]{1,0:T(1,128)} %get-tuple-element.595.bias_ref, bf16[832,1024]{1,0:T(8,128)(2,1)} %get-tuple-element.372.refs_0_.refs_1_, ...), custom_call_target="tpu_custom_call" | custom-call | tf_op jit(solution)/shard_map/mlp/pallas_call | solution.py:133
  198.3 2.2 collective-permute-done.20
  201.3 3.2 fusion.6
  206.8 21.1 %mlp.7 = (bf16[8,128,1024]{2,1,0:T(8,128)(2,1)}, bf16[8,128,1024]{2,1,0:T(8,128)(2,1)}, f32[1,1024]{1,0:T(1,128)}, f32[832,1024]{1,0:T(8,128)}, bf16[832,1024]{1,0:T(8,128)(2,1)}) custom-call(s32[9]{0:T(128)} %pad_add_fusion.1.order_ref, f32[1,1024]{1,0:T(1,128)} %get-tuple-element.594.bias_ref, f32[1,1024]{1,0:T(1,128)} %get-tuple-element.588.refs_0_, ...), custom_call_target="tpu_custom_call" | custom-call | tf_op jit(solution)/shard_map/mlp/pallas_call | solution.py:133
  228.5 2.2 fusion.21
  230.7 2.2 fusion.22
  233.3 2.1 collective-permute-done.23
  240.0 2.1 collective-permute-start.26
  242.9 11.0 %attention_out_back.1 = (f32[832,1024]{1,0:T(8,128)}, bf16[832,256]{1,0:T(8,128)(2,1)}, bf16[832,256]{1,0:T(8,128)(2,1)}, bf16[832,256]{1,0:T(8,128)(2,1)}, bf16...) custom-call(s32[9]{0:T(128)} %pad_add_fusion.1.order_ref, ...), custom_call_target="tpu_custom_call" | custom-call | tf_op jit(solution)/shard_map/attention_out_back/pallas_call | solution.py:133
  253.9 18.1 %attention_back.2 = (bf16[8,128,1024]{2,1,0:T(8,128)(2,1)}, bf16[8,128,1024]{2,1,0:T(8,128)(2,1)}, bf16[832,768]{1,0:T(8,128)(2,1)}, bf16[832,768]{1,0:T(8,128)(2,1)}, f32[2,1,768]{2,1,0:T(1,128)}) custom-call(s32[9]{0:T(128)} %pad_add_fusion.1.order_ref, bf16[832,1024]{1,0:T(8,128)(2,1)} %add_convert_fusion.normed_ref, ...), custom_call_target="tpu_custom_call" | custom-call | tf_op jit(solution)/shard_map/attention_back/pallas_call | solution.py:133
  274.8 2.4 fusion.4
  277.3 2.3 fusion.5
  279.6 2.4 add_convert_fusion.2
  283.5 2.1 collective-permute-start.30
  285.6 18.0 %attention_back.3 = (bf16[8,128,1024]{2,1,0:T(8,128)(2,1)}, bf16[8,128,1024]{2,1,0:T(8,128)(2,1)}, bf16[832,768]{1,0:T(8,128)(2,1)}, bf16[832,768]{1,0:T(8,128)(2,1)}, f32[2,1,768]{2,1,0:T(1,128)}) custom-call(s32[9]{0:T(128)} %pad_add_fusion.1.order_ref, bf16[832,1024]{1,0:T(8,128)(2,1)} %add_convert_fusion.normed_ref, ...), custom_call_target="tpu_custom_call" | custom-call | tf_op jit(solution)/shard_map/attention_back/pallas_call | solution.py:133
  303.6 3.9 collective-permute-done.32
  308.8 2.0 fusion.20
  319.3 16.0 %input_back.1 = (f32[832,1024]{1,0:T(8,128)}, f32[2,1,1024]{2,1,0:T(1,128)}) custom-call(s32[9]{0:T(128)} %pad_add_fusion.1.order_ref, f32[832,1024]{1,0:T(8,128)} %bitcast.230, f32[832,1024]{1,0:T(8,128)} %get-tuple-element.497.after_ref, f32[1,1024]{1,0:T(1,128)} %get-tuple-element.587.gain_ref, bf16[832,768]{1,0:T(8,128)(2,1)} %get-tuple-element.498.refs_0_, ...), custom_call_target="tpu_custom_call" | custom-call | tf_op jit(solution)/shard_map/input_back/pallas_call | solution.py:133
  336.8 4.2 %collective-permute-done.34 = bf16[128,1024]{1,0:T(8,128)(2,1)} collective-permute-done((bf16[128,1024]{1,0:T(8,128)(2,1)S(1)}, bf16[128,1024]{1,0:T(8,128)(2,1)}, u32[]{:S(2)}, u32[]{:S(2)}) %collective-permute-start.34) | collective-permute-done | bytes 262176 | tf_op jit(solution)/shard_map/ppermute | solution.py:19
  341.0 2.5 fusion.3
  352.4 6.9 %collective-permute-done.42 = bf16[2,128,1024]{2,1,0:T(8,128)(2,1)S(1)} collective-permute-done((bf16[2,128,1024]{2,1,0:T(8,128)(2,1)}, bf16[2,128,1024]{2,1,0:T(8,128)(2,1)S(1)}, u32[]{:S(2)}, u32[]{:S(2)}) %collective-permute-start.42) | collective-permute-done | bytes 524320 | tf_op jit(solution)/shard_map/ppermute | solution.py:19
  360.6 3.1 collective-permute-done.39
  363.8 2.2 fusion.25
  367.8 3.5 collective-permute-start.45
  372.7 4.9 %collective-permute-done.44 = f32[2,16,128]{2,1,0:T(8,128)S(1)} collective-permute-done((f32[2,16,128]{2,1,0:T(8,128)S(1)}, f32[2,16,128]{2,1,0:T(8,128)S(1)}, u32[]{:S(2)}, u32[]{:S(2)}) %collective-permute-start.44) | collective-permute-done | bytes 16416 | tf_op jit(solution)/shard_map/ppermute | solution.py:19
  377.6 5.8 %collective-permute-done.45 = bf16[128,1024]{1,0:T(8,128)(2,1)S(1)} collective-permute-done((bf16[128,1024]{1,0:T(8,128)(2,1)S(1)}, bf16[128,1024]{1,0:T(8,128)(2,1)S(1)}, u32[]{:S(2)}, u32[]{:S(2)}) %collective-permute-start.45) | collective-permute-done | bytes 262176 | tf_op jit(solution)/shard_map/ppermute | solution.py:19
  391.3 2.4 collective-permute-done.50.refs_2_
  397.4 3.9 finish_mlp.1
  401.3 2.6 finish_attention.1
  (231 shorter events, 86.0 us)
Async XLA Ops:
  7.2 99.6 %all-gather.5.cloned.1.call-start = ((), (), s32[]{:S(2)}) async-start(), calls=%async_computation | async-start | bytes 4718592 | tf_op jit(solution)/shard_map/all_gather | solution.py:963
  9.8 14.5 %collective-permute-start = (bf16[1,144,768]{2,1,0:T(8,128)(2,1)}, bf16[1,144,768]{2,1,0:T(8,128)(2,1)S(1)}, u32[]{:S(2)}, u32[]{:S(2)}) collective-permute-start(bf16[1,144,768]{2,1,0:T(8,128)(2,1)} %bitcast.263), channel_id=1, source_target_pairs={{0,4},{1,5},{2,6},{3,7},{4,0},{5,1},{6,2},{7,3},{8,12},{9,13},{10,... | collective-permute-start | bytes 663560 | tf_op jit(solution)/shard_map/ppermute | solution.py:19
  24.3 141.0 %all-gather.7.cloned.1.call-start = ((), (), s32[]{:S(2)}) async-start(), calls=%async_computation.1 | async-start | bytes 2359296 | tf_op jit(solution)/shard_map/all_gather | solution.py:964
  24.5 11.4 %collective-permute-start.1 = (bf16[2,144,768]{2,1,0:T(8,128)(2,1)S(1)}, bf16[2,144,768]{2,1,0:T(8,128)(2,1)S(1)}, u32[]{:S(2)}, u32[]{:S(2)}) collective-permute-start(bf16[2,144,768]{2,1,0:T(8,128)(2,1)S(1)} %pad_maximum_fusion.5), channel_id=1, source_target_pairs={{0,2},{1,3},{2,0},{3,1},{4,6},{5,7},{6,4},{7,5},{8,10},{9,11},{10,... | collective-permute-start | bytes 1327112 | tf_op jit(solution)/shard_map/ppermute | solution.py:19
  36.7 24.4 %collective-permute-start.2 = (bf16[4,144,768]{2,1,0:T(8,128)(2,1)}, bf16[4,144,768]{2,1,0:T(8,128)(2,1)}, u32[]{:S(2)}, u32[]{:S(2)}) collective-permute-start(bf16[4,144,768]{2,1,0:T(8,128)(2,1)} %constant_dynamic-update-slice_fusion.refs_0_.refs_4_), channel_id=1, source_target_pairs={{0,1},{1,0},{2,3},{3,2},{4,5},{5,4},{6,7},{7,6},{8,9},{9,8},{10,11... | collective-permute-start | bytes 2654216 | tf_op jit(solution)/shard_map/ppermute | solution.py:19
  38.1 23.0 %collective-permute-start.3 = (bf16[4,144,768]{2,1,0:T(8,128)(2,1)}, bf16[4,144,768]{2,1,0:T(8,128)(2,1)}, u32[]{:S(2)}, u32[]{:S(2)}) collective-permute-start(bf16[4,144,768]{2,1,0:T(8,128)(2,1)} %constant_dynamic-update-slice_fusion.refs_0_.refs_4_), channel_id=1, source_target_pairs={{0,8},{8,0},{16,24},{24,16},{1,9},{9,1},{17,25},{25,17},{2,10},{10... | collective-permute-start | bytes 2654216 | tf_op jit(solution)/shard_map/ppermute | solution.py:19
  39.7 42.3 %collective-permute-start.6 = (bf16[4,144,768]{2,1,0:T(8,128)(2,1)}, bf16[4,144,768]{2,1,0:T(8,128)(2,1)}, u32[]{:S(2)}, u32[]{:S(2)}) collective-permute-start(bf16[4,144,768]{2,1,0:T(8,128)(2,1)} %constant_dynamic-update-slice_fusion.refs_0_.refs_4_), channel_id=1, source_target_pairs={{0,16},{8,24},{16,0},{24,8},{1,17},{9,25},{17,1},{25,9},{2,18},{10... | collective-permute-start | bytes 2654216 | tf_op jit(solution)/shard_map/ppermute | solution.py:19
  41.3 19.0 %collective-permute-start.4 = (bf16[1,128,512]{2,1,0:T(8,128)(2,1)S(1)}, bf16[1,128,512]{2,1,0:T(8,128)(2,1)S(1)}, u32[]{:S(2)}, u32[]{:S(2)}) collective-permute-start(bf16[1,128,512]{2,1,0:T(8,128)(2,1)S(1)} %pad_maximum_fusion.7), channel_id=1, source_target_pairs={{0,4},{1,5},{2,6},{3,7},{4,0},{5,1},{6,2},{7,3},{8,12},{9,13},{10,... | collective-permute-start | bytes 393224 | tf_op jit(solution)/shard_map/ppermute | solution.py:19
  61.1 10.4 %collective-permute-start.5 = (bf16[4,144,768]{2,1,0:T(8,128)(2,1)}, bf16[4,144,768]{2,1,0:T(8,128)(2,1)}, u32[]{:S(2)}, u32[]{:S(2)}) collective-permute-start(bf16[4,144,768]{2,1,0:T(8,128)(2,1)} %collective-permute-done.2.refs_1_.refs_5_), channel_id=1, source_target_pairs={{0,8},{8,0},{16,24},{24,16},{1,9},{9,1},{17,25},{25,17},{2,10},{10... | collective-permute-start | bytes 2654216 | tf_op jit(solution)/shard_map/ppermute | solution.py:19
  61.1 29.8 %collective-permute-start.7 = (bf16[4,144,768]{2,1,0:T(8,128)(2,1)}, bf16[4,144,768]{2,1,0:T(8,128)(2,1)}, u32[]{:S(2)}, u32[]{:S(2)}) collective-permute-start(bf16[4,144,768]{2,1,0:T(8,128)(2,1)} %collective-permute-done.2.refs_1_.refs_5_), channel_id=1, source_target_pairs={{0,16},{8,24},{16,0},{24,8},{1,17},{9,25},{17,1},{25,9},{2,18},{10... | collective-permute-start | bytes 2654216 | tf_op jit(solution)/shard_map/ppermute | solution.py:19
  66.1 24.8 %collective-permute-start.8 = (bf16[2,128,512]{2,1,0:T(8,128)(2,1)S(1)}, bf16[2,128,512]{2,1,0:T(8,128)(2,1)S(1)}, u32[]{:S(2)}, u32[]{:S(2)}) collective-permute-start(bf16[2,128,512]{2,1,0:T(8,128)(2,1)S(1)} %pad_maximum_fusion.6), channel_id=1, source_target_pairs={{0,2},{1,3},{2,0},{3,1},{4,6},{5,7},{6,4},{7,5},{8,10},{9,11},{10,... | collective-permute-start | bytes 786440 | tf_op jit(solution)/shard_map/ppermute | solution.py:19
  91.5 15.3 %collective-permute-start.11 = (bf16[4,128,512]{2,1,0:T(8,128)(2,1)S(1)}, bf16[4,128,512]{2,1,0:T(8,128)(2,1)}, u32[]{:S(2)}, u32[]{:S(2)}) collective-permute-start(bf16[4,128,512]{2,1,0:T(8,128)(2,1)S(1)} %pad_maximum_fusion.2), channel_id=1, source_target_pairs={{0,1},{1,0},{2,3},{3,2},{4,5},{5,4},{6,7},{7,6},{8,9},{9,8},{10,11... | collective-permute-start | bytes 1572872 | tf_op jit(solution)/shard_map/ppermute | solution.py:19
  110.7 14.9 %collective-permute-start.13 = (bf16[8,128,2048]{2,1,0:T(8,128)(2,1)}, bf16[8,128,2048]{2,1,0:T(8,128)(2,1)}, u32[]{:S(2)}, u32[]{:S(2)}) collective-permute-start(bf16[8,128,2048]{2,1,0:T(8,128)(2,1)} %bitcast.236), channel_id=1, source_target_pairs={{0,8},{8,0},{16,24},{24,16},{1,9},{9,1},{17,25},{25,17},{2,10},{10... | collective-permute-start | bytes 12582920 | tf_op jit(solution)/shard_map/ppermute | solution.py:19
  114.2 51.2 %collective-permute-start.14 = (bf16[8,128,1024]{2,1,0:T(8,128)(2,1)}, bf16[8,128,1024]{2,1,0:T(8,128)(2,1)}, u32[]{:S(2)}, u32[]{:S(2)}) collective-permute-start(bf16[8,128,1024]{2,1,0:T(8,128)(2,1)} %slice.528), channel_id=1, source_target_pairs={{0,16},{8,24},{16,0},{24,8},{1,17},{9,25},{17,1},{25,9},{2,18},{10... | collective-permute-start | bytes 6291464 | tf_op jit(solution)/shard_map/ppermute | solution.py:19
  165.4 7.4 %collective-permute-start.15 = (bf16[8,128,1024]{2,1,0:T(8,128)(2,1)}, bf16[8,128,1024]{2,1,0:T(8,128)(2,1)S(1)}, u32[]{:S(2)}, u32[]{:S(2)}) collective-permute-start(bf16[8,128,1024]{2,1,0:T(8,128)(2,1)} %get-tuple-element.388), channel_id=1, source_target_pairs={{0,8},{8,0},{16,24},{24,16},{1,9},{9,1},{17,25},{25,17},{2,10},{10... | collective-permute-start | bytes 6291464 | tf_op jit(solution)/shard_map/ppermute | solution.py:19
  174.5 26.9 %collective-permute-start.17 = (bf16[8,128,1024]{2,1,0:T(8,128)(2,1)}, bf16[8,128,1024]{2,1,0:T(8,128)(2,1)S(1)}, u32[]{:S(2)}, u32[]{:S(2)}) collective-permute-start(bf16[8,128,1024]{2,1,0:T(8,128)(2,1)} %collective-permute-done.14.refs_2_), channel_id=1, source_target_pairs={{0,8},{8,0},{16,24},{24,16},{1,9},{9,1},{17,25},{25,17},{2,10},{10... | collective-permute-start | bytes 6291464 | tf_op jit(solution)/shard_map/ppermute | solution.py:19
  174.6 26.7 %collective-permute-start.18 = (bf16[8,128,1024]{2,1,0:T(8,128)(2,1)S(1)}, bf16[8,128,1024]{2,1,0:T(8,128)(2,1)}, u32[]{:S(2)}, u32[]{:S(2)}) collective-permute-start(bf16[8,128,1024]{2,1,0:T(8,128)(2,1)S(1)} %bitcast.243), channel_id=1, source_target_pairs={{0,8},{8,0},{16,24},{24,16},{1,9},{9,1},{17,25},{25,17},{2,10},{10... | collective-permute-start | bytes 6291464 | tf_op jit(solution)/shard_map/ppermute | solution.py:19
  175.0 25.5 %collective-permute-start.20 = (bf16[2,2,128,1024]{3,2,1,0:T(8,128)(2,1)}, bf16[2,2,128,1024]{3,2,1,0:T(8,128)(2,1)}, u32[]{:S(2)}, u32[]{:S(2)}) collective-permute-start(bf16[2,2,128,1024]{3,2,1,0:T(8,128)(2,1)} %fusion), channel_id=1, source_target_pairs={{0,2},{1,3},{2,0},{3,1},{4,6},{5,7},{6,4},{7,5},{8,10},{9,11},{10,... | collective-permute-start | bytes 3145736 | tf_op jit(solution)/shard_map/ppermute | solution.py:19
  176.3 25.0 %collective-permute-start.19 = (bf16[2,2,128,1024]{3,2,1,0:T(8,128)(2,1)S(1)}, bf16[2,2,128,1024]{3,2,1,0:T(8,128)(2,1)}, u32[]{:S(2)}, u32[]{:S(2)}) collective-permute-start(bf16[2,2,128,1024]{3,2,1,0:T(8,128)(2,1)S(1)} %bitcast.262), channel_id=1, source_target_pairs={{0,1},{1,0},{2,3},{3,2},{4,5},{5,4},{6,7},{7,6},{8,9},{9,8},{10,11... | collective-permute-start | bytes 3145736 | tf_op jit(solution)/shard_map/ppermute | solution.py:19
  204.6 23.3 %collective-permute-start.22 = (bf16[2,128,1024]{2,1,0:T(8,128)(2,1)S(1)}, bf16[2,128,1024]{2,1,0:T(8,128)(2,1)S(1)}, u32[]{:S(2)}, u32[]{:S(2)}) collective-permute-start(bf16[2,128,1024]{2,1,0:T(8,128)(2,1)S(1)} %get-tuple-element.426), channel_id=1, source_target_pairs={{0,1},{1,0},{2,3},{3,2},{4,5},{5,4},{6,7},{7,6},{8,9},{9,8},{10,11... | collective-permute-start | bytes 1572872 | tf_op jit(solution)/shard_map/ppermute | solution.py:19
  206.1 21.8 %collective-permute-start.21 = (bf16[2,128,1024]{2,1,0:T(8,128)(2,1)S(1)}, bf16[2,128,1024]{2,1,0:T(8,128)(2,1)S(1)}, u32[]{:S(2)}, u32[]{:S(2)}) collective-permute-start(bf16[2,128,1024]{2,1,0:T(8,128)(2,1)S(1)} %get-tuple-element.425), channel_id=1, source_target_pairs={{0,2},{1,3},{2,0},{3,1},{4,6},{5,7},{6,4},{7,5},{8,10},{9,11},{10,... | collective-permute-start | bytes 1572872 | tf_op jit(solution)/shard_map/ppermute | solution.py:19
  227.9 4.9 %collective-permute-start.24 = (bf16[8,128,1024]{2,1,0:T(8,128)(2,1)}, bf16[8,128,1024]{2,1,0:T(8,128)(2,1)S(1)}, u32[]{:S(2)}, u32[]{:S(2)}) collective-permute-start(bf16[8,128,1024]{2,1,0:T(8,128)(2,1)} %get-tuple-element.431), channel_id=1, source_target_pairs={{0,8},{8,0},{16,24},{24,16},{1,9},{9,1},{17,25},{25,17},{2,10},{10... | collective-permute-start | bytes 6291464 | tf_op jit(solution)/shard_map/ppermute | solution.py:19
  228.0 7.4 %collective-permute-start.23 = (bf16[8,128,1024]{2,1,0:T(8,128)(2,1)}, bf16[8,128,1024]{2,1,0:T(8,128)(2,1)S(1)}, u32[]{:S(2)}, u32[]{:S(2)}) collective-permute-start(bf16[8,128,1024]{2,1,0:T(8,128)(2,1)} %get-tuple-element.429), channel_id=1, source_target_pairs={{0,8},{8,0},{16,24},{24,16},{1,9},{9,1},{17,25},{25,17},{2,10},{10... | collective-permute-start | bytes 6291464 | tf_op jit(solution)/shard_map/ppermute | solution.py:19
  238.1 36.8 %collective-permute-start.28 = (bf16[2,2,128,1024]{3,2,1,0:T(8,128)(2,1)}, bf16[2,2,128,1024]{3,2,1,0:T(8,128)(2,1)}, u32[]{:S(2)}, u32[]{:S(2)}) collective-permute-start(bf16[2,2,128,1024]{3,2,1,0:T(8,128)(2,1)} %fusion.1), channel_id=1, source_target_pairs={{0,2},{1,3},{2,0},{3,1},{4,6},{5,7},{6,4},{7,5},{8,10},{9,11},{10,... | collective-permute-start | bytes 3145736 | tf_op jit(solution)/shard_map/ppermute | solution.py:19
  239.4 35.4 %collective-permute-start.27 = (bf16[2,2,128,1024]{3,2,1,0:T(8,128)(2,1)S(1)}, bf16[2,2,128,1024]{3,2,1,0:T(8,128)(2,1)}, u32[]{:S(2)}, u32[]{:S(2)}) collective-permute-start(bf16[2,2,128,1024]{3,2,1,0:T(8,128)(2,1)S(1)} %bitcast.261), channel_id=1, source_target_pairs={{0,1},{1,0},{2,3},{3,2},{4,5},{5,4},{6,7},{7,6},{8,9},{9,8},{10,11... | collective-permute-start | bytes 3145736 | tf_op jit(solution)/shard_map/ppermute | solution.py:19
  240.0 32.0 %collective-permute-start.26 = (bf16[128,1024]{1,0:T(8,128)(2,1)}, bf16[128,1024]{1,0:T(8,128)(2,1)S(1)}, u32[]{:S(2)}, u32[]{:S(2)}) collective-permute-start(bf16[128,1024]{1,0:T(8,128)(2,1)} %fusion.22), channel_id=1, source_target_pairs={{0,4},{1,5},{2,6},{3,7},{4,0},{5,1},{6,2},{7,3},{8,12},{9,13},{10,... | collective-permute-start | bytes 786440 | tf_op jit(solution)/shard_map/ppermute | solution.py:19
  242.1 31.6 %collective-permute-start.25 = (bf16[128,1024]{1,0:T(8,128)(2,1)}, bf16[128,1024]{1,0:T(8,128)(2,1)}, u32[]{:S(2)}, u32[]{:S(2)}) collective-permute-start(bf16[128,1024]{1,0:T(8,128)(2,1)} %fusion.21), channel_id=1, source_target_pairs={{0,4},{1,5},{2,6},{3,7},{4,0},{5,1},{6,2},{7,3},{8,12},{9,13},{10,... | collective-permute-start | bytes 786440 | tf_op jit(solution)/shard_map/ppermute | solution.py:19
  274.8 4.7 %collective-permute-start.29 = (bf16[8,128,1024]{2,1,0:T(8,128)(2,1)}, bf16[8,128,1024]{2,1,0:T(8,128)(2,1)S(1)}, u32[]{:S(2)}, u32[]{:S(2)}) collective-permute-start(bf16[8,128,1024]{2,1,0:T(8,128)(2,1)} %get-tuple-element.463), channel_id=1, source_target_pairs={{0,8},{8,0},{16,24},{24,16},{1,9},{9,1},{17,25},{25,17},{2,10},{10... | collective-permute-start | bytes 6291464 | tf_op jit(solution)/shard_map/ppermute | solution.py:19
  281.9 25.6 %collective-permute-start.32 = (bf16[4,128,1024]{2,1,0:T(8,128)(2,1)}, bf16[4,128,1024]{2,1,0:T(8,128)(2,1)S(1)}, u32[]{:S(2)}, u32[]{:S(2)}) collective-permute-start(bf16[4,128,1024]{2,1,0:T(8,128)(2,1)} %get-tuple-element.483), channel_id=1, source_target_pairs={{0,16},{8,24},{16,0},{24,8},{1,17},{9,25},{17,1},{25,9},{2,18},{10... | collective-permute-start | bytes 3145736 | tf_op jit(solution)/shard_map/ppermute | solution.py:19
  282.6 21.0 %collective-permute-start.31 = (bf16[2,128,1024]{2,1,0:T(8,128)(2,1)}, bf16[2,128,1024]{2,1,0:T(8,128)(2,1)}, u32[]{:S(2)}, u32[]{:S(2)}) collective-permute-start(bf16[2,128,1024]{2,1,0:T(8,128)(2,1)} %fusion.5), channel_id=1, source_target_pairs={{0,1},{1,0},{2,3},{3,2},{4,5},{5,4},{6,7},{7,6},{8,9},{9,8},{10,11... | collective-permute-start | bytes 1572872 | tf_op jit(solution)/shard_map/ppermute | solution.py:19
  283.5 20.1 %collective-permute-start.30 = (bf16[2,128,1024]{2,1,0:T(8,128)(2,1)}, bf16[2,128,1024]{2,1,0:T(8,128)(2,1)}, u32[]{:S(2)}, u32[]{:S(2)}) collective-permute-start(bf16[2,128,1024]{2,1,0:T(8,128)(2,1)} %fusion.4), channel_id=1, source_target_pairs={{0,2},{1,3},{2,0},{3,1},{4,6},{5,7},{6,4},{7,5},{8,10},{9,11},{10,... | collective-permute-start | bytes 1572872 | tf_op jit(solution)/shard_map/ppermute | solution.py:19
  313.6 27.4 %collective-permute-start.37 = (bf16[4,128,1024]{2,1,0:T(8,128)(2,1)}, bf16[4,128,1024]{2,1,0:T(8,128)(2,1)S(1)}, u32[]{:S(2)}, u32[]{:S(2)}) collective-permute-start(bf16[4,128,1024]{2,1,0:T(8,128)(2,1)} %get-tuple-element.514), channel_id=1, source_target_pairs={{0,16},{8,24},{16,0},{24,8},{1,17},{9,25},{17,1},{25,9},{2,18},{10... | collective-permute-start | bytes 3145736 | tf_op jit(solution)/shard_map/ppermute | solution.py:19
  314.2 26.8 %collective-permute-start.36 = (bf16[2,2,128,1024]{3,2,1,0:T(8,128)(2,1)}, bf16[2,2,128,1024]{3,2,1,0:T(8,128)(2,1)}, u32[]{:S(2)}, u32[]{:S(2)}) collective-permute-start(bf16[2,2,128,1024]{3,2,1,0:T(8,128)(2,1)} %bitcast.56), channel_id=1, source_target_pairs={{0,1},{1,0},{2,3},{3,2},{4,5},{5,4},{6,7},{7,6},{8,9},{9,8},{10,11... | collective-permute-start | bytes 3145736 | tf_op jit(solution)/shard_map/ppermute | solution.py:19
  315.1 21.7 %collective-permute-start.35 = (bf16[128,1024]{1,0:T(8,128)(2,1)}, bf16[128,1024]{1,0:T(8,128)(2,1)}, u32[]{:S(2)}, u32[]{:S(2)}) collective-permute-start(bf16[128,1024]{1,0:T(8,128)(2,1)} %fusion.20), channel_id=1, source_target_pairs={{0,4},{1,5},{2,6},{3,7},{4,0},{5,1},{6,2},{7,3},{8,12},{9,13},{10,... | collective-permute-start | bytes 786440 | tf_op jit(solution)/shard_map/ppermute | solution.py:19
  316.9 24.1 %collective-permute-start.34 = (bf16[128,1024]{1,0:T(8,128)(2,1)S(1)}, bf16[128,1024]{1,0:T(8,128)(2,1)}, u32[]{:S(2)}, u32[]{:S(2)}) collective-permute-start(bf16[128,1024]{1,0:T(8,128)(2,1)S(1)} %fusion.19), channel_id=1, source_target_pairs={{0,4},{1,5},{2,6},{3,7},{4,0},{5,1},{6,2},{7,3},{8,12},{9,13},{10,... | collective-permute-start | bytes 786440 | tf_op jit(solution)/shard_map/ppermute | solution.py:19
  346.5 12.8 %collective-permute-start.42 = (bf16[2,128,1024]{2,1,0:T(8,128)(2,1)}, bf16[2,128,1024]{2,1,0:T(8,128)(2,1)S(1)}, u32[]{:S(2)}, u32[]{:S(2)}) collective-permute-start(bf16[2,128,1024]{2,1,0:T(8,128)(2,1)} %fusion.3), channel_id=1, source_target_pairs={{0,2},{1,3},{2,0},{3,1},{4,6},{5,7},{6,4},{7,5},{8,10},{9,11},{10,... | collective-permute-start | bytes 1572872 | tf_op jit(solution)/shard_map/ppermute | solution.py:19
  348.9 14.8 %collective-permute-start.41 = (bf16[2,128,1024]{2,1,0:T(8,128)(2,1)S(1)}, bf16[2,128,1024]{2,1,0:T(8,128)(2,1)S(1)}, u32[]{:S(2)}, u32[]{:S(2)}) collective-permute-start(bf16[2,128,1024]{2,1,0:T(8,128)(2,1)S(1)} %pad_maximum_fusion.3), channel_id=1, source_target_pairs={{0,16},{8,24},{16,0},{24,8},{1,17},{9,25},{17,1},{25,9},{2,18},{10... | collective-permute-start | bytes 1572872 | tf_op jit(solution)/shard_map/ppermute | solution.py:19
  350.5 10.1 %collective-permute-start.38 = (f32[8,16,128]{2,1,0:T(8,128)S(1)}, f32[8,16,128]{2,1,0:T(8,128)S(1)}, u32[]{:S(2)}, u32[]{:S(2)}) collective-permute-start(f32[8,16,128]{2,1,0:T(8,128)S(1)} %copy-done.25), channel_id=1, source_target_pairs={{0,8},{8,0},{16,24},{24,16},{1,9},{9,1},{17,25},{25,17},{2,10},{10... | collective-permute-start | bytes 196616 | tf_op jit(solution)/shard_map/ppermute | solution.py:19
  350.5 13.2 %collective-permute-start.39 = (f32[8,16,128]{2,1,0:T(8,128)S(1)}, f32[8,16,128]{2,1,0:T(8,128)S(1)}, u32[]{:S(2)}, u32[]{:S(2)}) collective-permute-start(f32[8,16,128]{2,1,0:T(8,128)S(1)} %copy-done.25), channel_id=1, source_target_pairs={{0,16},{8,24},{16,0},{24,8},{1,17},{9,25},{17,1},{25,9},{2,18},{10... | collective-permute-start | bytes 196616 | tf_op jit(solution)/shard_map/ppermute | solution.py:19
  351.0 12.7 %collective-permute-start.40 = (f32[8,16,128]{2,1,0:T(8,128)S(1)}, f32[8,16,128]{2,1,0:T(8,128)S(1)}, u32[]{:S(2)}, u32[]{:S(2)}) collective-permute-start(f32[8,16,128]{2,1,0:T(8,128)S(1)} %copy-done.25), channel_id=1, source_target_pairs={{0,24},{8,16},{16,8},{24,0},{1,25},{9,17},{17,9},{25,1},{2,26},{10... | collective-permute-start | bytes 196616 | tf_op jit(solution)/shard_map/ppermute | solution.py:19
  366.8 4.4 %collective-permute-start.43 = (f32[2,2,16,128]{3,2,1,0:T(8,128)S(1)}, f32[2,2,16,128]{3,2,1,0:T(8,128)S(1)}, u32[]{:S(2)}, u32[]{:S(2)}) collective-permute-start(f32[2,2,16,128]{3,2,1,0:T(8,128)S(1)} %bitcast.265), channel_id=1, source_target_pairs={{0,1},{1,0},{2,3},{3,2},{4,5},{5,4},{6,7},{7,6},{8,9},{9,8},{10,11... | collective-permute-start | bytes 98312 | tf_op jit(solution)/shard_map/ppermute | solution.py:19
  367.8 15.6 %collective-permute-start.45 = (bf16[128,1024]{1,0:T(8,128)(2,1)S(1)}, bf16[128,1024]{1,0:T(8,128)(2,1)S(1)}, u32[]{:S(2)}, u32[]{:S(2)}) collective-permute-start(bf16[128,1024]{1,0:T(8,128)(2,1)S(1)} %fusion.14), channel_id=1, source_target_pairs={{0,4},{1,5},{2,6},{3,7},{4,0},{5,1},{6,2},{7,3},{8,12},{9,13},{10,... | collective-permute-start | bytes 786440 | tf_op jit(solution)/shard_map/ppermute | solution.py:19
  371.3 6.3 %collective-permute-start.44 = (f32[2,16,128]{2,1,0:T(8,128)S(1)}, f32[2,16,128]{2,1,0:T(8,128)S(1)}, u32[]{:S(2)}, u32[]{:S(2)}) collective-permute-start(f32[2,16,128]{2,1,0:T(8,128)S(1)} %bitcast_add_fusion), channel_id=1, source_target_pairs={{0,2},{1,3},{2,0},{3,1},{4,6},{5,7},{6,4},{7,5},{8,10},{9,11},{10,... | collective-permute-start | bytes 49160 | tf_op jit(solution)/shard_map/ppermute | solution.py:19
  371.7 22.0 %collective-permute-start.47 = (bf16[2,128,1024]{2,1,0:T(8,128)(2,1)}, bf16[2,128,1024]{2,1,0:T(8,128)(2,1)}, u32[]{:S(2)}, u32[]{:S(2)}) collective-permute-start(bf16[2,128,1024]{2,1,0:T(8,128)(2,1)} %pad_maximum_fusion.4.refs_0_), channel_id=1, source_target_pairs={{0,8},{8,0},{16,24},{24,16},{1,9},{9,1},{17,25},{25,17},{2,10},{10... | collective-permute-start | bytes 1572872 | tf_op jit(solution)/shard_map/ppermute | solution.py:19
  371.7 22.0 %collective-permute-start.48 = (bf16[2,128,1024]{2,1,0:T(8,128)(2,1)}, bf16[2,128,1024]{2,1,0:T(8,128)(2,1)}, u32[]{:S(2)}, u32[]{:S(2)}) collective-permute-start(bf16[2,128,1024]{2,1,0:T(8,128)(2,1)} %pad_maximum_fusion.4.refs_0_), channel_id=1, source_target_pairs={{0,16},{8,24},{16,0},{24,8},{1,17},{9,25},{17,1},{25,9},{2,18},{10... | collective-permute-start | bytes 1572872 | tf_op jit(solution)/shard_map/ppermute | solution.py:19
  384.8 6.5 %collective-permute-start.49 = (bf16[128,1024]{1,0:T(8,128)(2,1)S(1)}, bf16[128,1024]{1,0:T(8,128)(2,1)}, u32[]{:S(2)}, u32[]{:S(2)}) collective-permute-start(bf16[128,1024]{1,0:T(8,128)(2,1)S(1)} %fusion.9.refs_0_), channel_id=1, source_target_pairs={{0,8},{8,0},{16,24},{24,16},{1,9},{9,1},{17,25},{25,17},{2,10},{10... | collective-permute-start | bytes 786440 | tf_op jit(solution)/shard_map/ppermute | solution.py:19
  384.9 8.8 %collective-permute-start.50 = (bf16[128,1024]{1,0:T(8,128)(2,1)S(1)}, bf16[128,1024]{1,0:T(8,128)(2,1)}, u32[]{:S(2)}, u32[]{:S(2)}) collective-permute-start(bf16[128,1024]{1,0:T(8,128)(2,1)S(1)} %fusion.9.refs_0_), channel_id=1, source_target_pairs={{0,16},{8,24},{16,0},{24,8},{1,17},{9,25},{17,1},{25,9},{2,18},{10... | collective-permute-start | bytes 786440 | tf_op jit(solution)/shard_map/ppermute | solution.py:19
  386.1 5.2 %collective-permute-start.46 = (f32[16,128]{1,0:T(8,128)}, f32[16,128]{1,0:T(8,128)}, u32[]{:S(2)}, u32[]{:S(2)}) collective-permute-start(f32[16,128]{1,0:T(8,128)} %bitcast_add_fusion.3), channel_id=1, source_target_pairs={{0,4},{1,5},{2,6},{3,7},{4,0},{5,1},{6,2},{7,3},{8,12},{9,13},{10,... | collective-permute-start | bytes 24584 | tf_op jit(solution)/shard_map/ppermute | solution.py:19
  (48 other events, 346.3 us)
Sparse Core Ops, SparseCore 0:
  24.4 81.8 all-gather.4
  111.0 48.9 all-gather.6

commit v4 on v3

--- a/solution.py
+++ b/solution.py
@@ -1105,9 +1105,8 @@
         red_w.launch()
         seq.land((), red_w)
     red_w.launch()
-    two_up.terms[-1], two_down.terms[-1], sums_one = seq.at((two_up.terms[-1], two_down.terms[-1], sums_one))
     packed = pack_sums(
-        order,
+        seq.at(order),
         n,
         rows,
         ffq,
@@ -1115,32 +1114,34 @@
         (jnp.stack([g_bias_0, g_bias_1]), jnp.stack([g_bias_2, g_bias_3])),
         (sums_two, sums_one),
     )
-    packed = seq.at(packed)
-    peers = Sent([xor_swap(packed, "dp", 4, m) for m in (1, 2, 3)])
+    sums = Reduce(seq, (packed,), n, full)
+    while len(sums.axes) > 3:
+        sums.launch()
+        seq.land((), sums)
+    sums.launch()
     crossing = jnp.stack([two_up.rest().piece(), two_down.rest().piece()])
     cross = Sent(x_swap(seq.at(crossing)))
-    seq.land((), red_w)
-    if red_w.axes:
-        red_w.launch()
-    seq.land((), peers, cross)
+    seq.land((), red_w, sums)
+    red_w.launch()
+    sums.launch()
+    seq.land((), cross)
     owned = [
         rounded_sum([*red_up.rest().terms, cross.value[0]]),
         rounded_sum([*red_down.rest().terms, cross.value[1]]),
     ]
     mlp_spread = Spread(seq, jnp.stack(owned))
-    sums = Reduce(seq, (packed, *peers.value), n, full)
-    while len(sums.axes) > 1:
-        sums.launch()
-        if len(sums.axes) > 1:
-            seq.land((), sums)
-    seq.land((), *([sums, red_w] if len(bits) > 1 else []))
+    seq.land((), sums, red_w)
     w_spread = Spread(seq, red_w.piece())
     sums.launch()
     block, tokens_grad = seq.at((block, tokens_grad))
     block_out, grad_tokens = seq.land((compact(block), compact(tokens_grad)), sums, mlp_spread, w_spread)
     mlp_spread.cross()
     w_spread.cross()
-    small_sums = seq.land(sums.piece(), mlp_spread, w_spread)
+    packed = seq.at(sums.piece())
+    peers = Sent([xor_swap(packed, "dp", 4, m) for m in (1, 2, 3)])
+    seq.land((), mlp_spread, w_spread, peers)
+    beside, across, opposite = peers.value
+    small_sums = (packed + beside) + (across + opposite)
     out_fc1, out_fc2 = finish_mlp(q, mlp_spread.pieces, n)
     out_qkv, out_out = finish_attention(seq.value, w_spread.pieces)
     small_out = [small_sums[k, :rows] for k in range(8)]

time: 416 us -> 415 us (level)
  transfers between devices with their start and end apart: 55 -> 55, of which waited for: 23 -> 25; matrix products, arithmetic and copies ran while one was open for 12% -> 14% of each run, Pallas kernels for 44% -> 45%
where the time goes in v4:
time: 415 us; the launch traced here: 410 us
  Pallas kernels  191 us (46%)
  waiting for transfers between devices  75.8 us (18%)
  starting transfers between devices  51 us (12%)
  other arithmetic  48 us (12%)
  local copies, waits for them, and re-layouts  28.5 us (7%)
  between operations  14.9 us (4%)
    pallas_call x17, Pallas kernels, call(): pl.pallas_call(kernel, out_shape=[jax.ShapeDtypeStruct(shape, kind) for s...  191 us
    ppermute x53, waiting for transfers between devices, xor_swap(): return lax.ppermute(value, axis, [(i, i ^ mask) for i in range(size)])  75.7 us
    ppermute x53, starting transfers between devices, xor_swap(): return lax.ppermute(value, axis, [(i, i ^ mask) for i in range(size)])  50.9 us
    convert_element_type x16, other arithmetic, rounded_sum(): return sum((t.astype(full) for t in terms)).astype(kind)  30.7 us
  transfers between devices with their start and end apart: 55, of which 25 were waited for; matrix products, arithmetic and copies ran while one was open for 14% of the time, Pallas kernels for 45%

profile of v4, /device:TPU:0, one launch (start us, length us, event | category | flops | bytes accessed | tf_op | source)
XLA Modules:
  0.0 409.5 jit_solution(2856190943262989093)
XLA Ops:
  7.2 2.6 first_payload.1
  9.8 4.1 %collective-permute-start = (bf16[1,144,768]{2,1,0:T(8,128)(2,1)}, bf16[1,144,768]{2,1,0:T(8,128)(2,1)S(1)}, u32[]{:S(2)}, u32[]{:S(2)}) collective-permute-start(bf16[1,144,768]{2,1,0:T(8,128)(2,1)} %bitcast.267), channel_id=1, source_target_pairs={{0,4},{1,5},{2,6},{3,7},{4,0},{5,1},{6,2},{7,3},{8,12},{9,13},{10,... | collective-permute-start | bytes 663560 | tf_op jit(solution)/shard_map/ppermute | solution.py:19
  14.5 3.3 payloads.1
  17.8 6.5 %collective-permute-done = bf16[1,144,768]{2,1,0:T(8,128)(2,1)S(1)} collective-permute-done((bf16[1,144,768]{2,1,0:T(8,128)(2,1)}, bf16[1,144,768]{2,1,0:T(8,128)(2,1)S(1)}, u32[]{:S(2)}, u32[]{:S(2)}) %collective-permute-start) | collective-permute-done | bytes 221216 | tf_op jit(solution)/shard_map/ppermute | solution.py:19
  27.5 3.6 copy.32
  31.1 2.1 reshape.419
  41.3 6.6 %collective-permute-start.4 = (bf16[1,128,512]{2,1,0:T(8,128)(2,1)S(1)}, bf16[1,128,512]{2,1,0:T(8,128)(2,1)S(1)}, u32[]{:S(2)}, u32[]{:S(2)}) collective-permute-start(bf16[1,128,512]{2,1,0:T(8,128)(2,1)S(1)} %pad_maximum_fusion.7), channel_id=1, source_target_pairs={{0,4},{1,5},{2,6},{3,7},{4,0},{5,1},{6,2},{7,3},{8,12},{9,13},{10,... | collective-permute-start | bytes 393224 | tf_op jit(solution)/shard_map/ppermute | solution.py:19
  48.7 11.6 %collective-permute-done.4 = bf16[1,128,512]{2,1,0:T(8,128)(2,1)S(1)} collective-permute-done((bf16[1,128,512]{2,1,0:T(8,128)(2,1)S(1)}, bf16[1,128,512]{2,1,0:T(8,128)(2,1)S(1)}, u32[]{:S(2)}, u32[]{:S(2)}) %collective-permute-start.4) | collective-permute-done | bytes 131104 | tf_op jit(solution)/shard_map/ppermute | solution.py:19
  63.8 2.3 unpack_vectors.1
  71.5 10.5 %attention_forward.2 = (bf16[832,768]{1,0:T(8,128)(2,1)}, bf16[832,768]{1,0:T(8,128)(2,1)}, bf16[832,256]{1,0:T(8,128)(2,1)}, bf16[832,256]{1,0:T(8,128)(2,1)}, ...) custom-call(s32[9]{0:T(128)} %pad_add_fusion.1.order_ref, bf16[832,1024]{1,0:T(8,128)(2,1)} %add_convert_fusion.normed_ref, ...), custom_call_target="tpu_custom_call" | custom-call | tf_op jit(solution)/shard_map/attention_forward/pallas_call | solution.py:133
  82.0 8.9 %collective-permute-done.8 = bf16[2,128,512]{2,1,0:T(8,128)(2,1)S(1)} collective-permute-done((bf16[2,128,512]{2,1,0:T(8,128)(2,1)S(1)}, bf16[2,128,512]{2,1,0:T(8,128)(2,1)S(1)}, u32[]{:S(2)}, u32[]{:S(2)}) %collective-permute-start.8) | collective-permute-done | bytes 262176 | tf_op jit(solution)/shard_map/ppermute | solution.py:19
  96.3 10.5 %attention_forward.3 = (bf16[832,768]{1,0:T(8,128)(2,1)}, bf16[832,768]{1,0:T(8,128)(2,1)}, bf16[832,256]{1,0:T(8,128)(2,1)}, bf16[832,256]{1,0:T(8,128)(2,1)}, ...) custom-call(s32[9]{0:T(128)} %pad_add_fusion.1.order_ref, bf16[832,1024]{1,0:T(8,128)(2,1)} %add_convert_fusion.normed_ref, ...), custom_call_target="tpu_custom_call" | custom-call | tf_op jit(solution)/shard_map/attention_forward/pallas_call | solution.py:133
  108.1 2.6 collective-permute-done.12.refs_5_
  110.9 3.3 slice.459
  115.8 9.9 %attention_out.1 = (f32[832,1024]{1,0:T(8,128)}, bf16[832,1024]{1,0:T(8,128)(2,1)}) custom-call(s32[9]{0:T(128)} %pad_add_fusion.1.order_ref, f32[832,1024]{1,0:T(8,128)} %bitcast.233, f32[1,1024]{1,0:T(1,128)} %get-tuple-element.583.bias_ref, f32[1,1024]{1,0:T(1,128)} %get-tuple-element.582.gain_ref, f32[1,1024]{1,0:T(1,128)} %get-tuple-element.581.shift_ref, ...), custom_call_target="tpu_custom_call" | custom-call | tf_op jit(solution)/shard_map/attention_out/pallas_call | solution.py:133
  125.6 19.2 %mlp.4 = (bf16[8,128,1024]{2,1,0:T(8,128)(2,1)}, bf16[8,128,1024]{2,1,0:T(8,128)(2,1)}, f32[1,1024]{1,0:T(1,128)}, f32[832,1024]{1,0:T(8,128)}, f32[832,1024]{1,0:T(8,128)}) custom-call(s32[9]{0:T(128)} %pad_add_fusion.1.order_ref, f32[1,1024]{1,0:T(1,128)} %get-tuple-element.588.bias_ref, bf16[832,1024]{1,0:T(8,128)(2,1)} %get-tuple-element.368.refs_0_.refs_1_, ...), custom_call_target="tpu_custom_call" | custom-call | tf_op jit(solution)/shard_map/mlp/pallas_call | solution.py:133
  144.9 20.4 %mlp.5 = (bf16[8,128,1024]{2,1,0:T(8,128)(2,1)}, bf16[8,128,1024]{2,1,0:T(8,128)(2,1)}, f32[1,1024]{1,0:T(1,128)}, f32[832,1024]{1,0:T(8,128)}, f32[832,1024]{1,0:T(8,128)}) custom-call(s32[9]{0:T(128)} %pad_add_fusion.1.order_ref, f32[1,1024]{1,0:T(1,128)} %get-tuple-element.589.bias_ref, bf16[832,1024]{1,0:T(8,128)(2,1)} %get-tuple-element.368.refs_0_.refs_1_, ...), custom_call_target="tpu_custom_call" | custom-call | tf_op jit(solution)/shard_map/mlp/pallas_call | solution.py:133
  165.9 3.9 collective-permute-done.16
  169.8 2.4 add_convert_fusion.7
  177.8 20.5 %mlp.6 = (bf16[8,128,1024]{2,1,0:T(8,128)(2,1)}, bf16[8,128,1024]{2,1,0:T(8,128)(2,1)}, f32[1,1024]{1,0:T(1,128)}, f32[832,1024]{1,0:T(8,128)}, f32[832,1024]{1,0:T(8,128)}) custom-call(s32[9]{0:T(128)} %pad_add_fusion.1.order_ref, f32[1,1024]{1,0:T(1,128)} %get-tuple-element.587.bias_ref, bf16[832,1024]{1,0:T(8,128)(2,1)} %get-tuple-element.368.refs_0_.refs_1_, ...), custom_call_target="tpu_custom_call" | custom-call | tf_op jit(solution)/shard_map/mlp/pallas_call | solution.py:133
  198.3 2.2 collective-permute-done.20
  201.3 3.2 fusion.6
  206.8 21.0 %mlp.7 = (bf16[8,128,1024]{2,1,0:T(8,128)(2,1)}, bf16[8,128,1024]{2,1,0:T(8,128)(2,1)}, f32[1,1024]{1,0:T(1,128)}, f32[832,1024]{1,0:T(8,128)}, bf16[832,1024]{1,0:T(8,128)(2,1)}) custom-call(s32[9]{0:T(128)} %pad_add_fusion.1.order_ref, f32[1,1024]{1,0:T(1,128)} %get-tuple-element.586.bias_ref, f32[1,1024]{1,0:T(1,128)} %get-tuple-element.580.refs_0_, ...), custom_call_target="tpu_custom_call" | custom-call | tf_op jit(solution)/shard_map/mlp/pallas_call | solution.py:133
  228.5 2.2 fusion.21
  230.7 2.1 fusion.22
  233.2 2.1 collective-permute-done.23
  239.9 2.2 collective-permute-start.26
  242.9 11.0 %attention_out_back.1 = (f32[832,1024]{1,0:T(8,128)}, bf16[832,256]{1,0:T(8,128)(2,1)}, bf16[832,256]{1,0:T(8,128)(2,1)}, bf16[832,256]{1,0:T(8,128)(2,1)}, bf16...) custom-call(s32[9]{0:T(128)} %pad_add_fusion.1.order_ref, ...), custom_call_target="tpu_custom_call" | custom-call | tf_op jit(solution)/shard_map/attention_out_back/pallas_call | solution.py:133
  253.9 18.1 %attention_back.2 = (bf16[8,128,1024]{2,1,0:T(8,128)(2,1)}, bf16[8,128,1024]{2,1,0:T(8,128)(2,1)}, bf16[832,768]{1,0:T(8,128)(2,1)}, bf16[832,768]{1,0:T(8,128)(2,1)}, f32[2,1,768]{2,1,0:T(1,128)}) custom-call(s32[9]{0:T(128)} %pad_add_fusion.1.order_ref, bf16[832,1024]{1,0:T(8,128)(2,1)} %add_convert_fusion.normed_ref, ...), custom_call_target="tpu_custom_call" | custom-call | tf_op jit(solution)/shard_map/attention_back/pallas_call | solution.py:133
  274.8 2.4 fusion.4
  277.3 2.3 fusion.5
  279.5 2.4 add_convert_fusion.2
  283.5 2.1 collective-permute-start.30
  285.6 18.0 %attention_back.3 = (bf16[8,128,1024]{2,1,0:T(8,128)(2,1)}, bf16[8,128,1024]{2,1,0:T(8,128)(2,1)}, bf16[832,768]{1,0:T(8,128)(2,1)}, bf16[832,768]{1,0:T(8,128)(2,1)}, f32[2,1,768]{2,1,0:T(1,128)}) custom-call(s32[9]{0:T(128)} %pad_add_fusion.1.order_ref, bf16[832,1024]{1,0:T(8,128)(2,1)} %add_convert_fusion.normed_ref, ...), custom_call_target="tpu_custom_call" | custom-call | tf_op jit(solution)/shard_map/attention_back/pallas_call | solution.py:133
  303.6 4.0 collective-permute-done.32
  308.8 2.0 fusion.20
  319.3 15.9 %input_back.1 = (f32[832,1024]{1,0:T(8,128)}, f32[2,1,1024]{2,1,0:T(1,128)}) custom-call(s32[9]{0:T(128)} %pad_add_fusion.1.order_ref, f32[832,1024]{1,0:T(8,128)} %bitcast.234, f32[832,1024]{1,0:T(8,128)} %get-tuple-element.493.after_ref, f32[1,1024]{1,0:T(1,128)} %get-tuple-element.579.gain_ref, bf16[832,768]{1,0:T(8,128)(2,1)} %get-tuple-element.494.refs_0_, ...), custom_call_target="tpu_custom_call" | custom-call | tf_op jit(solution)/shard_map/input_back/pallas_call | solution.py:133
  336.9 4.2 %collective-permute-done.34 = bf16[128,1024]{1,0:T(8,128)(2,1)} collective-permute-done((bf16[128,1024]{1,0:T(8,128)(2,1)S(1)}, bf16[128,1024]{1,0:T(8,128)(2,1)}, u32[]{:S(2)}, u32[]{:S(2)}) %collective-permute-start.34) | collective-permute-done | bytes 262176 | tf_op jit(solution)/shard_map/ppermute | solution.py:19
  341.0 2.5 fusion.3
  351.8 3.4 collective-permute-done.39
  358.5 3.9 collective-permute-done.42
  362.4 3.1 collective-permute-start.41
  365.8 2.2 fusion.25
  370.3 6.0 %collective-permute-done.41 = bf16[128,1024]{1,0:T(8,128)(2,1)S(1)} collective-permute-done((bf16[128,1024]{1,0:T(8,128)(2,1)S(1)}, bf16[128,1024]{1,0:T(8,128)(2,1)S(1)}, u32[]{:S(2)}, u32[]{:S(2)}) %collective-permute-start.41) | collective-permute-done | bytes 262176 | tf_op jit(solution)/shard_map/ppermute | solution.py:19
  380.6 1.9 reshape.431
  385.4 3.7 collective-permute-done.47.refs_2_
  396.0 3.9 finish_mlp.1
  399.9 2.6 finish_attention.1
  (224 shorter events, 89.4 us)
Async XLA Ops:
  7.2 99.6 %all-gather.5.cloned.1.call-start = ((), (), s32[]{:S(2)}) async-start(), calls=%async_computation | async-start | bytes 4718592 | tf_op jit(solution)/shard_map/all_gather | solution.py:963
  9.8 14.5 %collective-permute-start = (bf16[1,144,768]{2,1,0:T(8,128)(2,1)}, bf16[1,144,768]{2,1,0:T(8,128)(2,1)S(1)}, u32[]{:S(2)}, u32[]{:S(2)}) collective-permute-start(bf16[1,144,768]{2,1,0:T(8,128)(2,1)} %bitcast.267), channel_id=1, source_target_pairs={{0,4},{1,5},{2,6},{3,7},{4,0},{5,1},{6,2},{7,3},{8,12},{9,13},{10,... | collective-permute-start | bytes 663560 | tf_op jit(solution)/shard_map/ppermute | solution.py:19
  24.3 141.0 %all-gather.7.cloned.1.call-start = ((), (), s32[]{:S(2)}) async-start(), calls=%async_computation.1 | async-start | bytes 2359296 | tf_op jit(solution)/shard_map/all_gather | solution.py:964
  24.5 11.4 %collective-permute-start.1 = (bf16[2,144,768]{2,1,0:T(8,128)(2,1)S(1)}, bf16[2,144,768]{2,1,0:T(8,128)(2,1)S(1)}, u32[]{:S(2)}, u32[]{:S(2)}) collective-permute-start(bf16[2,144,768]{2,1,0:T(8,128)(2,1)S(1)} %pad_maximum_fusion.5), channel_id=1, source_target_pairs={{0,2},{1,3},{2,0},{3,1},{4,6},{5,7},{6,4},{7,5},{8,10},{9,11},{10,... | collective-permute-start | bytes 1327112 | tf_op jit(solution)/shard_map/ppermute | solution.py:19
  36.8 24.4 %collective-permute-start.2 = (bf16[4,144,768]{2,1,0:T(8,128)(2,1)}, bf16[4,144,768]{2,1,0:T(8,128)(2,1)}, u32[]{:S(2)}, u32[]{:S(2)}) collective-permute-start(bf16[4,144,768]{2,1,0:T(8,128)(2,1)} %constant_dynamic-update-slice_fusion.refs_0_.refs_4_), channel_id=1, source_target_pairs={{0,1},{1,0},{2,3},{3,2},{4,5},{5,4},{6,7},{7,6},{8,9},{9,8},{10,11... | collective-permute-start | bytes 2654216 | tf_op jit(solution)/shard_map/ppermute | solution.py:19
  38.1 23.0 %collective-permute-start.3 = (bf16[4,144,768]{2,1,0:T(8,128)(2,1)}, bf16[4,144,768]{2,1,0:T(8,128)(2,1)}, u32[]{:S(2)}, u32[]{:S(2)}) collective-permute-start(bf16[4,144,768]{2,1,0:T(8,128)(2,1)} %constant_dynamic-update-slice_fusion.refs_0_.refs_4_), channel_id=1, source_target_pairs={{0,8},{8,0},{16,24},{24,16},{1,9},{9,1},{17,25},{25,17},{2,10},{10... | collective-permute-start | bytes 2654216 | tf_op jit(solution)/shard_map/ppermute | solution.py:19
  39.7 42.3 %collective-permute-start.6 = (bf16[4,144,768]{2,1,0:T(8,128)(2,1)}, bf16[4,144,768]{2,1,0:T(8,128)(2,1)}, u32[]{:S(2)}, u32[]{:S(2)}) collective-permute-start(bf16[4,144,768]{2,1,0:T(8,128)(2,1)} %constant_dynamic-update-slice_fusion.refs_0_.refs_4_), channel_id=1, source_target_pairs={{0,16},{8,24},{16,0},{24,8},{1,17},{9,25},{17,1},{25,9},{2,18},{10... | collective-permute-start | bytes 2654216 | tf_op jit(solution)/shard_map/ppermute | solution.py:19
  41.3 19.0 %collective-permute-start.4 = (bf16[1,128,512]{2,1,0:T(8,128)(2,1)S(1)}, bf16[1,128,512]{2,1,0:T(8,128)(2,1)S(1)}, u32[]{:S(2)}, u32[]{:S(2)}) collective-permute-start(bf16[1,128,512]{2,1,0:T(8,128)(2,1)S(1)} %pad_maximum_fusion.7), channel_id=1, source_target_pairs={{0,4},{1,5},{2,6},{3,7},{4,0},{5,1},{6,2},{7,3},{8,12},{9,13},{10,... | collective-permute-start | bytes 393224 | tf_op jit(solution)/shard_map/ppermute | solution.py:19
  61.1 10.4 %collective-permute-start.5 = (bf16[4,144,768]{2,1,0:T(8,128)(2,1)}, bf16[4,144,768]{2,1,0:T(8,128)(2,1)}, u32[]{:S(2)}, u32[]{:S(2)}) collective-permute-start(bf16[4,144,768]{2,1,0:T(8,128)(2,1)} %collective-permute-done.2.refs_1_.refs_5_), channel_id=1, source_target_pairs={{0,8},{8,0},{16,24},{24,16},{1,9},{9,1},{17,25},{25,17},{2,10},{10... | collective-permute-start | bytes 2654216 | tf_op jit(solution)/shard_map/ppermute | solution.py:19
  61.1 29.7 %collective-permute-start.7 = (bf16[4,144,768]{2,1,0:T(8,128)(2,1)}, bf16[4,144,768]{2,1,0:T(8,128)(2,1)}, u32[]{:S(2)}, u32[]{:S(2)}) collective-permute-start(bf16[4,144,768]{2,1,0:T(8,128)(2,1)} %collective-permute-done.2.refs_1_.refs_5_), channel_id=1, source_target_pairs={{0,16},{8,24},{16,0},{24,8},{1,17},{9,25},{17,1},{25,9},{2,18},{10... | collective-permute-start | bytes 2654216 | tf_op jit(solution)/shard_map/ppermute | solution.py:19
  66.1 24.8 %collective-permute-start.8 = (bf16[2,128,512]{2,1,0:T(8,128)(2,1)S(1)}, bf16[2,128,512]{2,1,0:T(8,128)(2,1)S(1)}, u32[]{:S(2)}, u32[]{:S(2)}) collective-permute-start(bf16[2,128,512]{2,1,0:T(8,128)(2,1)S(1)} %pad_maximum_fusion.6), channel_id=1, source_target_pairs={{0,2},{1,3},{2,0},{3,1},{4,6},{5,7},{6,4},{7,5},{8,10},{9,11},{10,... | collective-permute-start | bytes 786440 | tf_op jit(solution)/shard_map/ppermute | solution.py:19
  90.9 4.4 %collective-permute-start.10 = (bf16[4,144,768]{2,1,0:T(8,128)(2,1)}, bf16[4,144,768]{2,1,0:T(8,128)(2,1)S(1)}, u32[]{:S(2)}, u32[]{:S(2)}) collective-permute-start(bf16[4,144,768]{2,1,0:T(8,128)(2,1)} %collective-permute-done.7.refs_1_.refs_9_), channel_id=1, source_target_pairs={{0,8},{8,0},{16,24},{24,16},{1,9},{9,1},{17,25},{25,17},{2,10},{10... | collective-permute-start | bytes 2654216 | tf_op jit(solution)/shard_map/ppermute | solution.py:19
  90.9 4.4 %collective-permute-start.9 = (bf16[4,144,768]{2,1,0:T(8,128)(2,1)}, bf16[4,144,768]{2,1,0:T(8,128)(2,1)}, u32[]{:S(2)}, u32[]{:S(2)}) collective-permute-start(bf16[4,144,768]{2,1,0:T(8,128)(2,1)} %collective-permute-done.6.refs_0_.refs_8_), channel_id=1, source_target_pairs={{0,8},{8,0},{16,24},{24,16},{1,9},{9,1},{17,25},{25,17},{2,10},{10... | collective-permute-start | bytes 2654216 | tf_op jit(solution)/shard_map/ppermute | solution.py:19
  91.4 15.4 %collective-permute-start.11 = (bf16[4,128,512]{2,1,0:T(8,128)(2,1)S(1)}, bf16[4,128,512]{2,1,0:T(8,128)(2,1)}, u32[]{:S(2)}, u32[]{:S(2)}) collective-permute-start(bf16[4,128,512]{2,1,0:T(8,128)(2,1)S(1)} %pad_maximum_fusion.2), channel_id=1, source_target_pairs={{0,1},{1,0},{2,3},{3,2},{4,5},{5,4},{6,7},{7,6},{8,9},{9,8},{10,11... | collective-permute-start | bytes 1572872 | tf_op jit(solution)/shard_map/ppermute | solution.py:19
  110.7 14.9 %collective-permute-start.13 = (bf16[8,128,2048]{2,1,0:T(8,128)(2,1)}, bf16[8,128,2048]{2,1,0:T(8,128)(2,1)}, u32[]{:S(2)}, u32[]{:S(2)}) collective-permute-start(bf16[8,128,2048]{2,1,0:T(8,128)(2,1)} %bitcast.240), channel_id=1, source_target_pairs={{0,8},{8,0},{16,24},{24,16},{1,9},{9,1},{17,25},{25,17},{2,10},{10... | collective-permute-start | bytes 12582920 | tf_op jit(solution)/shard_map/ppermute | solution.py:19
  114.2 51.1 %collective-permute-start.14 = (bf16[8,128,1024]{2,1,0:T(8,128)(2,1)}, bf16[8,128,1024]{2,1,0:T(8,128)(2,1)}, u32[]{:S(2)}, u32[]{:S(2)}) collective-permute-start(bf16[8,128,1024]{2,1,0:T(8,128)(2,1)} %slice.459), channel_id=1, source_target_pairs={{0,16},{8,24},{16,0},{24,8},{1,17},{9,25},{17,1},{25,9},{2,18},{10... | collective-permute-start | bytes 6291464 | tf_op jit(solution)/shard_map/ppermute | solution.py:19
  165.4 7.4 %collective-permute-start.15 = (bf16[8,128,1024]{2,1,0:T(8,128)(2,1)}, bf16[8,128,1024]{2,1,0:T(8,128)(2,1)S(1)}, u32[]{:S(2)}, u32[]{:S(2)}) collective-permute-start(bf16[8,128,1024]{2,1,0:T(8,128)(2,1)} %get-tuple-element.384), channel_id=1, source_target_pairs={{0,8},{8,0},{16,24},{24,16},{1,9},{9,1},{17,25},{25,17},{2,10},{10... | collective-permute-start | bytes 6291464 | tf_op jit(solution)/shard_map/ppermute | solution.py:19
  174.4 26.9 %collective-permute-start.17 = (bf16[8,128,1024]{2,1,0:T(8,128)(2,1)}, bf16[8,128,1024]{2,1,0:T(8,128)(2,1)S(1)}, u32[]{:S(2)}, u32[]{:S(2)}) collective-permute-start(bf16[8,128,1024]{2,1,0:T(8,128)(2,1)} %collective-permute-done.14.refs_2_), channel_id=1, source_target_pairs={{0,8},{8,0},{16,24},{24,16},{1,9},{9,1},{17,25},{25,17},{2,10},{10... | collective-permute-start | bytes 6291464 | tf_op jit(solution)/shard_map/ppermute | solution.py:19
  174.6 26.7 %collective-permute-start.18 = (bf16[8,128,1024]{2,1,0:T(8,128)(2,1)S(1)}, bf16[8,128,1024]{2,1,0:T(8,128)(2,1)}, u32[]{:S(2)}, u32[]{:S(2)}) collective-permute-start(bf16[8,128,1024]{2,1,0:T(8,128)(2,1)S(1)} %bitcast.247), channel_id=1, source_target_pairs={{0,8},{8,0},{16,24},{24,16},{1,9},{9,1},{17,25},{25,17},{2,10},{10... | collective-permute-start | bytes 6291464 | tf_op jit(solution)/shard_map/ppermute | solution.py:19
  175.0 25.5 %collective-permute-start.20 = (bf16[2,2,128,1024]{3,2,1,0:T(8,128)(2,1)}, bf16[2,2,128,1024]{3,2,1,0:T(8,128)(2,1)}, u32[]{:S(2)}, u32[]{:S(2)}) collective-permute-start(bf16[2,2,128,1024]{3,2,1,0:T(8,128)(2,1)} %fusion), channel_id=1, source_target_pairs={{0,2},{1,3},{2,0},{3,1},{4,6},{5,7},{6,4},{7,5},{8,10},{9,11},{10,... | collective-permute-start | bytes 3145736 | tf_op jit(solution)/shard_map/ppermute | solution.py:19
  176.3 25.0 %collective-permute-start.19 = (bf16[2,2,128,1024]{3,2,1,0:T(8,128)(2,1)S(1)}, bf16[2,2,128,1024]{3,2,1,0:T(8,128)(2,1)}, u32[]{:S(2)}, u32[]{:S(2)}) collective-permute-start(bf16[2,2,128,1024]{3,2,1,0:T(8,128)(2,1)S(1)} %bitcast.266), channel_id=1, source_target_pairs={{0,1},{1,0},{2,3},{3,2},{4,5},{5,4},{6,7},{7,6},{8,9},{9,8},{10,11... | collective-permute-start | bytes 3145736 | tf_op jit(solution)/shard_map/ppermute | solution.py:19
  204.6 23.3 %collective-permute-start.22 = (bf16[2,128,1024]{2,1,0:T(8,128)(2,1)S(1)}, bf16[2,128,1024]{2,1,0:T(8,128)(2,1)S(1)}, u32[]{:S(2)}, u32[]{:S(2)}) collective-permute-start(bf16[2,128,1024]{2,1,0:T(8,128)(2,1)S(1)} %get-tuple-element.422), channel_id=1, source_target_pairs={{0,1},{1,0},{2,3},{3,2},{4,5},{5,4},{6,7},{7,6},{8,9},{9,8},{10,11... | collective-permute-start | bytes 1572872 | tf_op jit(solution)/shard_map/ppermute | solution.py:19
  206.1 21.8 %collective-permute-start.21 = (bf16[2,128,1024]{2,1,0:T(8,128)(2,1)S(1)}, bf16[2,128,1024]{2,1,0:T(8,128)(2,1)S(1)}, u32[]{:S(2)}, u32[]{:S(2)}) collective-permute-start(bf16[2,128,1024]{2,1,0:T(8,128)(2,1)S(1)} %get-tuple-element.421), channel_id=1, source_target_pairs={{0,2},{1,3},{2,0},{3,1},{4,6},{5,7},{6,4},{7,5},{8,10},{9,11},{10,... | collective-permute-start | bytes 1572872 | tf_op jit(solution)/shard_map/ppermute | solution.py:19
  227.9 4.9 %collective-permute-start.24 = (bf16[8,128,1024]{2,1,0:T(8,128)(2,1)}, bf16[8,128,1024]{2,1,0:T(8,128)(2,1)S(1)}, u32[]{:S(2)}, u32[]{:S(2)}) collective-permute-start(bf16[8,128,1024]{2,1,0:T(8,128)(2,1)} %get-tuple-element.427), channel_id=1, source_target_pairs={{0,8},{8,0},{16,24},{24,16},{1,9},{9,1},{17,25},{25,17},{2,10},{10... | collective-permute-start | bytes 6291464 | tf_op jit(solution)/shard_map/ppermute | solution.py:19
  228.0 7.4 %collective-permute-start.23 = (bf16[8,128,1024]{2,1,0:T(8,128)(2,1)}, bf16[8,128,1024]{2,1,0:T(8,128)(2,1)S(1)}, u32[]{:S(2)}, u32[]{:S(2)}) collective-permute-start(bf16[8,128,1024]{2,1,0:T(8,128)(2,1)} %get-tuple-element.425), channel_id=1, source_target_pairs={{0,8},{8,0},{16,24},{24,16},{1,9},{9,1},{17,25},{25,17},{2,10},{10... | collective-permute-start | bytes 6291464 | tf_op jit(solution)/shard_map/ppermute | solution.py:19
  238.1 36.8 %collective-permute-start.28 = (bf16[2,2,128,1024]{3,2,1,0:T(8,128)(2,1)}, bf16[2,2,128,1024]{3,2,1,0:T(8,128)(2,1)}, u32[]{:S(2)}, u32[]{:S(2)}) collective-permute-start(bf16[2,2,128,1024]{3,2,1,0:T(8,128)(2,1)} %fusion.1), channel_id=1, source_target_pairs={{0,2},{1,3},{2,0},{3,1},{4,6},{5,7},{6,4},{7,5},{8,10},{9,11},{10,... | collective-permute-start | bytes 3145736 | tf_op jit(solution)/shard_map/ppermute | solution.py:19
  239.4 35.4 %collective-permute-start.27 = (bf16[2,2,128,1024]{3,2,1,0:T(8,128)(2,1)S(1)}, bf16[2,2,128,1024]{3,2,1,0:T(8,128)(2,1)}, u32[]{:S(2)}, u32[]{:S(2)}) collective-permute-start(bf16[2,2,128,1024]{3,2,1,0:T(8,128)(2,1)S(1)} %bitcast.265), channel_id=1, source_target_pairs={{0,1},{1,0},{2,3},{3,2},{4,5},{5,4},{6,7},{7,6},{8,9},{9,8},{10,11... | collective-permute-start | bytes 3145736 | tf_op jit(solution)/shard_map/ppermute | solution.py:19
  239.9 32.1 %collective-permute-start.26 = (bf16[128,1024]{1,0:T(8,128)(2,1)}, bf16[128,1024]{1,0:T(8,128)(2,1)S(1)}, u32[]{:S(2)}, u32[]{:S(2)}) collective-permute-start(bf16[128,1024]{1,0:T(8,128)(2,1)} %fusion.22), channel_id=1, source_target_pairs={{0,4},{1,5},{2,6},{3,7},{4,0},{5,1},{6,2},{7,3},{8,12},{9,13},{10,... | collective-permute-start | bytes 786440 | tf_op jit(solution)/shard_map/ppermute | solution.py:19
  242.1 31.5 %collective-permute-start.25 = (bf16[128,1024]{1,0:T(8,128)(2,1)}, bf16[128,1024]{1,0:T(8,128)(2,1)}, u32[]{:S(2)}, u32[]{:S(2)}) collective-permute-start(bf16[128,1024]{1,0:T(8,128)(2,1)} %fusion.21), channel_id=1, source_target_pairs={{0,4},{1,5},{2,6},{3,7},{4,0},{5,1},{6,2},{7,3},{8,12},{9,13},{10,... | collective-permute-start | bytes 786440 | tf_op jit(solution)/shard_map/ppermute | solution.py:19
  274.8 4.7 %collective-permute-start.29 = (bf16[8,128,1024]{2,1,0:T(8,128)(2,1)}, bf16[8,128,1024]{2,1,0:T(8,128)(2,1)S(1)}, u32[]{:S(2)}, u32[]{:S(2)}) collective-permute-start(bf16[8,128,1024]{2,1,0:T(8,128)(2,1)} %get-tuple-element.459), channel_id=1, source_target_pairs={{0,8},{8,0},{16,24},{24,16},{1,9},{9,1},{17,25},{25,17},{2,10},{10... | collective-permute-start | bytes 6291464 | tf_op jit(solution)/shard_map/ppermute | solution.py:19
  281.9 25.6 %collective-permute-start.32 = (bf16[4,128,1024]{2,1,0:T(8,128)(2,1)}, bf16[4,128,1024]{2,1,0:T(8,128)(2,1)S(1)}, u32[]{:S(2)}, u32[]{:S(2)}) collective-permute-start(bf16[4,128,1024]{2,1,0:T(8,128)(2,1)} %get-tuple-element.479), channel_id=1, source_target_pairs={{0,16},{8,24},{16,0},{24,8},{1,17},{9,25},{17,1},{25,9},{2,18},{10... | collective-permute-start | bytes 3145736 | tf_op jit(solution)/shard_map/ppermute | solution.py:19
  282.6 20.9 %collective-permute-start.31 = (bf16[2,128,1024]{2,1,0:T(8,128)(2,1)}, bf16[2,128,1024]{2,1,0:T(8,128)(2,1)}, u32[]{:S(2)}, u32[]{:S(2)}) collective-permute-start(bf16[2,128,1024]{2,1,0:T(8,128)(2,1)} %fusion.5), channel_id=1, source_target_pairs={{0,1},{1,0},{2,3},{3,2},{4,5},{5,4},{6,7},{7,6},{8,9},{9,8},{10,11... | collective-permute-start | bytes 1572872 | tf_op jit(solution)/shard_map/ppermute | solution.py:19
  283.5 20.1 %collective-permute-start.30 = (bf16[2,128,1024]{2,1,0:T(8,128)(2,1)}, bf16[2,128,1024]{2,1,0:T(8,128)(2,1)}, u32[]{:S(2)}, u32[]{:S(2)}) collective-permute-start(bf16[2,128,1024]{2,1,0:T(8,128)(2,1)} %fusion.4), channel_id=1, source_target_pairs={{0,2},{1,3},{2,0},{3,1},{4,6},{5,7},{6,4},{7,5},{8,10},{9,11},{10,... | collective-permute-start | bytes 1572872 | tf_op jit(solution)/shard_map/ppermute | solution.py:19
  313.6 27.5 %collective-permute-start.37 = (bf16[4,128,1024]{2,1,0:T(8,128)(2,1)}, bf16[4,128,1024]{2,1,0:T(8,128)(2,1)S(1)}, u32[]{:S(2)}, u32[]{:S(2)}) collective-permute-start(bf16[4,128,1024]{2,1,0:T(8,128)(2,1)} %get-tuple-element.503), channel_id=1, source_target_pairs={{0,16},{8,24},{16,0},{24,8},{1,17},{9,25},{17,1},{25,9},{2,18},{10... | collective-permute-start | bytes 3145736 | tf_op jit(solution)/shard_map/ppermute | solution.py:19
  314.3 26.7 %collective-permute-start.36 = (bf16[2,2,128,1024]{3,2,1,0:T(8,128)(2,1)}, bf16[2,2,128,1024]{3,2,1,0:T(8,128)(2,1)}, u32[]{:S(2)}, u32[]{:S(2)}) collective-permute-start(bf16[2,2,128,1024]{3,2,1,0:T(8,128)(2,1)} %bitcast.56), channel_id=1, source_target_pairs={{0,1},{1,0},{2,3},{3,2},{4,5},{5,4},{6,7},{7,6},{8,9},{9,8},{10,11... | collective-permute-start | bytes 3145736 | tf_op jit(solution)/shard_map/ppermute | solution.py:19
  315.2 21.7 %collective-permute-start.35 = (bf16[128,1024]{1,0:T(8,128)(2,1)}, bf16[128,1024]{1,0:T(8,128)(2,1)}, u32[]{:S(2)}, u32[]{:S(2)}) collective-permute-start(bf16[128,1024]{1,0:T(8,128)(2,1)} %fusion.20), channel_id=1, source_target_pairs={{0,4},{1,5},{2,6},{3,7},{4,0},{5,1},{6,2},{7,3},{8,12},{9,13},{10,... | collective-permute-start | bytes 786440 | tf_op jit(solution)/shard_map/ppermute | solution.py:19
  316.9 24.1 %collective-permute-start.34 = (bf16[128,1024]{1,0:T(8,128)(2,1)S(1)}, bf16[128,1024]{1,0:T(8,128)(2,1)}, u32[]{:S(2)}, u32[]{:S(2)}) collective-permute-start(bf16[128,1024]{1,0:T(8,128)(2,1)S(1)} %fusion.19), channel_id=1, source_target_pairs={{0,4},{1,5},{2,6},{3,7},{4,0},{5,1},{6,2},{7,3},{8,12},{9,13},{10,... | collective-permute-start | bytes 786440 | tf_op jit(solution)/shard_map/ppermute | solution.py:19
  343.6 12.8 %collective-permute-start.38 = (bf16[2,128,1024]{2,1,0:T(8,128)(2,1)}, bf16[2,128,1024]{2,1,0:T(8,128)(2,1)}, u32[]{:S(2)}, u32[]{:S(2)}) collective-permute-start(bf16[2,128,1024]{2,1,0:T(8,128)(2,1)} %fusion.3), channel_id=1, source_target_pairs={{0,2},{1,3},{2,0},{3,1},{4,6},{5,7},{6,4},{7,5},{8,10},{9,11},{10,... | collective-permute-start | bytes 1572872 | tf_op jit(solution)/shard_map/ppermute | solution.py:19
  349.6 12.8 %collective-permute-start.42 = (bf16[2,128,1024]{2,1,0:T(8,128)(2,1)S(1)}, bf16[2,128,1024]{2,1,0:T(8,128)(2,1)S(1)}, u32[]{:S(2)}, u32[]{:S(2)}) collective-permute-start(bf16[2,128,1024]{2,1,0:T(8,128)(2,1)S(1)} %pad_maximum_fusion.3), channel_id=1, source_target_pairs={{0,16},{8,24},{16,0},{24,8},{1,17},{9,25},{17,1},{25,9},{2,18},{10... | collective-permute-start | bytes 1572872 | tf_op jit(solution)/shard_map/ppermute | solution.py:19
  362.4 13.9 %collective-permute-start.41 = (bf16[128,1024]{1,0:T(8,128)(2,1)S(1)}, bf16[128,1024]{1,0:T(8,128)(2,1)S(1)}, u32[]{:S(2)}, u32[]{:S(2)}) collective-permute-start(bf16[128,1024]{1,0:T(8,128)(2,1)S(1)} %fusion.14), channel_id=1, source_target_pairs={{0,4},{1,5},{2,6},{3,7},{4,0},{5,1},{6,2},{7,3},{8,12},{9,13},{10,... | collective-permute-start | bytes 786440 | tf_op jit(solution)/shard_map/ppermute | solution.py:19
  365.5 4.9 %collective-permute-start.40 = (f32[2,16,128]{2,1,0:T(8,128)S(1)}, f32[2,16,128]{2,1,0:T(8,128)S(1)}, u32[]{:S(2)}, u32[]{:S(2)}) collective-permute-start(f32[2,16,128]{2,1,0:T(8,128)S(1)} %slice_add_fusion), channel_id=1, source_target_pairs={{0,2},{1,3},{2,0},{3,1},{4,6},{5,7},{6,4},{7,5},{8,10},{9,11},{10,... | collective-permute-start | bytes 49160 | tf_op jit(solution)/shard_map/ppermute | solution.py:19
  368.8 20.3 %collective-permute-start.44 = (bf16[2,128,1024]{2,1,0:T(8,128)(2,1)}, bf16[2,128,1024]{2,1,0:T(8,128)(2,1)}, u32[]{:S(2)}, u32[]{:S(2)}) collective-permute-start(bf16[2,128,1024]{2,1,0:T(8,128)(2,1)} %pad_maximum_fusion.4.refs_0_), channel_id=1, source_target_pairs={{0,8},{8,0},{16,24},{24,16},{1,9},{9,1},{17,25},{25,17},{2,10},{10... | collective-permute-start | bytes 1572872 | tf_op jit(solution)/shard_map/ppermute | solution.py:19
  368.8 20.3 %collective-permute-start.45 = (bf16[2,128,1024]{2,1,0:T(8,128)(2,1)}, bf16[2,128,1024]{2,1,0:T(8,128)(2,1)}, u32[]{:S(2)}, u32[]{:S(2)}) collective-permute-start(bf16[2,128,1024]{2,1,0:T(8,128)(2,1)} %pad_maximum_fusion.4.refs_0_), channel_id=1, source_target_pairs={{0,16},{8,24},{16,0},{24,8},{1,17},{9,25},{17,1},{25,9},{2,18},{10... | collective-permute-start | bytes 1572872 | tf_op jit(solution)/shard_map/ppermute | solution.py:19
  377.7 7.6 %collective-permute-start.46 = (bf16[128,1024]{1,0:T(8,128)(2,1)S(1)}, bf16[128,1024]{1,0:T(8,128)(2,1)}, u32[]{:S(2)}, u32[]{:S(2)}) collective-permute-start(bf16[128,1024]{1,0:T(8,128)(2,1)S(1)} %fusion.9.refs_0_), channel_id=1, source_target_pairs={{0,8},{8,0},{16,24},{24,16},{1,9},{9,1},{17,25},{25,17},{2,10},{10... | collective-permute-start | bytes 786440 | tf_op jit(solution)/shard_map/ppermute | solution.py:19
  377.8 11.2 %collective-permute-start.47 = (bf16[128,1024]{1,0:T(8,128)(2,1)S(1)}, bf16[128,1024]{1,0:T(8,128)(2,1)}, u32[]{:S(2)}, u32[]{:S(2)}) collective-permute-start(bf16[128,1024]{1,0:T(8,128)(2,1)S(1)} %fusion.9.refs_0_), channel_id=1, source_target_pairs={{0,16},{8,24},{16,0},{24,8},{1,17},{9,25},{17,1},{25,9},{2,18},{10... | collective-permute-start | bytes 786440 | tf_op jit(solution)/shard_map/ppermute | solution.py:19
  380.2 5.2 %collective-permute-start.43 = (f32[16,128]{1,0:T(8,128)}, f32[16,128]{1,0:T(8,128)}, u32[]{:S(2)}, u32[]{:S(2)}) collective-permute-start(f32[16,128]{1,0:T(8,128)} %fusion.33), channel_id=1, source_target_pairs={{0,4},{1,5},{2,6},{3,7},{4,0},{5,1},{6,2},{7,3},{8,12},{9,13},{10,... | collective-permute-start | bytes 24584 | tf_op jit(solution)/shard_map/ppermute | solution.py:19
  389.1 5.6 %collective-permute-start.48 = (bf16[2,128,1024]{2,1,0:T(8,128)(2,1)}, bf16[2,128,1024]{2,1,0:T(8,128)(2,1)S(1)}, u32[]{:S(2)}, u32[]{:S(2)}) collective-permute-start(bf16[2,128,1024]{2,1,0:T(8,128)(2,1)} %collective-permute-done.45.refs_2_), channel_id=1, source_target_pairs={{0,8},{8,0},{16,24},{24,16},{1,9},{9,1},{17,25},{25,17},{2,10},{10... | collective-permute-start | bytes 1572872 | tf_op jit(solution)/shard_map/ppermute | solution.py:19
  389.1 5.6 %collective-permute-start.49 = (bf16[128,1024]{1,0:T(8,128)(2,1)}, bf16[128,1024]{1,0:T(8,128)(2,1)S(1)}, u32[]{:S(2)}, u32[]{:S(2)}) collective-permute-start(bf16[128,1024]{1,0:T(8,128)(2,1)} %collective-permute-done.47.refs_2_), channel_id=1, source_target_pairs={{0,8},{8,0},{16,24},{24,16},{1,9},{9,1},{17,25},{25,17},{2,10},{10... | collective-permute-start | bytes 786440 | tf_op jit(solution)/shard_map/ppermute | solution.py:19
  (44 other events, 275.7 us)
Sparse Core Ops, SparseCore 0:
  24.4 81.8 all-gather.4
  111.0 48.8 all-gather.6

commit v5 on v4

--- a/solution.py
+++ b/solution.py
@@ -1119,30 +1119,31 @@
         sums.launch()
         seq.land((), sums)
     sums.launch()
-    crossing = jnp.stack([two_up.rest().piece(), two_down.rest().piece()])
-    cross = Sent(x_swap(seq.at(crossing)))
+    own_part = jnp.stack([red_up.rest().piece(), red_down.rest().piece()])
+    across_part = jnp.stack([two_up.rest().piece(), two_down.rest().piece()])
+    pair = seq.at(jnp.stack([own_part, across_part]))
+    cross = Sent(x_swap(pair))
     seq.land((), red_w, sums)
     red_w.launch()
     sums.launch()
-    seq.land((), cross)
-    owned = [
-        rounded_sum([*red_up.rest().terms, cross.value[0]]),
-        rounded_sum([*red_down.rest().terms, cross.value[1]]),
-    ]
-    mlp_spread = Spread(seq, jnp.stack(owned))
     seq.land((), sums, red_w)
     w_spread = Spread(seq, red_w.piece())
     sums.launch()
+    seq.land((), cross)
+    totals = jnp.stack([rounded_sum([pair[0], cross.value[1]]), rounded_sum([pair[1], cross.value[0]])])
+    totals = seq.at(totals)
+    beside = Sent(core_swap(totals))
     block, tokens_grad = seq.at((block, tokens_grad))
-    block_out, grad_tokens = seq.land((compact(block), compact(tokens_grad)), sums, mlp_spread, w_spread)
-    mlp_spread.cross()
+    block_out, grad_tokens = seq.land((compact(block), compact(tokens_grad)), sums, beside)
+    mlp_pieces = seq.at((totals[0], beside.value[0], totals[1], beside.value[1]))
+    out_fc1, out_fc2 = finish_mlp(q, mlp_pieces, n)
+    packed = sums.piece()
+    out_fc2, packed = seq.land((out_fc2, packed), w_spread)
     w_spread.cross()
-    packed = seq.at(sums.piece())
     peers = Sent([xor_swap(packed, "dp", 4, m) for m in (1, 2, 3)])
-    seq.land((), mlp_spread, w_spread, peers)
-    beside, across, opposite = peers.value
-    small_sums = (packed + beside) + (across + opposite)
-    out_fc1, out_fc2 = finish_mlp(q, mlp_spread.pieces, n)
+    seq.land((), w_spread, peers)
+    beside, across, opposite_sum = peers.value
+    small_sums = (packed + beside) + (across + opposite_sum)
     out_qkv, out_out = finish_attention(seq.value, w_spread.pieces)
     small_out = [small_sums[k, :rows] for k in range(8)]
     out_bfc1 = small_sums[8:12, :ffq].reshape(-1)

time: 415 us -> 419 us (level)
  local copies, waits for them, and re-layouts: 28.5 us -> 33.1 us
    squeeze x0 -> x2, local copies, waits for them, and re-layouts: none -> 4.47 us  [the longest x1 2.24 us: local(): totals[1]]
    ppermute x53 -> x51, waiting for transfers between devices: 75.7 us -> 73.1 us  [xor_swap(): return lax.ppermute(value, axis, [(i, i ^ mask) for i in range(size)])]
    ppermute x53 -> x51, starting transfers between devices: 50.9 us -> 52.9 us  [xor_swap(): return lax.ppermute(value, axis, [(i, i ^ mask) for i in range(size)])]
    convert_element_type x16 -> x17, other arithmetic: 30.7 us -> 29.6 us  [rounded_sum(): return sum((t.astype(full) for t in terms)).astype(kind)]
  transfers between devices with their start and end apart: 55 -> 53, of which waited for: 25 -> 23; matrix products, arithmetic and copies ran while one was open for 14% -> 15% of each run, Pallas kernels for 45% -> 45%
where the time goes in v5:
time: 419 us; the launch traced here: 413 us
  Pallas kernels  191 us (46%)
  waiting for transfers between devices  73.2 us (17%)
  starting transfers between devices  53 us (13%)
  other arithmetic  47.7 us (11%)
  local copies, waits for them, and re-layouts  33.1 us (8%)
  between operations  15 us (4%)
    pallas_call x17, Pallas kernels, call(): pl.pallas_call(kernel, out_shape=[jax.ShapeDtypeStruct(shape, kind) for s...  191 us
    ppermute x51, waiting for transfers between devices, xor_swap(): return lax.ppermute(value, axis, [(i, i ^ mask) for i in range(size)])  73.1 us
    ppermute x51, starting transfers between devices, xor_swap(): return lax.ppermute(value, axis, [(i, i ^ mask) for i in range(size)])  52.9 us
    convert_element_type x17, other arithmetic, rounded_sum(): return sum((t.astype(full) for t in terms)).astype(kind)  29.6 us
  transfers between devices with their start and end apart: 53, of which 23 were waited for; matrix products, arithmetic and copies ran while one was open for 15% of the time, Pallas kernels for 45%

profile of v5, /device:TPU:0, one launch (start us, length us, event | category | flops | bytes accessed | tf_op | source)
XLA Modules:
  0.0 413.5 jit_solution(12740721500414502589)
XLA Ops:
  7.2 2.6 first_payload.1
  9.8 4.1 collective-permute-start
  14.5 3.3 payloads.1
  17.8 6.5 %collective-permute-done = bf16[1,144,768]{2,1,0:T(8,128)(2,1)S(1)} collective-permute-done((bf16[1,144,768]{2,1,0:T(8,128)(2,1)}, bf16[1,144,768]{2,1,0:T(8,128)(2,1)S(1)}, u32[]{:S(2)}, u32[]{:S(2)}) %collective-permute-start) | collective-permute-done | bytes 221216 | tf_op jit(solution)/shard_map/ppermute | solution.py:19
  27.5 3.6 copy.32
  31.1 2.1 reshape.415
  41.3 6.6 %collective-permute-start.4 = (bf16[1,128,512]{2,1,0:T(8,128)(2,1)S(1)}, bf16[1,128,512]{2,1,0:T(8,128)(2,1)S(1)}, u32[]{:S(2)}, u32[]{:S(2)}) collective-permute-start(bf16[1,128,512]{2,1,0:T(8,128)(2,1)S(1)} %pad_maximum_fusion.7), channel_id=1, source_target_pairs={{0,4},{1,5},{2,6},{3,7},{4,0},{5,1},{6,2},{7,3},{8,12},{9,13},{10,... | collective-permute-start | bytes 393224 | tf_op jit(solution)/shard_map/ppermute | solution.py:19
  48.7 11.6 %collective-permute-done.4 = bf16[1,128,512]{2,1,0:T(8,128)(2,1)S(1)} collective-permute-done((bf16[1,128,512]{2,1,0:T(8,128)(2,1)S(1)}, bf16[1,128,512]{2,1,0:T(8,128)(2,1)S(1)}, u32[]{:S(2)}, u32[]{:S(2)}) %collective-permute-start.4) | collective-permute-done | bytes 131104 | tf_op jit(solution)/shard_map/ppermute | solution.py:19
  63.8 2.3 unpack_vectors.1
  71.5 10.5 %attention_forward.2 = (bf16[832,768]{1,0:T(8,128)(2,1)}, bf16[832,768]{1,0:T(8,128)(2,1)}, bf16[832,256]{1,0:T(8,128)(2,1)}, bf16[832,256]{1,0:T(8,128)(2,1)}, ...) custom-call(s32[9]{0:T(128)} %pad_add_fusion.1.order_ref, bf16[832,1024]{1,0:T(8,128)(2,1)} %add_convert_fusion.normed_ref, ...), custom_call_target="tpu_custom_call" | custom-call | tf_op jit(solution)/shard_map/attention_forward/pallas_call | solution.py:133
  82.0 8.9 %collective-permute-done.8 = bf16[2,128,512]{2,1,0:T(8,128)(2,1)S(1)} collective-permute-done((bf16[2,128,512]{2,1,0:T(8,128)(2,1)S(1)}, bf16[2,128,512]{2,1,0:T(8,128)(2,1)S(1)}, u32[]{:S(2)}, u32[]{:S(2)}) %collective-permute-start.8) | collective-permute-done | bytes 262176 | tf_op jit(solution)/shard_map/ppermute | solution.py:19
  96.2 10.6 %attention_forward.3 = (bf16[832,768]{1,0:T(8,128)(2,1)}, bf16[832,768]{1,0:T(8,128)(2,1)}, bf16[832,256]{1,0:T(8,128)(2,1)}, bf16[832,256]{1,0:T(8,128)(2,1)}, ...) custom-call(s32[9]{0:T(128)} %pad_add_fusion.1.order_ref, bf16[832,1024]{1,0:T(8,128)(2,1)} %add_convert_fusion.normed_ref, ...), custom_call_target="tpu_custom_call" | custom-call | tf_op jit(solution)/shard_map/attention_forward/pallas_call | solution.py:133
  108.1 2.6 collective-permute-done.12.refs_5_
  110.9 3.3 slice.477
  115.8 9.8 %attention_out.1 = (f32[832,1024]{1,0:T(8,128)}, bf16[832,1024]{1,0:T(8,128)(2,1)}) custom-call(s32[9]{0:T(128)} %pad_add_fusion.1.order_ref, f32[832,1024]{1,0:T(8,128)} %bitcast.239, f32[1,1024]{1,0:T(1,128)} %get-tuple-element.591.bias_ref, f32[1,1024]{1,0:T(1,128)} %get-tuple-element.590.gain_ref, f32[1,1024]{1,0:T(1,128)} %get-tuple-element.589.shift_ref, ...), custom_call_target="tpu_custom_call" | custom-call | tf_op jit(solution)/shard_map/attention_out/pallas_call | solution.py:133
  125.6 19.2 %mlp.4 = (bf16[8,128,1024]{2,1,0:T(8,128)(2,1)}, bf16[8,128,1024]{2,1,0:T(8,128)(2,1)}, f32[1,1024]{1,0:T(1,128)}, f32[832,1024]{1,0:T(8,128)}, f32[832,1024]{1,0:T(8,128)}) custom-call(s32[9]{0:T(128)} %pad_add_fusion.1.order_ref, f32[1,1024]{1,0:T(1,128)} %get-tuple-element.596.bias_ref, bf16[832,1024]{1,0:T(8,128)(2,1)} %get-tuple-element.370.refs_0_.refs_1_, ...), custom_call_target="tpu_custom_call" | custom-call | tf_op jit(solution)/shard_map/mlp/pallas_call | solution.py:133
  144.8 20.4 %mlp.5 = (bf16[8,128,1024]{2,1,0:T(8,128)(2,1)}, bf16[8,128,1024]{2,1,0:T(8,128)(2,1)}, f32[1,1024]{1,0:T(1,128)}, f32[832,1024]{1,0:T(8,128)}, f32[832,1024]{1,0:T(8,128)}) custom-call(s32[9]{0:T(128)} %pad_add_fusion.1.order_ref, f32[1,1024]{1,0:T(1,128)} %get-tuple-element.597.bias_ref, bf16[832,1024]{1,0:T(8,128)(2,1)} %get-tuple-element.370.refs_0_.refs_1_, ...), custom_call_target="tpu_custom_call" | custom-call | tf_op jit(solution)/shard_map/mlp/pallas_call | solution.py:133
  165.9 3.9 collective-permute-done.16
  169.8 2.4 add_convert_fusion.7
  177.8 20.5 %mlp.6 = (bf16[8,128,1024]{2,1,0:T(8,128)(2,1)}, bf16[8,128,1024]{2,1,0:T(8,128)(2,1)}, f32[1,1024]{1,0:T(1,128)}, f32[832,1024]{1,0:T(8,128)}, f32[832,1024]{1,0:T(8,128)}) custom-call(s32[9]{0:T(128)} %pad_add_fusion.1.order_ref, f32[1,1024]{1,0:T(1,128)} %get-tuple-element.595.bias_ref, bf16[832,1024]{1,0:T(8,128)(2,1)} %get-tuple-element.370.refs_0_.refs_1_, ...), custom_call_target="tpu_custom_call" | custom-call | tf_op jit(solution)/shard_map/mlp/pallas_call | solution.py:133
  198.3 2.2 collective-permute-done.20
  201.4 3.2 fusion.6
  206.8 21.1 %mlp.7 = (bf16[8,128,1024]{2,1,0:T(8,128)(2,1)}, bf16[8,128,1024]{2,1,0:T(8,128)(2,1)}, f32[1,1024]{1,0:T(1,128)}, f32[832,1024]{1,0:T(8,128)}, bf16[832,1024]{1,0:T(8,128)(2,1)}) custom-call(s32[9]{0:T(128)} %pad_add_fusion.1.order_ref, f32[1,1024]{1,0:T(1,128)} %get-tuple-element.594.bias_ref, f32[1,1024]{1,0:T(1,128)} %get-tuple-element.588.refs_0_, ...), custom_call_target="tpu_custom_call" | custom-call | tf_op jit(solution)/shard_map/mlp/pallas_call | solution.py:133
  232.8 2.6 collective-permute-done.23
  240.1 2.2 collective-permute-start.26
  243.0 11.0 %attention_out_back.1 = (f32[832,1024]{1,0:T(8,128)}, bf16[832,256]{1,0:T(8,128)(2,1)}, bf16[832,256]{1,0:T(8,128)(2,1)}, bf16[832,256]{1,0:T(8,128)(2,1)}, bf16...) custom-call(s32[9]{0:T(128)} %pad_add_fusion.1.order_ref, ...), custom_call_target="tpu_custom_call" | custom-call | tf_op jit(solution)/shard_map/attention_out_back/pallas_call | solution.py:133
  254.0 18.1 %attention_back.2 = (bf16[8,128,1024]{2,1,0:T(8,128)(2,1)}, bf16[8,128,1024]{2,1,0:T(8,128)(2,1)}, bf16[832,768]{1,0:T(8,128)(2,1)}, bf16[832,768]{1,0:T(8,128)(2,1)}, f32[2,1,768]{2,1,0:T(1,128)}) custom-call(s32[9]{0:T(128)} %pad_add_fusion.1.order_ref, bf16[832,1024]{1,0:T(8,128)(2,1)} %add_convert_fusion.normed_ref, ...), custom_call_target="tpu_custom_call" | custom-call | tf_op jit(solution)/shard_map/attention_back/pallas_call | solution.py:133
  274.9 2.4 fusion.4
  277.4 2.3 fusion.5
  279.6 2.4 add_convert_fusion.2
  283.6 2.0 collective-permute-start.30
  285.7 18.0 %attention_back.3 = (bf16[8,128,1024]{2,1,0:T(8,128)(2,1)}, bf16[8,128,1024]{2,1,0:T(8,128)(2,1)}, bf16[832,768]{1,0:T(8,128)(2,1)}, bf16[832,768]{1,0:T(8,128)(2,1)}, f32[2,1,768]{2,1,0:T(1,128)}) custom-call(s32[9]{0:T(128)} %pad_add_fusion.1.order_ref, bf16[832,1024]{1,0:T(8,128)(2,1)} %add_convert_fusion.normed_ref, ...), custom_call_target="tpu_custom_call" | custom-call | tf_op jit(solution)/shard_map/attention_back/pallas_call | solution.py:133
  303.7 3.9 collective-permute-done.32
  308.9 1.9 fusion.20
  322.3 15.9 %input_back.1 = (f32[832,1024]{1,0:T(8,128)}, f32[2,1,1024]{2,1,0:T(1,128)}) custom-call(s32[9]{0:T(128)} %pad_add_fusion.1.order_ref, f32[832,1024]{1,0:T(8,128)} %bitcast.240, f32[832,1024]{1,0:T(8,128)} %get-tuple-element.495.after_ref, f32[1,1024]{1,0:T(1,128)} %get-tuple-element.587.gain_ref, bf16[832,768]{1,0:T(8,128)(2,1)} %get-tuple-element.496.refs_0_, ...), custom_call_target="tpu_custom_call" | custom-call | tf_op jit(solution)/shard_map/input_back/pallas_call | solution.py:133
  339.7 4.2 %collective-permute-done.34 = bf16[128,1024]{1,0:T(8,128)(2,1)} collective-permute-done((bf16[128,1024]{1,0:T(8,128)(2,1)S(1)}, bf16[128,1024]{1,0:T(8,128)(2,1)}, u32[]{:S(2)}, u32[]{:S(2)}) %collective-permute-start.34) | collective-permute-done | bytes 262176 | tf_op jit(solution)/shard_map/ppermute | solution.py:19
  343.9 2.5 fusion.3
  354.2 5.0 %collective-permute-done.39 = bf16[2,128,1024]{2,1,0:T(8,128)(2,1)} collective-permute-done((bf16[2,128,1024]{2,1,0:T(8,128)(2,1)}, bf16[2,128,1024]{2,1,0:T(8,128)(2,1)}, u32[]{:S(2)}, u32[]{:S(2)}) %collective-permute-start.39) | collective-permute-done | bytes 524320 | tf_op jit(solution)/shard_map/ppermute | solution.py:19
  360.6 2.7 collective-permute-start.42
  365.8 3.1 collective-permute-done.41
  368.9 6.0 %collective-permute-done.42 = bf16[128,1024]{1,0:T(8,128)(2,1)S(1)} collective-permute-done((bf16[128,1024]{1,0:T(8,128)(2,1)S(1)}, bf16[128,1024]{1,0:T(8,128)(2,1)S(1)}, u32[]{:S(2)}, u32[]{:S(2)}) %collective-permute-start.42) | collective-permute-done | bytes 262176 | tf_op jit(solution)/shard_map/ppermute | solution.py:19
  380.5 2.5 collective-permute-start.43
  383.0 2.2 slice_bitcast_fusion.1
  385.6 1.9 reshape.427
  390.3 2.2 slice_bitcast_fusion
  392.6 3.9 finish_mlp.1
  399.5 2.0 collective-permute-done.49
  403.8 2.6 finish_attention.1
  (230 shorter events, 93.6 us)
Async XLA Ops:
  7.2 99.6 %all-gather.5.cloned.1.call-start = ((), (), s32[]{:S(2)}) async-start(), calls=%async_computation | async-start | bytes 4718592 | tf_op jit(solution)/shard_map/all_gather | solution.py:963
  9.8 14.5 %collective-permute-start = (bf16[1,144,768]{2,1,0:T(8,128)(2,1)}, bf16[1,144,768]{2,1,0:T(8,128)(2,1)S(1)}, u32[]{:S(2)}, u32[]{:S(2)}) collective-permute-start(bf16[1,144,768]{2,1,0:T(8,128)(2,1)} %bitcast.273), channel_id=1, source_target_pairs={{0,4},{1,5},{2,6},{3,7},{4,0},{5,1},{6,2},{7,3},{8,12},{9,13},{10,... | collective-permute-start | bytes 663560 | tf_op jit(solution)/shard_map/ppermute | solution.py:19
  24.3 141.0 %all-gather.7.cloned.1.call-start = ((), (), s32[]{:S(2)}) async-start(), calls=%async_computation.1 | async-start | bytes 2359296 | tf_op jit(solution)/shard_map/all_gather | solution.py:964
  24.5 11.4 %collective-permute-start.1 = (bf16[2,144,768]{2,1,0:T(8,128)(2,1)S(1)}, bf16[2,144,768]{2,1,0:T(8,128)(2,1)S(1)}, u32[]{:S(2)}, u32[]{:S(2)}) collective-permute-start(bf16[2,144,768]{2,1,0:T(8,128)(2,1)S(1)} %pad_maximum_fusion.5), channel_id=1, source_target_pairs={{0,2},{1,3},{2,0},{3,1},{4,6},{5,7},{6,4},{7,5},{8,10},{9,11},{10,... | collective-permute-start | bytes 1327112 | tf_op jit(solution)/shard_map/ppermute | solution.py:19
  36.8 24.4 %collective-permute-start.2 = (bf16[4,144,768]{2,1,0:T(8,128)(2,1)}, bf16[4,144,768]{2,1,0:T(8,128)(2,1)}, u32[]{:S(2)}, u32[]{:S(2)}) collective-permute-start(bf16[4,144,768]{2,1,0:T(8,128)(2,1)} %constant_dynamic-update-slice_fusion.refs_0_.refs_4_), channel_id=1, source_target_pairs={{0,1},{1,0},{2,3},{3,2},{4,5},{5,4},{6,7},{7,6},{8,9},{9,8},{10,11... | collective-permute-start | bytes 2654216 | tf_op jit(solution)/shard_map/ppermute | solution.py:19
  38.1 23.0 %collective-permute-start.3 = (bf16[4,144,768]{2,1,0:T(8,128)(2,1)}, bf16[4,144,768]{2,1,0:T(8,128)(2,1)}, u32[]{:S(2)}, u32[]{:S(2)}) collective-permute-start(bf16[4,144,768]{2,1,0:T(8,128)(2,1)} %constant_dynamic-update-slice_fusion.refs_0_.refs_4_), channel_id=1, source_target_pairs={{0,8},{8,0},{16,24},{24,16},{1,9},{9,1},{17,25},{25,17},{2,10},{10... | collective-permute-start | bytes 2654216 | tf_op jit(solution)/shard_map/ppermute | solution.py:19
  39.7 42.3 %collective-permute-start.6 = (bf16[4,144,768]{2,1,0:T(8,128)(2,1)}, bf16[4,144,768]{2,1,0:T(8,128)(2,1)}, u32[]{:S(2)}, u32[]{:S(2)}) collective-permute-start(bf16[4,144,768]{2,1,0:T(8,128)(2,1)} %constant_dynamic-update-slice_fusion.refs_0_.refs_4_), channel_id=1, source_target_pairs={{0,16},{8,24},{16,0},{24,8},{1,17},{9,25},{17,1},{25,9},{2,18},{10... | collective-permute-start | bytes 2654216 | tf_op jit(solution)/shard_map/ppermute | solution.py:19
  41.3 19.0 %collective-permute-start.4 = (bf16[1,128,512]{2,1,0:T(8,128)(2,1)S(1)}, bf16[1,128,512]{2,1,0:T(8,128)(2,1)S(1)}, u32[]{:S(2)}, u32[]{:S(2)}) collective-permute-start(bf16[1,128,512]{2,1,0:T(8,128)(2,1)S(1)} %pad_maximum_fusion.7), channel_id=1, source_target_pairs={{0,4},{1,5},{2,6},{3,7},{4,0},{5,1},{6,2},{7,3},{8,12},{9,13},{10,... | collective-permute-start | bytes 393224 | tf_op jit(solution)/shard_map/ppermute | solution.py:19
  61.1 10.4 %collective-permute-start.5 = (bf16[4,144,768]{2,1,0:T(8,128)(2,1)}, bf16[4,144,768]{2,1,0:T(8,128)(2,1)}, u32[]{:S(2)}, u32[]{:S(2)}) collective-permute-start(bf16[4,144,768]{2,1,0:T(8,128)(2,1)} %collective-permute-done.2.refs_1_.refs_5_), channel_id=1, source_target_pairs={{0,8},{8,0},{16,24},{24,16},{1,9},{9,1},{17,25},{25,17},{2,10},{10... | collective-permute-start | bytes 2654216 | tf_op jit(solution)/shard_map/ppermute | solution.py:19
  61.1 29.8 %collective-permute-start.7 = (bf16[4,144,768]{2,1,0:T(8,128)(2,1)}, bf16[4,144,768]{2,1,0:T(8,128)(2,1)}, u32[]{:S(2)}, u32[]{:S(2)}) collective-permute-start(bf16[4,144,768]{2,1,0:T(8,128)(2,1)} %collective-permute-done.2.refs_1_.refs_5_), channel_id=1, source_target_pairs={{0,16},{8,24},{16,0},{24,8},{1,17},{9,25},{17,1},{25,9},{2,18},{10... | collective-permute-start | bytes 2654216 | tf_op jit(solution)/shard_map/ppermute | solution.py:19
  66.1 24.8 %collective-permute-start.8 = (bf16[2,128,512]{2,1,0:T(8,128)(2,1)S(1)}, bf16[2,128,512]{2,1,0:T(8,128)(2,1)S(1)}, u32[]{:S(2)}, u32[]{:S(2)}) collective-permute-start(bf16[2,128,512]{2,1,0:T(8,128)(2,1)S(1)} %pad_maximum_fusion.6), channel_id=1, source_target_pairs={{0,2},{1,3},{2,0},{3,1},{4,6},{5,7},{6,4},{7,5},{8,10},{9,11},{10,... | collective-permute-start | bytes 786440 | tf_op jit(solution)/shard_map/ppermute | solution.py:19
  90.9 4.4 %collective-permute-start.10 = (bf16[4,144,768]{2,1,0:T(8,128)(2,1)}, bf16[4,144,768]{2,1,0:T(8,128)(2,1)S(1)}, u32[]{:S(2)}, u32[]{:S(2)}) collective-permute-start(bf16[4,144,768]{2,1,0:T(8,128)(2,1)} %collective-permute-done.7.refs_1_.refs_9_), channel_id=1, source_target_pairs={{0,8},{8,0},{16,24},{24,16},{1,9},{9,1},{17,25},{25,17},{2,10},{10... | collective-permute-start | bytes 2654216 | tf_op jit(solution)/shard_map/ppermute | solution.py:19
  90.9 4.4 %collective-permute-start.9 = (bf16[4,144,768]{2,1,0:T(8,128)(2,1)}, bf16[4,144,768]{2,1,0:T(8,128)(2,1)}, u32[]{:S(2)}, u32[]{:S(2)}) collective-permute-start(bf16[4,144,768]{2,1,0:T(8,128)(2,1)} %collective-permute-done.6.refs_0_.refs_8_), channel_id=1, source_target_pairs={{0,8},{8,0},{16,24},{24,16},{1,9},{9,1},{17,25},{25,17},{2,10},{10... | collective-permute-start | bytes 2654216 | tf_op jit(solution)/shard_map/ppermute | solution.py:19
  91.4 15.4 %collective-permute-start.11 = (bf16[4,128,512]{2,1,0:T(8,128)(2,1)S(1)}, bf16[4,128,512]{2,1,0:T(8,128)(2,1)}, u32[]{:S(2)}, u32[]{:S(2)}) collective-permute-start(bf16[4,128,512]{2,1,0:T(8,128)(2,1)S(1)} %pad_maximum_fusion.4), channel_id=1, source_target_pairs={{0,1},{1,0},{2,3},{3,2},{4,5},{5,4},{6,7},{7,6},{8,9},{9,8},{10,11... | collective-permute-start | bytes 1572872 | tf_op jit(solution)/shard_map/ppermute | solution.py:19
  110.7 14.9 %collective-permute-start.13 = (bf16[8,128,2048]{2,1,0:T(8,128)(2,1)}, bf16[8,128,2048]{2,1,0:T(8,128)(2,1)}, u32[]{:S(2)}, u32[]{:S(2)}) collective-permute-start(bf16[8,128,2048]{2,1,0:T(8,128)(2,1)} %bitcast.246), channel_id=1, source_target_pairs={{0,8},{8,0},{16,24},{24,16},{1,9},{9,1},{17,25},{25,17},{2,10},{10... | collective-permute-start | bytes 12582920 | tf_op jit(solution)/shard_map/ppermute | solution.py:19
  114.2 51.1 %collective-permute-start.14 = (bf16[8,128,1024]{2,1,0:T(8,128)(2,1)}, bf16[8,128,1024]{2,1,0:T(8,128)(2,1)}, u32[]{:S(2)}, u32[]{:S(2)}) collective-permute-start(bf16[8,128,1024]{2,1,0:T(8,128)(2,1)} %slice.477), channel_id=1, source_target_pairs={{0,16},{8,24},{16,0},{24,8},{1,17},{9,25},{17,1},{25,9},{2,18},{10... | collective-permute-start | bytes 6291464 | tf_op jit(solution)/shard_map/ppermute | solution.py:19
  165.3 4.4 %collective-permute-start.16 = (bf16[8,128,1024]{2,1,0:T(8,128)(2,1)}, bf16[8,128,1024]{2,1,0:T(8,128)(2,1)S(1)}, u32[]{:S(2)}, u32[]{:S(2)}) collective-permute-start(bf16[8,128,1024]{2,1,0:T(8,128)(2,1)} %get-tuple-element.388), channel_id=1, source_target_pairs={{0,8},{8,0},{16,24},{24,16},{1,9},{9,1},{17,25},{25,17},{2,10},{10... | collective-permute-start | bytes 6291464 | tf_op jit(solution)/shard_map/ppermute | solution.py:19
  165.4 7.4 %collective-permute-start.15 = (bf16[8,128,1024]{2,1,0:T(8,128)(2,1)}, bf16[8,128,1024]{2,1,0:T(8,128)(2,1)S(1)}, u32[]{:S(2)}, u32[]{:S(2)}) collective-permute-start(bf16[8,128,1024]{2,1,0:T(8,128)(2,1)} %get-tuple-element.386), channel_id=1, source_target_pairs={{0,8},{8,0},{16,24},{24,16},{1,9},{9,1},{17,25},{25,17},{2,10},{10... | collective-permute-start | bytes 6291464 | tf_op jit(solution)/shard_map/ppermute | solution.py:19
  174.5 26.9 %collective-permute-start.17 = (bf16[8,128,1024]{2,1,0:T(8,128)(2,1)}, bf16[8,128,1024]{2,1,0:T(8,128)(2,1)S(1)}, u32[]{:S(2)}, u32[]{:S(2)}) collective-permute-start(bf16[8,128,1024]{2,1,0:T(8,128)(2,1)} %collective-permute-done.14.refs_2_), channel_id=1, source_target_pairs={{0,8},{8,0},{16,24},{24,16},{1,9},{9,1},{17,25},{25,17},{2,10},{10... | collective-permute-start | bytes 6291464 | tf_op jit(solution)/shard_map/ppermute | solution.py:19
  174.6 26.7 %collective-permute-start.18 = (bf16[8,128,1024]{2,1,0:T(8,128)(2,1)S(1)}, bf16[8,128,1024]{2,1,0:T(8,128)(2,1)}, u32[]{:S(2)}, u32[]{:S(2)}) collective-permute-start(bf16[8,128,1024]{2,1,0:T(8,128)(2,1)S(1)} %bitcast.253), channel_id=1, source_target_pairs={{0,8},{8,0},{16,24},{24,16},{1,9},{9,1},{17,25},{25,17},{2,10},{10... | collective-permute-start | bytes 6291464 | tf_op jit(solution)/shard_map/ppermute | solution.py:19
  175.0 25.5 %collective-permute-start.20 = (bf16[2,2,128,1024]{3,2,1,0:T(8,128)(2,1)}, bf16[2,2,128,1024]{3,2,1,0:T(8,128)(2,1)}, u32[]{:S(2)}, u32[]{:S(2)}) collective-permute-start(bf16[2,2,128,1024]{3,2,1,0:T(8,128)(2,1)} %fusion), channel_id=1, source_target_pairs={{0,2},{1,3},{2,0},{3,1},{4,6},{5,7},{6,4},{7,5},{8,10},{9,11},{10,... | collective-permute-start | bytes 3145736 | tf_op jit(solution)/shard_map/ppermute | solution.py:19
  176.3 25.0 %collective-permute-start.19 = (bf16[2,2,128,1024]{3,2,1,0:T(8,128)(2,1)S(1)}, bf16[2,2,128,1024]{3,2,1,0:T(8,128)(2,1)}, u32[]{:S(2)}, u32[]{:S(2)}) collective-permute-start(bf16[2,2,128,1024]{3,2,1,0:T(8,128)(2,1)S(1)} %bitcast.272), channel_id=1, source_target_pairs={{0,1},{1,0},{2,3},{3,2},{4,5},{5,4},{6,7},{7,6},{8,9},{9,8},{10,11... | collective-permute-start | bytes 3145736 | tf_op jit(solution)/shard_map/ppermute | solution.py:19
  204.6 23.3 %collective-permute-start.22 = (bf16[2,128,1024]{2,1,0:T(8,128)(2,1)S(1)}, bf16[2,128,1024]{2,1,0:T(8,128)(2,1)S(1)}, u32[]{:S(2)}, u32[]{:S(2)}) collective-permute-start(bf16[2,128,1024]{2,1,0:T(8,128)(2,1)S(1)} %get-tuple-element.424), channel_id=1, source_target_pairs={{0,1},{1,0},{2,3},{3,2},{4,5},{5,4},{6,7},{7,6},{8,9},{9,8},{10,11... | collective-permute-start | bytes 1572872 | tf_op jit(solution)/shard_map/ppermute | solution.py:19
  206.1 21.8 %collective-permute-start.21 = (bf16[2,128,1024]{2,1,0:T(8,128)(2,1)S(1)}, bf16[2,128,1024]{2,1,0:T(8,128)(2,1)S(1)}, u32[]{:S(2)}, u32[]{:S(2)}) collective-permute-start(bf16[2,128,1024]{2,1,0:T(8,128)(2,1)S(1)} %get-tuple-element.423), channel_id=1, source_target_pairs={{0,2},{1,3},{2,0},{3,1},{4,6},{5,7},{6,4},{7,5},{8,10},{9,11},{10,... | collective-permute-start | bytes 1572872 | tf_op jit(solution)/shard_map/ppermute | solution.py:19
  228.0 4.4 %collective-permute-start.24 = (bf16[8,128,1024]{2,1,0:T(8,128)(2,1)}, bf16[8,128,1024]{2,1,0:T(8,128)(2,1)S(1)}, u32[]{:S(2)}, u32[]{:S(2)}) collective-permute-start(bf16[8,128,1024]{2,1,0:T(8,128)(2,1)} %get-tuple-element.429), channel_id=1, source_target_pairs={{0,8},{8,0},{16,24},{24,16},{1,9},{9,1},{17,25},{25,17},{2,10},{10... | collective-permute-start | bytes 6291464 | tf_op jit(solution)/shard_map/ppermute | solution.py:19
  228.1 7.4 %collective-permute-start.23 = (bf16[8,128,1024]{2,1,0:T(8,128)(2,1)}, bf16[8,128,1024]{2,1,0:T(8,128)(2,1)S(1)}, u32[]{:S(2)}, u32[]{:S(2)}) collective-permute-start(bf16[8,128,1024]{2,1,0:T(8,128)(2,1)} %get-tuple-element.427), channel_id=1, source_target_pairs={{0,8},{8,0},{16,24},{24,16},{1,9},{9,1},{17,25},{25,17},{2,10},{10... | collective-permute-start | bytes 6291464 | tf_op jit(solution)/shard_map/ppermute | solution.py:19
  238.2 36.8 %collective-permute-start.28 = (bf16[2,2,128,1024]{3,2,1,0:T(8,128)(2,1)}, bf16[2,2,128,1024]{3,2,1,0:T(8,128)(2,1)}, u32[]{:S(2)}, u32[]{:S(2)}) collective-permute-start(bf16[2,2,128,1024]{3,2,1,0:T(8,128)(2,1)} %fusion.1), channel_id=1, source_target_pairs={{0,2},{1,3},{2,0},{3,1},{4,6},{5,7},{6,4},{7,5},{8,10},{9,11},{10,... | collective-permute-start | bytes 3145736 | tf_op jit(solution)/shard_map/ppermute | solution.py:19
  239.5 35.4 %collective-permute-start.27 = (bf16[2,2,128,1024]{3,2,1,0:T(8,128)(2,1)S(1)}, bf16[2,2,128,1024]{3,2,1,0:T(8,128)(2,1)}, u32[]{:S(2)}, u32[]{:S(2)}) collective-permute-start(bf16[2,2,128,1024]{3,2,1,0:T(8,128)(2,1)S(1)} %bitcast.271), channel_id=1, source_target_pairs={{0,1},{1,0},{2,3},{3,2},{4,5},{5,4},{6,7},{7,6},{8,9},{9,8},{10,11... | collective-permute-start | bytes 3145736 | tf_op jit(solution)/shard_map/ppermute | solution.py:19
  240.1 32.1 %collective-permute-start.26 = (bf16[128,1024]{1,0:T(8,128)(2,1)S(1)}, bf16[128,1024]{1,0:T(8,128)(2,1)S(1)}, u32[]{:S(2)}, u32[]{:S(2)}) collective-permute-start(bf16[128,1024]{1,0:T(8,128)(2,1)S(1)} %fusion.22), channel_id=1, source_target_pairs={{0,4},{1,5},{2,6},{3,7},{4,0},{5,1},{6,2},{7,3},{8,12},{9,13},{10,... | collective-permute-start | bytes 786440 | tf_op jit(solution)/shard_map/ppermute | solution.py:19
  242.2 31.4 %collective-permute-start.25 = (bf16[128,1024]{1,0:T(8,128)(2,1)S(1)}, bf16[128,1024]{1,0:T(8,128)(2,1)}, u32[]{:S(2)}, u32[]{:S(2)}) collective-permute-start(bf16[128,1024]{1,0:T(8,128)(2,1)S(1)} %fusion.21), channel_id=1, source_target_pairs={{0,4},{1,5},{2,6},{3,7},{4,0},{5,1},{6,2},{7,3},{8,12},{9,13},{10,... | collective-permute-start | bytes 786440 | tf_op jit(solution)/shard_map/ppermute | solution.py:19
  274.9 4.7 %collective-permute-start.29 = (bf16[8,128,1024]{2,1,0:T(8,128)(2,1)}, bf16[8,128,1024]{2,1,0:T(8,128)(2,1)S(1)}, u32[]{:S(2)}, u32[]{:S(2)}) collective-permute-start(bf16[8,128,1024]{2,1,0:T(8,128)(2,1)} %get-tuple-element.461), channel_id=1, source_target_pairs={{0,8},{8,0},{16,24},{24,16},{1,9},{9,1},{17,25},{25,17},{2,10},{10... | collective-permute-start | bytes 6291464 | tf_op jit(solution)/shard_map/ppermute | solution.py:19
  282.0 25.6 %collective-permute-start.32 = (bf16[4,128,1024]{2,1,0:T(8,128)(2,1)}, bf16[4,128,1024]{2,1,0:T(8,128)(2,1)S(1)}, u32[]{:S(2)}, u32[]{:S(2)}) collective-permute-start(bf16[4,128,1024]{2,1,0:T(8,128)(2,1)} %get-tuple-element.481), channel_id=1, source_target_pairs={{0,16},{8,24},{16,0},{24,8},{1,17},{9,25},{17,1},{25,9},{2,18},{10... | collective-permute-start | bytes 3145736 | tf_op jit(solution)/shard_map/ppermute | solution.py:19
  282.7 21.0 %collective-permute-start.31 = (bf16[2,128,1024]{2,1,0:T(8,128)(2,1)}, bf16[2,128,1024]{2,1,0:T(8,128)(2,1)S(1)}, u32[]{:S(2)}, u32[]{:S(2)}) collective-permute-start(bf16[2,128,1024]{2,1,0:T(8,128)(2,1)} %fusion.5), channel_id=1, source_target_pairs={{0,1},{1,0},{2,3},{3,2},{4,5},{5,4},{6,7},{7,6},{8,9},{9,8},{10,11... | collective-permute-start | bytes 1572872 | tf_op jit(solution)/shard_map/ppermute | solution.py:19
  283.6 20.1 %collective-permute-start.30 = (bf16[2,128,1024]{2,1,0:T(8,128)(2,1)}, bf16[2,128,1024]{2,1,0:T(8,128)(2,1)}, u32[]{:S(2)}, u32[]{:S(2)}) collective-permute-start(bf16[2,128,1024]{2,1,0:T(8,128)(2,1)} %fusion.4), channel_id=1, source_target_pairs={{0,2},{1,3},{2,0},{3,1},{4,6},{5,7},{6,4},{7,5},{8,10},{9,11},{10,... | collective-permute-start | bytes 1572872 | tf_op jit(solution)/shard_map/ppermute | solution.py:19
  313.7 30.2 %collective-permute-start.37 = (bf16[4,128,1024]{2,1,0:T(8,128)(2,1)}, bf16[4,128,1024]{2,1,0:T(8,128)(2,1)S(1)}, u32[]{:S(2)}, u32[]{:S(2)}) collective-permute-start(bf16[4,128,1024]{2,1,0:T(8,128)(2,1)} %get-tuple-element.507), channel_id=1, source_target_pairs={{0,16},{8,24},{16,0},{24,8},{1,17},{9,25},{17,1},{25,9},{2,18},{10... | collective-permute-start | bytes 3145736 | tf_op jit(solution)/shard_map/ppermute | solution.py:19
  314.4 29.5 %collective-permute-start.36 = (bf16[2,2,128,1024]{3,2,1,0:T(8,128)(2,1)}, bf16[2,2,128,1024]{3,2,1,0:T(8,128)(2,1)}, u32[]{:S(2)}, u32[]{:S(2)}) collective-permute-start(bf16[2,2,128,1024]{3,2,1,0:T(8,128)(2,1)} %bitcast.56), channel_id=1, source_target_pairs={{0,1},{1,0},{2,3},{3,2},{4,5},{5,4},{6,7},{7,6},{8,9},{9,8},{10,11... | collective-permute-start | bytes 3145736 | tf_op jit(solution)/shard_map/ppermute | solution.py:19
  317.9 21.8 %collective-permute-start.35 = (bf16[128,1024]{1,0:T(8,128)(2,1)}, bf16[128,1024]{1,0:T(8,128)(2,1)}, u32[]{:S(2)}, u32[]{:S(2)}) collective-permute-start(bf16[128,1024]{1,0:T(8,128)(2,1)} %fusion.20), channel_id=1, source_target_pairs={{0,4},{1,5},{2,6},{3,7},{4,0},{5,1},{6,2},{7,3},{8,12},{9,13},{10,... | collective-permute-start | bytes 786440 | tf_op jit(solution)/shard_map/ppermute | solution.py:19
  319.8 24.1 %collective-permute-start.34 = (bf16[128,1024]{1,0:T(8,128)(2,1)S(1)}, bf16[128,1024]{1,0:T(8,128)(2,1)}, u32[]{:S(2)}, u32[]{:S(2)}) collective-permute-start(bf16[128,1024]{1,0:T(8,128)(2,1)S(1)} %fusion.19), channel_id=1, source_target_pairs={{0,4},{1,5},{2,6},{3,7},{4,0},{5,1},{6,2},{7,3},{8,12},{9,13},{10,... | collective-permute-start | bytes 786440 | tf_op jit(solution)/shard_map/ppermute | solution.py:19
  346.4 12.8 %collective-permute-start.39 = (bf16[2,128,1024]{2,1,0:T(8,128)(2,1)}, bf16[2,128,1024]{2,1,0:T(8,128)(2,1)}, u32[]{:S(2)}, u32[]{:S(2)}) collective-permute-start(bf16[2,128,1024]{2,1,0:T(8,128)(2,1)} %fusion.3), channel_id=1, source_target_pairs={{0,2},{1,3},{2,0},{3,1},{4,6},{5,7},{6,4},{7,5},{8,10},{9,11},{10,... | collective-permute-start | bytes 1572872 | tf_op jit(solution)/shard_map/ppermute | solution.py:19
  348.7 5.5 %collective-permute-start.40 = (f32[2,2,16,128]{3,2,1,0:T(8,128)S(1)}, f32[2,2,16,128]{3,2,1,0:T(8,128)S(1)}, u32[]{:S(2)}, u32[]{:S(2)}) collective-permute-start(f32[2,2,16,128]{3,2,1,0:T(8,128)S(1)} %bitcast.275), channel_id=1, source_target_pairs={{0,1},{1,0},{2,3},{3,2},{4,5},{5,4},{6,7},{7,6},{8,9},{9,8},{10,11... | collective-permute-start | bytes 98312 | tf_op jit(solution)/shard_map/ppermute | solution.py:19
  352.8 24.9 %collective-permute-start.38 = (bf16[2,2,128,1024]{3,2,1,0:T(8,128)(2,1)S(1)}, bf16[2,2,128,1024]{3,2,1,0:T(8,128)(2,1)S(1)}, u32[]{:S(2)}, u32[]{:S(2)}) collective-permute-start(bf16[2,2,128,1024]{3,2,1,0:T(8,128)(2,1)S(1)} %pad_maximum_fusion.2), channel_id=1, source_target_pairs={{0,16},{8,24},{16,0},{24,8},{1,17},{9,25},{17,1},{25,9},{2,18},{10... | collective-permute-start | bytes 3145736 | tf_op jit(solution)/shard_map/ppermute | solution.py:19
  360.6 14.2 %collective-permute-start.42 = (bf16[128,1024]{1,0:T(8,128)(2,1)S(1)}, bf16[128,1024]{1,0:T(8,128)(2,1)S(1)}, u32[]{:S(2)}, u32[]{:S(2)}) collective-permute-start(bf16[128,1024]{1,0:T(8,128)(2,1)S(1)} %fusion.10), channel_id=1, source_target_pairs={{0,4},{1,5},{2,6},{3,7},{4,0},{5,1},{6,2},{7,3},{8,12},{9,13},{10,... | collective-permute-start | bytes 786440 | tf_op jit(solution)/shard_map/ppermute | solution.py:19
  364.1 4.8 %collective-permute-start.41 = (f32[2,16,128]{2,1,0:T(8,128)S(1)}, f32[2,16,128]{2,1,0:T(8,128)S(1)}, u32[]{:S(2)}, u32[]{:S(2)}) collective-permute-start(f32[2,16,128]{2,1,0:T(8,128)S(1)} %slice_add_fusion), channel_id=1, source_target_pairs={{0,2},{1,3},{2,0},{3,1},{4,6},{5,7},{6,4},{7,5},{8,10},{9,11},{10,... | collective-permute-start | bytes 49160 | tf_op jit(solution)/shard_map/ppermute | solution.py:19
  379.1 11.2 %collective-permute-start.44 = (bf16[2,2,128,1024]{3,2,1,0:T(8,128)(2,1)}, bf16[2,2,128,1024]{3,2,1,0:T(8,128)(2,1)}, u32[]{:S(2)}, u32[]{:S(2)}) collective-permute-start(bf16[2,2,128,1024]{3,2,1,0:T(8,128)(2,1)} %pad_maximum_fusion.3), channel_id=1, source_target_pairs={{0,8},{8,0},{16,24},{24,16},{1,9},{9,1},{17,25},{25,17},{2,10},{10... | collective-permute-start | bytes 3145736 | tf_op jit(solution)/shard_map/ppermute | solution.py:19
  379.1 18.1 %collective-permute-start.45 = (bf16[128,1024]{1,0:T(8,128)(2,1)S(1)}, bf16[128,1024]{1,0:T(8,128)(2,1)}, u32[]{:S(2)}, u32[]{:S(2)}) collective-permute-start(bf16[128,1024]{1,0:T(8,128)(2,1)S(1)} %fusion.9.refs_0_), channel_id=1, source_target_pairs={{0,8},{8,0},{16,24},{24,16},{1,9},{9,1},{17,25},{25,17},{2,10},{10... | collective-permute-start | bytes 786440 | tf_op jit(solution)/shard_map/ppermute | solution.py:19
  379.6 17.6 %collective-permute-start.46 = (bf16[128,1024]{1,0:T(8,128)(2,1)S(1)}, bf16[128,1024]{1,0:T(8,128)(2,1)}, u32[]{:S(2)}, u32[]{:S(2)}) collective-permute-start(bf16[128,1024]{1,0:T(8,128)(2,1)S(1)} %fusion.9.refs_0_), channel_id=1, source_target_pairs={{0,16},{8,24},{16,0},{24,8},{1,17},{9,25},{17,1},{25,9},{2,18},{10... | collective-permute-start | bytes 786440 | tf_op jit(solution)/shard_map/ppermute | solution.py:19
  380.5 9.9 %collective-permute-start.43 = (f32[16,128]{1,0:T(8,128)}, f32[16,128]{1,0:T(8,128)}, u32[]{:S(2)}, u32[]{:S(2)}) collective-permute-start(f32[16,128]{1,0:T(8,128)} %fusion.33), channel_id=1, source_target_pairs={{0,4},{1,5},{2,6},{3,7},{4,0},{5,1},{6,2},{7,3},{8,12},{9,13},{10,... | collective-permute-start | bytes 24584 | tf_op jit(solution)/shard_map/ppermute | solution.py:19
  397.2 5.4 %collective-permute-start.47 = (bf16[128,1024]{1,0:T(8,128)(2,1)}, bf16[128,1024]{1,0:T(8,128)(2,1)S(1)}, u32[]{:S(2)}, u32[]{:S(2)}) collective-permute-start(bf16[128,1024]{1,0:T(8,128)(2,1)} %collective-permute-done.46.refs_2_), channel_id=1, source_target_pairs={{0,8},{8,0},{16,24},{24,16},{1,9},{9,1},{17,25},{25,17},{2,10},{10... | collective-permute-start | bytes 786440 | tf_op jit(solution)/shard_map/ppermute | solution.py:19
  (44 other events, 241.3 us)
Sparse Core Ops, SparseCore 0:
  24.4 81.8 all-gather.4
  111.0 48.8 all-gather.6

commit v6 on v5

--- a/solution.py
+++ b/solution.py
@@ -718,28 +718,29 @@
     return [jnp.where(q >= 2, once[i ^ 2], once[i]) for i in range(4)]
 
 
-def finish_mlp(q, pieces, n):
-    _, rows, width = pieces[0].shape
+def finish_mlp(q, totals, swapped, n):
+    _, _, rows, width = totals.shape
     share = width // n
     if share % 128:
-        pieces = natural_quarters(q, pieces)
+        pieces = natural_quarters(q, [totals[0], swapped[0], totals[1], swapped[1]])
         fc1 = jnp.stack([p[0].reshape(rows, n, share) for p in pieces], axis=2).reshape(rows, 4 * width)
         return fc1.astype(full), jnp.concatenate([p[1] for p in pieces]).astype(full)
 
     def kernel(q_ref, *refs):
-        fc1_ref, fc2_ref = refs[4:]
+        fc1_ref, fc2_ref = refs[2:]
         for j in range(4):
             g = q_ref[0] ^ j
+            held = refs[j % 2].at[j // 2]
             for s in range(n):
                 at = pl.ds(pl.multiple_of((4 * s + g) * share, share), share)
-                fc1_ref[:, at] = refs[j][0, :, s * share : (s + 1) * share].astype(full)
-            fc2_ref[tile(g, rows), :] = refs[j][1].astype(full)
+                fc1_ref[:, at] = held[0, :, s * share : (s + 1) * share].astype(full)
+            fc2_ref[tile(g, rows), :] = held[1].astype(full)
 
     return call(
         kernel,
         "finish_mlp",
-        (q[None], *pieces),
-        [SCALARS] + [ON_CHIP] * 4,
+        (q[None], totals, swapped),
+        [SCALARS] + [ON_CHIP] * 2,
         [((rows, 4 * width), full), ((4 * rows, width), full)],
         [ON_CHIP] * 2,
         [],
@@ -1123,25 +1124,23 @@
     across_part = jnp.stack([two_up.rest().piece(), two_down.rest().piece()])
     pair = seq.at(jnp.stack([own_part, across_part]))
     cross = Sent(x_swap(pair))
-    seq.land((), red_w, sums)
+    grad_tokens = seq.land(compact(seq.at(tokens_grad)), red_w, sums)
     red_w.launch()
     sums.launch()
-    seq.land((), sums, red_w)
+    block_out = seq.land(compact(seq.at(block)), sums, red_w)
     w_spread = Spread(seq, red_w.piece())
     sums.launch()
     seq.land((), cross)
     totals = jnp.stack([rounded_sum([pair[0], cross.value[1]]), rounded_sum([pair[1], cross.value[0]])])
     totals = seq.at(totals)
-    beside = Sent(core_swap(totals))
-    block, tokens_grad = seq.at((block, tokens_grad))
-    block_out, grad_tokens = seq.land((compact(block), compact(tokens_grad)), sums, beside)
-    mlp_pieces = seq.at((totals[0], beside.value[0], totals[1], beside.value[1]))
-    out_fc1, out_fc2 = finish_mlp(q, mlp_pieces, n)
-    packed = sums.piece()
-    out_fc2, packed = seq.land((out_fc2, packed), w_spread)
+    swapped = Sent(core_swap(totals))
+    seq.land((), sums, swapped)
+    packed = seq.at(sums.piece())
+    peers = Sent([xor_swap(packed, "dp", 4, m) for m in (1, 2, 3)])
+    out_fc1, out_fc2 = finish_mlp(q, totals, seq.at(swapped.value), n)
+    out_fc2 = seq.land(out_fc2, w_spread, peers)
     w_spread.cross()
-    peers = Sent([xor_swap(packed, "dp", 4, m) for m in (1, 2, 3)])
-    seq.land((), w_spread, peers)
+    seq.land((), w_spread)
     beside, across, opposite_sum = peers.value
     small_sums = (packed + beside) + (across + opposite_sum)
     out_qkv, out_out = finish_attention(seq.value, w_spread.pieces)

time: 419 us -> 412 us (0.983)
    squeeze x2 -> x0, local copies, waits for them, and re-layouts: 4.47 us -> none  [the longest x1 2.24 us: local(): totals[1]]
  transfers between devices with their start and end apart: 53 -> 53, of which waited for: 23 -> 23; matrix products, arithmetic and copies ran while one was open for 15% -> 13% of each run, Pallas kernels for 45% -> 45%
where the time goes in v6:
time: 412 us; the launch traced here: 407 us
  Pallas kernels  191 us (46%)
  waiting for transfers between devices  72.5 us (18%)
  starting transfers between devices  51.3 us (12%)
  other arithmetic  47.1 us (11%)
  local copies, waits for them, and re-layouts  29.3 us (7%)
  between operations  15.1 us (4%)
    pallas_call x17, Pallas kernels, call(): pl.pallas_call(kernel, out_shape=[jax.ShapeDtypeStruct(shape, kind) for s...  191 us
    ppermute x51, waiting for transfers between devices, xor_swap(): return lax.ppermute(value, axis, [(i, i ^ mask) for i in range(size)])  72.4 us
    ppermute x51, starting transfers between devices, xor_swap(): return lax.ppermute(value, axis, [(i, i ^ mask) for i in range(size)])  51.3 us
    convert_element_type x17, other arithmetic, rounded_sum(): return sum((t.astype(full) for t in terms)).astype(kind)  31.7 us
  transfers between devices with their start and end apart: 53, of which 23 were waited for; matrix products, arithmetic and copies ran while one was open for 13% of the time, Pallas kernels for 45%

profile of v6, /device:TPU:0, one launch (start us, length us, event | category | flops | bytes accessed | tf_op | source)
XLA Modules:
  0.0 406.6 jit_solution(10128243588106730936)
XLA Ops:
  7.2 2.6 first_payload.1
  9.8 4.1 %collective-permute-start = (bf16[1,144,768]{2,1,0:T(8,128)(2,1)}, bf16[1,144,768]{2,1,0:T(8,128)(2,1)S(1)}, u32[]{:S(2)}, u32[]{:S(2)}) collective-permute-start(bf16[1,144,768]{2,1,0:T(8,128)(2,1)} %bitcast.265), channel_id=1, source_target_pairs={{0,4},{1,5},{2,6},{3,7},{4,0},{5,1},{6,2},{7,3},{8,12},{9,13},{10,... | collective-permute-start | bytes 663560 | tf_op jit(solution)/shard_map/ppermute | solution.py:19
  14.5 3.3 payloads.1
  17.8 6.5 %collective-permute-done = bf16[1,144,768]{2,1,0:T(8,128)(2,1)S(1)} collective-permute-done((bf16[1,144,768]{2,1,0:T(8,128)(2,1)}, bf16[1,144,768]{2,1,0:T(8,128)(2,1)S(1)}, u32[]{:S(2)}, u32[]{:S(2)}) %collective-permute-start) | collective-permute-done | bytes 221216 | tf_op jit(solution)/shard_map/ppermute | solution.py:19
  27.5 3.6 copy.32
  31.1 2.2 reshape.415
  41.3 6.6 %collective-permute-start.4 = (bf16[1,128,512]{2,1,0:T(8,128)(2,1)S(1)}, bf16[1,128,512]{2,1,0:T(8,128)(2,1)S(1)}, u32[]{:S(2)}, u32[]{:S(2)}) collective-permute-start(bf16[1,128,512]{2,1,0:T(8,128)(2,1)S(1)} %pad_maximum_fusion.7), channel_id=1, source_target_pairs={{0,4},{1,5},{2,6},{3,7},{4,0},{5,1},{6,2},{7,3},{8,12},{9,13},{10,... | collective-permute-start | bytes 393224 | tf_op jit(solution)/shard_map/ppermute | solution.py:19
  48.7 11.6 %collective-permute-done.4 = bf16[1,128,512]{2,1,0:T(8,128)(2,1)S(1)} collective-permute-done((bf16[1,128,512]{2,1,0:T(8,128)(2,1)S(1)}, bf16[1,128,512]{2,1,0:T(8,128)(2,1)S(1)}, u32[]{:S(2)}, u32[]{:S(2)}) %collective-permute-start.4) | collective-permute-done | bytes 131104 | tf_op jit(solution)/shard_map/ppermute | solution.py:19
  63.8 2.3 unpack_vectors.1
  69.1 1.8 add_convert_fusion.normed_ref
  71.5 10.5 %attention_forward.2 = (bf16[832,768]{1,0:T(8,128)(2,1)}, bf16[832,768]{1,0:T(8,128)(2,1)}, bf16[832,256]{1,0:T(8,128)(2,1)}, bf16[832,256]{1,0:T(8,128)(2,1)}, ...) custom-call(s32[9]{0:T(128)} %pad_add_fusion.1.order_ref, bf16[832,1024]{1,0:T(8,128)(2,1)} %add_convert_fusion.normed_ref, ...), custom_call_target="tpu_custom_call" | custom-call | tf_op jit(solution)/shard_map/attention_forward/pallas_call | solution.py:133
  82.0 8.9 %collective-permute-done.8 = bf16[2,128,512]{2,1,0:T(8,128)(2,1)S(1)} collective-permute-done((bf16[2,128,512]{2,1,0:T(8,128)(2,1)S(1)}, bf16[2,128,512]{2,1,0:T(8,128)(2,1)S(1)}, u32[]{:S(2)}, u32[]{:S(2)}) %collective-permute-start.8) | collective-permute-done | bytes 262176 | tf_op jit(solution)/shard_map/ppermute | solution.py:19
  96.3 10.5 %attention_forward.3 = (bf16[832,768]{1,0:T(8,128)(2,1)}, bf16[832,768]{1,0:T(8,128)(2,1)}, bf16[832,256]{1,0:T(8,128)(2,1)}, bf16[832,256]{1,0:T(8,128)(2,1)}, ...) custom-call(s32[9]{0:T(128)} %pad_add_fusion.1.order_ref, bf16[832,1024]{1,0:T(8,128)(2,1)} %add_convert_fusion.normed_ref, ...), custom_call_target="tpu_custom_call" | custom-call | tf_op jit(solution)/shard_map/attention_forward/pallas_call | solution.py:133
  108.1 2.6 collective-permute-done.12.refs_5_
  110.9 3.3 slice.465
  115.8 9.8 %attention_out.1 = (f32[832,1024]{1,0:T(8,128)}, bf16[832,1024]{1,0:T(8,128)(2,1)}) custom-call(s32[9]{0:T(128)} %pad_add_fusion.1.order_ref, f32[832,1024]{1,0:T(8,128)} %bitcast.231, f32[1,1024]{1,0:T(1,128)} %get-tuple-element.585.bias_ref, f32[1,1024]{1,0:T(1,128)} %get-tuple-element.584.gain_ref, f32[1,1024]{1,0:T(1,128)} %get-tuple-element.583.shift_ref, ...), custom_call_target="tpu_custom_call" | custom-call | tf_op jit(solution)/shard_map/attention_out/pallas_call | solution.py:133
  125.6 19.2 %mlp.4 = (bf16[8,128,1024]{2,1,0:T(8,128)(2,1)}, bf16[8,128,1024]{2,1,0:T(8,128)(2,1)}, f32[1,1024]{1,0:T(1,128)}, f32[832,1024]{1,0:T(8,128)}, f32[832,1024]{1,0:T(8,128)}) custom-call(s32[9]{0:T(128)} %pad_add_fusion.1.order_ref, f32[1,1024]{1,0:T(1,128)} %get-tuple-element.590.bias_ref, bf16[832,1024]{1,0:T(8,128)(2,1)} %get-tuple-element.369.refs_0_.refs_1_, ...), custom_call_target="tpu_custom_call" | custom-call | tf_op jit(solution)/shard_map/mlp/pallas_call | solution.py:133
  144.8 20.4 %mlp.5 = (bf16[8,128,1024]{2,1,0:T(8,128)(2,1)}, bf16[8,128,1024]{2,1,0:T(8,128)(2,1)}, f32[1,1024]{1,0:T(1,128)}, f32[832,1024]{1,0:T(8,128)}, f32[832,1024]{1,0:T(8,128)}) custom-call(s32[9]{0:T(128)} %pad_add_fusion.1.order_ref, f32[1,1024]{1,0:T(1,128)} %get-tuple-element.591.bias_ref, bf16[832,1024]{1,0:T(8,128)(2,1)} %get-tuple-element.369.refs_0_.refs_1_, ...), custom_call_target="tpu_custom_call" | custom-call | tf_op jit(solution)/shard_map/mlp/pallas_call | solution.py:133
  165.9 3.9 collective-permute-done.16
  169.8 2.4 add_convert_fusion.7
  177.8 20.5 %mlp.6 = (bf16[8,128,1024]{2,1,0:T(8,128)(2,1)}, bf16[8,128,1024]{2,1,0:T(8,128)(2,1)}, f32[1,1024]{1,0:T(1,128)}, f32[832,1024]{1,0:T(8,128)}, f32[832,1024]{1,0:T(8,128)}) custom-call(s32[9]{0:T(128)} %pad_add_fusion.1.order_ref, f32[1,1024]{1,0:T(1,128)} %get-tuple-element.589.bias_ref, bf16[832,1024]{1,0:T(8,128)(2,1)} %get-tuple-element.369.refs_0_.refs_1_, ...), custom_call_target="tpu_custom_call" | custom-call | tf_op jit(solution)/shard_map/mlp/pallas_call | solution.py:133
  198.3 2.2 collective-permute-done.20
  201.3 3.2 fusion.6
  206.8 21.0 %mlp.7 = (bf16[8,128,1024]{2,1,0:T(8,128)(2,1)}, bf16[8,128,1024]{2,1,0:T(8,128)(2,1)}, f32[1,1024]{1,0:T(1,128)}, f32[832,1024]{1,0:T(8,128)}, bf16[832,1024]{1,0:T(8,128)(2,1)}) custom-call(s32[9]{0:T(128)} %pad_add_fusion.1.order_ref, f32[1,1024]{1,0:T(1,128)} %get-tuple-element.588.bias_ref, f32[1,1024]{1,0:T(1,128)} %get-tuple-element.582.refs_0_, ...), custom_call_target="tpu_custom_call" | custom-call | tf_op jit(solution)/shard_map/mlp/pallas_call | solution.py:133
  232.8 2.6 collective-permute-done.23
  240.0 2.1 collective-permute-start.26
  242.9 11.0 %attention_out_back.1 = (f32[832,1024]{1,0:T(8,128)}, bf16[832,256]{1,0:T(8,128)(2,1)}, bf16[832,256]{1,0:T(8,128)(2,1)}, bf16[832,256]{1,0:T(8,128)(2,1)}, bf16...) custom-call(s32[9]{0:T(128)} %pad_add_fusion.1.order_ref, ...), custom_call_target="tpu_custom_call" | custom-call | tf_op jit(solution)/shard_map/attention_out_back/pallas_call | solution.py:133
  253.9 18.1 %attention_back.2 = (bf16[8,128,1024]{2,1,0:T(8,128)(2,1)}, bf16[8,128,1024]{2,1,0:T(8,128)(2,1)}, bf16[832,768]{1,0:T(8,128)(2,1)}, bf16[832,768]{1,0:T(8,128)(2,1)}, f32[2,1,768]{2,1,0:T(1,128)}) custom-call(s32[9]{0:T(128)} %pad_add_fusion.1.order_ref, bf16[832,1024]{1,0:T(8,128)(2,1)} %add_convert_fusion.normed_ref, ...), custom_call_target="tpu_custom_call" | custom-call | tf_op jit(solution)/shard_map/attention_back/pallas_call | solution.py:133
  274.8 2.4 fusion.4
  277.3 2.3 fusion.5
  279.6 2.4 add_convert_fusion.3
  283.5 2.1 collective-permute-start.30
  285.6 18.0 %attention_back.3 = (bf16[8,128,1024]{2,1,0:T(8,128)(2,1)}, bf16[8,128,1024]{2,1,0:T(8,128)(2,1)}, bf16[832,768]{1,0:T(8,128)(2,1)}, bf16[832,768]{1,0:T(8,128)(2,1)}, f32[2,1,768]{2,1,0:T(1,128)}) custom-call(s32[9]{0:T(128)} %pad_add_fusion.1.order_ref, bf16[832,1024]{1,0:T(8,128)(2,1)} %add_convert_fusion.normed_ref, ...), custom_call_target="tpu_custom_call" | custom-call | tf_op jit(solution)/shard_map/attention_back/pallas_call | solution.py:133
  303.6 3.9 collective-permute-done.32
  308.8 1.9 fusion.20
  317.8 1.8 collective-permute-start.35
  322.2 16.0 %input_back.1 = (f32[832,1024]{1,0:T(8,128)}, f32[2,1,1024]{2,1,0:T(1,128)}) custom-call(s32[9]{0:T(128)} %pad_add_fusion.1.order_ref, f32[832,1024]{1,0:T(8,128)} %bitcast.232, f32[832,1024]{1,0:T(8,128)} %get-tuple-element.494.after_ref, f32[1,1024]{1,0:T(1,128)} %get-tuple-element.581.gain_ref, bf16[832,768]{1,0:T(8,128)(2,1)} %get-tuple-element.495.refs_0_, ...), custom_call_target="tpu_custom_call" | custom-call | tf_op jit(solution)/shard_map/input_back/pallas_call | solution.py:133
  339.6 4.2 %collective-permute-done.34 = bf16[128,1024]{1,0:T(8,128)(2,1)} collective-permute-done((bf16[128,1024]{1,0:T(8,128)(2,1)S(1)}, bf16[128,1024]{1,0:T(8,128)(2,1)}, u32[]{:S(2)}, u32[]{:S(2)}) %collective-permute-start.34) | collective-permute-done | bytes 262176 | tf_op jit(solution)/shard_map/ppermute | solution.py:19
  343.8 2.9 fusion.3
  355.8 1.9 reshape.425
  357.7 6.4 %collective-permute-done.38 = bf16[2,128,1024]{2,1,0:T(8,128)(2,1)} collective-permute-done((bf16[2,128,1024]{2,1,0:T(8,128)(2,1)}, bf16[2,128,1024]{2,1,0:T(8,128)(2,1)}, u32[]{:S(2)}, u32[]{:S(2)}) %collective-permute-start.38) | collective-permute-done | bytes 524320 | tf_op jit(solution)/shard_map/ppermute | solution.py:19
  365.6 2.9 collective-permute-start.41
  373.6 6.0 %collective-permute-done.41 = bf16[128,1024]{1,0:T(8,128)(2,1)S(1)} collective-permute-done((bf16[128,1024]{1,0:T(8,128)(2,1)S(1)}, bf16[128,1024]{1,0:T(8,128)(2,1)S(1)}, u32[]{:S(2)}, u32[]{:S(2)}) %collective-permute-start.41) | collective-permute-done | bytes 262176 | tf_op jit(solution)/shard_map/ppermute | solution.py:19
  381.2 2.0 add_convert_fusion.9
  385.1 3.4 collective-permute-done.43
  388.6 2.0 collective-permute-start.48
  390.7 3.9 finish_mlp.1
  397.0 2.6 finish_attention.1
  (238 shorter events, 85.8 us)
Async XLA Ops:
  7.2 99.6 %all-gather.5.cloned.1.call-start = ((), (), s32[]{:S(2)}) async-start(), calls=%async_computation | async-start | bytes 4718592 | tf_op jit(solution)/shard_map/all_gather | solution.py:964
  9.8 14.5 %collective-permute-start = (bf16[1,144,768]{2,1,0:T(8,128)(2,1)}, bf16[1,144,768]{2,1,0:T(8,128)(2,1)S(1)}, u32[]{:S(2)}, u32[]{:S(2)}) collective-permute-start(bf16[1,144,768]{2,1,0:T(8,128)(2,1)} %bitcast.265), channel_id=1, source_target_pairs={{0,4},{1,5},{2,6},{3,7},{4,0},{5,1},{6,2},{7,3},{8,12},{9,13},{10,... | collective-permute-start | bytes 663560 | tf_op jit(solution)/shard_map/ppermute | solution.py:19
  24.3 141.0 %all-gather.7.cloned.1.call-start = ((), (), s32[]{:S(2)}) async-start(), calls=%async_computation.1 | async-start | bytes 2359296 | tf_op jit(solution)/shard_map/all_gather | solution.py:965
  24.5 11.4 %collective-permute-start.1 = (bf16[2,144,768]{2,1,0:T(8,128)(2,1)S(1)}, bf16[2,144,768]{2,1,0:T(8,128)(2,1)S(1)}, u32[]{:S(2)}, u32[]{:S(2)}) collective-permute-start(bf16[2,144,768]{2,1,0:T(8,128)(2,1)S(1)} %pad_maximum_fusion.5), channel_id=1, source_target_pairs={{0,2},{1,3},{2,0},{3,1},{4,6},{5,7},{6,4},{7,5},{8,10},{9,11},{10,... | collective-permute-start | bytes 1327112 | tf_op jit(solution)/shard_map/ppermute | solution.py:19
  36.7 24.4 %collective-permute-start.2 = (bf16[4,144,768]{2,1,0:T(8,128)(2,1)}, bf16[4,144,768]{2,1,0:T(8,128)(2,1)}, u32[]{:S(2)}, u32[]{:S(2)}) collective-permute-start(bf16[4,144,768]{2,1,0:T(8,128)(2,1)} %constant_dynamic-update-slice_fusion.refs_0_.refs_4_), channel_id=1, source_target_pairs={{0,1},{1,0},{2,3},{3,2},{4,5},{5,4},{6,7},{7,6},{8,9},{9,8},{10,11... | collective-permute-start | bytes 2654216 | tf_op jit(solution)/shard_map/ppermute | solution.py:19
  38.1 23.0 %collective-permute-start.3 = (bf16[4,144,768]{2,1,0:T(8,128)(2,1)}, bf16[4,144,768]{2,1,0:T(8,128)(2,1)}, u32[]{:S(2)}, u32[]{:S(2)}) collective-permute-start(bf16[4,144,768]{2,1,0:T(8,128)(2,1)} %constant_dynamic-update-slice_fusion.refs_0_.refs_4_), channel_id=1, source_target_pairs={{0,8},{8,0},{16,24},{24,16},{1,9},{9,1},{17,25},{25,17},{2,10},{10... | collective-permute-start | bytes 2654216 | tf_op jit(solution)/shard_map/ppermute | solution.py:19
  39.7 42.3 %collective-permute-start.6 = (bf16[4,144,768]{2,1,0:T(8,128)(2,1)}, bf16[4,144,768]{2,1,0:T(8,128)(2,1)}, u32[]{:S(2)}, u32[]{:S(2)}) collective-permute-start(bf16[4,144,768]{2,1,0:T(8,128)(2,1)} %constant_dynamic-update-slice_fusion.refs_0_.refs_4_), channel_id=1, source_target_pairs={{0,16},{8,24},{16,0},{24,8},{1,17},{9,25},{17,1},{25,9},{2,18},{10... | collective-permute-start | bytes 2654216 | tf_op jit(solution)/shard_map/ppermute | solution.py:19
  41.3 19.0 %collective-permute-start.4 = (bf16[1,128,512]{2,1,0:T(8,128)(2,1)S(1)}, bf16[1,128,512]{2,1,0:T(8,128)(2,1)S(1)}, u32[]{:S(2)}, u32[]{:S(2)}) collective-permute-start(bf16[1,128,512]{2,1,0:T(8,128)(2,1)S(1)} %pad_maximum_fusion.7), channel_id=1, source_target_pairs={{0,4},{1,5},{2,6},{3,7},{4,0},{5,1},{6,2},{7,3},{8,12},{9,13},{10,... | collective-permute-start | bytes 393224 | tf_op jit(solution)/shard_map/ppermute | solution.py:19
  61.1 10.4 %collective-permute-start.5 = (bf16[4,144,768]{2,1,0:T(8,128)(2,1)}, bf16[4,144,768]{2,1,0:T(8,128)(2,1)}, u32[]{:S(2)}, u32[]{:S(2)}) collective-permute-start(bf16[4,144,768]{2,1,0:T(8,128)(2,1)} %collective-permute-done.2.refs_1_.refs_5_), channel_id=1, source_target_pairs={{0,8},{8,0},{16,24},{24,16},{1,9},{9,1},{17,25},{25,17},{2,10},{10... | collective-permute-start | bytes 2654216 | tf_op jit(solution)/shard_map/ppermute | solution.py:19
  61.1 29.8 %collective-permute-start.7 = (bf16[4,144,768]{2,1,0:T(8,128)(2,1)}, bf16[4,144,768]{2,1,0:T(8,128)(2,1)}, u32[]{:S(2)}, u32[]{:S(2)}) collective-permute-start(bf16[4,144,768]{2,1,0:T(8,128)(2,1)} %collective-permute-done.2.refs_1_.refs_5_), channel_id=1, source_target_pairs={{0,16},{8,24},{16,0},{24,8},{1,17},{9,25},{17,1},{25,9},{2,18},{10... | collective-permute-start | bytes 2654216 | tf_op jit(solution)/shard_map/ppermute | solution.py:19
  66.1 24.8 %collective-permute-start.8 = (bf16[2,128,512]{2,1,0:T(8,128)(2,1)S(1)}, bf16[2,128,512]{2,1,0:T(8,128)(2,1)S(1)}, u32[]{:S(2)}, u32[]{:S(2)}) collective-permute-start(bf16[2,128,512]{2,1,0:T(8,128)(2,1)S(1)} %pad_maximum_fusion.6), channel_id=1, source_target_pairs={{0,2},{1,3},{2,0},{3,1},{4,6},{5,7},{6,4},{7,5},{8,10},{9,11},{10,... | collective-permute-start | bytes 786440 | tf_op jit(solution)/shard_map/ppermute | solution.py:19
  90.9 4.4 %collective-permute-start.10 = (bf16[4,144,768]{2,1,0:T(8,128)(2,1)}, bf16[4,144,768]{2,1,0:T(8,128)(2,1)S(1)}, u32[]{:S(2)}, u32[]{:S(2)}) collective-permute-start(bf16[4,144,768]{2,1,0:T(8,128)(2,1)} %collective-permute-done.7.refs_1_.refs_9_), channel_id=1, source_target_pairs={{0,8},{8,0},{16,24},{24,16},{1,9},{9,1},{17,25},{25,17},{2,10},{10... | collective-permute-start | bytes 2654216 | tf_op jit(solution)/shard_map/ppermute | solution.py:19
  90.9 4.4 %collective-permute-start.9 = (bf16[4,144,768]{2,1,0:T(8,128)(2,1)}, bf16[4,144,768]{2,1,0:T(8,128)(2,1)}, u32[]{:S(2)}, u32[]{:S(2)}) collective-permute-start(bf16[4,144,768]{2,1,0:T(8,128)(2,1)} %collective-permute-done.6.refs_0_.refs_8_), channel_id=1, source_target_pairs={{0,8},{8,0},{16,24},{24,16},{1,9},{9,1},{17,25},{25,17},{2,10},{10... | collective-permute-start | bytes 2654216 | tf_op jit(solution)/shard_map/ppermute | solution.py:19
  91.4 15.4 %collective-permute-start.11 = (bf16[4,128,512]{2,1,0:T(8,128)(2,1)S(1)}, bf16[4,128,512]{2,1,0:T(8,128)(2,1)}, u32[]{:S(2)}, u32[]{:S(2)}) collective-permute-start(bf16[4,128,512]{2,1,0:T(8,128)(2,1)S(1)} %pad_maximum_fusion.4), channel_id=1, source_target_pairs={{0,1},{1,0},{2,3},{3,2},{4,5},{5,4},{6,7},{7,6},{8,9},{9,8},{10,11... | collective-permute-start | bytes 1572872 | tf_op jit(solution)/shard_map/ppermute | solution.py:19
  110.7 14.9 %collective-permute-start.13 = (bf16[8,128,2048]{2,1,0:T(8,128)(2,1)}, bf16[8,128,2048]{2,1,0:T(8,128)(2,1)}, u32[]{:S(2)}, u32[]{:S(2)}) collective-permute-start(bf16[8,128,2048]{2,1,0:T(8,128)(2,1)} %bitcast.238), channel_id=1, source_target_pairs={{0,8},{8,0},{16,24},{24,16},{1,9},{9,1},{17,25},{25,17},{2,10},{10... | collective-permute-start | bytes 12582920 | tf_op jit(solution)/shard_map/ppermute | solution.py:19
  114.2 51.1 %collective-permute-start.14 = (bf16[8,128,1024]{2,1,0:T(8,128)(2,1)}, bf16[8,128,1024]{2,1,0:T(8,128)(2,1)}, u32[]{:S(2)}, u32[]{:S(2)}) collective-permute-start(bf16[8,128,1024]{2,1,0:T(8,128)(2,1)} %slice.465), channel_id=1, source_target_pairs={{0,16},{8,24},{16,0},{24,8},{1,17},{9,25},{17,1},{25,9},{2,18},{10... | collective-permute-start | bytes 6291464 | tf_op jit(solution)/shard_map/ppermute | solution.py:19
  165.3 4.4 %collective-permute-start.16 = (bf16[8,128,1024]{2,1,0:T(8,128)(2,1)}, bf16[8,128,1024]{2,1,0:T(8,128)(2,1)S(1)}, u32[]{:S(2)}, u32[]{:S(2)}) collective-permute-start(bf16[8,128,1024]{2,1,0:T(8,128)(2,1)} %get-tuple-element.387), channel_id=1, source_target_pairs={{0,8},{8,0},{16,24},{24,16},{1,9},{9,1},{17,25},{25,17},{2,10},{10... | collective-permute-start | bytes 6291464 | tf_op jit(solution)/shard_map/ppermute | solution.py:19
  165.4 7.4 %collective-permute-start.15 = (bf16[8,128,1024]{2,1,0:T(8,128)(2,1)}, bf16[8,128,1024]{2,1,0:T(8,128)(2,1)S(1)}, u32[]{:S(2)}, u32[]{:S(2)}) collective-permute-start(bf16[8,128,1024]{2,1,0:T(8,128)(2,1)} %get-tuple-element.385), channel_id=1, source_target_pairs={{0,8},{8,0},{16,24},{24,16},{1,9},{9,1},{17,25},{25,17},{2,10},{10... | collective-permute-start | bytes 6291464 | tf_op jit(solution)/shard_map/ppermute | solution.py:19
  174.5 26.9 %collective-permute-start.17 = (bf16[8,128,1024]{2,1,0:T(8,128)(2,1)}, bf16[8,128,1024]{2,1,0:T(8,128)(2,1)S(1)}, u32[]{:S(2)}, u32[]{:S(2)}) collective-permute-start(bf16[8,128,1024]{2,1,0:T(8,128)(2,1)} %collective-permute-done.14.refs_2_), channel_id=1, source_target_pairs={{0,8},{8,0},{16,24},{24,16},{1,9},{9,1},{17,25},{25,17},{2,10},{10... | collective-permute-start | bytes 6291464 | tf_op jit(solution)/shard_map/ppermute | solution.py:19
  174.6 26.7 %collective-permute-start.18 = (bf16[8,128,1024]{2,1,0:T(8,128)(2,1)S(1)}, bf16[8,128,1024]{2,1,0:T(8,128)(2,1)}, u32[]{:S(2)}, u32[]{:S(2)}) collective-permute-start(bf16[8,128,1024]{2,1,0:T(8,128)(2,1)S(1)} %bitcast.245), channel_id=1, source_target_pairs={{0,8},{8,0},{16,24},{24,16},{1,9},{9,1},{17,25},{25,17},{2,10},{10... | collective-permute-start | bytes 6291464 | tf_op jit(solution)/shard_map/ppermute | solution.py:19
  175.0 25.5 %collective-permute-start.20 = (bf16[2,2,128,1024]{3,2,1,0:T(8,128)(2,1)}, bf16[2,2,128,1024]{3,2,1,0:T(8,128)(2,1)}, u32[]{:S(2)}, u32[]{:S(2)}) collective-permute-start(bf16[2,2,128,1024]{3,2,1,0:T(8,128)(2,1)} %fusion), channel_id=1, source_target_pairs={{0,2},{1,3},{2,0},{3,1},{4,6},{5,7},{6,4},{7,5},{8,10},{9,11},{10,... | collective-permute-start | bytes 3145736 | tf_op jit(solution)/shard_map/ppermute | solution.py:19
  176.3 25.0 %collective-permute-start.19 = (bf16[2,2,128,1024]{3,2,1,0:T(8,128)(2,1)S(1)}, bf16[2,2,128,1024]{3,2,1,0:T(8,128)(2,1)}, u32[]{:S(2)}, u32[]{:S(2)}) collective-permute-start(bf16[2,2,128,1024]{3,2,1,0:T(8,128)(2,1)S(1)} %bitcast.264), channel_id=1, source_target_pairs={{0,1},{1,0},{2,3},{3,2},{4,5},{5,4},{6,7},{7,6},{8,9},{9,8},{10,11... | collective-permute-start | bytes 3145736 | tf_op jit(solution)/shard_map/ppermute | solution.py:19
  204.6 23.3 %collective-permute-start.22 = (bf16[2,128,1024]{2,1,0:T(8,128)(2,1)S(1)}, bf16[2,128,1024]{2,1,0:T(8,128)(2,1)S(1)}, u32[]{:S(2)}, u32[]{:S(2)}) collective-permute-start(bf16[2,128,1024]{2,1,0:T(8,128)(2,1)S(1)} %get-tuple-element.423), channel_id=1, source_target_pairs={{0,1},{1,0},{2,3},{3,2},{4,5},{5,4},{6,7},{7,6},{8,9},{9,8},{10,11... | collective-permute-start | bytes 1572872 | tf_op jit(solution)/shard_map/ppermute | solution.py:19
  206.1 21.8 %collective-permute-start.21 = (bf16[2,128,1024]{2,1,0:T(8,128)(2,1)S(1)}, bf16[2,128,1024]{2,1,0:T(8,128)(2,1)S(1)}, u32[]{:S(2)}, u32[]{:S(2)}) collective-permute-start(bf16[2,128,1024]{2,1,0:T(8,128)(2,1)S(1)} %get-tuple-element.422), channel_id=1, source_target_pairs={{0,2},{1,3},{2,0},{3,1},{4,6},{5,7},{6,4},{7,5},{8,10},{9,11},{10,... | collective-permute-start | bytes 1572872 | tf_op jit(solution)/shard_map/ppermute | solution.py:19
  228.0 7.4 %collective-permute-start.23 = (bf16[8,128,1024]{2,1,0:T(8,128)(2,1)}, bf16[8,128,1024]{2,1,0:T(8,128)(2,1)S(1)}, u32[]{:S(2)}, u32[]{:S(2)}) collective-permute-start(bf16[8,128,1024]{2,1,0:T(8,128)(2,1)} %get-tuple-element.426), channel_id=1, source_target_pairs={{0,8},{8,0},{16,24},{24,16},{1,9},{9,1},{17,25},{25,17},{2,10},{10... | collective-permute-start | bytes 6291464 | tf_op jit(solution)/shard_map/ppermute | solution.py:19
  238.1 36.8 %collective-permute-start.28 = (bf16[2,2,128,1024]{3,2,1,0:T(8,128)(2,1)}, bf16[2,2,128,1024]{3,2,1,0:T(8,128)(2,1)}, u32[]{:S(2)}, u32[]{:S(2)}) collective-permute-start(bf16[2,2,128,1024]{3,2,1,0:T(8,128)(2,1)} %fusion.1), channel_id=1, source_target_pairs={{0,2},{1,3},{2,0},{3,1},{4,6},{5,7},{6,4},{7,5},{8,10},{9,11},{10,... | collective-permute-start | bytes 3145736 | tf_op jit(solution)/shard_map/ppermute | solution.py:19
  239.4 35.4 %collective-permute-start.27 = (bf16[2,2,128,1024]{3,2,1,0:T(8,128)(2,1)S(1)}, bf16[2,2,128,1024]{3,2,1,0:T(8,128)(2,1)}, u32[]{:S(2)}, u32[]{:S(2)}) collective-permute-start(bf16[2,2,128,1024]{3,2,1,0:T(8,128)(2,1)S(1)} %bitcast.263), channel_id=1, source_target_pairs={{0,1},{1,0},{2,3},{3,2},{4,5},{5,4},{6,7},{7,6},{8,9},{9,8},{10,11... | collective-permute-start | bytes 3145736 | tf_op jit(solution)/shard_map/ppermute | solution.py:19
  240.0 32.0 %collective-permute-start.26 = (bf16[128,1024]{1,0:T(8,128)(2,1)S(1)}, bf16[128,1024]{1,0:T(8,128)(2,1)S(1)}, u32[]{:S(2)}, u32[]{:S(2)}) collective-permute-start(bf16[128,1024]{1,0:T(8,128)(2,1)S(1)} %fusion.22), channel_id=1, source_target_pairs={{0,4},{1,5},{2,6},{3,7},{4,0},{5,1},{6,2},{7,3},{8,12},{9,13},{10,... | collective-permute-start | bytes 786440 | tf_op jit(solution)/shard_map/ppermute | solution.py:19
  242.1 31.5 %collective-permute-start.25 = (bf16[128,1024]{1,0:T(8,128)(2,1)S(1)}, bf16[128,1024]{1,0:T(8,128)(2,1)}, u32[]{:S(2)}, u32[]{:S(2)}) collective-permute-start(bf16[128,1024]{1,0:T(8,128)(2,1)S(1)} %fusion.21), channel_id=1, source_target_pairs={{0,4},{1,5},{2,6},{3,7},{4,0},{5,1},{6,2},{7,3},{8,12},{9,13},{10,... | collective-permute-start | bytes 786440 | tf_op jit(solution)/shard_map/ppermute | solution.py:19
  274.8 4.7 %collective-permute-start.29 = (bf16[8,128,1024]{2,1,0:T(8,128)(2,1)}, bf16[8,128,1024]{2,1,0:T(8,128)(2,1)S(1)}, u32[]{:S(2)}, u32[]{:S(2)}) collective-permute-start(bf16[8,128,1024]{2,1,0:T(8,128)(2,1)} %get-tuple-element.460), channel_id=1, source_target_pairs={{0,8},{8,0},{16,24},{24,16},{1,9},{9,1},{17,25},{25,17},{2,10},{10... | collective-permute-start | bytes 6291464 | tf_op jit(solution)/shard_map/ppermute | solution.py:19
  281.9 25.6 %collective-permute-start.32 = (bf16[4,128,1024]{2,1,0:T(8,128)(2,1)}, bf16[4,128,1024]{2,1,0:T(8,128)(2,1)S(1)}, u32[]{:S(2)}, u32[]{:S(2)}) collective-permute-start(bf16[4,128,1024]{2,1,0:T(8,128)(2,1)} %get-tuple-element.480), channel_id=1, source_target_pairs={{0,16},{8,24},{16,0},{24,8},{1,17},{9,25},{17,1},{25,9},{2,18},{10... | collective-permute-start | bytes 3145736 | tf_op jit(solution)/shard_map/ppermute | solution.py:19
  282.6 21.0 %collective-permute-start.31 = (bf16[2,128,1024]{2,1,0:T(8,128)(2,1)}, bf16[2,128,1024]{2,1,0:T(8,128)(2,1)S(1)}, u32[]{:S(2)}, u32[]{:S(2)}) collective-permute-start(bf16[2,128,1024]{2,1,0:T(8,128)(2,1)} %fusion.5), channel_id=1, source_target_pairs={{0,1},{1,0},{2,3},{3,2},{4,5},{5,4},{6,7},{7,6},{8,9},{9,8},{10,11... | collective-permute-start | bytes 1572872 | tf_op jit(solution)/shard_map/ppermute | solution.py:19
  283.5 20.1 %collective-permute-start.30 = (bf16[2,128,1024]{2,1,0:T(8,128)(2,1)}, bf16[2,128,1024]{2,1,0:T(8,128)(2,1)}, u32[]{:S(2)}, u32[]{:S(2)}) collective-permute-start(bf16[2,128,1024]{2,1,0:T(8,128)(2,1)} %fusion.4), channel_id=1, source_target_pairs={{0,2},{1,3},{2,0},{3,1},{4,6},{5,7},{6,4},{7,5},{8,10},{9,11},{10,... | collective-permute-start | bytes 1572872 | tf_op jit(solution)/shard_map/ppermute | solution.py:19
  313.6 30.1 %collective-permute-start.37 = (bf16[4,128,1024]{2,1,0:T(8,128)(2,1)}, bf16[4,128,1024]{2,1,0:T(8,128)(2,1)S(1)}, u32[]{:S(2)}, u32[]{:S(2)}) collective-permute-start(bf16[4,128,1024]{2,1,0:T(8,128)(2,1)} %get-tuple-element.503), channel_id=1, source_target_pairs={{0,16},{8,24},{16,0},{24,8},{1,17},{9,25},{17,1},{25,9},{2,18},{10... | collective-permute-start | bytes 3145736 | tf_op jit(solution)/shard_map/ppermute | solution.py:19
  314.3 29.5 %collective-permute-start.36 = (bf16[2,2,128,1024]{3,2,1,0:T(8,128)(2,1)}, bf16[2,2,128,1024]{3,2,1,0:T(8,128)(2,1)}, u32[]{:S(2)}, u32[]{:S(2)}) collective-permute-start(bf16[2,2,128,1024]{3,2,1,0:T(8,128)(2,1)} %bitcast.56), channel_id=1, source_target_pairs={{0,1},{1,0},{2,3},{3,2},{4,5},{5,4},{6,7},{7,6},{8,9},{9,8},{10,11... | collective-permute-start | bytes 3145736 | tf_op jit(solution)/shard_map/ppermute | solution.py:19
  317.8 21.8 %collective-permute-start.35 = (bf16[128,1024]{1,0:T(8,128)(2,1)}, bf16[128,1024]{1,0:T(8,128)(2,1)}, u32[]{:S(2)}, u32[]{:S(2)}) collective-permute-start(bf16[128,1024]{1,0:T(8,128)(2,1)} %fusion.20), channel_id=1, source_target_pairs={{0,4},{1,5},{2,6},{3,7},{4,0},{5,1},{6,2},{7,3},{8,12},{9,13},{10,... | collective-permute-start | bytes 786440 | tf_op jit(solution)/shard_map/ppermute | solution.py:19
  319.6 24.1 %collective-permute-start.34 = (bf16[128,1024]{1,0:T(8,128)(2,1)S(1)}, bf16[128,1024]{1,0:T(8,128)(2,1)}, u32[]{:S(2)}, u32[]{:S(2)}) collective-permute-start(bf16[128,1024]{1,0:T(8,128)(2,1)S(1)} %fusion.19), channel_id=1, source_target_pairs={{0,4},{1,5},{2,6},{3,7},{4,0},{5,1},{6,2},{7,3},{8,12},{9,13},{10,... | collective-permute-start | bytes 786440 | tf_op jit(solution)/shard_map/ppermute | solution.py:19
  350.4 7.3 %collective-permute-start.39 = (f32[2,2,16,128]{3,2,1,0:T(8,128)S(1)}, f32[2,2,16,128]{3,2,1,0:T(8,128)S(1)}, u32[]{:S(2)}, u32[]{:S(2)}) collective-permute-start(f32[2,2,16,128]{3,2,1,0:T(8,128)S(1)} %bitcast.267), channel_id=1, source_target_pairs={{0,1},{1,0},{2,3},{3,2},{4,5},{5,4},{6,7},{7,6},{8,9},{9,8},{10,11... | collective-permute-start | bytes 98312 | tf_op jit(solution)/shard_map/ppermute | solution.py:19
  351.5 12.5 %collective-permute-start.38 = (bf16[2,128,1024]{2,1,0:T(8,128)(2,1)}, bf16[2,128,1024]{2,1,0:T(8,128)(2,1)}, u32[]{:S(2)}, u32[]{:S(2)}) collective-permute-start(bf16[2,128,1024]{2,1,0:T(8,128)(2,1)} %fusion.3), channel_id=1, source_target_pairs={{0,2},{1,3},{2,0},{3,1},{4,6},{5,7},{6,4},{7,5},{8,10},{9,11},{10,... | collective-permute-start | bytes 1572872 | tf_op jit(solution)/shard_map/ppermute | solution.py:19
  354.1 27.1 %collective-permute-start.42 = (bf16[2,2,128,1024]{3,2,1,0:T(8,128)(2,1)}, bf16[2,2,128,1024]{3,2,1,0:T(8,128)(2,1)}, u32[]{:S(2)}, u32[]{:S(2)}) collective-permute-start(bf16[2,2,128,1024]{3,2,1,0:T(8,128)(2,1)} %pad_maximum_fusion.2), channel_id=1, source_target_pairs={{0,16},{8,24},{16,0},{24,8},{1,17},{9,25},{17,1},{25,9},{2,18},{10... | collective-permute-start | bytes 3145736 | tf_op jit(solution)/shard_map/ppermute | solution.py:19
  365.6 14.1 %collective-permute-start.41 = (bf16[128,1024]{1,0:T(8,128)(2,1)S(1)}, bf16[128,1024]{1,0:T(8,128)(2,1)S(1)}, u32[]{:S(2)}, u32[]{:S(2)}) collective-permute-start(bf16[128,1024]{1,0:T(8,128)(2,1)S(1)} %fusion.10), channel_id=1, source_target_pairs={{0,4},{1,5},{2,6},{3,7},{4,0},{5,1},{6,2},{7,3},{8,12},{9,13},{10,... | collective-permute-start | bytes 786440 | tf_op jit(solution)/shard_map/ppermute | solution.py:19
  368.5 5.1 %collective-permute-start.40 = (f32[2,16,128]{2,1,0:T(8,128)S(1)}, f32[2,16,128]{2,1,0:T(8,128)S(1)}, u32[]{:S(2)}, u32[]{:S(2)}) collective-permute-start(f32[2,16,128]{2,1,0:T(8,128)S(1)} %slice_add_fusion), channel_id=1, source_target_pairs={{0,2},{1,3},{2,0},{3,1},{4,6},{5,7},{6,4},{7,5},{8,10},{9,11},{10,... | collective-permute-start | bytes 49160 | tf_op jit(solution)/shard_map/ppermute | solution.py:19
  383.3 5.2 %collective-permute-start.44 = (bf16[2,2,128,1024]{3,2,1,0:T(8,128)(2,1)S(1)}, bf16[2,2,128,1024]{3,2,1,0:T(8,128)(2,1)S(1)}, u32[]{:S(2)}, u32[]{:S(2)}) collective-permute-start(bf16[2,2,128,1024]{3,2,1,0:T(8,128)(2,1)S(1)} %pad_maximum_fusion.3.refs_0_), channel_id=1, source_target_pairs={{0,8},{8,0},{16,24},{24,16},{1,9},{9,1},{17,25},{25,17},{2,10},{10... | collective-permute-start | bytes 3145736 | tf_op jit(solution)/shard_map/ppermute | solution.py:19
  383.4 11.2 %collective-permute-start.45 = (bf16[128,1024]{1,0:T(8,128)(2,1)S(1)}, bf16[128,1024]{1,0:T(8,128)(2,1)S(1)}, u32[]{:S(2)}, u32[]{:S(2)}) collective-permute-start(bf16[128,1024]{1,0:T(8,128)(2,1)S(1)} %fusion.9.refs_0_), channel_id=1, source_target_pairs={{0,8},{8,0},{16,24},{24,16},{1,9},{9,1},{17,25},{25,17},{2,10},{10... | collective-permute-start | bytes 786440 | tf_op jit(solution)/shard_map/ppermute | solution.py:19
  383.9 10.7 %collective-permute-start.46 = (bf16[128,1024]{1,0:T(8,128)(2,1)S(1)}, bf16[128,1024]{1,0:T(8,128)(2,1)S(1)}, u32[]{:S(2)}, u32[]{:S(2)}) collective-permute-start(bf16[128,1024]{1,0:T(8,128)(2,1)S(1)} %fusion.9.refs_0_), channel_id=1, source_target_pairs={{0,16},{8,24},{16,0},{24,8},{1,17},{9,25},{17,1},{25,9},{2,18},{10... | collective-permute-start | bytes 786440 | tf_op jit(solution)/shard_map/ppermute | solution.py:19
  383.9 4.6 %collective-permute-start.43 = (f32[16,128]{1,0:T(8,128)S(1)}, f32[16,128]{1,0:T(8,128)S(1)}, u32[]{:S(2)}, u32[]{:S(2)}) collective-permute-start(f32[16,128]{1,0:T(8,128)S(1)} %fusion.33), channel_id=1, source_target_pairs={{0,4},{1,5},{2,6},{3,7},{4,0},{5,1},{6,2},{7,3},{8,12},{9,13},{10,... | collective-permute-start | bytes 24584 | tf_op jit(solution)/shard_map/ppermute | solution.py:19
  388.5 6.1 %collective-permute-start.47 = (f32[16,128]{1,0:T(8,128)S(1)}, f32[16,128]{1,0:T(8,128)S(1)}, u32[]{:S(2)}, u32[]{:S(2)}) collective-permute-start(f32[16,128]{1,0:T(8,128)S(1)} %fusion.31), channel_id=1, source_target_pairs={{0,8},{8,0},{16,24},{24,16},{1,9},{9,1},{17,25},{25,17},{2,10},{10... | collective-permute-start | bytes 24584 | tf_op jit(solution)/shard_map/ppermute | solution.py:19
  388.6 6.1 %collective-permute-start.48 = (f32[16,128]{1,0:T(8,128)S(1)}, f32[16,128]{1,0:T(8,128)S(1)}, u32[]{:S(2)}, u32[]{:S(2)}) collective-permute-start(f32[16,128]{1,0:T(8,128)S(1)} %fusion.31), channel_id=1, source_target_pairs={{0,16},{8,24},{16,0},{24,8},{1,17},{9,25},{17,1},{25,9},{2,18},{10... | collective-permute-start | bytes 24584 | tf_op jit(solution)/shard_map/ppermute | solution.py:19
  (49 other events, 247.3 us)
Sparse Core Ops, SparseCore 0:
  24.4 81.8 all-gather.4
  111.0 48.9 all-gather.6

commit v7 on v6

--- a/solution.py
+++ b/solution.py
@@ -1124,10 +1124,11 @@
     across_part = jnp.stack([two_up.rest().piece(), two_down.rest().piece()])
     pair = seq.at(jnp.stack([own_part, across_part]))
     cross = Sent(x_swap(pair))
-    grad_tokens = seq.land(compact(seq.at(tokens_grad)), red_w, sums)
+    seq.land((), red_w, sums)
     red_w.launch()
     sums.launch()
-    block_out = seq.land(compact(seq.at(block)), sums, red_w)
+    block, tokens_grad = seq.at((block, tokens_grad))
+    block_out, grad_tokens = seq.land((compact(block), compact(tokens_grad)), sums, red_w)
     w_spread = Spread(seq, red_w.piece())
     sums.launch()
     seq.land((), cross)

time: 412 us -> 413 us (level)
  transfers between devices with their start and end apart: 53 -> 53, of which waited for: 23 -> 22; matrix products, arithmetic and copies ran while one was open for 13% -> 14% of each run, Pallas kernels for 45% -> 45%
where the time goes in v7:
time: 413 us; the launch traced here: 408 us
  Pallas kernels  191 us (46%)
  waiting for transfers between devices  73 us (18%)
  starting transfers between devices  49.9 us (12%)
  other arithmetic  49.2 us (12%)
  local copies, waits for them, and re-layouts  29.3 us (7%)
  between operations  15.1 us (4%)
    pallas_call x17, Pallas kernels, call(): pl.pallas_call(kernel, out_shape=[jax.ShapeDtypeStruct(shape, kind) for s...  191 us
    ppermute x51, waiting for transfers between devices, xor_swap(): return lax.ppermute(value, axis, [(i, i ^ mask) for i in range(size)])  72.9 us
    ppermute x51, starting transfers between devices, xor_swap(): return lax.ppermute(value, axis, [(i, i ^ mask) for i in range(size)])  49.9 us
    convert_element_type x17, other arithmetic, rounded_sum(): return sum((t.astype(full) for t in terms)).astype(kind)  31.2 us
  transfers between devices with their start and end apart: 53, of which 22 were waited for; matrix products, arithmetic and copies ran while one was open for 14% of the time, Pallas kernels for 45%

profile of v7, /device:TPU:0, one launch (start us, length us, event | category | flops | bytes accessed | tf_op | source)
XLA Modules:
  0.0 407.8 jit_solution(11499228429173286685)
XLA Ops:
  7.2 2.6 first_payload.1
  9.8 4.1 %collective-permute-start = (bf16[1,144,768]{2,1,0:T(8,128)(2,1)}, bf16[1,144,768]{2,1,0:T(8,128)(2,1)S(1)}, u32[]{:S(2)}, u32[]{:S(2)}) collective-permute-start(bf16[1,144,768]{2,1,0:T(8,128)(2,1)} %bitcast.265), channel_id=1, source_target_pairs={{0,4},{1,5},{2,6},{3,7},{4,0},{5,1},{6,2},{7,3},{8,12},{9,13},{10,... | collective-permute-start | bytes 663560 | tf_op jit(solution)/shard_map/ppermute | solution.py:19
  14.5 3.3 payloads.1
  17.8 6.5 %collective-permute-done = bf16[1,144,768]{2,1,0:T(8,128)(2,1)S(1)} collective-permute-done((bf16[1,144,768]{2,1,0:T(8,128)(2,1)}, bf16[1,144,768]{2,1,0:T(8,128)(2,1)S(1)}, u32[]{:S(2)}, u32[]{:S(2)}) %collective-permute-start) | collective-permute-done | bytes 221216 | tf_op jit(solution)/shard_map/ppermute | solution.py:19
  27.5 3.6 copy.32
  31.1 2.2 reshape.415
  41.3 6.6 %collective-permute-start.4 = (bf16[1,128,512]{2,1,0:T(8,128)(2,1)S(1)}, bf16[1,128,512]{2,1,0:T(8,128)(2,1)S(1)}, u32[]{:S(2)}, u32[]{:S(2)}) collective-permute-start(bf16[1,128,512]{2,1,0:T(8,128)(2,1)S(1)} %pad_maximum_fusion.7), channel_id=1, source_target_pairs={{0,4},{1,5},{2,6},{3,7},{4,0},{5,1},{6,2},{7,3},{8,12},{9,13},{10,... | collective-permute-start | bytes 393224 | tf_op jit(solution)/shard_map/ppermute | solution.py:19
  48.7 11.6 %collective-permute-done.4 = bf16[1,128,512]{2,1,0:T(8,128)(2,1)S(1)} collective-permute-done((bf16[1,128,512]{2,1,0:T(8,128)(2,1)S(1)}, bf16[1,128,512]{2,1,0:T(8,128)(2,1)S(1)}, u32[]{:S(2)}, u32[]{:S(2)}) %collective-permute-start.4) | collective-permute-done | bytes 131104 | tf_op jit(solution)/shard_map/ppermute | solution.py:19
  63.8 2.3 unpack_vectors.1
  71.5 10.5 %attention_forward.2 = (bf16[832,768]{1,0:T(8,128)(2,1)}, bf16[832,768]{1,0:T(8,128)(2,1)}, bf16[832,256]{1,0:T(8,128)(2,1)}, bf16[832,256]{1,0:T(8,128)(2,1)}, ...) custom-call(s32[9]{0:T(128)} %pad_add_fusion.1.order_ref, bf16[832,1024]{1,0:T(8,128)(2,1)} %add_convert_fusion.normed_ref, ...), custom_call_target="tpu_custom_call" | custom-call | tf_op jit(solution)/shard_map/attention_forward/pallas_call | solution.py:133
  82.0 8.9 %collective-permute-done.8 = bf16[2,128,512]{2,1,0:T(8,128)(2,1)S(1)} collective-permute-done((bf16[2,128,512]{2,1,0:T(8,128)(2,1)S(1)}, bf16[2,128,512]{2,1,0:T(8,128)(2,1)S(1)}, u32[]{:S(2)}, u32[]{:S(2)}) %collective-permute-start.8) | collective-permute-done | bytes 262176 | tf_op jit(solution)/shard_map/ppermute | solution.py:19
  96.3 10.5 %attention_forward.3 = (bf16[832,768]{1,0:T(8,128)(2,1)}, bf16[832,768]{1,0:T(8,128)(2,1)}, bf16[832,256]{1,0:T(8,128)(2,1)}, bf16[832,256]{1,0:T(8,128)(2,1)}, ...) custom-call(s32[9]{0:T(128)} %pad_add_fusion.1.order_ref, bf16[832,1024]{1,0:T(8,128)(2,1)} %add_convert_fusion.normed_ref, ...), custom_call_target="tpu_custom_call" | custom-call | tf_op jit(solution)/shard_map/attention_forward/pallas_call | solution.py:133
  108.0 2.6 collective-permute-done.12.refs_5_
  110.9 3.3 slice.465
  115.8 9.8 %attention_out.1 = (f32[832,1024]{1,0:T(8,128)}, bf16[832,1024]{1,0:T(8,128)(2,1)}) custom-call(s32[9]{0:T(128)} %pad_add_fusion.1.order_ref, f32[832,1024]{1,0:T(8,128)} %bitcast.231, f32[1,1024]{1,0:T(1,128)} %get-tuple-element.583.bias_ref, f32[1,1024]{1,0:T(1,128)} %get-tuple-element.582.gain_ref, f32[1,1024]{1,0:T(1,128)} %get-tuple-element.581.shift_ref, ...), custom_call_target="tpu_custom_call" | custom-call | tf_op jit(solution)/shard_map/attention_out/pallas_call | solution.py:133
  125.6 19.2 %mlp.4 = (bf16[8,128,1024]{2,1,0:T(8,128)(2,1)}, bf16[8,128,1024]{2,1,0:T(8,128)(2,1)}, f32[1,1024]{1,0:T(1,128)}, f32[832,1024]{1,0:T(8,128)}, f32[832,1024]{1,0:T(8,128)}) custom-call(s32[9]{0:T(128)} %pad_add_fusion.1.order_ref, f32[1,1024]{1,0:T(1,128)} %get-tuple-element.588.bias_ref, bf16[832,1024]{1,0:T(8,128)(2,1)} %get-tuple-element.368.refs_0_.refs_1_, ...), custom_call_target="tpu_custom_call" | custom-call | tf_op jit(solution)/shard_map/mlp/pallas_call | solution.py:133
  144.8 20.4 %mlp.5 = (bf16[8,128,1024]{2,1,0:T(8,128)(2,1)}, bf16[8,128,1024]{2,1,0:T(8,128)(2,1)}, f32[1,1024]{1,0:T(1,128)}, f32[832,1024]{1,0:T(8,128)}, f32[832,1024]{1,0:T(8,128)}) custom-call(s32[9]{0:T(128)} %pad_add_fusion.1.order_ref, f32[1,1024]{1,0:T(1,128)} %get-tuple-element.589.bias_ref, bf16[832,1024]{1,0:T(8,128)(2,1)} %get-tuple-element.368.refs_0_.refs_1_, ...), custom_call_target="tpu_custom_call" | custom-call | tf_op jit(solution)/shard_map/mlp/pallas_call | solution.py:133
  165.9 3.9 collective-permute-done.16
  169.7 2.4 add_convert_fusion.7
  177.8 20.5 %mlp.6 = (bf16[8,128,1024]{2,1,0:T(8,128)(2,1)}, bf16[8,128,1024]{2,1,0:T(8,128)(2,1)}, f32[1,1024]{1,0:T(1,128)}, f32[832,1024]{1,0:T(8,128)}, f32[832,1024]{1,0:T(8,128)}) custom-call(s32[9]{0:T(128)} %pad_add_fusion.1.order_ref, f32[1,1024]{1,0:T(1,128)} %get-tuple-element.587.bias_ref, bf16[832,1024]{1,0:T(8,128)(2,1)} %get-tuple-element.368.refs_0_.refs_1_, ...), custom_call_target="tpu_custom_call" | custom-call | tf_op jit(solution)/shard_map/mlp/pallas_call | solution.py:133
  198.3 2.2 collective-permute-done.20
  201.3 3.2 fusion.6
  206.8 21.0 %mlp.7 = (bf16[8,128,1024]{2,1,0:T(8,128)(2,1)}, bf16[8,128,1024]{2,1,0:T(8,128)(2,1)}, f32[1,1024]{1,0:T(1,128)}, f32[832,1024]{1,0:T(8,128)}, bf16[832,1024]{1,0:T(8,128)(2,1)}) custom-call(s32[9]{0:T(128)} %pad_add_fusion.1.order_ref, f32[1,1024]{1,0:T(1,128)} %get-tuple-element.586.bias_ref, f32[1,1024]{1,0:T(1,128)} %get-tuple-element.580.refs_0_, ...), custom_call_target="tpu_custom_call" | custom-call | tf_op jit(solution)/shard_map/mlp/pallas_call | solution.py:133
  232.8 2.6 collective-permute-done.23
  240.0 2.1 collective-permute-start.26
  242.9 11.0 %attention_out_back.1 = (f32[832,1024]{1,0:T(8,128)}, bf16[832,256]{1,0:T(8,128)(2,1)}, bf16[832,256]{1,0:T(8,128)(2,1)}, bf16[832,256]{1,0:T(8,128)(2,1)}, bf16...) custom-call(s32[9]{0:T(128)} %pad_add_fusion.1.order_ref, ...), custom_call_target="tpu_custom_call" | custom-call | tf_op jit(solution)/shard_map/attention_out_back/pallas_call | solution.py:133
  253.9 18.1 %attention_back.2 = (bf16[8,128,1024]{2,1,0:T(8,128)(2,1)}, bf16[8,128,1024]{2,1,0:T(8,128)(2,1)}, bf16[832,768]{1,0:T(8,128)(2,1)}, bf16[832,768]{1,0:T(8,128)(2,1)}, f32[2,1,768]{2,1,0:T(1,128)}) custom-call(s32[9]{0:T(128)} %pad_add_fusion.1.order_ref, bf16[832,1024]{1,0:T(8,128)(2,1)} %add_convert_fusion.normed_ref, ...), custom_call_target="tpu_custom_call" | custom-call | tf_op jit(solution)/shard_map/attention_back/pallas_call | solution.py:133
  274.8 2.4 fusion.4
  277.3 2.3 fusion.5
  279.6 2.4 add_convert_fusion.2
  283.5 2.1 collective-permute-start.30
  285.6 18.0 %attention_back.3 = (bf16[8,128,1024]{2,1,0:T(8,128)(2,1)}, bf16[8,128,1024]{2,1,0:T(8,128)(2,1)}, bf16[832,768]{1,0:T(8,128)(2,1)}, bf16[832,768]{1,0:T(8,128)(2,1)}, f32[2,1,768]{2,1,0:T(1,128)}) custom-call(s32[9]{0:T(128)} %pad_add_fusion.1.order_ref, bf16[832,1024]{1,0:T(8,128)(2,1)} %add_convert_fusion.normed_ref, ...), custom_call_target="tpu_custom_call" | custom-call | tf_op jit(solution)/shard_map/attention_back/pallas_call | solution.py:133
  303.7 3.9 collective-permute-done.32
  308.9 1.9 fusion.20
  317.9 1.8 collective-permute-start.35
  322.2 16.0 %input_back.1 = (f32[832,1024]{1,0:T(8,128)}, f32[2,1,1024]{2,1,0:T(1,128)}) custom-call(s32[9]{0:T(128)} %pad_add_fusion.1.order_ref, f32[832,1024]{1,0:T(8,128)} %bitcast.232, f32[832,1024]{1,0:T(8,128)} %get-tuple-element.493.after_ref, f32[1,1024]{1,0:T(1,128)} %get-tuple-element.579.gain_ref, bf16[832,768]{1,0:T(8,128)(2,1)} %get-tuple-element.494.refs_0_, ...), custom_call_target="tpu_custom_call" | custom-call | tf_op jit(solution)/shard_map/input_back/pallas_call | solution.py:133
  339.6 4.2 %collective-permute-done.34 = bf16[128,1024]{1,0:T(8,128)(2,1)} collective-permute-done((bf16[128,1024]{1,0:T(8,128)(2,1)S(1)}, bf16[128,1024]{1,0:T(8,128)(2,1)}, u32[]{:S(2)}, u32[]{:S(2)}) %collective-permute-start.34) | collective-permute-done | bytes 262176 | tf_op jit(solution)/shard_map/ppermute | solution.py:19
  343.8 1.8 fusion.25
  354.6 8.4 %collective-permute-done.38 = bf16[2,128,1024]{2,1,0:T(8,128)(2,1)S(1)} collective-permute-done((bf16[2,128,1024]{2,1,0:T(8,128)(2,1)S(1)}, bf16[2,128,1024]{2,1,0:T(8,128)(2,1)S(1)}, u32[]{:S(2)}, u32[]{:S(2)}) %collective-permute-start.38) | collective-permute-done | bytes 524320 | tf_op jit(solution)/shard_map/ppermute | solution.py:19
  363.0 2.2 fusion.10
  365.2 2.9 collective-permute-start.41
  370.9 1.9 reshape.427
  375.7 3.8 collective-permute-done.41
  381.8 1.9 add_convert_fusion.9
  384.4 4.6 %collective-permute-done.43 = f32[16,128]{1,0:T(8,128)S(1)} collective-permute-done((f32[16,128]{1,0:T(8,128)S(1)}, f32[16,128]{1,0:T(8,128)S(1)}, u32[]{:S(2)}, u32[]{:S(2)}) %collective-permute-start.43) | collective-permute-done | bytes 8224 | tf_op jit(solution)/shard_map/ppermute | solution.py:19
  389.8 2.0 collective-permute-start.48
  391.9 3.9 finish_mlp.1
  398.2 2.6 finish_attention.1
  (246 shorter events, 86.8 us)
Async XLA Ops:
  7.2 99.6 %all-gather.5.cloned.1.call-start = ((), (), s32[]{:S(2)}) async-start(), calls=%async_computation | async-start | bytes 4718592 | tf_op jit(solution)/shard_map/all_gather | solution.py:964
  9.8 14.5 %collective-permute-start = (bf16[1,144,768]{2,1,0:T(8,128)(2,1)}, bf16[1,144,768]{2,1,0:T(8,128)(2,1)S(1)}, u32[]{:S(2)}, u32[]{:S(2)}) collective-permute-start(bf16[1,144,768]{2,1,0:T(8,128)(2,1)} %bitcast.265), channel_id=1, source_target_pairs={{0,4},{1,5},{2,6},{3,7},{4,0},{5,1},{6,2},{7,3},{8,12},{9,13},{10,... | collective-permute-start | bytes 663560 | tf_op jit(solution)/shard_map/ppermute | solution.py:19
  24.3 141.0 %all-gather.7.cloned.1.call-start = ((), (), s32[]{:S(2)}) async-start(), calls=%async_computation.1 | async-start | bytes 2359296 | tf_op jit(solution)/shard_map/all_gather | solution.py:965
  24.5 11.4 %collective-permute-start.1 = (bf16[2,144,768]{2,1,0:T(8,128)(2,1)S(1)}, bf16[2,144,768]{2,1,0:T(8,128)(2,1)S(1)}, u32[]{:S(2)}, u32[]{:S(2)}) collective-permute-start(bf16[2,144,768]{2,1,0:T(8,128)(2,1)S(1)} %pad_maximum_fusion.5), channel_id=1, source_target_pairs={{0,2},{1,3},{2,0},{3,1},{4,6},{5,7},{6,4},{7,5},{8,10},{9,11},{10,... | collective-permute-start | bytes 1327112 | tf_op jit(solution)/shard_map/ppermute | solution.py:19
  36.8 24.4 %collective-permute-start.2 = (bf16[4,144,768]{2,1,0:T(8,128)(2,1)}, bf16[4,144,768]{2,1,0:T(8,128)(2,1)}, u32[]{:S(2)}, u32[]{:S(2)}) collective-permute-start(bf16[4,144,768]{2,1,0:T(8,128)(2,1)} %constant_dynamic-update-slice_fusion.refs_0_.refs_4_), channel_id=1, source_target_pairs={{0,1},{1,0},{2,3},{3,2},{4,5},{5,4},{6,7},{7,6},{8,9},{9,8},{10,11... | collective-permute-start | bytes 2654216 | tf_op jit(solution)/shard_map/ppermute | solution.py:19
  38.1 23.0 %collective-permute-start.3 = (bf16[4,144,768]{2,1,0:T(8,128)(2,1)}, bf16[4,144,768]{2,1,0:T(8,128)(2,1)}, u32[]{:S(2)}, u32[]{:S(2)}) collective-permute-start(bf16[4,144,768]{2,1,0:T(8,128)(2,1)} %constant_dynamic-update-slice_fusion.refs_0_.refs_4_), channel_id=1, source_target_pairs={{0,8},{8,0},{16,24},{24,16},{1,9},{9,1},{17,25},{25,17},{2,10},{10... | collective-permute-start | bytes 2654216 | tf_op jit(solution)/shard_map/ppermute | solution.py:19
  39.7 42.3 %collective-permute-start.6 = (bf16[4,144,768]{2,1,0:T(8,128)(2,1)}, bf16[4,144,768]{2,1,0:T(8,128)(2,1)}, u32[]{:S(2)}, u32[]{:S(2)}) collective-permute-start(bf16[4,144,768]{2,1,0:T(8,128)(2,1)} %constant_dynamic-update-slice_fusion.refs_0_.refs_4_), channel_id=1, source_target_pairs={{0,16},{8,24},{16,0},{24,8},{1,17},{9,25},{17,1},{25,9},{2,18},{10... | collective-permute-start | bytes 2654216 | tf_op jit(solution)/shard_map/ppermute | solution.py:19
  41.3 19.0 %collective-permute-start.4 = (bf16[1,128,512]{2,1,0:T(8,128)(2,1)S(1)}, bf16[1,128,512]{2,1,0:T(8,128)(2,1)S(1)}, u32[]{:S(2)}, u32[]{:S(2)}) collective-permute-start(bf16[1,128,512]{2,1,0:T(8,128)(2,1)S(1)} %pad_maximum_fusion.7), channel_id=1, source_target_pairs={{0,4},{1,5},{2,6},{3,7},{4,0},{5,1},{6,2},{7,3},{8,12},{9,13},{10,... | collective-permute-start | bytes 393224 | tf_op jit(solution)/shard_map/ppermute | solution.py:19
  61.1 10.4 %collective-permute-start.5 = (bf16[4,144,768]{2,1,0:T(8,128)(2,1)}, bf16[4,144,768]{2,1,0:T(8,128)(2,1)}, u32[]{:S(2)}, u32[]{:S(2)}) collective-permute-start(bf16[4,144,768]{2,1,0:T(8,128)(2,1)} %collective-permute-done.2.refs_1_.refs_5_), channel_id=1, source_target_pairs={{0,8},{8,0},{16,24},{24,16},{1,9},{9,1},{17,25},{25,17},{2,10},{10... | collective-permute-start | bytes 2654216 | tf_op jit(solution)/shard_map/ppermute | solution.py:19
  61.1 29.8 %collective-permute-start.7 = (bf16[4,144,768]{2,1,0:T(8,128)(2,1)}, bf16[4,144,768]{2,1,0:T(8,128)(2,1)}, u32[]{:S(2)}, u32[]{:S(2)}) collective-permute-start(bf16[4,144,768]{2,1,0:T(8,128)(2,1)} %collective-permute-done.2.refs_1_.refs_5_), channel_id=1, source_target_pairs={{0,16},{8,24},{16,0},{24,8},{1,17},{9,25},{17,1},{25,9},{2,18},{10... | collective-permute-start | bytes 2654216 | tf_op jit(solution)/shard_map/ppermute | solution.py:19
  66.1 24.8 %collective-permute-start.8 = (bf16[2,128,512]{2,1,0:T(8,128)(2,1)S(1)}, bf16[2,128,512]{2,1,0:T(8,128)(2,1)S(1)}, u32[]{:S(2)}, u32[]{:S(2)}) collective-permute-start(bf16[2,128,512]{2,1,0:T(8,128)(2,1)S(1)} %pad_maximum_fusion.6), channel_id=1, source_target_pairs={{0,2},{1,3},{2,0},{3,1},{4,6},{5,7},{6,4},{7,5},{8,10},{9,11},{10,... | collective-permute-start | bytes 786440 | tf_op jit(solution)/shard_map/ppermute | solution.py:19
  90.9 4.5 %collective-permute-start.10 = (bf16[4,144,768]{2,1,0:T(8,128)(2,1)}, bf16[4,144,768]{2,1,0:T(8,128)(2,1)S(1)}, u32[]{:S(2)}, u32[]{:S(2)}) collective-permute-start(bf16[4,144,768]{2,1,0:T(8,128)(2,1)} %collective-permute-done.7.refs_1_.refs_9_), channel_id=1, source_target_pairs={{0,8},{8,0},{16,24},{24,16},{1,9},{9,1},{17,25},{25,17},{2,10},{10... | collective-permute-start | bytes 2654216 | tf_op jit(solution)/shard_map/ppermute | solution.py:19
  90.9 4.5 %collective-permute-start.9 = (bf16[4,144,768]{2,1,0:T(8,128)(2,1)}, bf16[4,144,768]{2,1,0:T(8,128)(2,1)}, u32[]{:S(2)}, u32[]{:S(2)}) collective-permute-start(bf16[4,144,768]{2,1,0:T(8,128)(2,1)} %collective-permute-done.6.refs_0_.refs_8_), channel_id=1, source_target_pairs={{0,8},{8,0},{16,24},{24,16},{1,9},{9,1},{17,25},{25,17},{2,10},{10... | collective-permute-start | bytes 2654216 | tf_op jit(solution)/shard_map/ppermute | solution.py:19
  91.4 15.3 %collective-permute-start.11 = (bf16[4,128,512]{2,1,0:T(8,128)(2,1)S(1)}, bf16[4,128,512]{2,1,0:T(8,128)(2,1)}, u32[]{:S(2)}, u32[]{:S(2)}) collective-permute-start(bf16[4,128,512]{2,1,0:T(8,128)(2,1)S(1)} %pad_maximum_fusion.4), channel_id=1, source_target_pairs={{0,1},{1,0},{2,3},{3,2},{4,5},{5,4},{6,7},{7,6},{8,9},{9,8},{10,11... | collective-permute-start | bytes 1572872 | tf_op jit(solution)/shard_map/ppermute | solution.py:19
  110.7 14.9 %collective-permute-start.13 = (bf16[8,128,2048]{2,1,0:T(8,128)(2,1)}, bf16[8,128,2048]{2,1,0:T(8,128)(2,1)}, u32[]{:S(2)}, u32[]{:S(2)}) collective-permute-start(bf16[8,128,2048]{2,1,0:T(8,128)(2,1)} %bitcast.238), channel_id=1, source_target_pairs={{0,8},{8,0},{16,24},{24,16},{1,9},{9,1},{17,25},{25,17},{2,10},{10... | collective-permute-start | bytes 12582920 | tf_op jit(solution)/shard_map/ppermute | solution.py:19
  114.2 51.1 %collective-permute-start.14 = (bf16[8,128,1024]{2,1,0:T(8,128)(2,1)}, bf16[8,128,1024]{2,1,0:T(8,128)(2,1)}, u32[]{:S(2)}, u32[]{:S(2)}) collective-permute-start(bf16[8,128,1024]{2,1,0:T(8,128)(2,1)} %slice.465), channel_id=1, source_target_pairs={{0,16},{8,24},{16,0},{24,8},{1,17},{9,25},{17,1},{25,9},{2,18},{10... | collective-permute-start | bytes 6291464 | tf_op jit(solution)/shard_map/ppermute | solution.py:19
  165.3 4.4 %collective-permute-start.16 = (bf16[8,128,1024]{2,1,0:T(8,128)(2,1)}, bf16[8,128,1024]{2,1,0:T(8,128)(2,1)S(1)}, u32[]{:S(2)}, u32[]{:S(2)}) collective-permute-start(bf16[8,128,1024]{2,1,0:T(8,128)(2,1)} %get-tuple-element.386), channel_id=1, source_target_pairs={{0,8},{8,0},{16,24},{24,16},{1,9},{9,1},{17,25},{25,17},{2,10},{10... | collective-permute-start | bytes 6291464 | tf_op jit(solution)/shard_map/ppermute | solution.py:19
  165.4 7.4 %collective-permute-start.15 = (bf16[8,128,1024]{2,1,0:T(8,128)(2,1)}, bf16[8,128,1024]{2,1,0:T(8,128)(2,1)S(1)}, u32[]{:S(2)}, u32[]{:S(2)}) collective-permute-start(bf16[8,128,1024]{2,1,0:T(8,128)(2,1)} %get-tuple-element.384), channel_id=1, source_target_pairs={{0,8},{8,0},{16,24},{24,16},{1,9},{9,1},{17,25},{25,17},{2,10},{10... | collective-permute-start | bytes 6291464 | tf_op jit(solution)/shard_map/ppermute | solution.py:19
  174.5 26.9 %collective-permute-start.17 = (bf16[8,128,1024]{2,1,0:T(8,128)(2,1)}, bf16[8,128,1024]{2,1,0:T(8,128)(2,1)S(1)}, u32[]{:S(2)}, u32[]{:S(2)}) collective-permute-start(bf16[8,128,1024]{2,1,0:T(8,128)(2,1)} %collective-permute-done.14.refs_2_), channel_id=1, source_target_pairs={{0,8},{8,0},{16,24},{24,16},{1,9},{9,1},{17,25},{25,17},{2,10},{10... | collective-permute-start | bytes 6291464 | tf_op jit(solution)/shard_map/ppermute | solution.py:19
  174.6 26.7 %collective-permute-start.18 = (bf16[8,128,1024]{2,1,0:T(8,128)(2,1)S(1)}, bf16[8,128,1024]{2,1,0:T(8,128)(2,1)}, u32[]{:S(2)}, u32[]{:S(2)}) collective-permute-start(bf16[8,128,1024]{2,1,0:T(8,128)(2,1)S(1)} %bitcast.245), channel_id=1, source_target_pairs={{0,8},{8,0},{16,24},{24,16},{1,9},{9,1},{17,25},{25,17},{2,10},{10... | collective-permute-start | bytes 6291464 | tf_op jit(solution)/shard_map/ppermute | solution.py:19
  175.0 25.5 %collective-permute-start.20 = (bf16[2,2,128,1024]{3,2,1,0:T(8,128)(2,1)}, bf16[2,2,128,1024]{3,2,1,0:T(8,128)(2,1)}, u32[]{:S(2)}, u32[]{:S(2)}) collective-permute-start(bf16[2,2,128,1024]{3,2,1,0:T(8,128)(2,1)} %fusion), channel_id=1, source_target_pairs={{0,2},{1,3},{2,0},{3,1},{4,6},{5,7},{6,4},{7,5},{8,10},{9,11},{10,... | collective-permute-start | bytes 3145736 | tf_op jit(solution)/shard_map/ppermute | solution.py:19
  176.3 25.0 %collective-permute-start.19 = (bf16[2,2,128,1024]{3,2,1,0:T(8,128)(2,1)S(1)}, bf16[2,2,128,1024]{3,2,1,0:T(8,128)(2,1)}, u32[]{:S(2)}, u32[]{:S(2)}) collective-permute-start(bf16[2,2,128,1024]{3,2,1,0:T(8,128)(2,1)S(1)} %bitcast.264), channel_id=1, source_target_pairs={{0,1},{1,0},{2,3},{3,2},{4,5},{5,4},{6,7},{7,6},{8,9},{9,8},{10,11... | collective-permute-start | bytes 3145736 | tf_op jit(solution)/shard_map/ppermute | solution.py:19
  204.6 23.3 %collective-permute-start.22 = (bf16[2,128,1024]{2,1,0:T(8,128)(2,1)S(1)}, bf16[2,128,1024]{2,1,0:T(8,128)(2,1)S(1)}, u32[]{:S(2)}, u32[]{:S(2)}) collective-permute-start(bf16[2,128,1024]{2,1,0:T(8,128)(2,1)S(1)} %get-tuple-element.422), channel_id=1, source_target_pairs={{0,1},{1,0},{2,3},{3,2},{4,5},{5,4},{6,7},{7,6},{8,9},{9,8},{10,11... | collective-permute-start | bytes 1572872 | tf_op jit(solution)/shard_map/ppermute | solution.py:19
  206.1 21.8 %collective-permute-start.21 = (bf16[2,128,1024]{2,1,0:T(8,128)(2,1)S(1)}, bf16[2,128,1024]{2,1,0:T(8,128)(2,1)S(1)}, u32[]{:S(2)}, u32[]{:S(2)}) collective-permute-start(bf16[2,128,1024]{2,1,0:T(8,128)(2,1)S(1)} %get-tuple-element.421), channel_id=1, source_target_pairs={{0,2},{1,3},{2,0},{3,1},{4,6},{5,7},{6,4},{7,5},{8,10},{9,11},{10,... | collective-permute-start | bytes 1572872 | tf_op jit(solution)/shard_map/ppermute | solution.py:19
  228.0 7.4 %collective-permute-start.23 = (bf16[8,128,1024]{2,1,0:T(8,128)(2,1)}, bf16[8,128,1024]{2,1,0:T(8,128)(2,1)S(1)}, u32[]{:S(2)}, u32[]{:S(2)}) collective-permute-start(bf16[8,128,1024]{2,1,0:T(8,128)(2,1)} %get-tuple-element.425), channel_id=1, source_target_pairs={{0,8},{8,0},{16,24},{24,16},{1,9},{9,1},{17,25},{25,17},{2,10},{10... | collective-permute-start | bytes 6291464 | tf_op jit(solution)/shard_map/ppermute | solution.py:19
  238.1 36.8 %collective-permute-start.28 = (bf16[2,2,128,1024]{3,2,1,0:T(8,128)(2,1)}, bf16[2,2,128,1024]{3,2,1,0:T(8,128)(2,1)}, u32[]{:S(2)}, u32[]{:S(2)}) collective-permute-start(bf16[2,2,128,1024]{3,2,1,0:T(8,128)(2,1)} %fusion.1), channel_id=1, source_target_pairs={{0,2},{1,3},{2,0},{3,1},{4,6},{5,7},{6,4},{7,5},{8,10},{9,11},{10,... | collective-permute-start | bytes 3145736 | tf_op jit(solution)/shard_map/ppermute | solution.py:19
  239.4 35.4 %collective-permute-start.27 = (bf16[2,2,128,1024]{3,2,1,0:T(8,128)(2,1)S(1)}, bf16[2,2,128,1024]{3,2,1,0:T(8,128)(2,1)}, u32[]{:S(2)}, u32[]{:S(2)}) collective-permute-start(bf16[2,2,128,1024]{3,2,1,0:T(8,128)(2,1)S(1)} %bitcast.263), channel_id=1, source_target_pairs={{0,1},{1,0},{2,3},{3,2},{4,5},{5,4},{6,7},{7,6},{8,9},{9,8},{10,11... | collective-permute-start | bytes 3145736 | tf_op jit(solution)/shard_map/ppermute | solution.py:19
  240.0 32.0 %collective-permute-start.26 = (bf16[128,1024]{1,0:T(8,128)(2,1)S(1)}, bf16[128,1024]{1,0:T(8,128)(2,1)S(1)}, u32[]{:S(2)}, u32[]{:S(2)}) collective-permute-start(bf16[128,1024]{1,0:T(8,128)(2,1)S(1)} %fusion.22), channel_id=1, source_target_pairs={{0,4},{1,5},{2,6},{3,7},{4,0},{5,1},{6,2},{7,3},{8,12},{9,13},{10,... | collective-permute-start | bytes 786440 | tf_op jit(solution)/shard_map/ppermute | solution.py:19
  242.1 31.4 %collective-permute-start.25 = (bf16[128,1024]{1,0:T(8,128)(2,1)S(1)}, bf16[128,1024]{1,0:T(8,128)(2,1)}, u32[]{:S(2)}, u32[]{:S(2)}) collective-permute-start(bf16[128,1024]{1,0:T(8,128)(2,1)S(1)} %fusion.21), channel_id=1, source_target_pairs={{0,4},{1,5},{2,6},{3,7},{4,0},{5,1},{6,2},{7,3},{8,12},{9,13},{10,... | collective-permute-start | bytes 786440 | tf_op jit(solution)/shard_map/ppermute | solution.py:19
  274.8 4.7 %collective-permute-start.29 = (bf16[8,128,1024]{2,1,0:T(8,128)(2,1)}, bf16[8,128,1024]{2,1,0:T(8,128)(2,1)S(1)}, u32[]{:S(2)}, u32[]{:S(2)}) collective-permute-start(bf16[8,128,1024]{2,1,0:T(8,128)(2,1)} %get-tuple-element.459), channel_id=1, source_target_pairs={{0,8},{8,0},{16,24},{24,16},{1,9},{9,1},{17,25},{25,17},{2,10},{10... | collective-permute-start | bytes 6291464 | tf_op jit(solution)/shard_map/ppermute | solution.py:19
  281.9 25.6 %collective-permute-start.32 = (bf16[4,128,1024]{2,1,0:T(8,128)(2,1)}, bf16[4,128,1024]{2,1,0:T(8,128)(2,1)S(1)}, u32[]{:S(2)}, u32[]{:S(2)}) collective-permute-start(bf16[4,128,1024]{2,1,0:T(8,128)(2,1)} %get-tuple-element.479), channel_id=1, source_target_pairs={{0,16},{8,24},{16,0},{24,8},{1,17},{9,25},{17,1},{25,9},{2,18},{10... | collective-permute-start | bytes 3145736 | tf_op jit(solution)/shard_map/ppermute | solution.py:19
  282.6 21.0 %collective-permute-start.31 = (bf16[2,128,1024]{2,1,0:T(8,128)(2,1)}, bf16[2,128,1024]{2,1,0:T(8,128)(2,1)S(1)}, u32[]{:S(2)}, u32[]{:S(2)}) collective-permute-start(bf16[2,128,1024]{2,1,0:T(8,128)(2,1)} %fusion.5), channel_id=1, source_target_pairs={{0,1},{1,0},{2,3},{3,2},{4,5},{5,4},{6,7},{7,6},{8,9},{9,8},{10,11... | collective-permute-start | bytes 1572872 | tf_op jit(solution)/shard_map/ppermute | solution.py:19
  283.5 20.1 %collective-permute-start.30 = (bf16[2,128,1024]{2,1,0:T(8,128)(2,1)}, bf16[2,128,1024]{2,1,0:T(8,128)(2,1)}, u32[]{:S(2)}, u32[]{:S(2)}) collective-permute-start(bf16[2,128,1024]{2,1,0:T(8,128)(2,1)} %fusion.4), channel_id=1, source_target_pairs={{0,2},{1,3},{2,0},{3,1},{4,6},{5,7},{6,4},{7,5},{8,10},{9,11},{10,... | collective-permute-start | bytes 1572872 | tf_op jit(solution)/shard_map/ppermute | solution.py:19
  313.6 30.2 %collective-permute-start.37 = (bf16[4,128,1024]{2,1,0:T(8,128)(2,1)}, bf16[4,128,1024]{2,1,0:T(8,128)(2,1)S(1)}, u32[]{:S(2)}, u32[]{:S(2)}) collective-permute-start(bf16[4,128,1024]{2,1,0:T(8,128)(2,1)} %get-tuple-element.503), channel_id=1, source_target_pairs={{0,16},{8,24},{16,0},{24,8},{1,17},{9,25},{17,1},{25,9},{2,18},{10... | collective-permute-start | bytes 3145736 | tf_op jit(solution)/shard_map/ppermute | solution.py:19
  314.3 29.5 %collective-permute-start.36 = (bf16[2,2,128,1024]{3,2,1,0:T(8,128)(2,1)}, bf16[2,2,128,1024]{3,2,1,0:T(8,128)(2,1)}, u32[]{:S(2)}, u32[]{:S(2)}) collective-permute-start(bf16[2,2,128,1024]{3,2,1,0:T(8,128)(2,1)} %bitcast.56), channel_id=1, source_target_pairs={{0,1},{1,0},{2,3},{3,2},{4,5},{5,4},{6,7},{7,6},{8,9},{9,8},{10,11... | collective-permute-start | bytes 3145736 | tf_op jit(solution)/shard_map/ppermute | solution.py:19
  317.9 21.8 %collective-permute-start.35 = (bf16[128,1024]{1,0:T(8,128)(2,1)}, bf16[128,1024]{1,0:T(8,128)(2,1)}, u32[]{:S(2)}, u32[]{:S(2)}) collective-permute-start(bf16[128,1024]{1,0:T(8,128)(2,1)} %fusion.20), channel_id=1, source_target_pairs={{0,4},{1,5},{2,6},{3,7},{4,0},{5,1},{6,2},{7,3},{8,12},{9,13},{10,... | collective-permute-start | bytes 786440 | tf_op jit(solution)/shard_map/ppermute | solution.py:19
  319.7 24.1 %collective-permute-start.34 = (bf16[128,1024]{1,0:T(8,128)(2,1)S(1)}, bf16[128,1024]{1,0:T(8,128)(2,1)}, u32[]{:S(2)}, u32[]{:S(2)}) collective-permute-start(bf16[128,1024]{1,0:T(8,128)(2,1)S(1)} %fusion.19), channel_id=1, source_target_pairs={{0,4},{1,5},{2,6},{3,7},{4,0},{5,1},{6,2},{7,3},{8,12},{9,13},{10,... | collective-permute-start | bytes 786440 | tf_op jit(solution)/shard_map/ppermute | solution.py:19
  349.7 4.9 %collective-permute-start.39 = (f32[2,2,16,128]{3,2,1,0:T(8,128)S(1)}, f32[2,2,16,128]{3,2,1,0:T(8,128)S(1)}, u32[]{:S(2)}, u32[]{:S(2)}) collective-permute-start(f32[2,2,16,128]{3,2,1,0:T(8,128)S(1)} %bitcast.267), channel_id=1, source_target_pairs={{0,1},{1,0},{2,3},{3,2},{4,5},{5,4},{6,7},{7,6},{8,9},{9,8},{10,11... | collective-permute-start | bytes 98312 | tf_op jit(solution)/shard_map/ppermute | solution.py:19
  350.8 12.2 %collective-permute-start.38 = (bf16[2,128,1024]{2,1,0:T(8,128)(2,1)S(1)}, bf16[2,128,1024]{2,1,0:T(8,128)(2,1)S(1)}, u32[]{:S(2)}, u32[]{:S(2)}) collective-permute-start(bf16[2,128,1024]{2,1,0:T(8,128)(2,1)S(1)} %fusion.3), channel_id=1, source_target_pairs={{0,2},{1,3},{2,0},{3,1},{4,6},{5,7},{6,4},{7,5},{8,10},{9,11},{10,... | collective-permute-start | bytes 1572872 | tf_op jit(solution)/shard_map/ppermute | solution.py:19
  353.2 28.5 %collective-permute-start.42 = (bf16[2,2,128,1024]{3,2,1,0:T(8,128)(2,1)}, bf16[2,2,128,1024]{3,2,1,0:T(8,128)(2,1)}, u32[]{:S(2)}, u32[]{:S(2)}) collective-permute-start(bf16[2,2,128,1024]{3,2,1,0:T(8,128)(2,1)} %pad_maximum_fusion.2), channel_id=1, source_target_pairs={{0,16},{8,24},{16,0},{24,8},{1,17},{9,25},{17,1},{25,9},{2,18},{10... | collective-permute-start | bytes 3145736 | tf_op jit(solution)/shard_map/ppermute | solution.py:19
  365.2 14.3 %collective-permute-start.41 = (bf16[128,1024]{1,0:T(8,128)(2,1)}, bf16[128,1024]{1,0:T(8,128)(2,1)S(1)}, u32[]{:S(2)}, u32[]{:S(2)}) collective-permute-start(bf16[128,1024]{1,0:T(8,128)(2,1)} %fusion.10), channel_id=1, source_target_pairs={{0,4},{1,5},{2,6},{3,7},{4,0},{5,1},{6,2},{7,3},{8,12},{9,13},{10,... | collective-permute-start | bytes 786440 | tf_op jit(solution)/shard_map/ppermute | solution.py:19
  368.8 6.9 %collective-permute-start.40 = (f32[2,16,128]{2,1,0:T(8,128)S(1)}, f32[2,16,128]{2,1,0:T(8,128)}, u32[]{:S(2)}, u32[]{:S(2)}) collective-permute-start(f32[2,16,128]{2,1,0:T(8,128)S(1)} %slice_add_fusion), channel_id=1, source_target_pairs={{0,2},{1,3},{2,0},{3,1},{4,6},{5,7},{6,4},{7,5},{8,10},{9,11},{10,... | collective-permute-start | bytes 49160 | tf_op jit(solution)/shard_map/ppermute | solution.py:19
  383.8 5.2 %collective-permute-start.44 = (bf16[2,2,128,1024]{3,2,1,0:T(8,128)(2,1)S(1)}, bf16[2,2,128,1024]{3,2,1,0:T(8,128)(2,1)S(1)}, u32[]{:S(2)}, u32[]{:S(2)}) collective-permute-start(bf16[2,2,128,1024]{3,2,1,0:T(8,128)(2,1)S(1)} %pad_maximum_fusion.3.refs_0_), channel_id=1, source_target_pairs={{0,8},{8,0},{16,24},{24,16},{1,9},{9,1},{17,25},{25,17},{2,10},{10... | collective-permute-start | bytes 3145736 | tf_op jit(solution)/shard_map/ppermute | solution.py:19
  383.9 11.9 %collective-permute-start.45 = (bf16[128,1024]{1,0:T(8,128)(2,1)S(1)}, bf16[128,1024]{1,0:T(8,128)(2,1)S(1)}, u32[]{:S(2)}, u32[]{:S(2)}) collective-permute-start(bf16[128,1024]{1,0:T(8,128)(2,1)S(1)} %fusion.9.refs_0_), channel_id=1, source_target_pairs={{0,8},{8,0},{16,24},{24,16},{1,9},{9,1},{17,25},{25,17},{2,10},{10... | collective-permute-start | bytes 786440 | tf_op jit(solution)/shard_map/ppermute | solution.py:19
  384.4 11.4 %collective-permute-start.46 = (bf16[128,1024]{1,0:T(8,128)(2,1)S(1)}, bf16[128,1024]{1,0:T(8,128)(2,1)S(1)}, u32[]{:S(2)}, u32[]{:S(2)}) collective-permute-start(bf16[128,1024]{1,0:T(8,128)(2,1)S(1)} %fusion.9.refs_0_), channel_id=1, source_target_pairs={{0,16},{8,24},{16,0},{24,8},{1,17},{9,25},{17,1},{25,9},{2,18},{10... | collective-permute-start | bytes 786440 | tf_op jit(solution)/shard_map/ppermute | solution.py:19
  384.4 4.6 %collective-permute-start.43 = (f32[16,128]{1,0:T(8,128)S(1)}, f32[16,128]{1,0:T(8,128)S(1)}, u32[]{:S(2)}, u32[]{:S(2)}) collective-permute-start(f32[16,128]{1,0:T(8,128)S(1)} %fusion.33), channel_id=1, source_target_pairs={{0,4},{1,5},{2,6},{3,7},{4,0},{5,1},{6,2},{7,3},{8,12},{9,13},{10,... | collective-permute-start | bytes 24584 | tf_op jit(solution)/shard_map/ppermute | solution.py:19
  389.8 6.1 %collective-permute-start.47 = (f32[16,128]{1,0:T(8,128)S(1)}, f32[16,128]{1,0:T(8,128)S(1)}, u32[]{:S(2)}, u32[]{:S(2)}) collective-permute-start(f32[16,128]{1,0:T(8,128)S(1)} %fusion.31), channel_id=1, source_target_pairs={{0,8},{8,0},{16,24},{24,16},{1,9},{9,1},{17,25},{25,17},{2,10},{10... | collective-permute-start | bytes 24584 | tf_op jit(solution)/shard_map/ppermute | solution.py:19
  389.8 6.1 %collective-permute-start.48 = (f32[16,128]{1,0:T(8,128)S(1)}, f32[16,128]{1,0:T(8,128)S(1)}, u32[]{:S(2)}, u32[]{:S(2)}) collective-permute-start(f32[16,128]{1,0:T(8,128)S(1)} %fusion.31), channel_id=1, source_target_pairs={{0,16},{8,24},{16,0},{24,8},{1,17},{9,25},{17,1},{25,9},{2,18},{10... | collective-permute-start | bytes 24584 | tf_op jit(solution)/shard_map/ppermute | solution.py:19
  (53 other events, 303.2 us)
Sparse Core Ops, SparseCore 0:
  24.4 81.8 all-gather.4
  111.0 48.8 all-gather.6
